TPU v7x, 256 devices: a whole 4x4x8 slice. The times are simulated.
256 devices in a mesh: expert: 64 (over x, z, core), tensor: 4 (over y).
Axes of the slice: x: 4, y: 4, z: 8, core: 2. Of those that a mesh axis runs over, the one named last changes fastest.
Arguments:
- tokens: bfloat16 [8192, 3584], P('expert', 'tensor'), may hold values from -6 to 6
- expert_ids: int32 [8192, 4], P('expert'), may hold values from 0 to 63, all different within a row; in each aligned block of 128 rows (0 to 127, 128 to 255, ...) at most 12 rows name the same one
- gate_values: bfloat16 [8192, 4], P('expert'), may hold values from 0.049804688 to 0.3984375
- w_gate: bfloat16 [64, 3584, 1024], P('expert', None, 'tensor'), may hold values from -0.09375 to 0.09375
- w_up: bfloat16 [64, 3584, 1024], P('expert', None, 'tensor'), may hold values from -0.09375 to 0.09375
- w_down: bfloat16 [64, 1024, 3584], P('expert', 'tensor'), may hold values from -0.1875 to 0.1875
- shared_gate: bfloat16 [3584, 1024], P(None, 'tensor'), may hold values from -0.09375 to 0.09375
- shared_up: bfloat16 [3584, 1024], P(None, 'tensor'), may hold values from -0.09375 to 0.09375
- shared_down: bfloat16 [1024, 3584], P('tensor'), may hold values from -0.1875 to 0.1875
Outputs:
- moe_output: bfloat16 [8192, 3584], P('expert', 'tensor')
Inputs may be any that keep to these rules, and one draw needn't show every extreme that they name: `expert_ids`: each token names 4 different experts. Among the 128 tokens of one index of the expert axis (aligned blocks of 128 rows) no expert is named by more than 12 tokens, a bound that some block reaches.
All inputs are finite; a program needn't handle non-finite values.
Results may differ from a plain program's by a relative error of at most 0.013.
Values may be sent and summed in bfloat16 or wider, within the bound.
No kernel may reach another device: no remote copies, remote signals or barrier semaphores. Data moves between devices by JAX's collectives and lax.ppermute only.
A program may use at most 64 MiB of HBM per device.

v0:
```python
import jax
import jax.numpy as jnp
from jax import lax
from jax.sharding import Mesh
from jax.sharding import PartitionSpec as P

EXPERT = ("expert_0", "expert_1", "expert_2")


def in_order(tiles, dim):
    shape = list(tiles.shape[1:])
    shape[dim] *= tiles.shape[0]
    return jnp.moveaxis(tiles, 0, dim).reshape(shape)


def from_everyone(x, axis):
    copies = jnp.broadcast_to(x, (lax.axis_size(axis), *x.shape))
    return lax.all_to_all(copies, axis, split_axis=0, concat_axis=0, tiled=True)


def collect(x, axis, dim):
    return in_order(from_everyone(x, axis), dim)


def in_blocks(x, dim, devices):
    before, after = (x.shape[:dim], x.shape[dim + 1 :])
    return jnp.moveaxis(x.reshape(*before, devices, -1, *after), dim, 0)


def sent_and_summed(x, axis, dim):
    tiles = in_blocks(x, dim, lax.axis_size(axis))
    arrived = lax.all_to_all(tiles, axis, split_axis=0, concat_axis=0, tiled=True)
    return arrived.astype(jnp.float32).sum(axis=0)


def turned_blocks(tiles, axes, sequence):
    shape = [lax.axis_size(a) for a in axes]
    tiles = tiles.reshape(*shape, *tiles.shape[1:])
    for k in sequence:
        tiles = lax.all_to_all(tiles, axes[k], split_axis=k, concat_axis=k, tiled=True)
    return tiles.reshape(-1, *tiles.shape[len(axes) :])


def core_and_chips(x, groups, sequence, split_dim, concat_dim):
    devices = lax.axis_size(groups[0]) * lax.axis_size(groups[1])
    tiles = in_blocks(x, split_dim, devices)
    return in_order(turned_blocks(tiles, groups, sequence), concat_dim)


def per_device(
    tokens, expert_ids, gate_values, w_gate, w_up, w_down, shared_gate, shared_up, shared_down
):
    tok_dev, narrow = tokens.shape
    top_count = expert_ids.shape[1]
    per_lane, features, quarter = w_gate.shape
    lane_count = lax.axis_size(EXPERT)
    experts_all = lane_count * per_lane
    capacity = min(tok_dev, 3 * tok_dev * top_count // (2 * experts_all))
    total_rows = experts_all * capacity
    numbers = jnp.arange(experts_all, dtype=jnp.int32)
    onehot = (expert_ids[:, :, None] == numbers).astype(jnp.int32)
    per_token = jnp.sum(onehot, axis=1)
    earlier = jnp.cumsum(per_token, axis=0) - per_token
    slot_index = jnp.sum(onehot * earlier[:, None, :], axis=2)
    target = expert_ids * capacity + slot_index
    token_index = jnp.repeat(jnp.arange(tok_dev, dtype=jnp.int32), top_count)
    owners = jnp.full((total_rows,), tok_dev, jnp.int32).at[target.reshape(-1)].set(token_index)
    features_all = collect(tokens, "tensor", 1)
    shared_gate_sums = jnp.dot(features_all, shared_gate, preferred_element_type=jnp.float32)
    shared_up_sums = jnp.dot(features_all, shared_up, preferred_element_type=jnp.float32)
    shared_hidden = (jax.nn.silu(shared_gate_sums) * shared_up_sums).astype(jnp.bfloat16)
    shared_partial = jnp.dot(shared_hidden, shared_down, preferred_element_type=jnp.float32)
    padded = jnp.concatenate([tokens, jnp.zeros((1, narrow), jnp.bfloat16)], axis=0)
    outgoing = padded[owners].reshape(lane_count, per_lane * capacity, narrow)
    arrived = lax.all_to_all(outgoing, EXPERT, split_axis=0, concat_axis=0, tiled=True)
    arrived = arrived.reshape(lane_count, per_lane, capacity, narrow)
    block_rows = lax.all_gather(arrived, "tensor", axis=3, tiled=True)
    gate_more = jnp.einsum("sjcd,jdf->sjcf", block_rows, w_gate, preferred_element_type=jnp.float32)
    up_more = jnp.einsum("sjcd,jdf->sjcf", block_rows, w_up, preferred_element_type=jnp.float32)
    hidden = (jax.nn.silu(gate_more) * up_more).astype(jnp.bfloat16)
    partial_value = jnp.einsum("sjcf,jfd->sjcd", hidden, w_down, preferred_element_type=jnp.float32)
    summed = sent_and_summed(partial_value.astype(jnp.bfloat16), "tensor", 3)
    returned = core_and_chips(
        summed.reshape(lane_count, per_lane * capacity, narrow).astype(jnp.bfloat16),
        (("expert_0", "expert_1"), "expert_2"),
        (1, 0),
        0,
        0,
    ).astype(jnp.float32)
    picked = returned.reshape(total_rows, narrow)[target]
    routed = jnp.sum(gate_values.astype(jnp.float32)[:, :, None] * picked, axis=1)
    shared_total = sent_and_summed(shared_partial.astype(jnp.bfloat16), "tensor", 1)
    return (routed + shared_total).astype(jnp.bfloat16)


def solution(mesh):
    torus = Mesh(
        mesh.devices.reshape(4, 8, 2, mesh.shape["tensor"]),
        ("expert_0", "expert_1", "expert_2", "tensor"),
    )
    placed = (
        P(EXPERT, "tensor"),
        P(EXPERT, None),
        P(EXPERT, None),
        P(EXPERT, None, "tensor"),
        P(EXPERT, None, "tensor"),
        P(EXPERT, "tensor", None),
        P(None, "tensor"),
        P(None, "tensor"),
        P("tensor", None),
    )
    return jax.shard_map(
        per_device, mesh=torus, in_specs=placed, out_specs=P(EXPERT, "tensor"), check_vma=False
    )
```

profile of v0, /device:TPU:32, one launch (start us, length us, event | category | flops | bytes accessed | tf_op | source)
XLA Modules:
  0.0 321.1 jit_solution(12613605834629810689)
XLA Ops:
  6.5 0.0 copy-start
  6.5 0.0 all-gather.3.cloned.1.call-start
  6.5 0.8 convert_reduce_fusion.1
  7.4 0.1 copy.45
  7.5 0.2 reduce_window_sum.11
  7.7 0.1 copy.47
  7.7 0.7 select_reduce_fusion
  8.5 0.7 compare_select_fusion.2
  9.1 0.1 copy.48
  9.3 0.1 reshape.98
  9.4 0.1 reshape.131
  9.5 2.4 scatter_custom_fusion
  12.0 1.0 concatenate.3
  12.9 2.8 gather_fusion
  15.8 1.4 reshape.100
  17.2 56.0 %all_to_all.30 = bf16[64,12,896]{2,1,0:T(8,128)(2,1)S(1)} all-to-all(bf16[64,12,896]{2,1,0:T(8,128)(2,1)} %reshape.100), channel_id=1, replica_groups=mesh['expert_0'=4,'expert_1'=8,'expert_2'=2,'tensor'=4] {'expert_0','exp..., dimensions={0} | all-to-all | bytes 2752512 | tf_op jit(solution)/shard_map/all_to_all | solution.py:75
  73.2 0.0 copy-start.3
  73.2 1.4 copy.49
  74.6 0.0 all-gather.3.cloned.1.call-update
  74.7 0.0 copy-done.3
  74.7 0.2 copy.57
  74.9 1.1 broadcast_in_dim.25
  75.9 4.5 %all-to-all-start.4 = ((bf16[4,128,896]{1,2,0:T(8,128)(2,1)}), bf16[4,128,896]{1,2,0:T(8,128)(2,1)S(1)}, u32[]{:S(2)}, u32[]{:S(2)}) async-start(bf16[4,128,896]{1,2,0:T(8,128)(2,1)} %broadcast_in_dim.25), calls=%async_computation.4 | async-start | bytes 1835008 | tf_op jit(solution)/shard_map/all_to_all | solution.py:18
  80.4 58.3 %all-gather.3.cloned.1.call-done = bf16[64,12,3584]{2,0,1:T(8,128)(2,1)} async-done(((bf16[64,12,896]{2,0,1:T(8,128)(2,1)}), bf16[64,12,3584]{2,0,1:T(8,128)(2,1)}) %all-gather.3.cloned.1.call-update) | async-done | bytes 5505040 | tf_op jit(solution)/shard_map/all_gather | solution.py:77
  138.6 5.6 %fusion.5 = f32[64,1,12,256]{3,0,2,1:T(8,128)} fusion(bf16[64,12,3584]{2,0,1:T(8,128)(2,1)} %all-gather.3.cloned.1.call-done, bf16[1,3584,256]{2,1,0:T(8,128)(2,1)} %param.12), kind=kOutput, calls=%fused_computation.14 | convolution fusion | flops 1409286144 | bytes 8126464 | tf_op jit(solution)/shard_map/sjcd,jdf->sjcf/dot_general | solution.py:78
  144.3 0.0 copy-done
  144.3 11.5 %convolution_convert_fusion = bf16[64,12,3584]{2,0,1:T(8,128)(2,1)} fusion(bf16[1,256,3584]{2,1,0:T(8,128)(2,1)S(1)} %copy-done, bf16[64,12,3584]{2,0,1:T(8,128)(2,1)} %all-gather.3.cloned.1.call-done, bf16[1,3584,256]{2,1,0:T(8,128)(2,1)} %param.13, f32[64,1,12,256]{3,0,2,1:T(8,128)} %fusion.5), kind=kOutput, calls=%fused_computation.3 | convolution fusion | flops 2822504448 | bytes 15466496 | tf_op jit(solution)/shard_map/sjcf,jfd->sjcd/dot_general | solution.py:81
  155.7 5.8 %copy.65 = bf16[1,12,8,4,8,896]{5,4,2,1,0,3:T(8,128)(2,1)} copy(bf16[1,12,8,4,8,896]{5,4,3,2,1,0:T(8,128)(2,1)} %bitcast.85) | data formatting | bytes 11010048 | tf_op jit(solution)/shard_map/reshape | solution.py:27
  161.6 0.0 all-to-all-done.4
  161.6 0.0 copy-start.2
  161.6 5.4 %all-to-all-start.1 = ((bf16[4,64,1,12,896]{4,1,3,2,0:T(8,128)(2,1)}), bf16[4,64,1,12,896]{4,1,3,2,0:T(8,128)(2,1)}, u32[]{:S(2)}, u32[]{:S(2)}) async-start(bf16[4,64,1,12,896]{4,1,3,2,0:T(8,128)(2,1)} %bitcast.82), calls=%async_computation.1 | async-start | bytes 11010048 | tf_op jit(solution)/shard_map/all_to_all | solution.py:32
  167.0 0.0 copy-done.2
  167.0 0.5 fusion.39
  167.5 3.3 %convolution_convert_fusion.1 = bf16[128,3584]{1,0:T(8,128)(2,1)S(1)} fusion(bf16[256,3584]{1,0:T(8,128)(2,1)} %param.17, bf16[128,3584]{0,1:T(8,128)(2,1)S(1)} %bitcast.84, bf16[3584,256]{1,0:T(8,128)(2,1)} %param.16, f32[128,256]{1,0:T(8,128)S(1)} %fusion.39), kind=kOutput, calls=%fused_computation.5 | convolution fusion | flops 470417408 | bytes 5636096 | tf_op jit(solution)/shard_map/dot_general | solution.py:72
  170.8 1.0 copy.66
  171.8 58.3 %all-to-all-done.1 = bf16[4,64,1,12,896]{4,1,3,2,0:T(8,128)(2,1)} async-done(((bf16[4,64,1,12,896]{4,1,3,2,0:T(8,128)(2,1)}), bf16[4,64,1,12,896]{4,1,3,2,0:T(8,128)(2,1)}, u32[]{:S(2)}, u32[]{:S(2)}) %all-to-all-start.1) | async-done | bytes 5505056 | tf_op jit(solution)/shard_map/all_to_all | solution.py:32
  230.1 3.6 %reduce_sum.50 = bf16[64,12,896]{2,0,1:T(8,128)(2,1)S(1)} reduce(bf16[4,64,1,12,896]{4,1,3,2,0:T(8,128)(2,1)} %all-to-all-done.1, bf16[]{:T(256)} %constant.8.clone.1), dimensions={0,2}, to_apply=%region_4.5 | reduce | flops 2064384 | bytes 6881282 | tf_op jit(solution)/shard_map/reduce_sum | solution.py:33
  233.7 0.6 convert_element_type.59
  234.3 0.2 copy.52
  234.5 4.8 %all_to_all.31 = bf16[32,2,1,12,896]{4,0,3,2,1:T(8,128)(2,1)S(1)} all-to-all(bf16[32,2,1,12,896]{4,0,3,2,1:T(8,128)(2,1)S(1)} %copy.52), channel_id=1, replica_groups=mesh['expert_0'=4,'expert_1'=8,'expert_2'=2,'tensor'=4] {'expert_2'}, dimensions={1} | all-to-all | bytes 2752512 | tf_op jit(solution)/shard_map/all_to_all | solution.py:40
  239.3 3.5 %all-to-all-start.5 = ((bf16[4,128,896]{2,1,0:T(8,128)(2,1)}), bf16[4,128,896]{2,1,0:T(8,128)(2,1)S(1)}, u32[]{:S(2)}, u32[]{:S(2)}) async-start(bf16[4,128,896]{2,1,0:T(8,128)(2,1)} %bitcast.81), calls=%async_computation.5 | async-start | bytes 1835008 | tf_op jit(solution)/shard_map/all_to_all | solution.py:32
  242.8 2.5 copy.53
  245.3 0.0 copy-start.4
  245.3 11.7 %all-to-all-done.5 = bf16[4,128,896]{2,1,0:T(8,128)(2,1)S(1)} async-done(((bf16[4,128,896]{2,1,0:T(8,128)(2,1)}), bf16[4,128,896]{2,1,0:T(8,128)(2,1)S(1)}, u32[]{:S(2)}, u32[]{:S(2)}) %all-to-all-start.5) | async-done | bytes 917536 | tf_op jit(solution)/shard_map/all_to_all | solution.py:32
  257.1 6.9 %all-to-all-start.3 = ((bf16[32,2,1,12,896]{4,1,3,2,0:T(2,128)(2,1)}), bf16[32,2,1,12,896]{4,1,3,2,0:T(2,128)(2,1)S(1)}, u32[]{:S(2)}, u32[]{:S(2)}) async-start(bf16[32,2,1,12,896]{4,1,3,2,0:T(2,128)(2,1)} %copy.53), calls=%async_computation.3 | async-start | bytes 2752512 | tf_op jit(solution)/shard_map/all_to_all | solution.py:40
  263.9 0.1 copy.56
  264.0 0.1 reshape.121
  264.1 0.0 copy-done.4
  264.2 0.1 copy.44
  264.3 0.1 convert_reduce_fusion
  264.4 34.2 %all-to-all-done.3 = bf16[32,2,1,12,896]{4,1,3,2,0:T(2,128)(2,1)S(1)} async-done(((bf16[32,2,1,12,896]{4,1,3,2,0:T(2,128)(2,1)}), bf16[32,2,1,12,896]{4,1,3,2,0:T(2,128)(2,1)S(1)}, u32[]{:S(2)}, u32[]{:S(2)}) %all-to-all-start.3) | async-done | bytes 1376288 | tf_op jit(solution)/shard_map/all_to_all | solution.py:40
  298.6 0.3 copy_convert_fusion
  299.0 3.4 %copy.55 = f32[32,2,1,12,896]{4,3,1,0,2:T(8,128)} copy(f32[32,2,1,12,896]{4,0,3,2,1:T(8,128)S(1)} %copy_convert_fusion) | data formatting | bytes 5505024 | tf_op jit(solution)/shard_map/convert_element_type | solution.py:89
  302.4 2.9 reshape.110
  305.3 2.7 gather_fusion.1
  307.9 0.0 copy-start.1
  307.9 2.9 reshape.120
  310.9 2.7 multiply_reduce_fusion
  313.6 0.7 add_convert_fusion
  314.3 0.0 copy-done.1
  (6 shorter events, 0.0 us)
Async XLA Ops:
  6.5 137.7 %copy-start = (bf16[1,256,3584]{2,1,0:T(8,128)(2,1)S(1)}, bf16[1,256,3584]{2,1,0:T(8,128)(2,1)}, u32[]{:S(2)}) copy-start(bf16[1,256,3584]{2,1,0:T(8,128)(2,1)} %param.14) | copy-start | bytes 5505028
  6.5 132.1 %all-gather.3.cloned.1.call-start = ((), (), s32[]{:S(2)}) async-start(), calls=%async_computation.6 | async-start | bytes 6881280 | tf_op jit(solution)/shard_map/all_gather | solution.py:77
  73.2 1.4 copy-start.3
  75.9 85.7 %all-to-all-start.4 = ((bf16[4,128,896]{1,2,0:T(8,128)(2,1)}), bf16[4,128,896]{1,2,0:T(8,128)(2,1)S(1)}, u32[]{:S(2)}, u32[]{:S(2)}) async-start(bf16[4,128,896]{1,2,0:T(8,128)(2,1)} %broadcast_in_dim.25), calls=%async_computation.4 | async-start | bytes 1835008 | tf_op jit(solution)/shard_map/all_to_all | solution.py:18
  161.6 5.5 %copy-start.2 = (bf16[3584,256]{1,0:T(8,128)(2,1)S(1)}, bf16[3584,256]{1,0:T(8,128)(2,1)}, u32[]{:S(2)}) copy-start(bf16[3584,256]{1,0:T(8,128)(2,1)} %param.15) | copy-start | bytes 5505028
  161.6 68.5 %all-to-all-start.1 = ((bf16[4,64,1,12,896]{4,1,3,2,0:T(8,128)(2,1)}), bf16[4,64,1,12,896]{4,1,3,2,0:T(8,128)(2,1)}, u32[]{:S(2)}, u32[]{:S(2)}) async-start(bf16[4,64,1,12,896]{4,1,3,2,0:T(8,128)(2,1)} %bitcast.82), calls=%async_computation.1 | async-start | bytes 11010048 | tf_op jit(solution)/shard_map/all_to_all | solution.py:32
  239.3 17.7 %all-to-all-start.5 = ((bf16[4,128,896]{2,1,0:T(8,128)(2,1)}), bf16[4,128,896]{2,1,0:T(8,128)(2,1)S(1)}, u32[]{:S(2)}, u32[]{:S(2)}) async-start(bf16[4,128,896]{2,1,0:T(8,128)(2,1)} %bitcast.81), calls=%async_computation.5 | async-start | bytes 1835008 | tf_op jit(solution)/shard_map/all_to_all | solution.py:32
  245.3 18.8 %copy-start.4 = (bf16[128,4]{0,1:T(4,128)(2,1)S(1)}, bf16[128,4]{0,1:T(4,128)(2,1)}, u32[]{:S(2)}) copy-start(bf16[128,4]{0,1:T(4,128)(2,1)} %param.11) | copy-start | bytes 3076
  257.1 41.6 %all-to-all-start.3 = ((bf16[32,2,1,12,896]{4,1,3,2,0:T(2,128)(2,1)}), bf16[32,2,1,12,896]{4,1,3,2,0:T(2,128)(2,1)S(1)}, u32[]{:S(2)}, u32[]{:S(2)}) async-start(bf16[32,2,1,12,896]{4,1,3,2,0:T(2,128)(2,1)} %copy.53), calls=%async_computation.3 | async-start | bytes 2752512 | tf_op jit(solution)/shard_map/all_to_all | solution.py:40
  307.9 6.4 %copy-start.1 = (bf16[1,256,3584]{2,1,0:T(8,128)(2,1)S(1)}, bf16[1,256,3584]{2,1,0:T(8,128)(2,1)}, u32[]{:S(2)}) copy-start(bf16[1,256,3584]{2,1,0:T(8,128)(2,1)} %param.14) | copy-start | bytes 5505028
Sparse Core Ops, SparseCore 0:
  74.8 63.8 all-gather.2
where the time goes:
time: 322 us; the launch traced here: 321 us
  waiting for transfers between devices  163 us (51%)
  blocking collectives  60.9 us (19%)
  local copies, waits for them, and re-layouts  33.1 us (10%)
  matrix products  20.8 us (6%)
  starting transfers between devices  20.3 us (6%)
  between operations  13.6 us (4%)
  other arithmetic  9.92 us (3%)
    all_to_all x2, waiting for transfers between devices, sent_and_summed(): lax.all_to_all(tiles, axis, split_axis=0, concat_axis=0, tiled=True)  70.1 us
    all_gather x1, waiting for transfers between devices, per_device(): block_rows = lax.all_gather(arrived, 'tensor', axis=3, tiled=True)  58.3 us
    all_to_all x1, blocking collectives, per_device(): lax.all_to_all(outgoing, EXPERT, split_axis=0, concat_axis=0, tiled=True)  56 us
    all_to_all x1, waiting for transfers between devices, turned_blocks(): lax.all_to_all(tiles, axes[k], split_axis=k, concat_axis=k, tiled=True)  34.2 us
    dot_general x1, matrix products, per_device(): jnp.einsum('sjcf,jfd->sjcd', hidden, w_down, preferred_element_type=jnp.f...  11.5 us
    all_to_all x2, starting transfers between devices, sent_and_summed(): lax.all_to_all(tiles, axis, split_axis=0, concat_axis=0, tiled=True)  8.94 us
    all_to_all x1, starting transfers between devices, turned_blocks(): lax.all_to_all(tiles, axes[k], split_axis=k, concat_axis=k, tiled=True)  6.87 us
    reshape x2, local copies, waits for them, and re-layouts, in_blocks(): return jnp.moveaxis(x.reshape(*before, devices, -1, *after), dim, 0)  6.86 us
  transfers between devices with their start and end apart: 5, of which 4 were waited for; matrix products, arithmetic and copies ran while one was open for 10% of the time, Pallas kernels for 0%

commit v1 on v0

v1 whole, which is shorter than its diff:
```python
import jax
import jax.numpy as jnp
from jax import lax
from jax.experimental import pallas as pl
from jax.experimental.pallas import tpu as pltpu
from jax.sharding import Mesh
from jax.sharding import PartitionSpec as P

EXPERT = ("expert_0", "expert_1", "expert_2")
CHUNKS = (8, 4)
F32 = jnp.float32
BF16 = jnp.bfloat16


def dot(a, b):
    return jnp.dot(a, b, preferred_element_type=F32)


def silu_times(gate, up):
    return (gate / (1.0 + jnp.exp(-gate)) * up).astype(BF16)


def kernel_call(body, outs, *args, smem=0):
    specs = [pl.BlockSpec(memory_space=pltpu.SMEM) for _ in range(smem)]
    specs += [pl.BlockSpec(memory_space=pltpu.VMEM) for _ in args[smem:]]
    return pl.pallas_call(
        body,
        in_specs=specs,
        out_specs=tuple(pl.BlockSpec(memory_space=pltpu.VMEM) for _ in outs),
        out_shape=tuple(jax.ShapeDtypeStruct(*o) for o in outs),
    )(*args)


def route_body(experts):
    def body(ids_ref, gates_ref, tokens_ref, *outs):
        ids = ids_ref[...]
        gates = gates_ref[...].astype(F32)
        rows, top = ids.shape
        numbers = lax.broadcasted_iota(jnp.int32, (rows, experts), 1)
        named = [ids[:, k : k + 1] == numbers for k in range(top)]
        onehot = [jnp.where(n, 1.0, 0.0) for n in named]
        per_token = sum(onehot[1:], onehot[0])
        before = lax.broadcasted_iota(jnp.int32, (rows, rows), 0) > lax.broadcasted_iota(
            jnp.int32, (rows, rows), 1
        )
        earlier = dot(jnp.where(before, 1.0, 0.0).astype(BF16), per_token.astype(BF16))
        slots = [
            jnp.sum(o * earlier, axis=1, keepdims=True).astype(jnp.int32) for o in onehot
        ]
        first = 0
        for j, size in enumerate(CHUNKS):
            place = lax.broadcasted_iota(jnp.int32, (rows, experts * size), 1)
            pick = jnp.zeros((rows, experts * size), F32)
            weight = jnp.zeros((rows, experts * size), F32)
            for k in range(top):
                local = slots[k] - first
                inside = (local >= 0) & (local < size)
                target = jnp.where(inside, ids[:, k : k + 1] * size + local, -1)
                here = target == place
                pick = jnp.where(here, 1.0, pick)
                weight = jnp.where(here, gates[:, k : k + 1], weight)
            outs[2 * j][...] = lax.dot_general(
                pick.astype(BF16),
                tokens_ref[...],
                (((0,), (0,)), ((), ())),
                preferred_element_type=F32,
            ).astype(BF16)
            outs[2 * j + 1][...] = weight.astype(BF16)
            first += size

    return body


def shared_body(x_ref, gate_ref, up_ref, down_ref, out_ref):
    pieces = x_ref.shape[0]
    gate = sum(dot(x_ref[s], gate_ref[s]) for s in range(pieces))
    up = sum(dot(x_ref[s], up_ref[s]) for s in range(pieces))
    hidden = silu_times(gate, up)
    width = out_ref.shape[2]
    for s in range(pieces):
        out_ref[s] = dot(hidden, down_ref[:, s * width : (s + 1) * width]).astype(BF16)


def hidden_body(q_ref, own_ref, left_ref, right_ref, o0_ref, o1_ref, gate_ref, up_ref, out_ref):
    q = q_ref[0]
    n = gate_ref.shape[0]
    half = o0_ref.shape[0]
    for part in range(2):
        span = pl.ds(part * half, half)
        opposite = (o0_ref, o1_ref)[part]
        rows = ((own_ref[span], 0), (left_ref[span], n - 1), (right_ref[span], 1), (opposite[...], 2))
        gate = sum(dot(x, gate_ref[lax.rem(q + s, n)]) for x, s in rows)
        up = sum(dot(x, up_ref[lax.rem(q + s, n)]) for x, s in rows)
        out_ref[span] = silu_times(gate, up)


def down_body(h_ref, down_ref, out_ref):
    out_ref[...] = sum(dot(h_ref[s], down_ref[s]) for s in range(h_ref.shape[0])).astype(BF16)


def combine_body(*refs):
    count = len(CHUNKS)
    parts_ref, out_ref = refs[2 * count :]
    total = sum(parts_ref[s].astype(F32) for s in range(parts_ref.shape[0]))
    for j in range(count):
        total = total + dot(refs[2 * j][...], refs[2 * j + 1][...])
    out_ref[...] = total.astype(BF16)


def exchange(x, axis):
    return lax.all_to_all(x, axis, split_axis=0, concat_axis=0, tiled=True)


def to_all(x, axis):
    return exchange(jnp.broadcast_to(x, (lax.axis_size(axis), *x.shape)), axis)


def shift(x, axis, by):
    n = lax.axis_size(axis)
    return lax.ppermute(x, axis, [(i, (i + by) % n) for i in range(n)])


def per_device(
    tokens, expert_ids, gate_values, w_gate, w_up, w_down, shared_gate, shared_up, shared_down
):
    tok_dev, narrow = tokens.shape
    _, features, quarter = w_gate.shape
    experts = lax.axis_size(EXPERT)
    n = lax.axis_size("tensor")
    q = lax.axis_index("tensor").reshape(1)

    tokens_all = to_all(tokens, "tensor")
    routed = kernel_call(
        route_body(experts),
        [
            o
            for size in CHUNKS
            for o in (((experts * size, narrow), BF16), ((tok_dev, experts * size), BF16))
        ],
        expert_ids,
        gate_values,
        tokens,
    )
    weights = routed[1::2]
    arrived = [
        exchange(rows.reshape(experts, size, narrow), EXPERT).reshape(-1, narrow)
        for rows, size in zip(routed[0::2], CHUNKS)
    ]
    down = exchange(jnp.moveaxis(w_down.reshape(quarter, n, narrow), 1, 0), "tensor")

    shared_parts = kernel_call(
        shared_body,
        [((n, tok_dev, narrow), BF16)],
        tokens_all,
        shared_gate.reshape(n, narrow, -1),
        shared_up.reshape(n, narrow, -1),
        shared_down,
    )[0]

    returned = []
    for rows, size in zip(arrived, CHUNKS):
        half = rows.shape[0] // 2
        left = shift(rows, "tensor", 1)
        right = shift(rows, "tensor", -1)
        o0 = shift(left[:half], "tensor", 1)
        o1 = shift(right[half:], "tensor", -1)
        hidden = kernel_call(
            hidden_body,
            [((rows.shape[0], quarter), BF16)],
            q,
            rows,
            left,
            right,
            o0,
            o1,
            w_gate.reshape(n, narrow, quarter),
            w_up.reshape(n, narrow, quarter),
            smem=1,
        )[0]
        hidden_all = to_all(hidden, "tensor")
        out = kernel_call(down_body, [((rows.shape[0], narrow), BF16)], hidden_all, down)[0]
        returned.append(exchange(out.reshape(experts, size, narrow), EXPERT).reshape(-1, narrow))
    shared_all = exchange(shared_parts, "tensor")
    pairs = [a for pair in zip(weights, returned) for a in pair]
    return kernel_call(combine_body, [((tok_dev, narrow), BF16)], *pairs, shared_all)[0]


def solution(mesh):
    torus = Mesh(
        mesh.devices.reshape(4, 8, 2, mesh.shape["tensor"]),
        ("expert_0", "expert_1", "expert_2", "tensor"),
    )
    placed = (
        P(EXPERT, "tensor"),
        P(EXPERT, None),
        P(EXPERT, None),
        P(EXPERT, None, "tensor"),
        P(EXPERT, None, "tensor"),
        P(EXPERT, "tensor", None),
        P(None, "tensor"),
        P(None, "tensor"),
        P("tensor", None),
    )
    return jax.shard_map(
        per_device, mesh=torus, in_specs=placed, out_specs=P(EXPERT, "tensor"), check_vma=False
    )
```

time: 322 us -> 251 us (0.78)
  waiting for transfers between devices: 163 us -> 115 us
  blocking collectives: 60.9 us -> 27.2 us
  starting transfers between devices: 20.3 us -> 53.9 us
  Pallas kernels: 0 us -> 28.9 us
  matrix products: 20.8 us -> 0 us
  between operations: 13.6 us -> 0.19 us
  other arithmetic: 9.92 us -> 0 us
  local copies, waits for them, and re-layouts: 33.1 us -> 23.2 us
    all_gather x1 -> x0, waiting for transfers between devices: 58.3 us -> none  [per_device(): block_rows = lax.all_gather(arrived, 'tensor', axis=3, tiled=True)]
    all_to_all x2 -> x1, blocking collectives: 60.9 us -> 27.2 us  [exchange(): return lax.all_to_all(x, axis, split_axis=0, concat_axis=0, tiled=True)]
    pallas_call x0 -> x7, Pallas kernels: none -> 28.9 us  [kernel_call(): pl.pallas_call(body, in_specs=specs, out_specs=tuple((pl.BlockSpec(memory...]
    ppermute x0 -> x8, waiting for transfers between devices: none -> 28.7 us  [shift(): return lax.ppermute(x, axis, [(i, (i + by) % n) for i in range(n)])]
    dot_general x4 -> x0, matrix products: 20.8 us -> none  [the longest x1 11.5 us: per_device(): jnp.einsum('sjcf,jfd->sjcd', hidden, w_down, preferred_element_type=jnp.f...]
    all_to_all x4 -> x8, starting transfers between devices: 20.3 us -> 40.4 us  [exchange(): return lax.all_to_all(x, axis, split_axis=0, concat_axis=0, tiled=True)]
    all_to_all x4 -> x8, waiting for transfers between devices: 104 us -> 86.1 us  [exchange(): return lax.all_to_all(x, axis, split_axis=0, concat_axis=0, tiled=True)]
    ppermute x0 -> x8, starting transfers between devices: none -> 13.5 us  [shift(): return lax.ppermute(x, axis, [(i, (i + by) % n) for i in range(n)])]
  transfers between devices with their start and end apart: 5 -> 16, of which waited for: 4 -> 9; matrix products, arithmetic and copies ran while one was open for 10% -> 7% of each run, Pallas kernels for 0% -> 11%
where the time goes in v1:
time: 251 us; the launch traced here: 248 us
  waiting for transfers between devices  115 us (46%)
  starting transfers between devices  53.9 us (21%)
  Pallas kernels  28.9 us (12%)
  blocking collectives  27.2 us (11%)
  local copies, waits for them, and re-layouts  23.2 us (9%)
    all_to_all x8, waiting for transfers between devices, exchange(): return lax.all_to_all(x, axis, split_axis=0, concat_axis=0, tiled=True)  86.1 us
    all_to_all x8, starting transfers between devices, exchange(): return lax.all_to_all(x, axis, split_axis=0, concat_axis=0, tiled=True)  40.4 us
    pallas_call x7, Pallas kernels, kernel_call(): pl.pallas_call(body, in_specs=specs, out_specs=tuple((pl.BlockSpec(memory...  28.9 us
    ppermute x8, waiting for transfers between devices, shift(): return lax.ppermute(x, axis, [(i, (i + by) % n) for i in range(n)])  28.7 us
    all_to_all x1, blocking collectives, exchange(): return lax.all_to_all(x, axis, split_axis=0, concat_axis=0, tiled=True)  27.2 us
    ppermute x8, starting transfers between devices, shift(): return lax.ppermute(x, axis, [(i, (i + by) % n) for i in range(n)])  13.5 us
    unnamed x25, local copies, waits for them, and re-layouts  6.09 us
    broadcast_in_dim x3, local copies, waits for them, and re-layouts, to_all(): return exchange(jnp.broadcast_to(x, (lax.axis_size(axis), *x.shape)), axis)  5.98 us
  transfers between devices with their start and end apart: 16, of which 9 were waited for; matrix products, arithmetic and copies ran while one was open for 7% of the time, Pallas kernels for 11%

profile of v1, /device:TPU:32, one launch (start us, length us, event | category | flops | bytes accessed | tf_op | source)
XLA Modules:
  0.0 248.1 jit_solution(7707129462596839452)
XLA Ops:
  0.0 2.0 broadcast_in_dim.11
  2.0 4.5 %all-to-all-start.7 = ((bf16[4,128,896]{2,1,0:T(8,128)(2,1)}), bf16[4,128,896]{2,1,0:T(8,128)(2,1)S(1)}, u32[]{:S(2)}, u32[]{:S(2)}) async-start(bf16[4,128,896]{2,1,0:T(8,128)(2,1)} %broadcast_in_dim.11), calls=%async_computation.7 | async-start | bytes 1835008 | tf_op jit(solution)/shard_map/all_to_all | solution.py:111
  6.4 0.0 copy-done.9
  6.4 0.7 copy.12.ids_ref
  7.2 0.0 copy-done.10
  7.2 0.7 copy.13.gates_ref
  7.9 3.2 %shard_map.91 = (bf16[512,896]{1,0:T(8,128)(2,1)}, bf16[128,512]{1,0:T(8,128)(2,1)}, bf16[256,896]{1,0:T(8,128)(2,1)}, bf16[128,256]{1,0:T(8,128)(2,1)}) custom-call(s32[128,4]{1,0:T(8,128)} %copy.12.ids_ref, bf16[128,4]{1,0:T(8,128)(2,1)} %copy.13.gates_ref, bf16[128,896]{1,0:T(8,128)(2,1)} %tokens_ref.1), custom_call_target="tpu_custom_call" | custom-call | tf_op jit(solution)/shard_map/pallas_call | solution.py:26
  11.1 1.1 reshape.52
  12.3 7.9 %all-to-all-done.7.x_ref = bf16[4,128,896]{2,1,0:T(8,128)(2,1)S(1)} async-done(((bf16[4,128,896]{2,1,0:T(8,128)(2,1)}), bf16[4,128,896]{2,1,0:T(8,128)(2,1)S(1)}, u32[]{:S(2)}, u32[]{:S(2)}) %all-to-all-start.7) | async-done | bytes 917536 | tf_op jit(solution)/shard_map/all_to_all | solution.py:111
  20.1 27.2 %all_to_all.45 = bf16[64,4,896]{2,1,0:T(4,128)(2,1)} all-to-all(bf16[64,4,896]{2,1,0:T(4,128)(2,1)S(1)} %reshape.52), channel_id=1, replica_groups=mesh['expert_0'=4,'expert_1'=8,'expert_2'=2,'tensor'=4] {'expert_0','exp..., dimensions={0} | all-to-all | bytes 917504 | tf_op jit(solution)/shard_map/all_to_all | solution.py:111
  47.3 6.7 %all-to-all-start = ((bf16[64,8,896]{2,1,0:T(8,128)(2,1)}), bf16[64,8,896]{2,1,0:T(8,128)(2,1)}, u32[]{:S(2)}, u32[]{:S(2)}) async-start(bf16[64,8,896]{2,1,0:T(8,128)(2,1)} %bitcast.1), calls=%async_computation | async-start | bytes 1835008 | tf_op jit(solution)/shard_map/all_to_all | solution.py:111
  54.0 2.9 %copy.14 = bf16[1,256,3584]{1,2,0:T(8,128)(2,1)S(1)} copy(bf16[1,256,3584]{2,1,0:T(8,128)(2,1)} %param.14) | data formatting | bytes 3670016 | tf_op args[5]
  56.9 0.0 copy-done.2
  56.9 2.4 copy.15
  59.3 19.9 %all-to-all-done = bf16[64,8,896]{2,1,0:T(8,128)(2,1)} async-done(((bf16[64,8,896]{2,1,0:T(8,128)(2,1)}), bf16[64,8,896]{2,1,0:T(8,128)(2,1)}, u32[]{:S(2)}, u32[]{:S(2)}) %all-to-all-start) | async-done | bytes 917536 | tf_op jit(solution)/shard_map/all_to_all | solution.py:111
  79.2 3.7 %all-to-all-start.2 = ((bf16[4,256,896]{2,1,0:T(8,128)(2,1)}), bf16[4,256,896]{2,1,0:T(8,128)(2,1)S(1)}, u32[]{:S(2)}, u32[]{:S(2)}) async-start(bf16[4,256,896]{2,1,0:T(8,128)(2,1)} %bitcast.11), calls=%async_computation.2 | async-start | bytes 3670016 | tf_op jit(solution)/shard_map/all_to_all | solution.py:111
  82.9 2.0 collective-permute-start
  84.9 1.3 collective-permute-start.1
  86.2 0.0 copy-done.7
  86.2 0.1 reshape.53.own_ref
  86.3 0.0 copy-start.6
  86.4 0.8 collective-permute-start.4
  87.1 2.5 %collective-permute-start.5 = (bf16[256,896]{1,0:T(8,128)(2,1)S(1)}, bf16[256,896]{1,0:T(8,128)(2,1)}, u32[]{:S(2)}, u32[]{:S(2)}) collective-permute-start(bf16[256,896]{1,0:T(8,128)(2,1)S(1)} %reshape.53.own_ref), channel_id=1, source_target_pairs={{0,3},{1,0},{2,1},{3,2},{4,7},{5,4},{6,5},{7,6},{8,11},{9,8},{10,9... | collective-permute-start | bytes 1376264 | tf_op jit(solution)/shard_map/ppermute | solution.py:120
  89.7 4.9 %shard_map.96 = bf16[4,128,896]{2,1,0:T(8,128)(2,1)} custom-call(bf16[4,128,896]{2,1,0:T(8,128)(2,1)} %copy-done.2, bf16[4,896,256]{2,1,0:T(8,128)(2,1)} %bitcast.19, bf16[4,896,256]{2,1,0:T(8,128)(2,1)} %bitcast.20, bf16[256,3584]{1,0:T(8,128)(2,1)} %down_ref.1), custom_call_target="tpu_custom_call" | custom-call | tf_op jit(solution)/shard_map/pallas_call | solution.py:26
  94.6 13.2 %all-to-all-done.2.down_ref = bf16[4,256,896]{2,1,0:T(8,128)(2,1)S(1)} async-done(((bf16[4,256,896]{2,1,0:T(8,128)(2,1)}), bf16[4,256,896]{2,1,0:T(8,128)(2,1)S(1)}, u32[]{:S(2)}, u32[]{:S(2)}) %all-to-all-start.2) | async-done | bytes 1835040 | tf_op jit(solution)/shard_map/all_to_all | solution.py:111
  107.9 3.5 %all-to-all-start.8 = ((bf16[4,128,896]{2,1,0:T(8,128)(2,1)}), bf16[4,128,896]{2,1,0:T(8,128)(2,1)S(1)}, u32[]{:S(2)}, u32[]{:S(2)}) async-start(bf16[4,128,896]{2,1,0:T(8,128)(2,1)} %shard_map.96), calls=%async_computation.8 | async-start | bytes 1835008 | tf_op jit(solution)/shard_map/all_to_all | solution.py:111
  111.4 25.7 %collective-permute-done.4.left_ref = bf16[256,896]{1,0:T(8,128)(2,1)} collective-permute-done((bf16[256,896]{1,0:T(8,128)(2,1)S(1)}, bf16[256,896]{1,0:T(8,128)(2,1)}, u32[]{:S(2)}, u32[]{:S(2)}) %collective-permute-start.4) | collective-permute-done | bytes 458784 | tf_op jit(solution)/shard_map/ppermute | solution.py:120
  137.1 1.0 slice.18
  138.1 0.1 collective-permute-start.6
  138.2 0.0 collective-permute-done.5.right_ref
  138.2 1.6 slice.19
  139.8 3.2 %collective-permute-start.7 = (bf16[128,896]{1,0:T(8,128)(2,1)}, bf16[128,896]{1,0:T(8,128)(2,1)}, u32[]{:S(2)}, u32[]{:S(2)}) collective-permute-start(bf16[128,896]{1,0:T(8,128)(2,1)} %slice.19), channel_id=1, source_target_pairs={{0,3},{1,0},{2,1},{3,2},{4,7},{5,4},{6,5},{7,6},{8,11},{9,8},{10,9... | collective-permute-start | bytes 688136 | tf_op jit(solution)/shard_map/ppermute | solution.py:120
  143.0 0.0 collective-permute-done.left_ref
  143.0 1.1 slice.16
  144.1 0.1 collective-permute-start.2
  144.2 0.0 collective-permute-done.1.right_ref
  144.2 1.1 slice.17
  145.3 3.5 %collective-permute-start.3 = (bf16[256,896]{1,0:T(8,128)(2,1)S(1)}, bf16[256,896]{1,0:T(8,128)(2,1)S(1)}, u32[]{:S(2)}, u32[]{:S(2)}) collective-permute-start(bf16[256,896]{1,0:T(8,128)(2,1)S(1)} %slice.17), channel_id=1, source_target_pairs={{0,3},{1,0},{2,1},{3,2},{4,7},{5,4},{6,5},{7,6},{8,11},{9,8},{10,9... | collective-permute-start | bytes 1376264 | tf_op jit(solution)/shard_map/ppermute | solution.py:120
  148.7 3.0 %collective-permute-done.6.o0_ref = bf16[128,896]{1,0:T(8,128)(2,1)} collective-permute-done((bf16[128,896]{1,0:T(8,128)(2,1)S(1)}, bf16[128,896]{1,0:T(8,128)(2,1)}, u32[]{:S(2)}, u32[]{:S(2)}) %collective-permute-start.6) | collective-permute-done | bytes 229408 | tf_op jit(solution)/shard_map/ppermute | solution.py:120
  151.7 0.0 collective-permute-done.7.o1_ref
  151.7 4.6 %shard_map.94 = bf16[256,256]{1,0:T(8,128)(2,1)} custom-call(s32[1]{0:T(128)} %bitcast.q_ref, bf16[256,896]{1,0:T(8,128)(2,1)} %copy-done.6, bf16[256,896]{1,0:T(8,128)(2,1)} %collective-permute-done.4.left_ref, bf16[256,896]{1,0:T(8,128)(2,1)} %collective-permute-done.5.right_ref, bf16[128,896]{1,0:T(8,128)(2,1)} %collective-permute-done.6.o0_ref, ...), custom_call_target="tpu_custom_call" | custom-call | tf_op jit(solution)/shard_map/pallas_call | solution.py:26
  156.3 0.0 all-to-all-done.8.refs_4_
  156.3 1.9 broadcast_in_dim.10
  158.2 3.5 %all-to-all-start.5 = ((bf16[4,256,256]{2,1,0:T(8,128)(2,1)}), bf16[4,256,256]{2,1,0:T(8,128)(2,1)S(1)}, u32[]{:S(2)}, u32[]{:S(2)}) async-start(bf16[4,256,256]{2,1,0:T(8,128)(2,1)} %broadcast_in_dim.10), calls=%async_computation.5 | async-start | bytes 1048576 | tf_op jit(solution)/shard_map/all_to_all | solution.py:111
  161.7 0.0 collective-permute-done.2.o0_ref
  161.7 0.0 collective-permute-done.3.o1_ref
  161.7 0.8 copy-done.8
  162.5 6.2 %shard_map.92 = bf16[512,256]{1,0:T(8,128)(2,1)} custom-call(s32[1]{0:T(128)} %bitcast.q_ref, bf16[512,896]{1,0:T(8,128)(2,1)} %bitcast.2.own_ref, bf16[512,896]{1,0:T(8,128)(2,1)} %collective-permute-done.left_ref, bf16[512,896]{1,0:T(8,128)(2,1)} %collective-permute-done.1.right_ref, bf16[256,896]{1,0:T(8,128)(2,1)} %collective-permute-done.2.o0_ref, ...), custom_call_target="tpu_custom_call" | custom-call | tf_op jit(solution)/shard_map/pallas_call | solution.py:26
  168.7 1.0 all-to-all-done.5.h_ref
  169.7 2.1 broadcast_in_dim.9
  171.9 3.7 %all-to-all-start.1 = ((bf16[4,512,256]{2,1,0:T(8,128)(2,1)}), bf16[4,512,256]{2,1,0:T(8,128)(2,1)S(1)}, u32[]{:S(2)}, u32[]{:S(2)}) async-start(bf16[4,512,256]{2,1,0:T(8,128)(2,1)} %broadcast_in_dim.9), calls=%async_computation.1 | async-start | bytes 2097152 | tf_op jit(solution)/shard_map/all_to_all | solution.py:111
  175.6 0.0 copy-done.5
  175.6 3.2 %shard_map.95 = bf16[256,896]{1,0:T(8,128)(2,1)} custom-call(bf16[4,256,256]{2,1,0:T(8,128)(2,1)} %copy-done.5, bf16[4,256,896]{2,1,0:T(8,128)(2,1)} %copy-done), custom_call_target="tpu_custom_call" | custom-call | tf_op jit(solution)/shard_map/pallas_call | solution.py:26
  178.7 1.9 reshape.54
  180.7 7.9 %all-to-all-done.1.h_ref = bf16[4,512,256]{2,1,0:T(8,128)(2,1)S(1)} async-done(((bf16[4,512,256]{2,1,0:T(8,128)(2,1)}), bf16[4,512,256]{2,1,0:T(8,128)(2,1)S(1)}, u32[]{:S(2)}, u32[]{:S(2)}) %all-to-all-start.1) | async-done | bytes 1048608 | tf_op jit(solution)/shard_map/all_to_all | solution.py:111
  188.6 8.4 %all-to-all-start.6 = ((bf16[64,4,896]{2,1,0:T(4,128)(2,1)}), bf16[64,4,896]{2,1,0:T(4,128)(2,1)S(1)}, u32[]{:S(2)}, u32[]{:S(2)}) async-start(bf16[64,4,896]{2,1,0:T(4,128)(2,1)} %reshape.54), calls=%async_computation.6 | async-start | bytes 917504 | tf_op jit(solution)/shard_map/all_to_all | solution.py:111
  197.0 0.0 copy-done.1
  197.0 4.0 %shard_map.93 = bf16[512,896]{1,0:T(8,128)(2,1)} custom-call(bf16[4,512,256]{2,1,0:T(8,128)(2,1)} %copy-done.1, bf16[4,256,896]{2,1,0:T(8,128)(2,1)} %copy-done), custom_call_target="tpu_custom_call" | custom-call | tf_op jit(solution)/shard_map/pallas_call | solution.py:26
  201.0 11.7 %all-to-all-done.6 = bf16[64,4,896]{2,1,0:T(4,128)(2,1)S(1)} async-done(((bf16[64,4,896]{2,1,0:T(4,128)(2,1)}), bf16[64,4,896]{2,1,0:T(4,128)(2,1)S(1)}, u32[]{:S(2)}, u32[]{:S(2)}) %all-to-all-start.6) | async-done | bytes 458784 | tf_op jit(solution)/shard_map/all_to_all | solution.py:111
  212.7 6.5 %all-to-all-start.3 = ((bf16[64,8,896]{2,1,0:T(8,128)(2,1)}), bf16[64,8,896]{2,1,0:T(8,128)(2,1)S(1)}, u32[]{:S(2)}, u32[]{:S(2)}) async-start(bf16[64,8,896]{2,1,0:T(8,128)(2,1)} %bitcast.18), calls=%async_computation.3 | async-start | bytes 1835008 | tf_op jit(solution)/shard_map/all_to_all | solution.py:111
  219.2 0.9 reshape.55.refs_3_
  220.1 24.4 %all-to-all-done.3 = bf16[64,8,896]{2,1,0:T(8,128)(2,1)S(1)} async-done(((bf16[64,8,896]{2,1,0:T(8,128)(2,1)}), bf16[64,8,896]{2,1,0:T(8,128)(2,1)S(1)}, u32[]{:S(2)}, u32[]{:S(2)}) %all-to-all-start.3) | async-done | bytes 917536 | tf_op jit(solution)/shard_map/all_to_all | solution.py:111
  244.5 0.9 copy-done.4
  245.4 2.7 %shard_map.97 = bf16[128,896]{1,0:T(8,128)(2,1)} custom-call(bf16[128,512]{1,0:T(8,128)(2,1)} %get-tuple-element.9.refs_0_, bf16[512,896]{1,0:T(8,128)(2,1)} %bitcast.17, bf16[128,256]{1,0:T(8,128)(2,1)} %get-tuple-element.11.refs_2_, bf16[256,896]{1,0:T(8,128)(2,1)} %reshape.55.refs_3_, bf16[4,128,896]{2,1,0:T(8,128)(2,1)} %copy-done.3), custom_call_target="tpu_custom_call" | custom-call | tf_op jit(solution)/shard_map/pallas_call | solution.py:26
  (13 shorter events, 0.0 us)
Async XLA Ops:
  0.0 6.4 %copy-start.9 = (s32[128,4]{0,1:T(4,128)S(1)}, s32[128,4]{0,1:T(4,128)}, u32[]{:S(2)}) copy-start(s32[128,4]{0,1:T(4,128)} %param.10) | copy-start | bytes 6148
  0.0 7.2 %copy-start.10 = (bf16[128,4]{0,1:T(4,128)(2,1)S(1)}, bf16[128,4]{0,1:T(4,128)(2,1)}, u32[]{:S(2)}) copy-start(bf16[128,4]{0,1:T(4,128)(2,1)} %param.11) | copy-start | bytes 3076
  2.0 18.2 %all-to-all-start.7 = ((bf16[4,128,896]{2,1,0:T(8,128)(2,1)}), bf16[4,128,896]{2,1,0:T(8,128)(2,1)S(1)}, u32[]{:S(2)}, u32[]{:S(2)}) async-start(bf16[4,128,896]{2,1,0:T(8,128)(2,1)} %broadcast_in_dim.11), calls=%async_computation.7 | async-start | bytes 1835008 | tf_op jit(solution)/shard_map/all_to_all | solution.py:111
  20.1 36.7 %copy-start.2 = (bf16[4,128,896]{2,1,0:T(8,128)(2,1)}, bf16[4,128,896]{2,1,0:T(8,128)(2,1)S(1)}, u32[]{:S(2)}) copy-start(bf16[4,128,896]{2,1,0:T(8,128)(2,1)S(1)} %all-to-all-done.7.x_ref) | copy-start | bytes 2752516
  47.3 31.9 %all-to-all-start = ((bf16[64,8,896]{2,1,0:T(8,128)(2,1)}), bf16[64,8,896]{2,1,0:T(8,128)(2,1)}, u32[]{:S(2)}, u32[]{:S(2)}) async-start(bf16[64,8,896]{2,1,0:T(8,128)(2,1)} %bitcast.1), calls=%async_computation | async-start | bytes 1835008 | tf_op jit(solution)/shard_map/all_to_all | solution.py:111
  79.2 7.0 %copy-start.7 = (bf16[64,4,896]{2,1,0:T(4,128)(2,1)S(1)}, bf16[64,4,896]{2,1,0:T(4,128)(2,1)}, u32[]{:S(2)}) copy-start(bf16[64,4,896]{2,1,0:T(4,128)(2,1)} %all_to_all.45) | copy-start | bytes 1376260
  79.2 28.7 %all-to-all-start.2 = ((bf16[4,256,896]{2,1,0:T(8,128)(2,1)}), bf16[4,256,896]{2,1,0:T(8,128)(2,1)S(1)}, u32[]{:S(2)}, u32[]{:S(2)}) async-start(bf16[4,256,896]{2,1,0:T(8,128)(2,1)} %bitcast.11), calls=%async_computation.2 | async-start | bytes 3670016 | tf_op jit(solution)/shard_map/all_to_all | solution.py:111
  82.9 60.1 %collective-permute-start = (bf16[512,896]{1,0:T(8,128)(2,1)}, bf16[512,896]{1,0:T(8,128)(2,1)}, u32[]{:S(2)}, u32[]{:S(2)}) collective-permute-start(bf16[512,896]{1,0:T(8,128)(2,1)} %bitcast.2.own_ref), channel_id=1, source_target_pairs={{0,1},{1,2},{2,3},{3,0},{4,5},{5,6},{6,7},{7,4},{8,9},{9,10},{10,1... | collective-permute-start | bytes 2752520 | tf_op jit(solution)/shard_map/ppermute | solution.py:120
  84.9 59.3 %collective-permute-start.1 = (bf16[512,896]{1,0:T(8,128)(2,1)}, bf16[512,896]{1,0:T(8,128)(2,1)}, u32[]{:S(2)}, u32[]{:S(2)}) collective-permute-start(bf16[512,896]{1,0:T(8,128)(2,1)} %bitcast.2.own_ref), channel_id=1, source_target_pairs={{0,3},{1,0},{2,1},{3,2},{4,7},{5,4},{6,5},{7,6},{8,11},{9,8},{10,9... | collective-permute-start | bytes 2752520 | tf_op jit(solution)/shard_map/ppermute | solution.py:120
  86.3 8.3 %copy-start.6 = (bf16[256,896]{1,0:T(8,128)(2,1)}, bf16[256,896]{1,0:T(8,128)(2,1)S(1)}, u32[]{:S(2)}) copy-start(bf16[256,896]{1,0:T(8,128)(2,1)S(1)} %reshape.53.own_ref) | copy-start | bytes 1376260
  86.4 50.8 %collective-permute-start.4 = (bf16[256,896]{1,0:T(8,128)(2,1)S(1)}, bf16[256,896]{1,0:T(8,128)(2,1)}, u32[]{:S(2)}, u32[]{:S(2)}) collective-permute-start(bf16[256,896]{1,0:T(8,128)(2,1)S(1)} %reshape.53.own_ref), channel_id=1, source_target_pairs={{0,1},{1,2},{2,3},{3,0},{4,5},{5,6},{6,7},{7,4},{8,9},{9,10},{10,1... | collective-permute-start | bytes 1376264 | tf_op jit(solution)/shard_map/ppermute | solution.py:120
  87.1 51.0 %collective-permute-start.5 = (bf16[256,896]{1,0:T(8,128)(2,1)S(1)}, bf16[256,896]{1,0:T(8,128)(2,1)}, u32[]{:S(2)}, u32[]{:S(2)}) collective-permute-start(bf16[256,896]{1,0:T(8,128)(2,1)S(1)} %reshape.53.own_ref), channel_id=1, source_target_pairs={{0,3},{1,0},{2,1},{3,2},{4,7},{5,4},{6,5},{7,6},{8,11},{9,8},{10,9... | collective-permute-start | bytes 1376264 | tf_op jit(solution)/shard_map/ppermute | solution.py:120
  107.9 36.2 %copy-start = (bf16[4,256,896]{2,1,0:T(8,128)(2,1)}, bf16[4,256,896]{2,1,0:T(8,128)(2,1)S(1)}, u32[]{:S(2)}) copy-start(bf16[4,256,896]{2,1,0:T(8,128)(2,1)S(1)} %all-to-all-done.2.down_ref) | copy-start | bytes 5505028
  107.9 48.5 %all-to-all-start.8 = ((bf16[4,128,896]{2,1,0:T(8,128)(2,1)}), bf16[4,128,896]{2,1,0:T(8,128)(2,1)S(1)}, u32[]{:S(2)}, u32[]{:S(2)}) async-start(bf16[4,128,896]{2,1,0:T(8,128)(2,1)} %shard_map.96), calls=%async_computation.8 | async-start | bytes 1835008 | tf_op jit(solution)/shard_map/all_to_all | solution.py:111
  138.1 13.6 %collective-permute-start.6 = (bf16[128,896]{1,0:T(8,128)(2,1)S(1)}, bf16[128,896]{1,0:T(8,128)(2,1)}, u32[]{:S(2)}, u32[]{:S(2)}) collective-permute-start(bf16[128,896]{1,0:T(8,128)(2,1)S(1)} %slice.18), channel_id=1, source_target_pairs={{0,1},{1,2},{2,3},{3,0},{4,5},{5,6},{6,7},{7,4},{8,9},{9,10},{10,1... | collective-permute-start | bytes 688136 | tf_op jit(solution)/shard_map/ppermute | solution.py:120
  139.8 11.9 %collective-permute-start.7 = (bf16[128,896]{1,0:T(8,128)(2,1)}, bf16[128,896]{1,0:T(8,128)(2,1)}, u32[]{:S(2)}, u32[]{:S(2)}) collective-permute-start(bf16[128,896]{1,0:T(8,128)(2,1)} %slice.19), channel_id=1, source_target_pairs={{0,3},{1,0},{2,1},{3,2},{4,7},{5,4},{6,5},{7,6},{8,11},{9,8},{10,9... | collective-permute-start | bytes 688136 | tf_op jit(solution)/shard_map/ppermute | solution.py:120
  144.1 17.5 %collective-permute-start.2 = (bf16[256,896]{1,0:T(8,128)(2,1)S(1)}, bf16[256,896]{1,0:T(8,128)(2,1)}, u32[]{:S(2)}, u32[]{:S(2)}) collective-permute-start(bf16[256,896]{1,0:T(8,128)(2,1)S(1)} %slice.16), channel_id=1, source_target_pairs={{0,1},{1,2},{2,3},{3,0},{4,5},{5,6},{6,7},{7,4},{8,9},{9,10},{10,1... | collective-permute-start | bytes 1376264 | tf_op jit(solution)/shard_map/ppermute | solution.py:120
  145.3 16.4 %collective-permute-start.3 = (bf16[256,896]{1,0:T(8,128)(2,1)S(1)}, bf16[256,896]{1,0:T(8,128)(2,1)S(1)}, u32[]{:S(2)}, u32[]{:S(2)}) collective-permute-start(bf16[256,896]{1,0:T(8,128)(2,1)S(1)} %slice.17), channel_id=1, source_target_pairs={{0,3},{1,0},{2,1},{3,2},{4,7},{5,4},{6,5},{7,6},{8,11},{9,8},{10,9... | collective-permute-start | bytes 1376264 | tf_op jit(solution)/shard_map/ppermute | solution.py:120
  156.3 12.4 %copy-start.3 = (bf16[4,128,896]{2,1,0:T(8,128)(2,1)}, bf16[4,128,896]{2,1,0:T(8,128)(2,1)S(1)}, u32[]{:S(2)}) copy-start(bf16[4,128,896]{2,1,0:T(8,128)(2,1)S(1)} %all-to-all-done.8.refs_4_) | copy-start | bytes 2752516
  158.2 11.5 %all-to-all-start.5 = ((bf16[4,256,256]{2,1,0:T(8,128)(2,1)}), bf16[4,256,256]{2,1,0:T(8,128)(2,1)S(1)}, u32[]{:S(2)}, u32[]{:S(2)}) async-start(bf16[4,256,256]{2,1,0:T(8,128)(2,1)} %broadcast_in_dim.10), calls=%async_computation.5 | async-start | bytes 1048576 | tf_op jit(solution)/shard_map/all_to_all | solution.py:111
  161.7 0.8 copy-start.8
  169.7 5.9 %copy-start.5 = (bf16[4,256,256]{2,1,0:T(8,128)(2,1)}, bf16[4,256,256]{2,1,0:T(8,128)(2,1)S(1)}, u32[]{:S(2)}) copy-start(bf16[4,256,256]{2,1,0:T(8,128)(2,1)S(1)} %all-to-all-done.5.h_ref) | copy-start | bytes 1572868
  171.9 16.7 %all-to-all-start.1 = ((bf16[4,512,256]{2,1,0:T(8,128)(2,1)}), bf16[4,512,256]{2,1,0:T(8,128)(2,1)S(1)}, u32[]{:S(2)}, u32[]{:S(2)}) async-start(bf16[4,512,256]{2,1,0:T(8,128)(2,1)} %broadcast_in_dim.9), calls=%async_computation.1 | async-start | bytes 2097152 | tf_op jit(solution)/shard_map/all_to_all | solution.py:111
  188.6 8.4 %copy-start.1 = (bf16[4,512,256]{2,1,0:T(8,128)(2,1)}, bf16[4,512,256]{2,1,0:T(8,128)(2,1)S(1)}, u32[]{:S(2)}) copy-start(bf16[4,512,256]{2,1,0:T(8,128)(2,1)S(1)} %all-to-all-done.1.h_ref) | copy-start | bytes 3145732
  188.6 24.1 %all-to-all-start.6 = ((bf16[64,4,896]{2,1,0:T(4,128)(2,1)}), bf16[64,4,896]{2,1,0:T(4,128)(2,1)S(1)}, u32[]{:S(2)}, u32[]{:S(2)}) async-start(bf16[64,4,896]{2,1,0:T(4,128)(2,1)} %reshape.54), calls=%async_computation.6 | async-start | bytes 917504 | tf_op jit(solution)/shard_map/all_to_all | solution.py:111
  212.7 31.8 %all-to-all-start.3 = ((bf16[64,8,896]{2,1,0:T(8,128)(2,1)}), bf16[64,8,896]{2,1,0:T(8,128)(2,1)S(1)}, u32[]{:S(2)}, u32[]{:S(2)}) async-start(bf16[64,8,896]{2,1,0:T(8,128)(2,1)} %bitcast.18), calls=%async_computation.3 | async-start | bytes 1835008 | tf_op jit(solution)/shard_map/all_to_all | solution.py:111
  244.5 0.9 copy-start.4

commit v2 on v1

v2 whole, which is shorter than its diff:
```python
import jax
import jax.numpy as jnp
from jax import lax
from jax.experimental import pallas as pl
from jax.experimental.pallas import tpu as pltpu
from jax.sharding import Mesh
from jax.sharding import PartitionSpec as P

EXPERT = ("expert_0", "expert_1", "expert_2")
CHUNKS = (4, 4, 4)
TURNS = (0, 3, 1, 2)
F32 = jnp.float32
BF16 = jnp.bfloat16


def dot(a, b):
    return jnp.dot(a, b, preferred_element_type=F32)


def flat(ref):
    x = ref[...]
    return x.reshape(-1, x.shape[-1])


def silu_times(gate, up):
    return (gate / (1.0 + jnp.exp(-gate)) * up).astype(BF16)


def kernel_call(body, outs, *args, smem=0, vmem=16, flops=1):
    specs = [pl.BlockSpec(memory_space=pltpu.SMEM) for _ in range(smem)]
    specs += [pl.BlockSpec(memory_space=pltpu.VMEM) for _ in args[smem:]]
    return pl.pallas_call(
        body,
        in_specs=specs,
        out_specs=[pl.BlockSpec(memory_space=pltpu.VMEM) for _ in outs],
        out_shape=[jax.ShapeDtypeStruct(o, BF16) for o in outs],
        compiler_params=pltpu.CompilerParams(vmem_limit_bytes=vmem << 20),
        cost_estimate=pl.CostEstimate(flops=flops, transcendentals=0, bytes_accessed=0),
    )(*args)


def block(ref, index, width):
    return ref[:, pl.ds(pl.multiple_of(index * width, 128), width)]


def columns_body(q_ref, x_ref, *outs):
    n = len(outs)
    for s, out_ref in enumerate(outs):
        out_ref[...] = block(x_ref, lax.rem(q_ref[0] + s, n), out_ref.shape[1])


def gather_body(experts, first):
    def body(ids_ref, tokens_ref, out_ref):
        ids = ids_ref[...]
        top, rows = ids.shape
        size = out_ref.shape[1]
        numbers = lax.broadcasted_iota(jnp.int32, (experts, rows), 0)
        onehot = [jnp.where(ids[k : k + 1] == numbers, 1.0, 0.0) for k in range(top)]
        per_token = sum(onehot[1:], onehot[0])
        before = lax.broadcasted_iota(jnp.int32, (rows, rows), 0) < lax.broadcasted_iota(
            jnp.int32, (rows, rows), 1
        )
        earlier = dot(per_token.astype(BF16), jnp.where(before, 1.0, 0.0).astype(BF16))
        place = lax.broadcasted_iota(jnp.int32, (experts * size, rows), 0)
        pick = jnp.zeros((experts * size, rows), F32)
        for k in range(top):
            slot = jnp.sum(onehot[k] * earlier, axis=0, keepdims=True).astype(jnp.int32)
            local = slot - first
            inside = (local >= 0) & (local < size)
            target = jnp.where(inside, ids[k : k + 1] * size + local, -1)
            pick = jnp.where(target == place, 1.0, pick)
        out_ref[...] = dot(pick.astype(BF16), tokens_ref[...]).astype(BF16).reshape(out_ref.shape)

    return body


def weight_body(experts):
    def body(ids_ref, gates_ref, out_ref):
        ids = ids_ref[...]
        gates = gates_ref[...].astype(F32)
        rows, top = ids.shape
        numbers = lax.broadcasted_iota(jnp.int32, (rows, experts), 1)
        onehot = [jnp.where(ids[:, k : k + 1] == numbers, 1.0, 0.0) for k in range(top)]
        per_token = sum(onehot[1:], onehot[0])
        before = lax.broadcasted_iota(jnp.int32, (rows, rows), 0) > lax.broadcasted_iota(
            jnp.int32, (rows, rows), 1
        )
        earlier = dot(jnp.where(before, 1.0, 0.0).astype(BF16), per_token.astype(BF16))
        slots = [
            jnp.sum(o * earlier, axis=1, keepdims=True).astype(jnp.int32) for o in onehot
        ]
        first = start = 0
        for size in CHUNKS:
            width = experts * size
            place = lax.broadcasted_iota(jnp.int32, (rows, width), 1)
            weight = jnp.zeros((rows, width), F32)
            for k in range(top):
                local = slots[k] - first
                inside = (local >= 0) & (local < size)
                target = jnp.where(inside, ids[:, k : k + 1] * size + local, -1)
                weight = jnp.where(target == place, gates[:, k : k + 1], weight)
            out_ref[:, start : start + width] = weight.astype(BF16)
            first += size
            start += width

    return body


def matmul_halves(q_ref, xs, gate_ref, up_ref):
    n = gate_ref.shape[0]
    at = [lax.rem(q_ref[0] + s, n) for s in TURNS]
    gate = sum(dot(x, gate_ref[i]) for x, i in zip(xs, at))
    up = sum(dot(x, up_ref[i]) for x, i in zip(xs, at))
    return silu_times(gate, up)


def shared_body(q_ref, *refs):
    n = len(TURNS)
    gate_ref, up_ref, down_ref = refs[n : n + 3]
    outs = refs[n + 3 :]
    hidden = matmul_halves(q_ref, [r[...] for r in refs[:n]], gate_ref, up_ref)
    for s, out_ref in enumerate(outs):
        part = block(down_ref, lax.rem(q_ref[0] + s, n), out_ref.shape[1])
        out_ref[...] = dot(hidden, part).astype(BF16)


def hidden_body(q_ref, *refs):
    n = len(TURNS)
    gate_ref, up_ref, out_ref = refs[n:]
    out_ref[...] = matmul_halves(q_ref, [flat(r) for r in refs[:n]], gate_ref, up_ref)


def down_body(*refs):
    *ins, out_ref = refs
    n = len(TURNS)
    total = sum(dot(h[...], w[...]) for h, w in zip(ins[:n], ins[n:]))
    out_ref[...] = total.astype(BF16).reshape(out_ref.shape)


def combine_body(weight_ref, *refs):
    *ins, out_ref = refs
    rows_refs, parts = ins[: len(CHUNKS)], ins[len(CHUNKS) :]
    total = sum(p[...].astype(F32) for p in parts)
    start = 0
    for rows_ref in rows_refs:
        rows = flat(rows_ref)
        total = total + dot(weight_ref[:, start : start + rows.shape[0]], rows)
        start += rows.shape[0]
    out_ref[...] = total.astype(BF16)


def exchange(x, axis):
    return lax.all_to_all(x, axis, split_axis=0, concat_axis=0, tiled=True)


def shift(x, axis, by):
    n = lax.axis_size(axis)
    return lax.ppermute(x, axis, [(i, (i + by) % n) for i in range(n)])


def spread(x):
    return [x, shift(x, "tensor", 1), shift(x, "tensor", -1), shift(x, "tensor", 2)]


def deal(xs):
    return [xs[0], shift(xs[1], "tensor", 1), shift(xs[3], "tensor", -1), shift(xs[2], "tensor", 2)]


def ring(x, turn):
    left = shift(x, "tensor", 1)
    right = shift(x, "tensor", -1)
    return [x, left, right, shift(left if turn == 1 else right, "tensor", turn)]


def per_device(tokens, expert_ids, gate_values, w_gate, w_up, w_down, *shared):
    return layer(tokens, expert_ids, gate_values, w_gate, w_up, w_down[0], *shared)


def layer(
    tokens, expert_ids, gate_values, w_gate, w_up, w_down, shared_gate, shared_up, shared_down
):
    tok_dev, narrow = tokens.shape
    _, _, quarter = w_gate.shape
    experts = lax.axis_size(EXPERT)
    n = lax.axis_size("tensor")
    q = lax.axis_index("tensor").reshape(1)
    w_gate = w_gate.reshape(n, narrow, quarter)
    w_up = w_up.reshape(n, narrow, quarter)

    ids_t = expert_ids.T
    arrived = []
    for j, size in enumerate(CHUNKS):
        (rows,) = kernel_call(
            gather_body(experts, sum(CHUNKS[:j])), [(experts, size, narrow)], ids_t, tokens
        )
        arrived.append(exchange(rows, EXPERT))
    tokens_all = spread(tokens)
    columns = kernel_call(columns_body, [(quarter, narrow)] * n, q, w_down, smem=1)
    down = deal(columns)
    (weight,) = kernel_call(
        weight_body(experts), [(tok_dev, experts * sum(CHUNKS))], expert_ids, gate_values
    )
    shared_parts = kernel_call(
        shared_body,
        [(tok_dev, narrow)] * n,
        q,
        *tokens_all,
        shared_gate.reshape(n, narrow, -1),
        shared_up.reshape(n, narrow, -1),
        shared_down,
        smem=1,
        flops=10**9,
    )

    returned = []
    for j, (rows, size) in enumerate(zip(arrived, CHUNKS)):
        rows_all = ring(rows, 1 - 2 * (j % 2))
        (hidden,) = kernel_call(
            hidden_body,
            [(experts * size, quarter)],
            q,
            *rows_all,
            w_gate,
            w_up,
            smem=1,
            flops=10**9,
        )
        hidden_all = spread(hidden)
        (out,) = kernel_call(down_body, [(experts, size, narrow)], *hidden_all, *down, flops=10**9)
        returned.append(exchange(out, EXPERT))
    shared_all = deal(shared_parts)
    return kernel_call(combine_body, [(tok_dev, narrow)], weight, *returned, *shared_all)[0]


def solution(mesh):
    torus = Mesh(
        mesh.devices.reshape(4, 8, 2, mesh.shape["tensor"]),
        ("expert_0", "expert_1", "expert_2", "tensor"),
    )
    placed = (
        P(EXPERT, "tensor"),
        P(EXPERT, None),
        P(EXPERT, None),
        P(EXPERT, None, "tensor"),
        P(EXPERT, None, "tensor"),
        P(EXPERT, "tensor", None),
        P(None, "tensor"),
        P(None, "tensor"),
        P("tensor", None),
    )
    return jax.shard_map(
        per_device, mesh=torus, in_specs=placed, out_specs=P(EXPERT, "tensor"), check_vma=False
    )
```

time: 251 us -> 242 us (0.964)
  starting transfers between devices: 53.9 us -> 91 us
  blocking collectives: 27.2 us -> 0 us
  Pallas kernels: 28.9 us -> 16.2 us
  local copies, waits for them, and re-layouts: 23.2 us -> 20.4 us
    all_to_all x8 -> x6, waiting for transfers between devices: 86.1 us -> 26.4 us  [exchange(): return lax.all_to_all(x, axis, split_axis=0, concat_axis=0, tiled=True)]
    ppermute x8 -> x27, waiting for transfers between devices: 28.7 us -> 86.8 us  [shift(): return lax.ppermute(x, axis, [(i, (i + by) % n) for i in range(n)])]
    all_to_all x1 -> x0, blocking collectives: 27.2 us -> none  [exchange(): return lax.all_to_all(x, axis, split_axis=0, concat_axis=0, tiled=True)]
    ppermute x8 -> x27, starting transfers between devices: 13.5 us -> 35.4 us  [shift(): return lax.ppermute(x, axis, [(i, (i + by) % n) for i in range(n)])]
    all_to_all x8 -> x6, starting transfers between devices: 40.4 us -> 55.6 us  [exchange(): return lax.all_to_all(x, axis, split_axis=0, concat_axis=0, tiled=True)]
    unnamed x25 -> x66, local copies, waits for them, and re-layouts: 6.09 us -> 20.4 us
    pallas_call x7 -> x13, Pallas kernels: 28.9 us -> 16.2 us  [kernel_call(): pl.pallas_call(body, in_specs=specs, out_specs=[pl.BlockSpec(memory_space...]
    reshape x5 -> x0, local copies, waits for them, and re-layouts: 6.4 us -> none  [the longest x1 2.38 us: per_device(): w_down.reshape(quarter, n, narrow)]
  transfers between devices with their start and end apart: 16 -> 33, of which waited for: 9 -> 22; matrix products, arithmetic and copies ran while one was open for 7% -> 0% of each run, Pallas kernels for 11% -> 6%
where the time goes in v2:
time: 242 us; the launch traced here: 241 us
  waiting for transfers between devices  113 us (47%)
  starting transfers between devices  91 us (38%)
  local copies, waits for them, and re-layouts  20.4 us (8%)
  Pallas kernels  16.2 us (7%)
    ppermute x27, waiting for transfers between devices, shift(): return lax.ppermute(x, axis, [(i, (i + by) % n) for i in range(n)])  86.8 us
    all_to_all x6, starting transfers between devices, exchange(): return lax.all_to_all(x, axis, split_axis=0, concat_axis=0, tiled=True)  55.6 us
    ppermute x27, starting transfers between devices, shift(): return lax.ppermute(x, axis, [(i, (i + by) % n) for i in range(n)])  35.4 us
    all_to_all x6, waiting for transfers between devices, exchange(): return lax.all_to_all(x, axis, split_axis=0, concat_axis=0, tiled=True)  26.4 us
    unnamed x66, local copies, waits for them, and re-layouts  20.4 us
    pallas_call x13, Pallas kernels, kernel_call(): pl.pallas_call(body, in_specs=specs, out_specs=[pl.BlockSpec(memory_space...  16.2 us
  transfers between devices with their start and end apart: 33, of which 22 were waited for; matrix products, arithmetic and copies ran while one was open for 0% of the time, Pallas kernels for 6%

profile of v2, /device:TPU:32, one launch (start us, length us, event | category | flops | bytes accessed | tf_op | source)
XLA Modules:
  0.0 240.9 jit_solution(9468063488245769326)
XLA Ops:
  0.0 0.9 copy-done.4
  1.6 1.2 shard_map.99
  2.8 11.6 %all-to-all-start.4 = ((bf16[64,4,896]{2,1,0:T(4,128)(2,1)}), bf16[64,4,896]{2,1,0:T(4,128)(2,1)S(1)}, u32[]{:S(2)}, u32[]{:S(2)}) async-start(bf16[64,4,896]{2,1,0:T(4,128)(2,1)} %shard_map.99), calls=%async_computation.4 | async-start | bytes 917504 | tf_op jit(solution)/shard_map/all_to_all | solution.py:153
  14.4 0.9 copy-done.5
  15.4 1.2 shard_map.96
  16.6 13.5 %all-to-all-done.4.refs_0_ = bf16[64,4,896]{2,1,0:T(4,128)(2,1)S(1)} async-done(((bf16[64,4,896]{2,1,0:T(4,128)(2,1)}), bf16[64,4,896]{2,1,0:T(4,128)(2,1)S(1)}, u32[]{:S(2)}, u32[]{:S(2)}) %all-to-all-start.4) | async-done | bytes 458784 | tf_op jit(solution)/shard_map/all_to_all | solution.py:153
  30.1 6.5 %all-to-all-start.2 = ((bf16[64,4,896]{2,1,0:T(4,128)(2,1)}), bf16[64,4,896]{2,1,0:T(4,128)(2,1)S(1)}, u32[]{:S(2)}, u32[]{:S(2)}) async-start(bf16[64,4,896]{2,1,0:T(4,128)(2,1)} %shard_map.96), calls=%async_computation.2 | async-start | bytes 917504 | tf_op jit(solution)/shard_map/all_to_all | solution.py:153
  36.6 1.7 collective-permute-start.15
  38.7 0.8 copy-done.7
  39.5 12.8 %all-to-all-done.2.refs_0_ = bf16[64,4,896]{2,1,0:T(4,128)(2,1)S(1)} async-done(((bf16[64,4,896]{2,1,0:T(4,128)(2,1)}), bf16[64,4,896]{2,1,0:T(4,128)(2,1)S(1)}, u32[]{:S(2)}, u32[]{:S(2)}) %all-to-all-start.2) | async-done | bytes 458784 | tf_op jit(solution)/shard_map/all_to_all | solution.py:153
  52.3 6.5 %all-to-all-start = ((bf16[64,4,896]{2,1,0:T(4,128)(2,1)}), bf16[64,4,896]{2,1,0:T(4,128)(2,1)S(1)}, u32[]{:S(2)}, u32[]{:S(2)}) async-start(bf16[64,4,896]{2,1,0:T(4,128)(2,1)} %copy-done.7), calls=%async_computation | async-start | bytes 917504 | tf_op jit(solution)/shard_map/all_to_all | solution.py:153
  58.8 3.1 %collective-permute-start.16 = (bf16[64,4,896]{2,1,0:T(4,128)(2,1)S(1)}, bf16[64,4,896]{2,1,0:T(4,128)(2,1)}, u32[]{:S(2)}, u32[]{:S(2)}) collective-permute-start(bf16[64,4,896]{2,1,0:T(4,128)(2,1)S(1)} %all-to-all-done.4.refs_0_), channel_id=1, source_target_pairs={{0,3},{1,0},{2,1},{3,2},{4,7},{5,4},{6,5},{7,6},{8,11},{9,8},{10,9... | collective-permute-start | bytes 1376264 | tf_op jit(solution)/shard_map/ppermute | solution.py:158
  61.9 1.5 copy-done.8
  64.2 2.7 %collective-permute-start.7 = (bf16[256,896]{1,0:T(8,128)(2,1)S(1)}, bf16[256,896]{1,0:T(8,128)(2,1)S(1)}, u32[]{:S(2)}, u32[]{:S(2)}) collective-permute-start(bf16[256,896]{1,0:T(8,128)(2,1)S(1)} %get-tuple-element.15), channel_id=1, source_target_pairs={{0,3},{1,0},{2,1},{3,2},{4,7},{5,4},{6,5},{7,6},{8,11},{9,8},{10,9... | collective-permute-start | bytes 1376264 | tf_op jit(solution)/shard_map/ppermute | solution.py:158
  67.0 1.4 collective-permute-start.8
  68.3 4.5 %collective-permute-done.16.refs_2_ = bf16[64,4,896]{2,1,0:T(4,128)(2,1)} collective-permute-done((bf16[64,4,896]{2,1,0:T(4,128)(2,1)S(1)}, bf16[64,4,896]{2,1,0:T(4,128)(2,1)}, u32[]{:S(2)}, u32[]{:S(2)}) %collective-permute-start.16) | collective-permute-done | bytes 458784 | tf_op jit(solution)/shard_map/ppermute | solution.py:158
  72.8 3.8 %collective-permute-start.10 = (bf16[64,4,896]{2,1,0:T(4,128)(2,1)S(1)}, bf16[64,4,896]{2,1,0:T(4,128)(2,1)}, u32[]{:S(2)}, u32[]{:S(2)}) collective-permute-start(bf16[64,4,896]{2,1,0:T(4,128)(2,1)S(1)} %all-to-all-done.2.refs_0_), channel_id=1, source_target_pairs={{0,3},{1,0},{2,1},{3,2},{4,7},{5,4},{6,5},{7,6},{8,11},{9,8},{10,9... | collective-permute-start | bytes 1376264 | tf_op jit(solution)/shard_map/ppermute | solution.py:158
  76.8 1.5 copy-done.1
  78.3 2.6 %shard_map.100.refs_0_ = bf16[256,256]{1,0:T(8,128)(2,1)S(1)} custom-call(s32[1]{0:T(128)} %bitcast.q_ref, bf16[64,4,896]{2,1,0:T(4,128)(2,1)S(1)} %all-to-all-done.4.refs_0_, bf16[64,4,896]{2,1,0:T(4,128)(2,1)} %collective-permute-done.15.refs_1_, bf16[64,4,896]{2,1,0:T(4,128)(2,1)} %collective-permute-done.16.refs_2_, ...), custom_call_target="tpu_custom_call" | custom-call | flops 1000000000 | tf_op jit(solution)/shard_map/pallas_call | solution.py:32
  81.0 15.8 %collective-permute-done.6.refs_5_ = bf16[256,896]{1,0:T(8,128)(2,1)S(1)} collective-permute-done((bf16[256,896]{1,0:T(8,128)(2,1)S(1)}, bf16[256,896]{1,0:T(8,128)(2,1)S(1)}, u32[]{:S(2)}, u32[]{:S(2)}) %collective-permute-start.6) | collective-permute-done | bytes 458784 | tf_op jit(solution)/shard_map/ppermute | solution.py:158
  96.8 2.6 %collective-permute-done.18.refs_1_ = bf16[256,256]{1,0:T(8,128)(2,1)S(1)} collective-permute-done((bf16[256,256]{1,0:T(8,128)(2,1)S(1)}, bf16[256,256]{1,0:T(8,128)(2,1)S(1)}, u32[]{:S(2)}, u32[]{:S(2)}) %collective-permute-start.18) | collective-permute-done | bytes 131104 | tf_op jit(solution)/shard_map/ppermute | solution.py:158
  99.5 7.6 %collective-permute-done.19.refs_2_ = bf16[256,256]{1,0:T(8,128)(2,1)S(1)} collective-permute-done((bf16[256,256]{1,0:T(8,128)(2,1)S(1)}, bf16[256,256]{1,0:T(8,128)(2,1)S(1)}, u32[]{:S(2)}, u32[]{:S(2)}) %collective-permute-start.19) | collective-permute-done | bytes 131104 | tf_op jit(solution)/shard_map/ppermute | solution.py:158
  107.8 0.8 copy-done.13
  109.3 0.8 copy-done.25
  110.1 0.8 copy-done.28
  110.9 10.3 %all-to-all-start.5 = ((bf16[64,4,896]{2,1,0:T(4,128)(2,1)}), bf16[64,4,896]{2,1,0:T(4,128)(2,1)S(1)}, u32[]{:S(2)}, u32[]{:S(2)}) async-start(bf16[64,4,896]{2,1,0:T(4,128)(2,1)} %copy-done.13), calls=%async_computation.5 | async-start | bytes 917504 | tf_op jit(solution)/shard_map/all_to_all | solution.py:153
  121.2 2.2 collective-permute-start.9
  123.4 1.7 collective-permute-start.11
  125.4 10.9 %collective-permute-done.9.refs_1_ = bf16[64,4,896]{2,1,0:T(4,128)(2,1)S(1)} collective-permute-done((bf16[64,4,896]{2,1,0:T(4,128)(2,1)S(1)}, bf16[64,4,896]{2,1,0:T(4,128)(2,1)S(1)}, u32[]{:S(2)}, u32[]{:S(2)}) %collective-permute-start.9) | collective-permute-done | bytes 458784 | tf_op jit(solution)/shard_map/ppermute | solution.py:158
  136.4 1.5 copy-done.2
  137.9 2.4 %shard_map.97.refs_0_ = bf16[256,256]{1,0:T(8,128)(2,1)S(1)} custom-call(s32[1]{0:T(128)} %bitcast.q_ref, bf16[64,4,896]{2,1,0:T(4,128)(2,1)S(1)} %all-to-all-done.2.refs_0_, bf16[64,4,896]{2,1,0:T(4,128)(2,1)S(1)} %collective-permute-done.9.refs_1_, bf16[64,4,896]{2,1,0:T(4,128)(2,1)} %collective-permute-done.10.refs_2_, ...), custom_call_target="tpu_custom_call" | custom-call | flops 1000000000 | tf_op jit(solution)/shard_map/pallas_call | solution.py:32
  140.3 0.9 collective-permute-start.12
  141.2 2.5 %collective-permute-start.13 = (bf16[256,256]{1,0:T(8,128)(2,1)S(1)}, bf16[256,256]{1,0:T(8,128)(2,1)S(1)}, u32[]{:S(2)}, u32[]{:S(2)}) collective-permute-start(bf16[256,256]{1,0:T(8,128)(2,1)S(1)} %shard_map.97.refs_0_), channel_id=1, source_target_pairs={{0,3},{1,0},{2,1},{3,2},{4,7},{5,4},{6,5},{7,6},{8,11},{9,8},{10,9... | collective-permute-start | bytes 393224 | tf_op jit(solution)/shard_map/ppermute | solution.py:158
  143.6 1.4 collective-permute-start.14
  145.0 3.5 %collective-permute-done.12.refs_1_ = bf16[256,256]{1,0:T(8,128)(2,1)S(1)} collective-permute-done((bf16[256,256]{1,0:T(8,128)(2,1)S(1)}, bf16[256,256]{1,0:T(8,128)(2,1)S(1)}, u32[]{:S(2)}, u32[]{:S(2)}) %collective-permute-start.12) | collective-permute-done | bytes 131104 | tf_op jit(solution)/shard_map/ppermute | solution.py:158
  148.7 3.7 %collective-permute-done.14.refs_3_ = bf16[256,256]{1,0:T(8,128)(2,1)S(1)} collective-permute-done((bf16[256,256]{1,0:T(8,128)(2,1)S(1)}, bf16[256,256]{1,0:T(8,128)(2,1)S(1)}, u32[]{:S(2)}, u32[]{:S(2)}) %collective-permute-start.14) | collective-permute-done | bytes 131104 | tf_op jit(solution)/shard_map/ppermute | solution.py:158
  153.2 0.8 copy-done.14
  153.9 10.3 %all-to-all-start.3 = ((bf16[64,4,896]{2,1,0:T(4,128)(2,1)}), bf16[64,4,896]{2,1,0:T(4,128)(2,1)S(1)}, u32[]{:S(2)}, u32[]{:S(2)}) async-start(bf16[64,4,896]{2,1,0:T(4,128)(2,1)} %copy-done.14), calls=%async_computation.3 | async-start | bytes 917504 | tf_op jit(solution)/shard_map/all_to_all | solution.py:153
  164.4 2.0 collective-permute-start.2
  166.4 10.5 %collective-permute-done.1.refs_2_ = bf16[64,4,896]{2,1,0:T(4,128)(2,1)S(1)} collective-permute-done((bf16[64,4,896]{2,1,0:T(4,128)(2,1)S(1)}, bf16[64,4,896]{2,1,0:T(4,128)(2,1)S(1)}, u32[]{:S(2)}, u32[]{:S(2)}) %collective-permute-start.1) | collective-permute-done | bytes 458784 | tf_op jit(solution)/shard_map/ppermute | solution.py:158
  176.9 1.5 collective-permute-done.2.refs_3_
  178.4 1.5 copy-done.3
  179.9 2.4 %shard_map.93.refs_0_ = bf16[256,256]{1,0:T(8,128)(2,1)S(1)} custom-call(s32[1]{0:T(128)} %bitcast.q_ref, bf16[64,4,896]{2,1,0:T(4,128)(2,1)S(1)} %all-to-all-done.refs_0_, bf16[64,4,896]{2,1,0:T(4,128)(2,1)} %collective-permute-done.refs_1_, bf16[64,4,896]{2,1,0:T(4,128)(2,1)S(1)} %collective-permute-done.1.refs_2_, ...), custom_call_target="tpu_custom_call" | custom-call | flops 1000000000 | tf_op jit(solution)/shard_map/pallas_call | solution.py:32
  182.9 2.8 %collective-permute-start.4 = (bf16[256,256]{1,0:T(8,128)(2,1)S(1)}, bf16[256,256]{1,0:T(8,128)(2,1)S(1)}, u32[]{:S(2)}, u32[]{:S(2)}) collective-permute-start(bf16[256,256]{1,0:T(8,128)(2,1)S(1)} %shard_map.93.refs_0_), channel_id=1, source_target_pairs={{0,3},{1,0},{2,1},{3,2},{4,7},{5,4},{6,5},{7,6},{8,11},{9,8},{10,9... | collective-permute-start | bytes 393224 | tf_op jit(solution)/shard_map/ppermute | solution.py:158
  185.7 4.3 %collective-permute-done.3.refs_1_ = bf16[256,256]{1,0:T(8,128)(2,1)S(1)} collective-permute-done((bf16[256,256]{1,0:T(8,128)(2,1)S(1)}, bf16[256,256]{1,0:T(8,128)(2,1)S(1)}, u32[]{:S(2)}, u32[]{:S(2)}) %collective-permute-start.3) | collective-permute-done | bytes 131104 | tf_op jit(solution)/shard_map/ppermute | solution.py:158
  190.4 1.7 collective-permute-done.5.refs_3_
  192.9 0.8 copy-done.12
  193.7 10.3 %all-to-all-start.1 = ((bf16[64,4,896]{2,1,0:T(4,128)(2,1)}), bf16[64,4,896]{2,1,0:T(4,128)(2,1)S(1)}, u32[]{:S(2)}, u32[]{:S(2)}) async-start(bf16[64,4,896]{2,1,0:T(4,128)(2,1)} %copy-done.12), calls=%async_computation.1 | async-start | bytes 917504 | tf_op jit(solution)/shard_map/all_to_all | solution.py:153
  204.1 3.2 %collective-permute-start.22 = (bf16[128,896]{1,0:T(8,128)(2,1)S(1)}, bf16[128,896]{1,0:T(8,128)(2,1)S(1)}, u32[]{:S(2)}, u32[]{:S(2)}) collective-permute-start(bf16[128,896]{1,0:T(8,128)(2,1)S(1)} %copy-done.6), channel_id=1, source_target_pairs={{0,3},{1,0},{2,1},{3,2},{4,7},{5,4},{6,5},{7,6},{8,11},{9,8},{10,9... | collective-permute-start | bytes 688136 | tf_op jit(solution)/shard_map/ppermute | solution.py:158
  207.5 6.1 %collective-permute-done.21.refs_1_ = bf16[128,896]{1,0:T(8,128)(2,1)S(1)} collective-permute-done((bf16[128,896]{1,0:T(8,128)(2,1)S(1)}, bf16[128,896]{1,0:T(8,128)(2,1)S(1)}, u32[]{:S(2)}, u32[]{:S(2)}) %collective-permute-start.21) | collective-permute-done | bytes 229408 | tf_op jit(solution)/shard_map/ppermute | solution.py:158
  213.6 3.5 %collective-permute-done.22.refs_2_ = bf16[128,896]{1,0:T(8,128)(2,1)S(1)} collective-permute-done((bf16[128,896]{1,0:T(8,128)(2,1)S(1)}, bf16[128,896]{1,0:T(8,128)(2,1)S(1)}, u32[]{:S(2)}, u32[]{:S(2)}) %collective-permute-start.22) | collective-permute-done | bytes 229408 | tf_op jit(solution)/shard_map/ppermute | solution.py:158
  217.1 0.9 collective-permute-done.23.refs_3_
  218.0 1.5 copy-done.9
  219.5 1.5 copy-done.10
  221.0 1.5 copy-done.11
  222.5 1.8 shard_map.102
  225.1 1.1 collective-permute-start.24
  226.2 2.1 collective-permute-start.25
  228.3 1.0 collective-permute-start.26
  230.3 4.2 %collective-permute-done.24.refs_4_ = bf16[128,896]{1,0:T(8,128)(2,1)S(1)} collective-permute-done((bf16[128,896]{1,0:T(8,128)(2,1)}, bf16[128,896]{1,0:T(8,128)(2,1)S(1)}, u32[]{:S(2)}, u32[]{:S(2)}) %collective-permute-start.24) | collective-permute-done | bytes 229408 | tf_op jit(solution)/shard_map/ppermute | solution.py:158
  234.5 3.1 %collective-permute-done.25.refs_5_ = bf16[128,896]{1,0:T(8,128)(2,1)S(1)} collective-permute-done((bf16[128,896]{1,0:T(8,128)(2,1)}, bf16[128,896]{1,0:T(8,128)(2,1)S(1)}, u32[]{:S(2)}, u32[]{:S(2)}) %collective-permute-start.25) | collective-permute-done | bytes 229408 | tf_op jit(solution)/shard_map/ppermute | solution.py:158
  237.6 1.3 collective-permute-done.26.refs_6_
  238.9 0.9 copy-done.16
  239.9 1.1 shard_map.103
  (81 shorter events, 8.8 us)
Async XLA Ops:
  0.0 0.9 copy-start.4
  1.6 36.7 %copy-start.6 = (bf16[128,896]{1,0:T(8,128)(2,1)S(1)}, bf16[128,896]{1,0:T(8,128)(2,1)}, u32[]{:S(2)}) copy-start(bf16[128,896]{1,0:T(8,128)(2,1)} %refs_0_.1) | copy-start | bytes 688132
  1.6 36.7 %copy-start.18 = (s32[128,4]{0,1:T(4,128)S(1)}, s32[128,4]{0,1:T(4,128)}, u32[]{:S(2)}) copy-start(s32[128,4]{0,1:T(4,128)} %param.10) | copy-start | bytes 6148
  2.8 27.3 %all-to-all-start.4 = ((bf16[64,4,896]{2,1,0:T(4,128)(2,1)}), bf16[64,4,896]{2,1,0:T(4,128)(2,1)S(1)}, u32[]{:S(2)}, u32[]{:S(2)}) async-start(bf16[64,4,896]{2,1,0:T(4,128)(2,1)} %shard_map.99), calls=%async_computation.4 | async-start | bytes 917504 | tf_op jit(solution)/shard_map/all_to_all | solution.py:153
  14.4 0.9 copy-start.5
  30.1 22.2 %all-to-all-start.2 = ((bf16[64,4,896]{2,1,0:T(4,128)(2,1)}), bf16[64,4,896]{2,1,0:T(4,128)(2,1)S(1)}, u32[]{:S(2)}, u32[]{:S(2)}) async-start(bf16[64,4,896]{2,1,0:T(4,128)(2,1)} %shard_map.96), calls=%async_computation.2 | async-start | bytes 917504 | tf_op jit(solution)/shard_map/all_to_all | solution.py:153
  36.6 40.2 %copy-start = (bf16[1,3584,256]{2,1,0:T(8,128)(2,1)S(1)}, bf16[1,3584,256]{2,1,0:T(8,128)(2,1)}, u32[]{:S(2)}) copy-start(bf16[1,3584,256]{2,1,0:T(8,128)(2,1)} %param.12) | copy-start | bytes 5505028
  36.6 25.3 %collective-permute-start.15 = (bf16[64,4,896]{2,1,0:T(4,128)(2,1)S(1)}, bf16[64,4,896]{2,1,0:T(4,128)(2,1)}, u32[]{:S(2)}, u32[]{:S(2)}) collective-permute-start(bf16[64,4,896]{2,1,0:T(4,128)(2,1)S(1)} %all-to-all-done.4.refs_0_), channel_id=1, source_target_pairs={{0,1},{1,2},{2,3},{3,0},{4,5},{5,6},{6,7},{7,4},{8,9},{9,10},{10,1... | collective-permute-start | bytes 1376264 | tf_op jit(solution)/shard_map/ppermute | solution.py:158
  38.7 0.8 copy-start.7
  52.3 58.6 %all-to-all-start = ((bf16[64,4,896]{2,1,0:T(4,128)(2,1)}), bf16[64,4,896]{2,1,0:T(4,128)(2,1)S(1)}, u32[]{:S(2)}, u32[]{:S(2)}) async-start(bf16[64,4,896]{2,1,0:T(4,128)(2,1)} %copy-done.7), calls=%async_computation | async-start | bytes 917504 | tf_op jit(solution)/shard_map/all_to_all | solution.py:153
  58.8 14.0 %collective-permute-start.16 = (bf16[64,4,896]{2,1,0:T(4,128)(2,1)S(1)}, bf16[64,4,896]{2,1,0:T(4,128)(2,1)}, u32[]{:S(2)}, u32[]{:S(2)}) collective-permute-start(bf16[64,4,896]{2,1,0:T(4,128)(2,1)S(1)} %all-to-all-done.4.refs_0_), channel_id=1, source_target_pairs={{0,3},{1,0},{2,1},{3,2},{4,7},{5,4},{6,5},{7,6},{8,11},{9,8},{10,9... | collective-permute-start | bytes 1376264 | tf_op jit(solution)/shard_map/ppermute | solution.py:158
  61.9 14.9 %collective-permute-start.17 = (bf16[64,4,896]{2,1,0:T(4,128)(2,1)}, bf16[64,4,896]{2,1,0:T(4,128)(2,1)}, u32[]{:S(2)}, u32[]{:S(2)}) collective-permute-start(bf16[64,4,896]{2,1,0:T(4,128)(2,1)} %collective-permute-done.15.refs_1_), channel_id=1, source_target_pairs={{0,1},{1,2},{2,3},{3,0},{4,5},{5,6},{6,7},{7,4},{8,9},{9,10},{10,1... | collective-permute-start | bytes 1376264 | tf_op jit(solution)/shard_map/ppermute | solution.py:158
  61.9 1.5 copy-start.8
  63.5 43.5 %copy-start.19 = (bf16[256,896]{1,0:T(8,128)(2,1)}, bf16[256,896]{1,0:T(8,128)(2,1)S(1)}, u32[]{:S(2)}) copy-start(bf16[256,896]{1,0:T(8,128)(2,1)S(1)} %get-tuple-element.13.refs_4_) | copy-start | bytes 1376260
  63.6 33.3 %collective-permute-start.6 = (bf16[256,896]{1,0:T(8,128)(2,1)S(1)}, bf16[256,896]{1,0:T(8,128)(2,1)S(1)}, u32[]{:S(2)}, u32[]{:S(2)}) collective-permute-start(bf16[256,896]{1,0:T(8,128)(2,1)S(1)} %get-tuple-element.14), channel_id=1, source_target_pairs={{0,1},{1,2},{2,3},{3,0},{4,5},{5,6},{6,7},{7,4},{8,9},{9,10},{10,1... | collective-permute-start | bytes 1376264 | tf_op jit(solution)/shard_map/ppermute | solution.py:158
  64.2 32.6 %collective-permute-start.7 = (bf16[256,896]{1,0:T(8,128)(2,1)S(1)}, bf16[256,896]{1,0:T(8,128)(2,1)S(1)}, u32[]{:S(2)}, u32[]{:S(2)}) collective-permute-start(bf16[256,896]{1,0:T(8,128)(2,1)S(1)} %get-tuple-element.15), channel_id=1, source_target_pairs={{0,3},{1,0},{2,1},{3,2},{4,7},{5,4},{6,5},{7,6},{8,11},{9,8},{10,9... | collective-permute-start | bytes 1376264 | tf_op jit(solution)/shard_map/ppermute | solution.py:158
  67.0 29.9 %collective-permute-start.8 = (bf16[256,896]{1,0:T(8,128)(2,1)S(1)}, bf16[256,896]{1,0:T(8,128)(2,1)S(1)}, u32[]{:S(2)}, u32[]{:S(2)}) collective-permute-start(bf16[256,896]{1,0:T(8,128)(2,1)S(1)} %get-tuple-element.16), channel_id=1, source_target_pairs={{0,2},{1,3},{2,0},{3,1},{4,6},{5,7},{6,4},{7,5},{8,10},{9,11},{10,... | collective-permute-start | bytes 1376264 | tf_op jit(solution)/shard_map/ppermute | solution.py:158
  72.8 50.6 %collective-permute-start.10 = (bf16[64,4,896]{2,1,0:T(4,128)(2,1)S(1)}, bf16[64,4,896]{2,1,0:T(4,128)(2,1)}, u32[]{:S(2)}, u32[]{:S(2)}) collective-permute-start(bf16[64,4,896]{2,1,0:T(4,128)(2,1)S(1)} %all-to-all-done.2.refs_0_), channel_id=1, source_target_pairs={{0,3},{1,0},{2,1},{3,2},{4,7},{5,4},{6,5},{7,6},{8,11},{9,8},{10,9... | collective-permute-start | bytes 1376264 | tf_op jit(solution)/shard_map/ppermute | solution.py:158
  76.8 1.5 copy-start.1
  80.9 18.6 %collective-permute-start.18 = (bf16[256,256]{1,0:T(8,128)(2,1)S(1)}, bf16[256,256]{1,0:T(8,128)(2,1)S(1)}, u32[]{:S(2)}, u32[]{:S(2)}) collective-permute-start(bf16[256,256]{1,0:T(8,128)(2,1)S(1)} %shard_map.100.refs_0_), channel_id=1, source_target_pairs={{0,1},{1,2},{2,3},{3,0},{4,5},{5,6},{6,7},{7,4},{8,9},{9,10},{10,1... | collective-permute-start | bytes 393224 | tf_op jit(solution)/shard_map/ppermute | solution.py:158
  96.8 10.3 %collective-permute-start.19 = (bf16[256,256]{1,0:T(8,128)(2,1)S(1)}, bf16[256,256]{1,0:T(8,128)(2,1)S(1)}, u32[]{:S(2)}, u32[]{:S(2)}) collective-permute-start(bf16[256,256]{1,0:T(8,128)(2,1)S(1)} %shard_map.100.refs_0_), channel_id=1, source_target_pairs={{0,3},{1,0},{2,1},{3,2},{4,7},{5,4},{6,5},{7,6},{8,11},{9,8},{10,9... | collective-permute-start | bytes 393224 | tf_op jit(solution)/shard_map/ppermute | solution.py:158
  96.8 10.3 %collective-permute-start.20 = (bf16[256,256]{1,0:T(8,128)(2,1)S(1)}, bf16[256,256]{1,0:T(8,128)(2,1)S(1)}, u32[]{:S(2)}, u32[]{:S(2)}) collective-permute-start(bf16[256,256]{1,0:T(8,128)(2,1)S(1)} %shard_map.100.refs_0_), channel_id=1, source_target_pairs={{0,2},{1,3},{2,0},{3,1},{4,6},{5,7},{6,4},{7,5},{8,10},{9,11},{10,... | collective-permute-start | bytes 393224 | tf_op jit(solution)/shard_map/ppermute | solution.py:158
  107.8 0.8 copy-start.13
  108.6 0.8 copy-start.22
  109.3 0.8 copy-start.25
  110.1 0.8 copy-start.28
  110.9 43.1 %all-to-all-start.5 = ((bf16[64,4,896]{2,1,0:T(4,128)(2,1)}), bf16[64,4,896]{2,1,0:T(4,128)(2,1)S(1)}, u32[]{:S(2)}, u32[]{:S(2)}) async-start(bf16[64,4,896]{2,1,0:T(4,128)(2,1)} %copy-done.13), calls=%async_computation.5 | async-start | bytes 917504 | tf_op jit(solution)/shard_map/all_to_all | solution.py:153
  121.2 15.1 %collective-permute-start.9 = (bf16[64,4,896]{2,1,0:T(4,128)(2,1)S(1)}, bf16[64,4,896]{2,1,0:T(4,128)(2,1)S(1)}, u32[]{:S(2)}, u32[]{:S(2)}) collective-permute-start(bf16[64,4,896]{2,1,0:T(4,128)(2,1)S(1)} %all-to-all-done.2.refs_0_), channel_id=1, source_target_pairs={{0,1},{1,2},{2,3},{3,0},{4,5},{5,6},{6,7},{7,4},{8,9},{9,10},{10,1... | collective-permute-start | bytes 1376264 | tf_op jit(solution)/shard_map/ppermute | solution.py:158
  123.4 13.0 %collective-permute-start.11 = (bf16[64,4,896]{2,1,0:T(4,128)(2,1)}, bf16[64,4,896]{2,1,0:T(4,128)(2,1)S(1)}, u32[]{:S(2)}, u32[]{:S(2)}) collective-permute-start(bf16[64,4,896]{2,1,0:T(4,128)(2,1)} %collective-permute-done.10.refs_2_), channel_id=1, source_target_pairs={{0,3},{1,0},{2,1},{3,2},{4,7},{5,4},{6,5},{7,6},{8,11},{9,8},{10,9... | collective-permute-start | bytes 1376264 | tf_op jit(solution)/shard_map/ppermute | solution.py:158
  125.1 39.3 %collective-permute-start = (bf16[64,4,896]{2,1,0:T(4,128)(2,1)S(1)}, bf16[64,4,896]{2,1,0:T(4,128)(2,1)}, u32[]{:S(2)}, u32[]{:S(2)}) collective-permute-start(bf16[64,4,896]{2,1,0:T(4,128)(2,1)S(1)} %all-to-all-done.refs_0_), channel_id=1, source_target_pairs={{0,1},{1,2},{2,3},{3,0},{4,5},{5,6},{6,7},{7,4},{8,9},{9,10},{10,1... | collective-permute-start | bytes 1376264 | tf_op jit(solution)/shard_map/ppermute | solution.py:158
  136.4 1.5 copy-start.2
  137.9 14.6 %copy-start.20 = (bf16[256,896]{1,0:T(8,128)(2,1)S(1)}, bf16[256,896]{1,0:T(8,128)(2,1)}, u32[]{:S(2)}) copy-start(bf16[256,896]{1,0:T(8,128)(2,1)} %copy-done.19) | copy-start | bytes 1376260
  137.9 14.6 %copy-start.23 = (bf16[256,896]{1,0:T(8,128)(2,1)S(1)}, bf16[256,896]{1,0:T(8,128)(2,1)}, u32[]{:S(2)}) copy-start(bf16[256,896]{1,0:T(8,128)(2,1)} %copy-done.22) | copy-start | bytes 1376260
  137.9 14.6 %copy-start.26 = (bf16[256,896]{1,0:T(8,128)(2,1)S(1)}, bf16[256,896]{1,0:T(8,128)(2,1)}, u32[]{:S(2)}) copy-start(bf16[256,896]{1,0:T(8,128)(2,1)} %copy-done.25) | copy-start | bytes 1376260
  137.9 14.6 %copy-start.29 = (bf16[256,896]{1,0:T(8,128)(2,1)S(1)}, bf16[256,896]{1,0:T(8,128)(2,1)}, u32[]{:S(2)}) copy-start(bf16[256,896]{1,0:T(8,128)(2,1)} %copy-done.28) | copy-start | bytes 1376260
  140.3 8.1 %collective-permute-start.12 = (bf16[256,256]{1,0:T(8,128)(2,1)S(1)}, bf16[256,256]{1,0:T(8,128)(2,1)S(1)}, u32[]{:S(2)}, u32[]{:S(2)}) collective-permute-start(bf16[256,256]{1,0:T(8,128)(2,1)S(1)} %shard_map.97.refs_0_), channel_id=1, source_target_pairs={{0,1},{1,2},{2,3},{3,0},{4,5},{5,6},{6,7},{7,4},{8,9},{9,10},{10,1... | collective-permute-start | bytes 393224 | tf_op jit(solution)/shard_map/ppermute | solution.py:158
  141.2 7.5 %collective-permute-start.13 = (bf16[256,256]{1,0:T(8,128)(2,1)S(1)}, bf16[256,256]{1,0:T(8,128)(2,1)S(1)}, u32[]{:S(2)}, u32[]{:S(2)}) collective-permute-start(bf16[256,256]{1,0:T(8,128)(2,1)S(1)} %shard_map.97.refs_0_), channel_id=1, source_target_pairs={{0,3},{1,0},{2,1},{3,2},{4,7},{5,4},{6,5},{7,6},{8,11},{9,8},{10,9... | collective-permute-start | bytes 393224 | tf_op jit(solution)/shard_map/ppermute | solution.py:158
  143.6 8.8 %collective-permute-start.14 = (bf16[256,256]{1,0:T(8,128)(2,1)S(1)}, bf16[256,256]{1,0:T(8,128)(2,1)S(1)}, u32[]{:S(2)}, u32[]{:S(2)}) collective-permute-start(bf16[256,256]{1,0:T(8,128)(2,1)S(1)} %shard_map.97.refs_0_), channel_id=1, source_target_pairs={{0,2},{1,3},{2,0},{3,1},{4,6},{5,7},{6,4},{7,5},{8,10},{9,11},{10,... | collective-permute-start | bytes 393224 | tf_op jit(solution)/shard_map/ppermute | solution.py:158
  153.2 0.8 copy-start.14
  153.9 39.8 %all-to-all-start.3 = ((bf16[64,4,896]{2,1,0:T(4,128)(2,1)}), bf16[64,4,896]{2,1,0:T(4,128)(2,1)S(1)}, u32[]{:S(2)}, u32[]{:S(2)}) async-start(bf16[64,4,896]{2,1,0:T(4,128)(2,1)} %copy-done.14), calls=%async_computation.3 | async-start | bytes 917504 | tf_op jit(solution)/shard_map/all_to_all | solution.py:153
  164.3 12.6 %collective-permute-start.1 = (bf16[64,4,896]{2,1,0:T(4,128)(2,1)S(1)}, bf16[64,4,896]{2,1,0:T(4,128)(2,1)S(1)}, u32[]{:S(2)}, u32[]{:S(2)}) collective-permute-start(bf16[64,4,896]{2,1,0:T(4,128)(2,1)S(1)} %all-to-all-done.refs_0_), channel_id=1, source_target_pairs={{0,3},{1,0},{2,1},{3,2},{4,7},{5,4},{6,5},{7,6},{8,11},{9,8},{10,9... | collective-permute-start | bytes 1376264 | tf_op jit(solution)/shard_map/ppermute | solution.py:158
  164.4 14.0 %collective-permute-start.2 = (bf16[64,4,896]{2,1,0:T(4,128)(2,1)}, bf16[64,4,896]{2,1,0:T(4,128)(2,1)S(1)}, u32[]{:S(2)}, u32[]{:S(2)}) collective-permute-start(bf16[64,4,896]{2,1,0:T(4,128)(2,1)} %collective-permute-done.refs_1_), channel_id=1, source_target_pairs={{0,1},{1,2},{2,3},{3,0},{4,5},{5,6},{6,7},{7,4},{8,9},{9,10},{10,1... | collective-permute-start | bytes 1376264 | tf_op jit(solution)/shard_map/ppermute | solution.py:158
  178.4 1.5 copy-start.3
  179.9 12.2 %copy-start.21 = (bf16[256,896]{1,0:T(8,128)(2,1)S(1)}, bf16[256,896]{1,0:T(8,128)(2,1)}, u32[]{:S(2)}) copy-start(bf16[256,896]{1,0:T(8,128)(2,1)} %copy-done.19) | copy-start | bytes 1376260
  179.9 12.2 %copy-start.24 = (bf16[256,896]{1,0:T(8,128)(2,1)S(1)}, bf16[256,896]{1,0:T(8,128)(2,1)}, u32[]{:S(2)}) copy-start(bf16[256,896]{1,0:T(8,128)(2,1)} %copy-done.22) | copy-start | bytes 1376260
  179.9 12.2 %copy-start.27 = (bf16[256,896]{1,0:T(8,128)(2,1)S(1)}, bf16[256,896]{1,0:T(8,128)(2,1)}, u32[]{:S(2)}) copy-start(bf16[256,896]{1,0:T(8,128)(2,1)} %copy-done.25) | copy-start | bytes 1376260
  179.9 12.2 %copy-start.30 = (bf16[256,896]{1,0:T(8,128)(2,1)S(1)}, bf16[256,896]{1,0:T(8,128)(2,1)}, u32[]{:S(2)}) copy-start(bf16[256,896]{1,0:T(8,128)(2,1)} %copy-done.28) | copy-start | bytes 1376260
  182.4 7.7 %collective-permute-start.3 = (bf16[256,256]{1,0:T(8,128)(2,1)S(1)}, bf16[256,256]{1,0:T(8,128)(2,1)S(1)}, u32[]{:S(2)}, u32[]{:S(2)}) collective-permute-start(bf16[256,256]{1,0:T(8,128)(2,1)S(1)} %shard_map.93.refs_0_), channel_id=1, source_target_pairs={{0,1},{1,2},{2,3},{3,0},{4,5},{5,6},{6,7},{7,4},{8,9},{9,10},{10,1... | collective-permute-start | bytes 393224 | tf_op jit(solution)/shard_map/ppermute | solution.py:158
  182.9 7.5 %collective-permute-start.4 = (bf16[256,256]{1,0:T(8,128)(2,1)S(1)}, bf16[256,256]{1,0:T(8,128)(2,1)S(1)}, u32[]{:S(2)}, u32[]{:S(2)}) collective-permute-start(bf16[256,256]{1,0:T(8,128)(2,1)S(1)} %shard_map.93.refs_0_), channel_id=1, source_target_pairs={{0,3},{1,0},{2,1},{3,2},{4,7},{5,4},{6,5},{7,6},{8,11},{9,8},{10,9... | collective-permute-start | bytes 393224 | tf_op jit(solution)/shard_map/ppermute | solution.py:158
  185.7 6.5 %collective-permute-start.5 = (bf16[256,256]{1,0:T(8,128)(2,1)S(1)}, bf16[256,256]{1,0:T(8,128)(2,1)S(1)}, u32[]{:S(2)}, u32[]{:S(2)}) collective-permute-start(bf16[256,256]{1,0:T(8,128)(2,1)S(1)} %shard_map.93.refs_0_), channel_id=1, source_target_pairs={{0,2},{1,3},{2,0},{3,1},{4,6},{5,7},{6,4},{7,5},{8,10},{9,11},{10,... | collective-permute-start | bytes 393224 | tf_op jit(solution)/shard_map/ppermute | solution.py:158
  192.9 0.8 copy-start.12
  193.7 45.2 %all-to-all-start.1 = ((bf16[64,4,896]{2,1,0:T(4,128)(2,1)}), bf16[64,4,896]{2,1,0:T(4,128)(2,1)S(1)}, u32[]{:S(2)}, u32[]{:S(2)}) async-start(bf16[64,4,896]{2,1,0:T(4,128)(2,1)} %copy-done.12), calls=%async_computation.1 | async-start | bytes 917504 | tf_op jit(solution)/shard_map/all_to_all | solution.py:153
  204.0 9.6 %collective-permute-start.21 = (bf16[128,896]{1,0:T(8,128)(2,1)S(1)}, bf16[128,896]{1,0:T(8,128)(2,1)S(1)}, u32[]{:S(2)}, u32[]{:S(2)}) collective-permute-start(bf16[128,896]{1,0:T(8,128)(2,1)S(1)} %copy-done.6), channel_id=1, source_target_pairs={{0,1},{1,2},{2,3},{3,0},{4,5},{5,6},{6,7},{7,4},{8,9},{9,10},{10,1... | collective-permute-start | bytes 688136 | tf_op jit(solution)/shard_map/ppermute | solution.py:158
  204.1 13.0 %collective-permute-start.22 = (bf16[128,896]{1,0:T(8,128)(2,1)S(1)}, bf16[128,896]{1,0:T(8,128)(2,1)S(1)}, u32[]{:S(2)}, u32[]{:S(2)}) collective-permute-start(bf16[128,896]{1,0:T(8,128)(2,1)S(1)} %copy-done.6), channel_id=1, source_target_pairs={{0,3},{1,0},{2,1},{3,2},{4,7},{5,4},{6,5},{7,6},{8,11},{9,8},{10,9... | collective-permute-start | bytes 688136 | tf_op jit(solution)/shard_map/ppermute | solution.py:158
  207.4 10.7 %collective-permute-start.23 = (bf16[128,896]{1,0:T(8,128)(2,1)S(1)}, bf16[128,896]{1,0:T(8,128)(2,1)S(1)}, u32[]{:S(2)}, u32[]{:S(2)}) collective-permute-start(bf16[128,896]{1,0:T(8,128)(2,1)S(1)} %copy-done.6), channel_id=1, source_target_pairs={{0,2},{1,3},{2,0},{3,1},{4,6},{5,7},{6,4},{7,5},{8,10},{9,11},{10,... | collective-permute-start | bytes 688136 | tf_op jit(solution)/shard_map/ppermute | solution.py:158
  218.0 1.5 copy-start.9
  219.5 1.5 copy-start.10
  221.0 1.5 copy-start.11
  222.5 6.9 %copy-start.31 = (bf16[128,4]{0,1:T(4,128)(2,1)S(1)}, bf16[128,4]{0,1:T(4,128)(2,1)}, u32[]{:S(2)}) copy-start(bf16[128,4]{0,1:T(4,128)(2,1)} %param.11) | copy-start | bytes 3076
  224.4 0.7 copy-start.15
  225.1 9.4 %collective-permute-start.24 = (bf16[128,896]{1,0:T(8,128)(2,1)}, bf16[128,896]{1,0:T(8,128)(2,1)S(1)}, u32[]{:S(2)}, u32[]{:S(2)}) collective-permute-start(bf16[128,896]{1,0:T(8,128)(2,1)} %get-tuple-element.18), channel_id=1, source_target_pairs={{0,1},{1,2},{2,3},{3,0},{4,5},{5,6},{6,7},{7,4},{8,9},{9,10},{10,1... | collective-permute-start | bytes 688136 | tf_op jit(solution)/shard_map/ppermute | solution.py:158
  226.2 11.4 %collective-permute-start.25 = (bf16[128,896]{1,0:T(8,128)(2,1)}, bf16[128,896]{1,0:T(8,128)(2,1)S(1)}, u32[]{:S(2)}, u32[]{:S(2)}) collective-permute-start(bf16[128,896]{1,0:T(8,128)(2,1)} %get-tuple-element.19), channel_id=1, source_target_pairs={{0,3},{1,0},{2,1},{3,2},{4,7},{5,4},{6,5},{7,6},{8,11},{9,8},{10,9... | collective-permute-start | bytes 688136 | tf_op jit(solution)/shard_map/ppermute | solution.py:158
  228.3 10.6 %collective-permute-start.26 = (bf16[128,896]{1,0:T(8,128)(2,1)}, bf16[128,896]{1,0:T(8,128)(2,1)S(1)}, u32[]{:S(2)}, u32[]{:S(2)}) collective-permute-start(bf16[128,896]{1,0:T(8,128)(2,1)} %get-tuple-element.20), channel_id=1, source_target_pairs={{0,2},{1,3},{2,0},{3,1},{4,6},{5,7},{6,4},{7,5},{8,10},{9,11},{10,... | collective-permute-start | bytes 688136 | tf_op jit(solution)/shard_map/ppermute | solution.py:158
  238.9 0.9 copy-start.16
  (1 other events, 0.7 us)

commit v3 on v2

--- a/solution.py
+++ b/solution.py
@@ -7,7 +7,8 @@
 from jax.sharding import PartitionSpec as P
 
 EXPERT = ("expert_0", "expert_1", "expert_2")
-CHUNKS = (4, 4, 4)
+CHUNKS = (6, 6)
+PAIR = 2
 TURNS = (0, 3, 1, 2)
 F32 = jnp.float32
 BF16 = jnp.bfloat16
@@ -17,23 +18,34 @@
     return jnp.dot(a, b, preferred_element_type=F32)
 
 
-def flat(ref):
+def flat(ref, width):
     x = ref[...]
-    return x.reshape(-1, x.shape[-1])
+    count = x.shape[2] // width
+    parts = [x[:, :, p * width : (p + 1) * width].reshape(-1, width) for p in range(count)]
+    return jnp.concatenate(parts, axis=0)
+
+
+def unflat(out_ref, x):
+    width = x.shape[1]
+    count = out_ref.shape[2] // width
+    rows = x.shape[0] // count
+    for p in range(count):
+        part = x[p * rows : (p + 1) * rows]
+        out_ref[:, :, p * width : (p + 1) * width] = part.reshape(-1, PAIR, width)
 
 
 def silu_times(gate, up):
     return (gate / (1.0 + jnp.exp(-gate)) * up).astype(BF16)
 
 
-def kernel_call(body, outs, *args, smem=0, vmem=16, flops=1):
-    specs = [pl.BlockSpec(memory_space=pltpu.SMEM) for _ in range(smem)]
-    specs += [pl.BlockSpec(memory_space=pltpu.VMEM) for _ in args[smem:]]
+def kernel_call(body, outs, *args, smem=0, hbm=0, scratch=(), vmem=16, flops=1):
+    places = [pltpu.SMEM] * smem + [pltpu.VMEM] * (len(args) - smem - hbm) + [pltpu.HBM] * hbm
     return pl.pallas_call(
         body,
-        in_specs=specs,
+        in_specs=[pl.BlockSpec(memory_space=m) for m in places],
         out_specs=[pl.BlockSpec(memory_space=pltpu.VMEM) for _ in outs],
         out_shape=[jax.ShapeDtypeStruct(o, BF16) for o in outs],
+        scratch_shapes=scratch,
         compiler_params=pltpu.CompilerParams(vmem_limit_bytes=vmem << 20),
         cost_estimate=pl.CostEstimate(flops=flops, transcendentals=0, bytes_accessed=0),
     )(*args)
@@ -49,11 +61,10 @@
         out_ref[...] = block(x_ref, lax.rem(q_ref[0] + s, n), out_ref.shape[1])
 
 
-def gather_body(experts, first):
+def gather_body(experts, first, size):
     def body(ids_ref, tokens_ref, out_ref):
         ids = ids_ref[...]
         top, rows = ids.shape
-        size = out_ref.shape[1]
         numbers = lax.broadcasted_iota(jnp.int32, (experts, rows), 0)
         onehot = [jnp.where(ids[k : k + 1] == numbers, 1.0, 0.0) for k in range(top)]
         per_token = sum(onehot[1:], onehot[0])
@@ -61,15 +72,20 @@
             jnp.int32, (rows, rows), 1
         )
         earlier = dot(per_token.astype(BF16), jnp.where(before, 1.0, 0.0).astype(BF16))
-        place = lax.broadcasted_iota(jnp.int32, (experts * size, rows), 0)
-        pick = jnp.zeros((experts * size, rows), F32)
-        for k in range(top):
-            slot = jnp.sum(onehot[k] * earlier, axis=0, keepdims=True).astype(jnp.int32)
-            local = slot - first
-            inside = (local >= 0) & (local < size)
-            target = jnp.where(inside, ids[k : k + 1] * size + local, -1)
-            pick = jnp.where(target == place, 1.0, pick)
-        out_ref[...] = dot(pick.astype(BF16), tokens_ref[...]).astype(BF16).reshape(out_ref.shape)
+        slots = [
+            jnp.sum(o * earlier, axis=0, keepdims=True).astype(jnp.int32) for o in onehot
+        ]
+        place = lax.broadcasted_iota(jnp.int32, (experts * PAIR, rows), 0)
+        picks = []
+        for p in range(first, first + size, PAIR):
+            pick = jnp.zeros((experts * PAIR, rows), F32)
+            for k in range(top):
+                local = slots[k] - p
+                inside = (local >= 0) & (local < PAIR)
+                target = jnp.where(inside, ids[k : k + 1] * PAIR + local, -1)
+                pick = jnp.where(target == place, 1.0, pick)
+            picks.append(pick.astype(BF16))
+        unflat(out_ref, dot(jnp.concatenate(picks, axis=0), tokens_ref[...]).astype(BF16))
 
     return body
 
@@ -89,19 +105,16 @@
         slots = [
             jnp.sum(o * earlier, axis=1, keepdims=True).astype(jnp.int32) for o in onehot
         ]
-        first = start = 0
-        for size in CHUNKS:
-            width = experts * size
-            place = lax.broadcasted_iota(jnp.int32, (rows, width), 1)
+        width = experts * PAIR
+        place = lax.broadcasted_iota(jnp.int32, (rows, width), 1)
+        for i in range(sum(CHUNKS) // PAIR):
             weight = jnp.zeros((rows, width), F32)
             for k in range(top):
-                local = slots[k] - first
-                inside = (local >= 0) & (local < size)
-                target = jnp.where(inside, ids[:, k : k + 1] * size + local, -1)
+                local = slots[k] - i * PAIR
+                inside = (local >= 0) & (local < PAIR)
+                target = jnp.where(inside, ids[:, k : k + 1] * PAIR + local, -1)
                 weight = jnp.where(target == place, gates[:, k : k + 1], weight)
-            out_ref[:, start : start + width] = weight.astype(BF16)
-            first += size
-            start += width
+            out_ref[:, i * width : (i + 1) * width] = weight.astype(BF16)
 
     return body
 
@@ -126,15 +139,33 @@
 
 def hidden_body(q_ref, *refs):
     n = len(TURNS)
-    gate_ref, up_ref, out_ref = refs[n:]
-    out_ref[...] = matmul_halves(q_ref, [flat(r) for r in refs[:n]], gate_ref, up_ref)
+    gate_hbm, up_hbm, out_ref, gate_ref, up_ref, sems = refs[n:]
+    width = gate_ref.shape[1]
+    at = [lax.rem(q_ref[0] + s, n) for s in TURNS]
+    copies = []
+    for i in range(n):
+        pair = (
+            pltpu.make_async_copy(gate_hbm.at[at[i]], gate_ref.at[i], sems.at[i, 0]),
+            pltpu.make_async_copy(up_hbm.at[at[i]], up_ref.at[i], sems.at[i, 1]),
+        )
+        for c in pair:
+            c.start()
+        copies.append(pair)
+    gate = up = 0.0
+    for i in range(n):
+        x = flat(refs[i], width)
+        for c in copies[i]:
+            c.wait()
+        gate = gate + dot(x, gate_ref[i])
+        up = up + dot(x, up_ref[i])
+    out_ref[...] = silu_times(gate, up)
 
 
 def down_body(*refs):
     *ins, out_ref = refs
     n = len(TURNS)
     total = sum(dot(h[...], w[...]) for h, w in zip(ins[:n], ins[n:]))
-    out_ref[...] = total.astype(BF16).reshape(out_ref.shape)
+    unflat(out_ref, total.astype(BF16))
 
 
 def combine_body(weight_ref, *refs):
@@ -143,7 +174,7 @@
     total = sum(p[...].astype(F32) for p in parts)
     start = 0
     for rows_ref in rows_refs:
-        rows = flat(rows_ref)
+        rows = flat(rows_ref, out_ref.shape[1])
         total = total + dot(weight_ref[:, start : start + rows.shape[0]], rows)
         start += rows.shape[0]
     out_ref[...] = total.astype(BF16)
@@ -188,13 +219,16 @@
     w_up = w_up.reshape(n, narrow, quarter)
 
     ids_t = expert_ids.T
+    tokens_all = spread(tokens)
     arrived = []
     for j, size in enumerate(CHUNKS):
         (rows,) = kernel_call(
-            gather_body(experts, sum(CHUNKS[:j])), [(experts, size, narrow)], ids_t, tokens
+            gather_body(experts, sum(CHUNKS[:j]), size),
+            [(experts, PAIR, size // PAIR * narrow)],
+            ids_t,
+            tokens,
         )
         arrived.append(exchange(rows, EXPERT))
-    tokens_all = spread(tokens)
     columns = kernel_call(columns_body, [(quarter, narrow)] * n, q, w_down, smem=1)
     down = deal(columns)
     (weight,) = kernel_call(
@@ -223,10 +257,19 @@
             w_gate,
             w_up,
             smem=1,
+            hbm=2,
+            scratch=[
+                pltpu.VMEM((n, narrow, quarter), BF16),
+                pltpu.VMEM((n, narrow, quarter), BF16),
+                pltpu.SemaphoreType.DMA((n, 2)),
+            ],
+            vmem=24,
             flops=10**9,
         )
         hidden_all = spread(hidden)
-        (out,) = kernel_call(down_body, [(experts, size, narrow)], *hidden_all, *down, flops=10**9)
+        (out,) = kernel_call(
+            down_body, [(experts, PAIR, size // PAIR * narrow)], *hidden_all, *down, flops=10**9
+        )
         returned.append(exchange(out, EXPERT))
     shared_all = deal(shared_parts)
     return kernel_call(combine_body, [(tok_dev, narrow)], weight, *returned, *shared_all)[0]

time: 242 us -> 207 us (0.86)
  starting transfers between devices: 91 us -> 56.1 us
  waiting for transfers between devices: 113 us -> 80.5 us
  blocking collectives: 0 us -> 32 us
  Pallas kernels: 16.2 us -> 24.8 us
  local copies, waits for them, and re-layouts: 20.4 us -> 12.5 us
    all_to_all x0 -> x1, blocking collectives: none -> 32 us  [exchange(): return lax.all_to_all(x, axis, split_axis=0, concat_axis=0, tiled=True)]
    all_to_all x6 -> x3, starting transfers between devices: 55.6 us -> 27.3 us  [exchange(): return lax.all_to_all(x, axis, split_axis=0, concat_axis=0, tiled=True)]
    all_to_all x6 -> x3, waiting for transfers between devices: 26.4 us -> 3.15 us  [exchange(): return lax.all_to_all(x, axis, split_axis=0, concat_axis=0, tiled=True)]
    ppermute x27 -> x21, waiting for transfers between devices: 86.8 us -> 77.4 us  [shift(): return lax.ppermute(x, axis, [(i, (i + by) % n) for i in range(n)])]
    pallas_call x13 -> x10, Pallas kernels: 16.2 us -> 24.8 us  [kernel_call(): pl.pallas_call(body, in_specs=[pl.BlockSpec(memory_space=m) for m in plac...]
    unnamed x66 -> x34, local copies, waits for them, and re-layouts: 20.4 us -> 12.5 us
    ppermute x27 -> x21, starting transfers between devices: 35.4 us -> 28.8 us  [shift(): return lax.ppermute(x, axis, [(i, (i + by) % n) for i in range(n)])]
  transfers between devices with their start and end apart: 33 -> 24, of which waited for: 22 -> 14; matrix products, arithmetic and copies ran while one was open for 0% -> 0% of each run, Pallas kernels for 6% -> 11%
where the time goes in v3:
time: 207 us; the launch traced here: 206 us
  waiting for transfers between devices  80.5 us (39%)
  starting transfers between devices  56.1 us (27%)
  blocking collectives  32 us (15%)
  Pallas kernels  24.8 us (12%)
  local copies, waits for them, and re-layouts  12.5 us (6%)
    ppermute x21, waiting for transfers between devices, shift(): return lax.ppermute(x, axis, [(i, (i + by) % n) for i in range(n)])  77.4 us
    all_to_all x1, blocking collectives, exchange(): return lax.all_to_all(x, axis, split_axis=0, concat_axis=0, tiled=True)  32 us
    ppermute x21, starting transfers between devices, shift(): return lax.ppermute(x, axis, [(i, (i + by) % n) for i in range(n)])  28.8 us
    all_to_all x3, starting transfers between devices, exchange(): return lax.all_to_all(x, axis, split_axis=0, concat_axis=0, tiled=True)  27.3 us
    pallas_call x10, Pallas kernels, kernel_call(): pl.pallas_call(body, in_specs=[pl.BlockSpec(memory_space=m) for m in plac...  24.8 us
    unnamed x34, local copies, waits for them, and re-layouts  12.5 us
  transfers between devices with their start and end apart: 24, of which 14 were waited for; matrix products, arithmetic and copies ran while one was open for 0% of the time, Pallas kernels for 11%

profile of v3, /device:TPU:32, one launch (start us, length us, event | category | flops | bytes accessed | tf_op | source)
XLA Modules:
  0.0 206.1 jit_solution(6752379883344289890)
XLA Ops:
  0.0 0.9 copy-done.3
  0.9 0.7 copy-done.10
  1.6 0.5 shard_map.92
  2.2 32.0 %all_to_all.20.refs_0_ = bf16[64,2,2688]{2,1,0:T(2,128)(2,1)S(1)} all-to-all(bf16[64,2,2688]{2,1,0:T(2,128)(2,1)S(1)} %shard_map.92), channel_id=1, replica_groups=mesh['expert_0'=4,'expert_1'=8,'expert_2'=2,'tensor'=4] {'expert_0','exp..., dimensions={0} | all-to-all | bytes 1376256 | tf_op jit(solution)/shard_map/all_to_all | solution.py:184
  34.1 1.6 collective-permute-start
  35.7 1.4 shard_map.96
  37.1 6.6 %all-to-all-start.2 = ((bf16[64,2,2688]{2,1,0:T(2,128)(2,1)}), bf16[64,2,2688]{2,1,0:T(2,128)(2,1)S(1)}, u32[]{:S(2)}, u32[]{:S(2)}) async-start(bf16[64,2,2688]{2,1,0:T(2,128)(2,1)} %shard_map.96), calls=%async_computation.2 | async-start | bytes 1376256 | tf_op jit(solution)/shard_map/all_to_all | solution.py:184
  43.7 1.7 collective-permute-start.1
  45.4 7.0 %collective-permute-done.refs_1_ = bf16[64,2,2688]{2,1,0:T(2,128)(2,1)} collective-permute-done((bf16[64,2,2688]{2,1,0:T(2,128)(2,1)S(1)}, bf16[64,2,2688]{2,1,0:T(2,128)(2,1)}, u32[]{:S(2)}, u32[]{:S(2)}) %collective-permute-start) | collective-permute-done | bytes 688160 | tf_op jit(solution)/shard_map/ppermute | solution.py:189
  52.4 0.3 collective-permute-start.2
  52.7 1.5 copy-done.5
  54.2 1.2 shard_map.94
  55.4 0.8 copy-done.12
  56.2 1.6 collective-permute-start.6
  57.8 1.7 collective-permute-start.7
  59.5 1.7 collective-permute-start.8
  61.1 3.1 %all-to-all-done.2.refs_0_ = bf16[64,2,2688]{2,1,0:T(2,128)(2,1)S(1)} async-done(((bf16[64,2,2688]{2,1,0:T(2,128)(2,1)}), bf16[64,2,2688]{2,1,0:T(2,128)(2,1)S(1)}, u32[]{:S(2)}, u32[]{:S(2)}) %all-to-all-start.2) | async-done | bytes 688160 | tf_op jit(solution)/shard_map/all_to_all | solution.py:184
  64.3 1.7 collective-permute-start.10
  66.0 6.3 %collective-permute-done.2.refs_3_ = bf16[64,2,2688]{2,1,0:T(2,128)(2,1)} collective-permute-done((bf16[64,2,2688]{2,1,0:T(2,128)(2,1)}, bf16[64,2,2688]{2,1,0:T(2,128)(2,1)}, u32[]{:S(2)}, u32[]{:S(2)}) %collective-permute-start.2) | collective-permute-done | bytes 688160 | tf_op jit(solution)/shard_map/ppermute | solution.py:189
  72.2 1.5 copy-done.1
  73.7 6.4 %shard_map.93.refs_0_ = bf16[384,256]{1,0:T(8,128)(2,1)S(1)} custom-call(s32[1]{0:T(128)} %bitcast.q_ref, bf16[64,2,2688]{2,1,0:T(2,128)(2,1)S(1)} %all_to_all.20.refs_0_, bf16[64,2,2688]{2,1,0:T(2,128)(2,1)} %collective-permute-done.refs_1_, bf16[64,2,2688]{2,1,0:T(2,128)(2,1)} %collective-permute-done.1.refs_2_, ...), custom_call_target="tpu_custom_call" | custom-call | flops 1000000000 | tf_op jit(solution)/shard_map/pallas_call | solution.py:43
  80.1 0.8 collective-permute-start.5
  80.9 11.2 %collective-permute-done.6.refs_5_ = bf16[256,896]{1,0:T(8,128)(2,1)} collective-permute-done((bf16[256,896]{1,0:T(8,128)(2,1)}, bf16[256,896]{1,0:T(8,128)(2,1)}, u32[]{:S(2)}, u32[]{:S(2)}) %collective-permute-start.6) | collective-permute-done | bytes 458784 | tf_op jit(solution)/shard_map/ppermute | solution.py:189
  92.1 0.0 collective-permute-start.4
  92.1 0.0 collective-permute-done.7.refs_6_
  92.1 2.0 collective-permute-start.3
  94.1 0.0 collective-permute-done.8.refs_7_
  94.1 1.8 collective-permute-done.5.refs_3_
  95.9 8.3 %collective-permute-done.4.refs_2_ = bf16[384,256]{1,0:T(8,128)(2,1)S(1)} collective-permute-done((bf16[384,256]{1,0:T(8,128)(2,1)S(1)}, bf16[384,256]{1,0:T(8,128)(2,1)S(1)}, u32[]{:S(2)}, u32[]{:S(2)}) %collective-permute-start.4) | collective-permute-done | bytes 196640 | tf_op jit(solution)/shard_map/ppermute | solution.py:189
  104.2 2.3 %shard_map.95 = bf16[64,2,2688]{2,1,0:T(2,128)(2,1)S(1)} custom-call(bf16[384,256]{1,0:T(8,128)(2,1)S(1)} %shard_map.93.refs_0_, bf16[384,256]{1,0:T(8,128)(2,1)S(1)} %collective-permute-done.3.refs_1_, bf16[384,256]{1,0:T(8,128)(2,1)S(1)} %collective-permute-done.4.refs_2_, bf16[384,256]{1,0:T(8,128)(2,1)S(1)} %collective-permute-done.5.refs_3_, ...), custom_call_target="tpu_custom_call" | custom-call | flops 1000000000 | tf_op jit(solution)/shard_map/pallas_call | solution.py:43
  106.5 0.8 copy-done.9
  107.3 10.3 %all-to-all-start.1 = ((bf16[64,2,2688]{2,1,0:T(2,128)(2,1)}), bf16[64,2,2688]{2,1,0:T(2,128)(2,1)S(1)}, u32[]{:S(2)}, u32[]{:S(2)}) async-start(bf16[64,2,2688]{2,1,0:T(2,128)(2,1)} %copy-done.9), calls=%async_computation.1 | async-start | bytes 1376256 | tf_op jit(solution)/shard_map/all_to_all | solution.py:184
  117.7 1.6 collective-permute-start.9
  119.2 1.7 collective-permute-start.11
  121.0 15.4 %collective-permute-done.9.refs_1_ = bf16[64,2,2688]{2,1,0:T(2,128)(2,1)S(1)} collective-permute-done((bf16[64,2,2688]{2,1,0:T(2,128)(2,1)S(1)}, bf16[64,2,2688]{2,1,0:T(2,128)(2,1)S(1)}, u32[]{:S(2)}, u32[]{:S(2)}) %collective-permute-start.9) | collective-permute-done | bytes 688160 | tf_op jit(solution)/shard_map/ppermute | solution.py:189
  136.4 0.2 collective-permute-done.11.refs_3_
  136.6 1.5 copy-done.2
  138.1 6.0 %shard_map.97.refs_0_ = bf16[384,256]{1,0:T(8,128)(2,1)S(1)} custom-call(s32[1]{0:T(128)} %bitcast.q_ref, bf16[64,2,2688]{2,1,0:T(2,128)(2,1)S(1)} %all-to-all-done.2.refs_0_, bf16[64,2,2688]{2,1,0:T(2,128)(2,1)S(1)} %collective-permute-done.9.refs_1_, bf16[64,2,2688]{2,1,0:T(2,128)(2,1)} %collective-permute-done.10.refs_2_, ...), custom_call_target="tpu_custom_call" | custom-call | flops 1000000000 | tf_op jit(solution)/shard_map/pallas_call | solution.py:43
  144.1 0.0 copy-start.4
  144.1 2.8 %collective-permute-start.14 = (bf16[384,256]{1,0:T(8,128)(2,1)S(1)}, bf16[384,256]{1,0:T(8,128)(2,1)S(1)}, u32[]{:S(2)}, u32[]{:S(2)}) collective-permute-start(bf16[384,256]{1,0:T(8,128)(2,1)S(1)} %shard_map.97.refs_0_), channel_id=1, source_target_pairs={{0,2},{1,3},{2,0},{3,1},{4,6},{5,7},{6,4},{7,5},{8,10},{9,11},{10,... | collective-permute-start | bytes 589832 | tf_op jit(solution)/shard_map/ppermute | solution.py:189
  146.9 1.3 collective-permute-start.13
  148.2 0.7 collective-permute-start.12
  149.0 4.5 %collective-permute-done.14.refs_3_ = bf16[384,256]{1,0:T(8,128)(2,1)S(1)} collective-permute-done((bf16[384,256]{1,0:T(8,128)(2,1)S(1)}, bf16[384,256]{1,0:T(8,128)(2,1)S(1)}, u32[]{:S(2)}, u32[]{:S(2)}) %collective-permute-start.14) | collective-permute-done | bytes 196640 | tf_op jit(solution)/shard_map/ppermute | solution.py:189
  153.5 2.5 %collective-permute-done.13.refs_2_ = bf16[384,256]{1,0:T(8,128)(2,1)S(1)} collective-permute-done((bf16[384,256]{1,0:T(8,128)(2,1)S(1)}, bf16[384,256]{1,0:T(8,128)(2,1)S(1)}, u32[]{:S(2)}, u32[]{:S(2)}) %collective-permute-start.13) | collective-permute-done | bytes 196640 | tf_op jit(solution)/shard_map/ppermute | solution.py:189
  156.0 0.2 collective-permute-done.12.refs_1_
  156.2 3.2 %shard_map.98 = bf16[64,2,2688]{2,1,0:T(2,128)(2,1)} custom-call(bf16[384,256]{1,0:T(8,128)(2,1)S(1)} %shard_map.97.refs_0_, bf16[384,256]{1,0:T(8,128)(2,1)S(1)} %collective-permute-done.12.refs_1_, bf16[384,256]{1,0:T(8,128)(2,1)S(1)} %collective-permute-done.13.refs_2_, bf16[384,256]{1,0:T(8,128)(2,1)S(1)} %collective-permute-done.14.refs_3_, ...), custom_call_target="tpu_custom_call" | custom-call | flops 1000000000 | tf_op jit(solution)/shard_map/pallas_call | solution.py:43
  159.3 0.0 all-to-all-done.1.refs_0_
  159.3 10.3 %all-to-all-start.3 = ((bf16[64,2,2688]{2,1,0:T(2,128)(2,1)}), bf16[64,2,2688]{2,1,0:T(2,128)(2,1)S(1)}, u32[]{:S(2)}, u32[]{:S(2)}) async-start(bf16[64,2,2688]{2,1,0:T(2,128)(2,1)} %shard_map.98), calls=%async_computation.3 | async-start | bytes 1376256 | tf_op jit(solution)/shard_map/all_to_all | solution.py:184
  169.7 2.6 %collective-permute-start.16 = (bf16[128,896]{1,0:T(8,128)(2,1)S(1)}, bf16[128,896]{1,0:T(8,128)(2,1)S(1)}, u32[]{:S(2)}, u32[]{:S(2)}) collective-permute-start(bf16[128,896]{1,0:T(8,128)(2,1)S(1)} %copy-done.4), channel_id=1, source_target_pairs={{0,3},{1,0},{2,1},{3,2},{4,7},{5,4},{6,5},{7,6},{8,11},{9,8},{10,9... | collective-permute-start | bytes 688136 | tf_op jit(solution)/shard_map/ppermute | solution.py:189
  172.2 1.8 collective-permute-start.17
  174.1 8.3 %collective-permute-done.16.refs_2_ = bf16[128,896]{1,0:T(8,128)(2,1)S(1)} collective-permute-done((bf16[128,896]{1,0:T(8,128)(2,1)S(1)}, bf16[128,896]{1,0:T(8,128)(2,1)S(1)}, u32[]{:S(2)}, u32[]{:S(2)}) %collective-permute-start.16) | collective-permute-done | bytes 229408 | tf_op jit(solution)/shard_map/ppermute | solution.py:189
  182.3 3.4 %collective-permute-done.15.refs_1_ = bf16[128,896]{1,0:T(8,128)(2,1)S(1)} collective-permute-done((bf16[128,896]{1,0:T(8,128)(2,1)S(1)}, bf16[128,896]{1,0:T(8,128)(2,1)S(1)}, u32[]{:S(2)}, u32[]{:S(2)}) %collective-permute-start.15) | collective-permute-done | bytes 229408 | tf_op jit(solution)/shard_map/ppermute | solution.py:189
  185.7 0.0 collective-permute-done.17.refs_3_
  185.7 1.5 copy-done.6
  187.2 1.5 copy-done.7
  188.7 1.5 copy-done.8
  190.2 1.7 shard_map.99
  191.9 0.0 collective-permute-start.18
  191.9 3.2 %collective-permute-start.19 = (bf16[128,896]{1,0:T(8,128)(2,1)S(1)}, bf16[128,896]{1,0:T(8,128)(2,1)S(1)}, u32[]{:S(2)}, u32[]{:S(2)}) collective-permute-start(bf16[128,896]{1,0:T(8,128)(2,1)S(1)} %get-tuple-element.19), channel_id=1, source_target_pairs={{0,3},{1,0},{2,1},{3,2},{4,7},{5,4},{6,5},{7,6},{8,11},{9,8},{10,9... | collective-permute-start | bytes 688136 | tf_op jit(solution)/shard_map/ppermute | solution.py:189
  195.1 0.1 copy.10.ids_ref
  195.3 0.1 copy.11.gates_ref
  195.4 0.9 shard_map.91.weight_ref
  196.3 8.4 %collective-permute-done.18.refs_3_ = bf16[128,896]{1,0:T(8,128)(2,1)S(1)} collective-permute-done((bf16[128,896]{1,0:T(8,128)(2,1)}, bf16[128,896]{1,0:T(8,128)(2,1)S(1)}, u32[]{:S(2)}, u32[]{:S(2)}) %collective-permute-start.18) | collective-permute-done | bytes 229408 | tf_op jit(solution)/shard_map/ppermute | solution.py:189
  204.7 1.4 shard_map.100
  (29 shorter events, 0.1 us)
Async XLA Ops:
  0.0 0.9 copy-start.3
  0.9 0.7 copy-start.10
  34.1 18.3 %collective-permute-start = (bf16[64,2,2688]{2,1,0:T(2,128)(2,1)S(1)}, bf16[64,2,2688]{2,1,0:T(2,128)(2,1)}, u32[]{:S(2)}, u32[]{:S(2)}) collective-permute-start(bf16[64,2,2688]{2,1,0:T(2,128)(2,1)S(1)} %all_to_all.20.refs_0_), channel_id=1, source_target_pairs={{0,1},{1,2},{2,3},{3,0},{4,5},{5,6},{6,7},{7,4},{8,9},{9,10},{10,1... | collective-permute-start | bytes 2064392 | tf_op jit(solution)/shard_map/ppermute | solution.py:189
  37.1 35.1 %copy-start = (bf16[1,3584,256]{2,1,0:T(8,128)(2,1)S(1)}, bf16[1,3584,256]{2,1,0:T(8,128)(2,1)}, u32[]{:S(2)}) copy-start(bf16[1,3584,256]{2,1,0:T(8,128)(2,1)} %param.12) | copy-start | bytes 5505028
  37.1 27.2 %all-to-all-start.2 = ((bf16[64,2,2688]{2,1,0:T(2,128)(2,1)}), bf16[64,2,2688]{2,1,0:T(2,128)(2,1)S(1)}, u32[]{:S(2)}, u32[]{:S(2)}) async-start(bf16[64,2,2688]{2,1,0:T(2,128)(2,1)} %shard_map.96), calls=%async_computation.2 | async-start | bytes 1376256 | tf_op jit(solution)/shard_map/all_to_all | solution.py:184
  43.7 20.6 %collective-permute-start.1 = (bf16[64,2,2688]{2,1,0:T(2,128)(2,1)S(1)}, bf16[64,2,2688]{2,1,0:T(2,128)(2,1)}, u32[]{:S(2)}, u32[]{:S(2)}) collective-permute-start(bf16[64,2,2688]{2,1,0:T(2,128)(2,1)S(1)} %all_to_all.20.refs_0_), channel_id=1, source_target_pairs={{0,3},{1,0},{2,1},{3,2},{4,7},{5,4},{6,5},{7,6},{8,11},{9,8},{10,9... | collective-permute-start | bytes 2064392 | tf_op jit(solution)/shard_map/ppermute | solution.py:189
  52.4 19.8 %collective-permute-start.2 = (bf16[64,2,2688]{2,1,0:T(2,128)(2,1)}, bf16[64,2,2688]{2,1,0:T(2,128)(2,1)}, u32[]{:S(2)}, u32[]{:S(2)}) collective-permute-start(bf16[64,2,2688]{2,1,0:T(2,128)(2,1)} %collective-permute-done.refs_1_), channel_id=1, source_target_pairs={{0,1},{1,2},{2,3},{3,0},{4,5},{5,6},{6,7},{7,4},{8,9},{9,10},{10,1... | collective-permute-start | bytes 2064392 | tf_op jit(solution)/shard_map/ppermute | solution.py:189
  52.7 1.5 copy-start.5
  55.4 0.8 copy-start.12
  56.2 35.8 %collective-permute-start.6 = (bf16[256,896]{1,0:T(8,128)(2,1)}, bf16[256,896]{1,0:T(8,128)(2,1)}, u32[]{:S(2)}, u32[]{:S(2)}) collective-permute-start(bf16[256,896]{1,0:T(8,128)(2,1)} %get-tuple-element.14), channel_id=1, source_target_pairs={{0,1},{1,2},{2,3},{3,0},{4,5},{5,6},{6,7},{7,4},{8,9},{9,10},{10,1... | collective-permute-start | bytes 1376264 | tf_op jit(solution)/shard_map/ppermute | solution.py:189
  57.8 34.3 %collective-permute-start.7 = (bf16[256,896]{1,0:T(8,128)(2,1)}, bf16[256,896]{1,0:T(8,128)(2,1)}, u32[]{:S(2)}, u32[]{:S(2)}) collective-permute-start(bf16[256,896]{1,0:T(8,128)(2,1)} %get-tuple-element.15), channel_id=1, source_target_pairs={{0,3},{1,0},{2,1},{3,2},{4,7},{5,4},{6,5},{7,6},{8,11},{9,8},{10,9... | collective-permute-start | bytes 1376264 | tf_op jit(solution)/shard_map/ppermute | solution.py:189
  59.5 34.6 %collective-permute-start.8 = (bf16[256,896]{1,0:T(8,128)(2,1)}, bf16[256,896]{1,0:T(8,128)(2,1)}, u32[]{:S(2)}, u32[]{:S(2)}) collective-permute-start(bf16[256,896]{1,0:T(8,128)(2,1)} %get-tuple-element.16), channel_id=1, source_target_pairs={{0,2},{1,3},{2,0},{3,1},{4,6},{5,7},{6,4},{7,5},{8,10},{9,11},{10,... | collective-permute-start | bytes 1376264 | tf_op jit(solution)/shard_map/ppermute | solution.py:189
  64.3 54.9 %collective-permute-start.10 = (bf16[64,2,2688]{2,1,0:T(2,128)(2,1)S(1)}, bf16[64,2,2688]{2,1,0:T(2,128)(2,1)}, u32[]{:S(2)}, u32[]{:S(2)}) collective-permute-start(bf16[64,2,2688]{2,1,0:T(2,128)(2,1)S(1)} %all-to-all-done.2.refs_0_), channel_id=1, source_target_pairs={{0,3},{1,0},{2,1},{3,2},{4,7},{5,4},{6,5},{7,6},{8,11},{9,8},{10,9... | collective-permute-start | bytes 2064392 | tf_op jit(solution)/shard_map/ppermute | solution.py:189
  72.2 1.5 copy-start.1
  73.7 30.4 %copy-start.13 = (bf16[256,896]{1,0:T(8,128)(2,1)S(1)}, bf16[256,896]{1,0:T(8,128)(2,1)}, u32[]{:S(2)}) copy-start(bf16[256,896]{1,0:T(8,128)(2,1)} %copy-done.12) | copy-start | bytes 1376260
  80.1 15.8 %collective-permute-start.5 = (bf16[384,256]{1,0:T(8,128)(2,1)S(1)}, bf16[384,256]{1,0:T(8,128)(2,1)S(1)}, u32[]{:S(2)}, u32[]{:S(2)}) collective-permute-start(bf16[384,256]{1,0:T(8,128)(2,1)S(1)} %shard_map.93.refs_0_), channel_id=1, source_target_pairs={{0,2},{1,3},{2,0},{3,1},{4,6},{5,7},{6,4},{7,5},{8,10},{9,11},{10,... | collective-permute-start | bytes 589832 | tf_op jit(solution)/shard_map/ppermute | solution.py:189
  92.1 12.1 %collective-permute-start.4 = (bf16[384,256]{1,0:T(8,128)(2,1)S(1)}, bf16[384,256]{1,0:T(8,128)(2,1)S(1)}, u32[]{:S(2)}, u32[]{:S(2)}) collective-permute-start(bf16[384,256]{1,0:T(8,128)(2,1)S(1)} %shard_map.93.refs_0_), channel_id=1, source_target_pairs={{0,3},{1,0},{2,1},{3,2},{4,7},{5,4},{6,5},{7,6},{8,11},{9,8},{10,9... | collective-permute-start | bytes 589832 | tf_op jit(solution)/shard_map/ppermute | solution.py:189
  92.1 12.1 %collective-permute-start.3 = (bf16[384,256]{1,0:T(8,128)(2,1)S(1)}, bf16[384,256]{1,0:T(8,128)(2,1)S(1)}, u32[]{:S(2)}, u32[]{:S(2)}) collective-permute-start(bf16[384,256]{1,0:T(8,128)(2,1)S(1)} %shard_map.93.refs_0_), channel_id=1, source_target_pairs={{0,1},{1,2},{2,3},{3,0},{4,5},{5,6},{6,7},{7,4},{8,9},{9,10},{10,1... | collective-permute-start | bytes 589832 | tf_op jit(solution)/shard_map/ppermute | solution.py:189
  106.5 0.9 copy-start.9
  107.3 52.0 %all-to-all-start.1 = ((bf16[64,2,2688]{2,1,0:T(2,128)(2,1)}), bf16[64,2,2688]{2,1,0:T(2,128)(2,1)S(1)}, u32[]{:S(2)}, u32[]{:S(2)}) async-start(bf16[64,2,2688]{2,1,0:T(2,128)(2,1)} %copy-done.9), calls=%async_computation.1 | async-start | bytes 1376256 | tf_op jit(solution)/shard_map/all_to_all | solution.py:184
  117.7 18.7 %collective-permute-start.9 = (bf16[64,2,2688]{2,1,0:T(2,128)(2,1)S(1)}, bf16[64,2,2688]{2,1,0:T(2,128)(2,1)S(1)}, u32[]{:S(2)}, u32[]{:S(2)}) collective-permute-start(bf16[64,2,2688]{2,1,0:T(2,128)(2,1)S(1)} %all-to-all-done.2.refs_0_), channel_id=1, source_target_pairs={{0,1},{1,2},{2,3},{3,0},{4,5},{5,6},{6,7},{7,4},{8,9},{9,10},{10,1... | collective-permute-start | bytes 2064392 | tf_op jit(solution)/shard_map/ppermute | solution.py:189
  119.2 17.4 %collective-permute-start.11 = (bf16[64,2,2688]{2,1,0:T(2,128)(2,1)}, bf16[64,2,2688]{2,1,0:T(2,128)(2,1)S(1)}, u32[]{:S(2)}, u32[]{:S(2)}) collective-permute-start(bf16[64,2,2688]{2,1,0:T(2,128)(2,1)} %collective-permute-done.10.refs_2_), channel_id=1, source_target_pairs={{0,3},{1,0},{2,1},{3,2},{4,7},{5,4},{6,5},{7,6},{8,11},{9,8},{10,9... | collective-permute-start | bytes 2064392 | tf_op jit(solution)/shard_map/ppermute | solution.py:189
  136.6 1.5 copy-start.2
  138.1 18.0 %copy-start.14 = (bf16[256,896]{1,0:T(8,128)(2,1)S(1)}, bf16[256,896]{1,0:T(8,128)(2,1)}, u32[]{:S(2)}) copy-start(bf16[256,896]{1,0:T(8,128)(2,1)} %copy-done.12) | copy-start | bytes 1376260
  144.1 25.6 %copy-start.4 = (bf16[128,896]{1,0:T(8,128)(2,1)S(1)}, bf16[128,896]{1,0:T(8,128)(2,1)}, u32[]{:S(2)}) copy-start(bf16[128,896]{1,0:T(8,128)(2,1)} %refs_0_.1) | copy-start | bytes 688132
  144.1 9.4 %collective-permute-start.14 = (bf16[384,256]{1,0:T(8,128)(2,1)S(1)}, bf16[384,256]{1,0:T(8,128)(2,1)S(1)}, u32[]{:S(2)}, u32[]{:S(2)}) collective-permute-start(bf16[384,256]{1,0:T(8,128)(2,1)S(1)} %shard_map.97.refs_0_), channel_id=1, source_target_pairs={{0,2},{1,3},{2,0},{3,1},{4,6},{5,7},{6,4},{7,5},{8,10},{9,11},{10,... | collective-permute-start | bytes 589832 | tf_op jit(solution)/shard_map/ppermute | solution.py:189
  146.9 9.1 %collective-permute-start.13 = (bf16[384,256]{1,0:T(8,128)(2,1)S(1)}, bf16[384,256]{1,0:T(8,128)(2,1)S(1)}, u32[]{:S(2)}, u32[]{:S(2)}) collective-permute-start(bf16[384,256]{1,0:T(8,128)(2,1)S(1)} %shard_map.97.refs_0_), channel_id=1, source_target_pairs={{0,3},{1,0},{2,1},{3,2},{4,7},{5,4},{6,5},{7,6},{8,11},{9,8},{10,9... | collective-permute-start | bytes 589832 | tf_op jit(solution)/shard_map/ppermute | solution.py:189
  148.2 7.9 %collective-permute-start.12 = (bf16[384,256]{1,0:T(8,128)(2,1)S(1)}, bf16[384,256]{1,0:T(8,128)(2,1)S(1)}, u32[]{:S(2)}, u32[]{:S(2)}) collective-permute-start(bf16[384,256]{1,0:T(8,128)(2,1)S(1)} %shard_map.97.refs_0_), channel_id=1, source_target_pairs={{0,1},{1,2},{2,3},{3,0},{4,5},{5,6},{6,7},{7,4},{8,9},{9,10},{10,1... | collective-permute-start | bytes 589832 | tf_op jit(solution)/shard_map/ppermute | solution.py:189
  159.3 45.4 %all-to-all-start.3 = ((bf16[64,2,2688]{2,1,0:T(2,128)(2,1)}), bf16[64,2,2688]{2,1,0:T(2,128)(2,1)S(1)}, u32[]{:S(2)}, u32[]{:S(2)}) async-start(bf16[64,2,2688]{2,1,0:T(2,128)(2,1)} %shard_map.98), calls=%async_computation.3 | async-start | bytes 1376256 | tf_op jit(solution)/shard_map/all_to_all | solution.py:184
  169.7 12.7 %collective-permute-start.16 = (bf16[128,896]{1,0:T(8,128)(2,1)S(1)}, bf16[128,896]{1,0:T(8,128)(2,1)S(1)}, u32[]{:S(2)}, u32[]{:S(2)}) collective-permute-start(bf16[128,896]{1,0:T(8,128)(2,1)S(1)} %copy-done.4), channel_id=1, source_target_pairs={{0,3},{1,0},{2,1},{3,2},{4,7},{5,4},{6,5},{7,6},{8,11},{9,8},{10,9... | collective-permute-start | bytes 688136 | tf_op jit(solution)/shard_map/ppermute | solution.py:189
  172.2 13.5 %collective-permute-start.15 = (bf16[128,896]{1,0:T(8,128)(2,1)S(1)}, bf16[128,896]{1,0:T(8,128)(2,1)S(1)}, u32[]{:S(2)}, u32[]{:S(2)}) collective-permute-start(bf16[128,896]{1,0:T(8,128)(2,1)S(1)} %copy-done.4), channel_id=1, source_target_pairs={{0,1},{1,2},{2,3},{3,0},{4,5},{5,6},{6,7},{7,4},{8,9},{9,10},{10,1... | collective-permute-start | bytes 688136 | tf_op jit(solution)/shard_map/ppermute | solution.py:189
  172.2 13.5 %collective-permute-start.17 = (bf16[128,896]{1,0:T(8,128)(2,1)S(1)}, bf16[128,896]{1,0:T(8,128)(2,1)S(1)}, u32[]{:S(2)}, u32[]{:S(2)}) collective-permute-start(bf16[128,896]{1,0:T(8,128)(2,1)S(1)} %copy-done.4), channel_id=1, source_target_pairs={{0,2},{1,3},{2,0},{3,1},{4,6},{5,7},{6,4},{7,5},{8,10},{9,11},{10,... | collective-permute-start | bytes 688136 | tf_op jit(solution)/shard_map/ppermute | solution.py:189
  185.7 1.5 copy-start.6
  187.2 1.5 copy-start.7
  188.7 1.5 copy-start.8
  190.2 4.9 %copy-start.11 = (s32[128,4]{0,1:T(4,128)S(1)}, s32[128,4]{0,1:T(4,128)}, u32[]{:S(2)}) copy-start(s32[128,4]{0,1:T(4,128)} %param.10) | copy-start | bytes 6148
  190.2 5.0 %copy-start.15 = (bf16[128,4]{0,1:T(4,128)(2,1)S(1)}, bf16[128,4]{0,1:T(4,128)(2,1)}, u32[]{:S(2)}) copy-start(bf16[128,4]{0,1:T(4,128)(2,1)} %param.11) | copy-start | bytes 3076
  191.9 12.8 %collective-permute-start.18 = (bf16[128,896]{1,0:T(8,128)(2,1)}, bf16[128,896]{1,0:T(8,128)(2,1)S(1)}, u32[]{:S(2)}, u32[]{:S(2)}) collective-permute-start(bf16[128,896]{1,0:T(8,128)(2,1)} %get-tuple-element.18), channel_id=1, source_target_pairs={{0,1},{1,2},{2,3},{3,0},{4,5},{5,6},{6,7},{7,4},{8,9},{9,10},{10,1... | collective-permute-start | bytes 688136 | tf_op jit(solution)/shard_map/ppermute | solution.py:189
  191.9 12.8 %collective-permute-start.19 = (bf16[128,896]{1,0:T(8,128)(2,1)S(1)}, bf16[128,896]{1,0:T(8,128)(2,1)S(1)}, u32[]{:S(2)}, u32[]{:S(2)}) collective-permute-start(bf16[128,896]{1,0:T(8,128)(2,1)S(1)} %get-tuple-element.19), channel_id=1, source_target_pairs={{0,3},{1,0},{2,1},{3,2},{4,7},{5,4},{6,5},{7,6},{8,11},{9,8},{10,9... | collective-permute-start | bytes 688136 | tf_op jit(solution)/shard_map/ppermute | solution.py:189
  195.1 9.6 %collective-permute-start.20 = (bf16[128,896]{1,0:T(8,128)(2,1)S(1)}, bf16[128,896]{1,0:T(8,128)(2,1)S(1)}, u32[]{:S(2)}, u32[]{:S(2)}) collective-permute-start(bf16[128,896]{1,0:T(8,128)(2,1)S(1)} %get-tuple-element.20), channel_id=1, source_target_pairs={{0,2},{1,3},{2,0},{3,1},{4,6},{5,7},{6,4},{7,5},{8,10},{9,11},{10,... | collective-permute-start | bytes 688136 | tf_op jit(solution)/shard_map/ppermute | solution.py:189

commit v4 on v3

--- a/solution.py
+++ b/solution.py
@@ -18,34 +18,36 @@
     return jnp.dot(a, b, preferred_element_type=F32)
 
 
-def flat(ref, width):
-    x = ref[...]
+def flat(x, width):
     count = x.shape[2] // width
     parts = [x[:, :, p * width : (p + 1) * width].reshape(-1, width) for p in range(count)]
     return jnp.concatenate(parts, axis=0)
 
 
-def unflat(out_ref, x):
+def unflat(out_ref, x, start=0):
     width = x.shape[1]
     count = out_ref.shape[2] // width
     rows = x.shape[0] // count
+    span = pl.ds(start, rows // PAIR)
     for p in range(count):
         part = x[p * rows : (p + 1) * rows]
-        out_ref[:, :, p * width : (p + 1) * width] = part.reshape(-1, PAIR, width)
+        out_ref[span, :, p * width : (p + 1) * width] = part.reshape(-1, PAIR, width)
 
 
 def silu_times(gate, up):
     return (gate / (1.0 + jnp.exp(-gate)) * up).astype(BF16)
 
 
-def kernel_call(body, outs, *args, smem=0, hbm=0, scratch=(), vmem=16, flops=1):
-    places = [pltpu.SMEM] * smem + [pltpu.VMEM] * (len(args) - smem - hbm) + [pltpu.HBM] * hbm
+def kernel_call(body, outs, *args, smem=0, vmem=12, flops=1):
+    places = [pltpu.SMEM] * smem + [pltpu.VMEM] * (len(args) - smem)
     return pl.pallas_call(
         body,
         in_specs=[pl.BlockSpec(memory_space=m) for m in places],
         out_specs=[pl.BlockSpec(memory_space=pltpu.VMEM) for _ in outs],
-        out_shape=[jax.ShapeDtypeStruct(o, BF16) for o in outs],
-        scratch_shapes=scratch,
+        out_shape=[
+            o if isinstance(o, jax.ShapeDtypeStruct) else jax.ShapeDtypeStruct(o, BF16)
+            for o in outs
+        ],
         compiler_params=pltpu.CompilerParams(vmem_limit_bytes=vmem << 20),
         cost_estimate=pl.CostEstimate(flops=flops, transcendentals=0, bytes_accessed=0),
     )(*args)
@@ -137,35 +139,40 @@
         out_ref[...] = dot(hidden, part).astype(BF16)
 
 
-def hidden_body(q_ref, *refs):
-    n = len(TURNS)
-    gate_hbm, up_hbm, out_ref, gate_ref, up_ref, sems = refs[n:]
-    width = gate_ref.shape[1]
+def partial_body(q_ref, own_ref, left_ref, right_ref, gate_ref, up_ref, sums_ref, far_ref):
+    n, width, quarter = gate_ref.shape
     at = [lax.rem(q_ref[0] + s, n) for s in TURNS]
-    copies = []
-    for i in range(n):
-        pair = (
-            pltpu.make_async_copy(gate_hbm.at[at[i]], gate_ref.at[i], sems.at[i, 0]),
-            pltpu.make_async_copy(up_hbm.at[at[i]], up_ref.at[i], sems.at[i, 1]),
-        )
-        for c in pair:
-            c.start()
-        copies.append(pair)
-    gate = up = 0.0
-    for i in range(n):
-        x = flat(refs[i], width)
-        for c in copies[i]:
-            c.wait()
-        gate = gate + dot(x, gate_ref[i])
-        up = up + dot(x, up_ref[i])
-    out_ref[...] = silu_times(gate, up)
+    half = own_ref.shape[0] // 2
+    rows = sums_ref.shape[0] // 2
+    for h in range(2):
+        span = pl.ds(h * half, half)
+        xs = [flat(r[span], width) for r in (own_ref, left_ref, right_ref)]
+        out = pl.ds(h * rows, rows)
+        sums_ref[out, :quarter] = sum(dot(x, gate_ref[i]) for x, i in zip(xs, at))
+        sums_ref[out, quarter:] = sum(dot(x, up_ref[i]) for x, i in zip(xs, at))
+    far_ref[0] = gate_ref[at[3]]
+    far_ref[1] = up_ref[at[3]]
+
+
+def hidden_body(sums_ref, o0_ref, o1_ref, far_ref, out_ref):
+    _, width, quarter = far_ref.shape
+    rows = sums_ref.shape[0] // 2
+    for h, o_ref in enumerate((o0_ref, o1_ref)):
+        span = pl.ds(h * rows, rows)
+        x = flat(o_ref[...], width)
+        gate = sums_ref[span, :quarter] + dot(x, far_ref[0])
+        up = sums_ref[span, quarter:] + dot(x, far_ref[1])
+        out_ref[span] = silu_times(gate, up)
 
 
 def down_body(*refs):
     *ins, out_ref = refs
     n = len(TURNS)
-    total = sum(dot(h[...], w[...]) for h, w in zip(ins[:n], ins[n:]))
-    unflat(out_ref, total.astype(BF16))
+    rows = ins[0].shape[0] // 2
+    for h in range(2):
+        span = pl.ds(h * rows, rows)
+        total = sum(dot(a[span], w[...]) for a, w in zip(ins[:n], ins[n:]))
+        unflat(out_ref, total.astype(BF16), h * out_ref.shape[0] // 2)
 
 
 def combine_body(weight_ref, *refs):
@@ -174,7 +181,7 @@
     total = sum(p[...].astype(F32) for p in parts)
     start = 0
     for rows_ref in rows_refs:
-        rows = flat(rows_ref, out_ref.shape[1])
+        rows = flat(rows_ref[...], out_ref.shape[1])
         total = total + dot(weight_ref[:, start : start + rows.shape[0]], rows)
         start += rows.shape[0]
     out_ref[...] = total.astype(BF16)
@@ -197,10 +204,13 @@
     return [xs[0], shift(xs[1], "tensor", 1), shift(xs[3], "tensor", -1), shift(xs[2], "tensor", 2)]
 
 
-def ring(x, turn):
+def ring(x):
+    half = x.shape[0] // 2
     left = shift(x, "tensor", 1)
     right = shift(x, "tensor", -1)
-    return [x, left, right, shift(left if turn == 1 else right, "tensor", turn)]
+    o0 = shift(left[:half], "tensor", 1)
+    o1 = shift(right[half:], "tensor", -1)
+    return left, right, o0, o1
 
 
 def per_device(tokens, expert_ids, gate_values, w_gate, w_up, w_down, *shared):
@@ -247,24 +257,25 @@
     )
 
     returned = []
-    for j, (rows, size) in enumerate(zip(arrived, CHUNKS)):
-        rows_all = ring(rows, 1 - 2 * (j % 2))
-        (hidden,) = kernel_call(
-            hidden_body,
-            [(experts * size, quarter)],
+    for rows, size in zip(arrived, CHUNKS):
+        left, right, o0, o1 = ring(rows)
+        sums, far = kernel_call(
+            partial_body,
+            [
+                jax.ShapeDtypeStruct((experts * size, 2 * quarter), F32),
+                (2, narrow, quarter),
+            ],
             q,
-            *rows_all,
+            rows,
+            left,
+            right,
             w_gate,
             w_up,
             smem=1,
-            hbm=2,
-            scratch=[
-                pltpu.VMEM((n, narrow, quarter), BF16),
-                pltpu.VMEM((n, narrow, quarter), BF16),
-                pltpu.SemaphoreType.DMA((n, 2)),
-            ],
-            vmem=24,
             flops=10**9,
+        )
+        (hidden,) = kernel_call(
+            hidden_body, [(experts * size, quarter)], sums, o0, o1, far, flops=10**9
         )
         hidden_all = spread(hidden)
         (out,) = kernel_call(

time: 207 us -> 199 us (0.961)
  blocking collectives: 32 us -> 0 us
  waiting for transfers between devices: 80.5 us -> 92.8 us
  local copies, waits for them, and re-layouts: 12.5 us -> 21.2 us
  starting transfers between devices: 56.1 us -> 64.6 us
  Pallas kernels: 24.8 us -> 18.9 us
    all_to_all x1 -> x0, blocking collectives: 32 us -> none  [exchange(): return lax.all_to_all(x, axis, split_axis=0, concat_axis=0, tiled=True)]
    all_to_all x3 -> x4, waiting for transfers between devices: 3.15 us -> 19.2 us  [exchange(): return lax.all_to_all(x, axis, split_axis=0, concat_axis=0, tiled=True)]
    all_to_all x3 -> x4, starting transfers between devices: 27.3 us -> 38.7 us  [exchange(): return lax.all_to_all(x, axis, split_axis=0, concat_axis=0, tiled=True)]
    pallas_call x10 -> x12, Pallas kernels: 24.8 us -> 18.9 us  [kernel_call(): pl.pallas_call(body, in_specs=[pl.BlockSpec(memory_space=m) for m in plac...]
    slice x0 -> x4, local copies, waits for them, and re-layouts: none -> 4.87 us  [the longest x2 2.43 us: ring(): o0 = shift(left[:half], 'tensor', 1)]
    unnamed x34 -> x52, local copies, waits for them, and re-layouts: 12.5 us -> 16.3 us
    ppermute x21 -> x23, waiting for transfers between devices: 77.4 us -> 73.7 us  [shift(): return lax.ppermute(x, axis, [(i, (i + by) % n) for i in range(n)])]
    ppermute x21 -> x23, starting transfers between devices: 28.8 us -> 25.9 us  [shift(): return lax.ppermute(x, axis, [(i, (i + by) % n) for i in range(n)])]
  transfers between devices with their start and end apart: 24 -> 27, of which waited for: 14 -> 13; matrix products, arithmetic and copies ran while one was open for 0% -> 3% of each run, Pallas kernels for 11% -> 8%
where the time goes in v4:
time: 199 us; the launch traced here: 198 us
  waiting for transfers between devices  92.8 us (47%)
  starting transfers between devices  64.6 us (32%)
  local copies, waits for them, and re-layouts  21.2 us (11%)
  Pallas kernels  18.9 us (9%)
    ppermute x23, waiting for transfers between devices, shift(): return lax.ppermute(x, axis, [(i, (i + by) % n) for i in range(n)])  73.7 us
    all_to_all x4, starting transfers between devices, exchange(): return lax.all_to_all(x, axis, split_axis=0, concat_axis=0, tiled=True)  38.7 us
    ppermute x23, starting transfers between devices, shift(): return lax.ppermute(x, axis, [(i, (i + by) % n) for i in range(n)])  25.9 us
    all_to_all x4, waiting for transfers between devices, exchange(): return lax.all_to_all(x, axis, split_axis=0, concat_axis=0, tiled=True)  19.2 us
    pallas_call x12, Pallas kernels, kernel_call(): pl.pallas_call(body, in_specs=[pl.BlockSpec(memory_space=m) for m in plac...  18.9 us
    unnamed x52, local copies, waits for them, and re-layouts  16.3 us
  transfers between devices with their start and end apart: 27, of which 13 were waited for; matrix products, arithmetic and copies ran while one was open for 3% of the time, Pallas kernels for 8%

profile of v4, /device:TPU:32, one launch (start us, length us, event | category | flops | bytes accessed | tf_op | source)
XLA Modules:
  0.0 197.8 jit_solution(6503996808805392358)
XLA Ops:
  0.0 0.9 copy-done.3
  0.9 0.7 copy-done.13
  1.6 1.4 shard_map.92
  3.0 11.6 %all-to-all-start = ((bf16[64,2,2688]{2,1,0:T(2,128)(2,1)}), bf16[64,2,2688]{2,1,0:T(2,128)(2,1)S(1)}, u32[]{:S(2)}, u32[]{:S(2)}) async-start(bf16[64,2,2688]{2,1,0:T(2,128)(2,1)} %shard_map.92), calls=%async_computation | async-start | bytes 1376256 | tf_op jit(solution)/shard_map/all_to_all | solution.py:191
  14.6 1.4 shard_map.97
  16.0 19.2 %all-to-all-done.own_ref = bf16[64,2,2688]{2,1,0:T(2,128)(2,1)S(1)} async-done(((bf16[64,2,2688]{2,1,0:T(2,128)(2,1)}), bf16[64,2,2688]{2,1,0:T(2,128)(2,1)S(1)}, u32[]{:S(2)}, u32[]{:S(2)}) %all-to-all-start) | async-done | bytes 688160 | tf_op jit(solution)/shard_map/all_to_all | solution.py:191
  35.2 6.5 %all-to-all-start.2 = ((bf16[64,2,2688]{2,1,0:T(2,128)(2,1)}), bf16[64,2,2688]{2,1,0:T(2,128)(2,1)S(1)}, u32[]{:S(2)}, u32[]{:S(2)}) async-start(bf16[64,2,2688]{2,1,0:T(2,128)(2,1)} %shard_map.97), calls=%async_computation.2 | async-start | bytes 1376256 | tf_op jit(solution)/shard_map/all_to_all | solution.py:191
  41.7 3.1 %collective-permute-start.1 = (bf16[64,2,2688]{2,1,0:T(2,128)(2,1)S(1)}, bf16[64,2,2688]{2,1,0:T(2,128)(2,1)}, u32[]{:S(2)}, u32[]{:S(2)}) collective-permute-start(bf16[64,2,2688]{2,1,0:T(2,128)(2,1)S(1)} %all-to-all-done.own_ref), channel_id=1, source_target_pairs={{0,3},{1,0},{2,1},{3,2},{4,7},{5,4},{6,5},{7,6},{8,11},{9,8},{10,9... | collective-permute-start | bytes 2064392 | tf_op jit(solution)/shard_map/ppermute | solution.py:196
  44.8 1.5 copy-done.5
  46.3 0.9 shard_map.95
  47.2 0.6 collective-permute-start.7
  47.8 12.0 %collective-permute-done.1.right_ref = bf16[64,2,2688]{2,1,0:T(2,128)(2,1)} collective-permute-done((bf16[64,2,2688]{2,1,0:T(2,128)(2,1)S(1)}, bf16[64,2,2688]{2,1,0:T(2,128)(2,1)}, u32[]{:S(2)}, u32[]{:S(2)}) %collective-permute-start.1) | collective-permute-done | bytes 688160 | tf_op jit(solution)/shard_map/ppermute | solution.py:196
  59.8 1.2 slice.17
  61.0 3.9 %collective-permute-start.3 = (bf16[32,2,2688]{2,1,0:T(2,128)(2,1)S(1)}, bf16[32,2,2688]{2,1,0:T(2,128)(2,1)S(1)}, u32[]{:S(2)}, u32[]{:S(2)}) collective-permute-start(bf16[32,2,2688]{2,1,0:T(2,128)(2,1)S(1)} %slice.17), channel_id=1, source_target_pairs={{0,3},{1,0},{2,1},{3,2},{4,7},{5,4},{6,5},{7,6},{8,11},{9,8},{10,9... | collective-permute-start | bytes 1032200 | tf_op jit(solution)/shard_map/ppermute | solution.py:196
  64.9 1.2 slice.16
  66.2 3.2 %collective-permute-start.8 = (bf16[256,896]{1,0:T(8,128)(2,1)S(1)}, bf16[256,896]{1,0:T(8,128)(2,1)S(1)}, u32[]{:S(2)}, u32[]{:S(2)}) collective-permute-start(bf16[256,896]{1,0:T(8,128)(2,1)S(1)} %get-tuple-element.21), channel_id=1, source_target_pairs={{0,3},{1,0},{2,1},{3,2},{4,7},{5,4},{6,5},{7,6},{8,11},{9,8},{10,9... | collective-permute-start | bytes 1376264 | tf_op jit(solution)/shard_map/ppermute | solution.py:196
  69.4 1.5 copy-done.1
  70.9 2.8 %shard_map.93 = (f32[384,512]{1,0:T(8,128)S(1)}, bf16[2,896,256]{2,1,0:T(8,128)(2,1)S(1)}) custom-call(s32[1]{0:T(128)} %bitcast.q_ref, bf16[64,2,2688]{2,1,0:T(2,128)(2,1)S(1)} %all-to-all-done.own_ref, bf16[64,2,2688]{2,1,0:T(2,128)(2,1)} %collective-permute-done.left_ref, bf16[64,2,2688]{2,1,0:T(2,128)(2,1)} %collective-permute-done.1.right_ref, ...), custom_call_target="tpu_custom_call" | custom-call | flops 1000000000 | tf_op jit(solution)/shard_map/pallas_call | solution.py:43
  73.7 19.6 %collective-permute-done.2.o0_ref = bf16[32,2,2688]{2,1,0:T(2,128)(2,1)S(1)} collective-permute-done((bf16[32,2,2688]{2,1,0:T(2,128)(2,1)S(1)}, bf16[32,2,2688]{2,1,0:T(2,128)(2,1)S(1)}, u32[]{:S(2)}, u32[]{:S(2)}) %collective-permute-start.2) | collective-permute-done | bytes 344096 | tf_op jit(solution)/shard_map/ppermute | solution.py:196
  93.2 0.6 shard_map.94.refs_0_
  94.1 0.8 copy-done.18
  94.9 2.0 %collective-permute-start.4 = (bf16[384,256]{1,0:T(8,128)(2,1)S(1)}, bf16[384,256]{1,0:T(8,128)(2,1)}, u32[]{:S(2)}, u32[]{:S(2)}) collective-permute-start(bf16[384,256]{1,0:T(8,128)(2,1)S(1)} %shard_map.94.refs_0_), channel_id=1, source_target_pairs={{0,1},{1,2},{2,3},{3,0},{4,5},{5,6},{6,7},{7,4},{8,9},{9,10},{10,1... | collective-permute-start | bytes 589832 | tf_op jit(solution)/shard_map/ppermute | solution.py:196
  96.9 0.8 copy-done.21
  97.6 2.1 %collective-permute-start.11 = (bf16[64,2,2688]{2,1,0:T(2,128)(2,1)S(1)}, bf16[64,2,2688]{2,1,0:T(2,128)(2,1)}, u32[]{:S(2)}, u32[]{:S(2)}) collective-permute-start(bf16[64,2,2688]{2,1,0:T(2,128)(2,1)S(1)} %all-to-all-done.2.own_ref), channel_id=1, source_target_pairs={{0,3},{1,0},{2,1},{3,2},{4,7},{5,4},{6,5},{7,6},{8,11},{9,8},{10,9... | collective-permute-start | bytes 2064392 | tf_op jit(solution)/shard_map/ppermute | solution.py:196
  99.7 3.6 %collective-permute-done.6.refs_3_ = bf16[384,256]{1,0:T(8,128)(2,1)} collective-permute-done((bf16[384,256]{1,0:T(8,128)(2,1)S(1)}, bf16[384,256]{1,0:T(8,128)(2,1)}, u32[]{:S(2)}, u32[]{:S(2)}) %collective-permute-start.6) | collective-permute-done | bytes 196640 | tf_op jit(solution)/shard_map/ppermute | solution.py:196
  103.4 1.1 collective-permute-done.5.refs_2_
  104.4 1.7 collective-permute-done.4.refs_1_
  106.1 1.0 copy-done.19
  107.2 1.0 copy-done.22
  108.2 2.3 %shard_map.96 = bf16[64,2,2688]{2,1,0:T(2,128)(2,1)S(1)} custom-call(bf16[384,256]{1,0:T(8,128)(2,1)S(1)} %shard_map.94.refs_0_, bf16[384,256]{1,0:T(8,128)(2,1)} %collective-permute-done.4.refs_1_, bf16[384,256]{1,0:T(8,128)(2,1)} %collective-permute-done.5.refs_2_, bf16[384,256]{1,0:T(8,128)(2,1)} %collective-permute-done.6.refs_3_, ...), custom_call_target="tpu_custom_call" | custom-call | flops 1000000000 | tf_op jit(solution)/shard_map/pallas_call | solution.py:43
  110.5 0.9 copy-done.10
  111.4 10.3 %all-to-all-start.1 = ((bf16[64,2,2688]{2,1,0:T(2,128)(2,1)}), bf16[64,2,2688]{2,1,0:T(2,128)(2,1)S(1)}, u32[]{:S(2)}, u32[]{:S(2)}) async-start(bf16[64,2,2688]{2,1,0:T(2,128)(2,1)} %copy-done.10), calls=%async_computation.1 | async-start | bytes 1376256 | tf_op jit(solution)/shard_map/all_to_all | solution.py:191
  121.7 1.2 slice.19
  122.9 2.1 %collective-permute-start.13 = (bf16[32,2,2688]{2,1,0:T(2,128)(2,1)S(1)}, bf16[32,2,2688]{2,1,0:T(2,128)(2,1)S(1)}, u32[]{:S(2)}, u32[]{:S(2)}) collective-permute-start(bf16[32,2,2688]{2,1,0:T(2,128)(2,1)S(1)} %slice.19), channel_id=1, source_target_pairs={{0,3},{1,0},{2,1},{3,2},{4,7},{5,4},{6,5},{7,6},{8,11},{9,8},{10,9... | collective-permute-start | bytes 1032200 | tf_op jit(solution)/shard_map/ppermute | solution.py:196
  125.0 1.2 slice.18
  126.3 1.5 copy-done.2
  127.8 2.8 %shard_map.98 = (f32[384,512]{1,0:T(8,128)S(1)}, bf16[2,896,256]{2,1,0:T(8,128)(2,1)S(1)}) custom-call(s32[1]{0:T(128)} %bitcast.q_ref, bf16[64,2,2688]{2,1,0:T(2,128)(2,1)S(1)} %all-to-all-done.2.own_ref, bf16[64,2,2688]{2,1,0:T(2,128)(2,1)} %collective-permute-done.10.left_ref, bf16[64,2,2688]{2,1,0:T(2,128)(2,1)} %collective-permute-done.11.right_ref, ...), custom_call_target="tpu_custom_call" | custom-call | flops 1000000000 | tf_op jit(solution)/shard_map/pallas_call | solution.py:43
  130.6 2.5 %collective-permute-done.13.o1_ref = bf16[32,2,2688]{2,1,0:T(2,128)(2,1)S(1)} collective-permute-done((bf16[32,2,2688]{2,1,0:T(2,128)(2,1)S(1)}, bf16[32,2,2688]{2,1,0:T(2,128)(2,1)S(1)}, u32[]{:S(2)}, u32[]{:S(2)}) %collective-permute-start.13) | collective-permute-done | bytes 344096 | tf_op jit(solution)/shard_map/ppermute | solution.py:196
  133.1 4.2 %collective-permute-done.12.o0_ref = bf16[32,2,2688]{2,1,0:T(2,128)(2,1)S(1)} collective-permute-done((bf16[32,2,2688]{2,1,0:T(2,128)(2,1)S(1)}, bf16[32,2,2688]{2,1,0:T(2,128)(2,1)S(1)}, u32[]{:S(2)}, u32[]{:S(2)}) %collective-permute-start.12) | collective-permute-done | bytes 344096 | tf_op jit(solution)/shard_map/ppermute | solution.py:196
  137.3 0.6 shard_map.99.refs_0_
  138.1 1.7 collective-permute-start.15
  139.8 0.4 collective-permute-start.14
  140.2 7.2 %collective-permute-done.16.refs_3_ = bf16[384,256]{1,0:T(8,128)(2,1)S(1)} collective-permute-done((bf16[384,256]{1,0:T(8,128)(2,1)S(1)}, bf16[384,256]{1,0:T(8,128)(2,1)S(1)}, u32[]{:S(2)}, u32[]{:S(2)}) %collective-permute-start.16) | collective-permute-done | bytes 196640 | tf_op jit(solution)/shard_map/ppermute | solution.py:196
  147.4 2.2 %collective-permute-done.14.refs_1_ = bf16[384,256]{1,0:T(8,128)(2,1)S(1)} collective-permute-done((bf16[384,256]{1,0:T(8,128)(2,1)S(1)}, bf16[384,256]{1,0:T(8,128)(2,1)S(1)}, u32[]{:S(2)}, u32[]{:S(2)}) %collective-permute-start.14) | collective-permute-done | bytes 196640 | tf_op jit(solution)/shard_map/ppermute | solution.py:196
  149.6 2.0 %shard_map.100 = bf16[64,2,2688]{2,1,0:T(2,128)(2,1)S(1)} custom-call(bf16[384,256]{1,0:T(8,128)(2,1)S(1)} %shard_map.99.refs_0_, bf16[384,256]{1,0:T(8,128)(2,1)S(1)} %collective-permute-done.14.refs_1_, bf16[384,256]{1,0:T(8,128)(2,1)S(1)} %collective-permute-done.15.refs_2_, bf16[384,256]{1,0:T(8,128)(2,1)S(1)} %collective-permute-done.16.refs_3_, ...), custom_call_target="tpu_custom_call" | custom-call | flops 1000000000 | tf_op jit(solution)/shard_map/pallas_call | solution.py:43
  151.6 0.9 copy-done.9
  152.5 10.3 %all-to-all-start.3 = ((bf16[64,2,2688]{2,1,0:T(2,128)(2,1)}), bf16[64,2,2688]{2,1,0:T(2,128)(2,1)S(1)}, u32[]{:S(2)}, u32[]{:S(2)}) async-start(bf16[64,2,2688]{2,1,0:T(2,128)(2,1)} %copy-done.9), calls=%async_computation.3 | async-start | bytes 1376256 | tf_op jit(solution)/shard_map/all_to_all | solution.py:191
  162.8 0.9 collective-permute-start.18
  163.7 1.5 collective-permute-start.17
  165.2 0.3 collective-permute-start.19
  165.5 6.2 %collective-permute-done.18.refs_2_ = bf16[128,896]{1,0:T(8,128)(2,1)S(1)} collective-permute-done((bf16[128,896]{1,0:T(8,128)(2,1)S(1)}, bf16[128,896]{1,0:T(8,128)(2,1)S(1)}, u32[]{:S(2)}, u32[]{:S(2)}) %collective-permute-start.18) | collective-permute-done | bytes 229408 | tf_op jit(solution)/shard_map/ppermute | solution.py:196
  171.6 5.6 %collective-permute-done.17.refs_1_ = bf16[128,896]{1,0:T(8,128)(2,1)S(1)} collective-permute-done((bf16[128,896]{1,0:T(8,128)(2,1)S(1)}, bf16[128,896]{1,0:T(8,128)(2,1)S(1)}, u32[]{:S(2)}, u32[]{:S(2)}) %collective-permute-start.17) | collective-permute-done | bytes 229408 | tf_op jit(solution)/shard_map/ppermute | solution.py:196
  177.2 1.5 copy-done.7
  178.7 1.5 copy-done.8
  180.2 1.8 shard_map.101
  182.0 0.7 copy-done.11
  182.7 3.2 %collective-permute-start.21 = (bf16[128,896]{1,0:T(8,128)(2,1)}, bf16[128,896]{1,0:T(8,128)(2,1)S(1)}, u32[]{:S(2)}, u32[]{:S(2)}) collective-permute-start(bf16[128,896]{1,0:T(8,128)(2,1)} %get-tuple-element.27), channel_id=1, source_target_pairs={{0,3},{1,0},{2,1},{3,2},{4,7},{5,4},{6,5},{7,6},{8,11},{9,8},{10,9... | collective-permute-start | bytes 688136 | tf_op jit(solution)/shard_map/ppermute | solution.py:196
  185.9 0.6 collective-permute-start.22
  186.5 0.1 copy.10.ids_ref
  186.6 0.1 copy.11.gates_ref
  186.8 0.9 shard_map.91.weight_ref
  187.7 7.9 %collective-permute-done.20.refs_3_ = bf16[128,896]{1,0:T(8,128)(2,1)S(1)} collective-permute-done((bf16[128,896]{1,0:T(8,128)(2,1)}, bf16[128,896]{1,0:T(8,128)(2,1)S(1)}, u32[]{:S(2)}, u32[]{:S(2)}) %collective-permute-start.20) | collective-permute-done | bytes 229408 | tf_op jit(solution)/shard_map/ppermute | solution.py:196
  195.6 0.9 copy-done.12
  196.5 1.3 shard_map.102
  (58 shorter events, 0.6 us)
Async XLA Ops:
  0.0 0.9 copy-start.3
  0.9 0.7 copy-start.13
  1.6 13.0 %copy-start.4 = (bf16[128,896]{1,0:T(8,128)(2,1)S(1)}, bf16[128,896]{1,0:T(8,128)(2,1)}, u32[]{:S(2)}) copy-start(bf16[128,896]{1,0:T(8,128)(2,1)} %refs_0_.1) | copy-start | bytes 688132
  1.6 13.0 %copy-start.14 = (s32[128,4]{0,1:T(4,128)S(1)}, s32[128,4]{0,1:T(4,128)}, u32[]{:S(2)}) copy-start(s32[128,4]{0,1:T(4,128)} %param.10) | copy-start | bytes 6148
  3.0 32.2 %all-to-all-start = ((bf16[64,2,2688]{2,1,0:T(2,128)(2,1)}), bf16[64,2,2688]{2,1,0:T(2,128)(2,1)S(1)}, u32[]{:S(2)}, u32[]{:S(2)}) async-start(bf16[64,2,2688]{2,1,0:T(2,128)(2,1)} %shard_map.92), calls=%async_computation | async-start | bytes 1376256 | tf_op jit(solution)/shard_map/all_to_all | solution.py:191
  35.2 62.4 %all-to-all-start.2 = ((bf16[64,2,2688]{2,1,0:T(2,128)(2,1)}), bf16[64,2,2688]{2,1,0:T(2,128)(2,1)S(1)}, u32[]{:S(2)}, u32[]{:S(2)}) async-start(bf16[64,2,2688]{2,1,0:T(2,128)(2,1)} %shard_map.97), calls=%async_computation.2 | async-start | bytes 1376256 | tf_op jit(solution)/shard_map/all_to_all | solution.py:191
  41.7 27.7 %copy-start = (bf16[1,3584,256]{2,1,0:T(8,128)(2,1)S(1)}, bf16[1,3584,256]{2,1,0:T(8,128)(2,1)}, u32[]{:S(2)}) copy-start(bf16[1,3584,256]{2,1,0:T(8,128)(2,1)} %param.12) | copy-start | bytes 5505028
  41.7 18.1 %collective-permute-start.1 = (bf16[64,2,2688]{2,1,0:T(2,128)(2,1)S(1)}, bf16[64,2,2688]{2,1,0:T(2,128)(2,1)}, u32[]{:S(2)}, u32[]{:S(2)}) collective-permute-start(bf16[64,2,2688]{2,1,0:T(2,128)(2,1)S(1)} %all-to-all-done.own_ref), channel_id=1, source_target_pairs={{0,3},{1,0},{2,1},{3,2},{4,7},{5,4},{6,5},{7,6},{8,11},{9,8},{10,9... | collective-permute-start | bytes 2064392 | tf_op jit(solution)/shard_map/ppermute | solution.py:196
  44.8 20.1 %collective-permute-start = (bf16[64,2,2688]{2,1,0:T(2,128)(2,1)S(1)}, bf16[64,2,2688]{2,1,0:T(2,128)(2,1)}, u32[]{:S(2)}, u32[]{:S(2)}) collective-permute-start(bf16[64,2,2688]{2,1,0:T(2,128)(2,1)S(1)} %all-to-all-done.own_ref), channel_id=1, source_target_pairs={{0,1},{1,2},{2,3},{3,0},{4,5},{5,6},{6,7},{7,4},{8,9},{9,10},{10,1... | collective-permute-start | bytes 2064392 | tf_op jit(solution)/shard_map/ppermute | solution.py:196
  44.8 1.5 copy-start.5
  47.2 26.5 %copy-start.15 = (bf16[256,896]{1,0:T(8,128)(2,1)}, bf16[256,896]{1,0:T(8,128)(2,1)S(1)}, u32[]{:S(2)}) copy-start(bf16[256,896]{1,0:T(8,128)(2,1)S(1)} %get-tuple-element.19.refs_4_) | copy-start | bytes 1376260
  47.2 46.9 %collective-permute-start.7 = (bf16[256,896]{1,0:T(8,128)(2,1)S(1)}, bf16[256,896]{1,0:T(8,128)(2,1)S(1)}, u32[]{:S(2)}, u32[]{:S(2)}) collective-permute-start(bf16[256,896]{1,0:T(8,128)(2,1)S(1)} %get-tuple-element.20), channel_id=1, source_target_pairs={{0,1},{1,2},{2,3},{3,0},{4,5},{5,6},{6,7},{7,4},{8,9},{9,10},{10,1... | collective-permute-start | bytes 1376264 | tf_op jit(solution)/shard_map/ppermute | solution.py:196
  61.0 12.7 %collective-permute-start.3 = (bf16[32,2,2688]{2,1,0:T(2,128)(2,1)S(1)}, bf16[32,2,2688]{2,1,0:T(2,128)(2,1)S(1)}, u32[]{:S(2)}, u32[]{:S(2)}) collective-permute-start(bf16[32,2,2688]{2,1,0:T(2,128)(2,1)S(1)} %slice.17), channel_id=1, source_target_pairs={{0,3},{1,0},{2,1},{3,2},{4,7},{5,4},{6,5},{7,6},{8,11},{9,8},{10,9... | collective-permute-start | bytes 1032200 | tf_op jit(solution)/shard_map/ppermute | solution.py:196
  66.1 27.2 %collective-permute-start.2 = (bf16[32,2,2688]{2,1,0:T(2,128)(2,1)S(1)}, bf16[32,2,2688]{2,1,0:T(2,128)(2,1)S(1)}, u32[]{:S(2)}, u32[]{:S(2)}) collective-permute-start(bf16[32,2,2688]{2,1,0:T(2,128)(2,1)S(1)} %slice.16), channel_id=1, source_target_pairs={{0,1},{1,2},{2,3},{3,0},{4,5},{5,6},{6,7},{7,4},{8,9},{9,10},{10,1... | collective-permute-start | bytes 1032200 | tf_op jit(solution)/shard_map/ppermute | solution.py:196
  66.2 30.7 %collective-permute-start.8 = (bf16[256,896]{1,0:T(8,128)(2,1)S(1)}, bf16[256,896]{1,0:T(8,128)(2,1)S(1)}, u32[]{:S(2)}, u32[]{:S(2)}) collective-permute-start(bf16[256,896]{1,0:T(8,128)(2,1)S(1)} %get-tuple-element.21), channel_id=1, source_target_pairs={{0,3},{1,0},{2,1},{3,2},{4,7},{5,4},{6,5},{7,6},{8,11},{9,8},{10,9... | collective-permute-start | bytes 1376264 | tf_op jit(solution)/shard_map/ppermute | solution.py:196
  69.4 30.3 %collective-permute-start.9 = (bf16[256,896]{1,0:T(8,128)(2,1)}, bf16[256,896]{1,0:T(8,128)(2,1)}, u32[]{:S(2)}, u32[]{:S(2)}) collective-permute-start(bf16[256,896]{1,0:T(8,128)(2,1)} %get-tuple-element.22), channel_id=1, source_target_pairs={{0,2},{1,3},{2,0},{3,1},{4,6},{5,7},{6,4},{7,5},{8,10},{9,11},{10,... | collective-permute-start | bytes 1376264 | tf_op jit(solution)/shard_map/ppermute | solution.py:196
  69.4 1.5 copy-start.1
  93.2 12.9 %copy-start.16 = (bf16[256,896]{1,0:T(8,128)(2,1)S(1)}, bf16[256,896]{1,0:T(8,128)(2,1)}, u32[]{:S(2)}) copy-start(bf16[256,896]{1,0:T(8,128)(2,1)} %copy-done.15) | copy-start | bytes 1376260
  93.9 9.5 %collective-permute-start.6 = (bf16[384,256]{1,0:T(8,128)(2,1)S(1)}, bf16[384,256]{1,0:T(8,128)(2,1)}, u32[]{:S(2)}, u32[]{:S(2)}) collective-permute-start(bf16[384,256]{1,0:T(8,128)(2,1)S(1)} %shard_map.94.refs_0_), channel_id=1, source_target_pairs={{0,2},{1,3},{2,0},{3,1},{4,6},{5,7},{6,4},{7,5},{8,10},{9,11},{10,... | collective-permute-start | bytes 589832 | tf_op jit(solution)/shard_map/ppermute | solution.py:196
  94.0 10.5 %collective-permute-start.5 = (bf16[384,256]{1,0:T(8,128)(2,1)S(1)}, bf16[384,256]{1,0:T(8,128)(2,1)}, u32[]{:S(2)}, u32[]{:S(2)}) collective-permute-start(bf16[384,256]{1,0:T(8,128)(2,1)S(1)} %shard_map.94.refs_0_), channel_id=1, source_target_pairs={{0,3},{1,0},{2,1},{3,2},{4,7},{5,4},{6,5},{7,6},{8,11},{9,8},{10,9... | collective-permute-start | bytes 589832 | tf_op jit(solution)/shard_map/ppermute | solution.py:196
  94.1 0.8 copy-start.18
  94.9 11.3 %collective-permute-start.4 = (bf16[384,256]{1,0:T(8,128)(2,1)S(1)}, bf16[384,256]{1,0:T(8,128)(2,1)}, u32[]{:S(2)}, u32[]{:S(2)}) collective-permute-start(bf16[384,256]{1,0:T(8,128)(2,1)S(1)} %shard_map.94.refs_0_), channel_id=1, source_target_pairs={{0,1},{1,2},{2,3},{3,0},{4,5},{5,6},{6,7},{7,4},{8,9},{9,10},{10,1... | collective-permute-start | bytes 589832 | tf_op jit(solution)/shard_map/ppermute | solution.py:196
  96.9 0.8 copy-start.21
  97.6 24.1 %collective-permute-start.11 = (bf16[64,2,2688]{2,1,0:T(2,128)(2,1)S(1)}, bf16[64,2,2688]{2,1,0:T(2,128)(2,1)}, u32[]{:S(2)}, u32[]{:S(2)}) collective-permute-start(bf16[64,2,2688]{2,1,0:T(2,128)(2,1)S(1)} %all-to-all-done.2.own_ref), channel_id=1, source_target_pairs={{0,3},{1,0},{2,1},{3,2},{4,7},{5,4},{6,5},{7,6},{8,11},{9,8},{10,9... | collective-permute-start | bytes 2064392 | tf_op jit(solution)/shard_map/ppermute | solution.py:196
  99.7 25.3 %collective-permute-start.10 = (bf16[64,2,2688]{2,1,0:T(2,128)(2,1)S(1)}, bf16[64,2,2688]{2,1,0:T(2,128)(2,1)}, u32[]{:S(2)}, u32[]{:S(2)}) collective-permute-start(bf16[64,2,2688]{2,1,0:T(2,128)(2,1)S(1)} %all-to-all-done.2.own_ref), channel_id=1, source_target_pairs={{0,1},{1,2},{2,3},{3,0},{4,5},{5,6},{6,7},{7,4},{8,9},{9,10},{10,1... | collective-permute-start | bytes 2064392 | tf_op jit(solution)/shard_map/ppermute | solution.py:196
  106.1 1.0 copy-start.19
  107.1 1.0 copy-start.22
  110.5 0.9 copy-start.10
  111.4 41.1 %all-to-all-start.1 = ((bf16[64,2,2688]{2,1,0:T(2,128)(2,1)}), bf16[64,2,2688]{2,1,0:T(2,128)(2,1)S(1)}, u32[]{:S(2)}, u32[]{:S(2)}) async-start(bf16[64,2,2688]{2,1,0:T(2,128)(2,1)} %copy-done.10), calls=%async_computation.1 | async-start | bytes 1376256 | tf_op jit(solution)/shard_map/all_to_all | solution.py:191
  122.9 10.2 %collective-permute-start.13 = (bf16[32,2,2688]{2,1,0:T(2,128)(2,1)S(1)}, bf16[32,2,2688]{2,1,0:T(2,128)(2,1)S(1)}, u32[]{:S(2)}, u32[]{:S(2)}) collective-permute-start(bf16[32,2,2688]{2,1,0:T(2,128)(2,1)S(1)} %slice.19), channel_id=1, source_target_pairs={{0,3},{1,0},{2,1},{3,2},{4,7},{5,4},{6,5},{7,6},{8,11},{9,8},{10,9... | collective-permute-start | bytes 1032200 | tf_op jit(solution)/shard_map/ppermute | solution.py:196
  126.2 11.1 %collective-permute-start.12 = (bf16[32,2,2688]{2,1,0:T(2,128)(2,1)S(1)}, bf16[32,2,2688]{2,1,0:T(2,128)(2,1)S(1)}, u32[]{:S(2)}, u32[]{:S(2)}) collective-permute-start(bf16[32,2,2688]{2,1,0:T(2,128)(2,1)S(1)} %slice.18), channel_id=1, source_target_pairs={{0,1},{1,2},{2,3},{3,0},{4,5},{5,6},{6,7},{7,4},{8,9},{9,10},{10,1... | collective-permute-start | bytes 1032200 | tf_op jit(solution)/shard_map/ppermute | solution.py:196
  126.3 1.5 copy-start.2
  137.3 12.3 %copy-start.17 = (bf16[256,896]{1,0:T(8,128)(2,1)S(1)}, bf16[256,896]{1,0:T(8,128)(2,1)}, u32[]{:S(2)}) copy-start(bf16[256,896]{1,0:T(8,128)(2,1)} %copy-done.15) | copy-start | bytes 1376260
  137.3 12.3 %copy-start.20 = (bf16[256,896]{1,0:T(8,128)(2,1)S(1)}, bf16[256,896]{1,0:T(8,128)(2,1)}, u32[]{:S(2)}) copy-start(bf16[256,896]{1,0:T(8,128)(2,1)} %copy-done.18) | copy-start | bytes 1376260
  137.3 12.3 %copy-start.23 = (bf16[256,896]{1,0:T(8,128)(2,1)S(1)}, bf16[256,896]{1,0:T(8,128)(2,1)}, u32[]{:S(2)}) copy-start(bf16[256,896]{1,0:T(8,128)(2,1)} %copy-done.21) | copy-start | bytes 1376260
  138.0 39.2 %copy-start.6 = (bf16[3584,256]{1,0:T(8,128)(2,1)S(1)}, bf16[3584,256]{1,0:T(8,128)(2,1)}, u32[]{:S(2)}) copy-start(bf16[3584,256]{1,0:T(8,128)(2,1)} %param.15) | copy-start | bytes 5505028
  138.0 9.4 %collective-permute-start.16 = (bf16[384,256]{1,0:T(8,128)(2,1)S(1)}, bf16[384,256]{1,0:T(8,128)(2,1)S(1)}, u32[]{:S(2)}, u32[]{:S(2)}) collective-permute-start(bf16[384,256]{1,0:T(8,128)(2,1)S(1)} %shard_map.99.refs_0_), channel_id=1, source_target_pairs={{0,2},{1,3},{2,0},{3,1},{4,6},{5,7},{6,4},{7,5},{8,10},{9,11},{10,... | collective-permute-start | bytes 589832 | tf_op jit(solution)/shard_map/ppermute | solution.py:196
  138.1 9.3 %collective-permute-start.15 = (bf16[384,256]{1,0:T(8,128)(2,1)S(1)}, bf16[384,256]{1,0:T(8,128)(2,1)S(1)}, u32[]{:S(2)}, u32[]{:S(2)}) collective-permute-start(bf16[384,256]{1,0:T(8,128)(2,1)S(1)} %shard_map.99.refs_0_), channel_id=1, source_target_pairs={{0,3},{1,0},{2,1},{3,2},{4,7},{5,4},{6,5},{7,6},{8,11},{9,8},{10,9... | collective-permute-start | bytes 589832 | tf_op jit(solution)/shard_map/ppermute | solution.py:196
  139.8 9.8 %collective-permute-start.14 = (bf16[384,256]{1,0:T(8,128)(2,1)S(1)}, bf16[384,256]{1,0:T(8,128)(2,1)S(1)}, u32[]{:S(2)}, u32[]{:S(2)}) collective-permute-start(bf16[384,256]{1,0:T(8,128)(2,1)S(1)} %shard_map.99.refs_0_), channel_id=1, source_target_pairs={{0,1},{1,2},{2,3},{3,0},{4,5},{5,6},{6,7},{7,4},{8,9},{9,10},{10,1... | collective-permute-start | bytes 589832 | tf_op jit(solution)/shard_map/ppermute | solution.py:196
  151.6 0.9 copy-start.9
  152.5 43.1 %all-to-all-start.3 = ((bf16[64,2,2688]{2,1,0:T(2,128)(2,1)}), bf16[64,2,2688]{2,1,0:T(2,128)(2,1)S(1)}, u32[]{:S(2)}, u32[]{:S(2)}) async-start(bf16[64,2,2688]{2,1,0:T(2,128)(2,1)} %copy-done.9), calls=%async_computation.3 | async-start | bytes 1376256 | tf_op jit(solution)/shard_map/all_to_all | solution.py:191
  162.8 8.8 %collective-permute-start.18 = (bf16[128,896]{1,0:T(8,128)(2,1)S(1)}, bf16[128,896]{1,0:T(8,128)(2,1)S(1)}, u32[]{:S(2)}, u32[]{:S(2)}) collective-permute-start(bf16[128,896]{1,0:T(8,128)(2,1)S(1)} %copy-done.4), channel_id=1, source_target_pairs={{0,3},{1,0},{2,1},{3,2},{4,7},{5,4},{6,5},{7,6},{8,11},{9,8},{10,9... | collective-permute-start | bytes 688136 | tf_op jit(solution)/shard_map/ppermute | solution.py:196
  163.7 13.5 %collective-permute-start.17 = (bf16[128,896]{1,0:T(8,128)(2,1)S(1)}, bf16[128,896]{1,0:T(8,128)(2,1)S(1)}, u32[]{:S(2)}, u32[]{:S(2)}) collective-permute-start(bf16[128,896]{1,0:T(8,128)(2,1)S(1)} %copy-done.4), channel_id=1, source_target_pairs={{0,1},{1,2},{2,3},{3,0},{4,5},{5,6},{6,7},{7,4},{8,9},{9,10},{10,1... | collective-permute-start | bytes 688136 | tf_op jit(solution)/shard_map/ppermute | solution.py:196
  165.2 12.0 %collective-permute-start.19 = (bf16[128,896]{1,0:T(8,128)(2,1)S(1)}, bf16[128,896]{1,0:T(8,128)(2,1)S(1)}, u32[]{:S(2)}, u32[]{:S(2)}) collective-permute-start(bf16[128,896]{1,0:T(8,128)(2,1)S(1)} %copy-done.4), channel_id=1, source_target_pairs={{0,2},{1,3},{2,0},{3,1},{4,6},{5,7},{6,4},{7,5},{8,10},{9,11},{10,... | collective-permute-start | bytes 688136 | tf_op jit(solution)/shard_map/ppermute | solution.py:196
  177.2 1.5 copy-start.7
  178.7 1.5 copy-start.8
  180.2 6.4 %copy-start.24 = (bf16[128,4]{0,1:T(4,128)(2,1)S(1)}, bf16[128,4]{0,1:T(4,128)(2,1)}, u32[]{:S(2)}) copy-start(bf16[128,4]{0,1:T(4,128)(2,1)} %param.11) | copy-start | bytes 3076
  182.0 0.7 copy-start.11
  182.7 12.8 %collective-permute-start.20 = (bf16[128,896]{1,0:T(8,128)(2,1)}, bf16[128,896]{1,0:T(8,128)(2,1)S(1)}, u32[]{:S(2)}, u32[]{:S(2)}) collective-permute-start(bf16[128,896]{1,0:T(8,128)(2,1)} %get-tuple-element.26), channel_id=1, source_target_pairs={{0,1},{1,2},{2,3},{3,0},{4,5},{5,6},{6,7},{7,4},{8,9},{9,10},{10,1... | collective-permute-start | bytes 688136 | tf_op jit(solution)/shard_map/ppermute | solution.py:196
  182.7 12.8 %collective-permute-start.21 = (bf16[128,896]{1,0:T(8,128)(2,1)}, bf16[128,896]{1,0:T(8,128)(2,1)S(1)}, u32[]{:S(2)}, u32[]{:S(2)}) collective-permute-start(bf16[128,896]{1,0:T(8,128)(2,1)} %get-tuple-element.27), channel_id=1, source_target_pairs={{0,3},{1,0},{2,1},{3,2},{4,7},{5,4},{6,5},{7,6},{8,11},{9,8},{10,9... | collective-permute-start | bytes 688136 | tf_op jit(solution)/shard_map/ppermute | solution.py:196
  185.9 9.6 %collective-permute-start.22 = (bf16[128,896]{1,0:T(8,128)(2,1)}, bf16[128,896]{1,0:T(8,128)(2,1)S(1)}, u32[]{:S(2)}, u32[]{:S(2)}) collective-permute-start(bf16[128,896]{1,0:T(8,128)(2,1)} %get-tuple-element.28), channel_id=1, source_target_pairs={{0,2},{1,3},{2,0},{3,1},{4,6},{5,7},{6,4},{7,5},{8,10},{9,11},{10,... | collective-permute-start | bytes 688136 | tf_op jit(solution)/shard_map/ppermute | solution.py:196
  195.6 0.9 copy-start.12

commit v5 on v4

--- a/solution.py
+++ b/solution.py
@@ -24,14 +24,12 @@
     return jnp.concatenate(parts, axis=0)
 
 
-def unflat(out_ref, x, start=0):
+def unflat(out_ref, x, lane=0):
+    rows = out_ref.shape[0] * PAIR
     width = x.shape[1]
-    count = out_ref.shape[2] // width
-    rows = x.shape[0] // count
-    span = pl.ds(start, rows // PAIR)
-    for p in range(count):
-        part = x[p * rows : (p + 1) * rows]
-        out_ref[span, :, p * width : (p + 1) * width] = part.reshape(-1, PAIR, width)
+    for p in range(x.shape[0] // rows):
+        part = x[p * rows : (p + 1) * rows].reshape(-1, PAIR, width)
+        out_ref[:, :, lane + p * width : lane + (p + 1) * width] = part
 
 
 def silu_times(gate, up):
@@ -64,7 +62,8 @@
 
 
 def gather_body(experts, first, size):
-    def body(ids_ref, tokens_ref, out_ref):
+    def body(ids_ref, *refs):
+        *tokens_refs, out_ref = refs
         ids = ids_ref[...]
         top, rows = ids.shape
         numbers = lax.broadcasted_iota(jnp.int32, (experts, rows), 0)
@@ -87,7 +86,10 @@
                 target = jnp.where(inside, ids[k : k + 1] * PAIR + local, -1)
                 pick = jnp.where(target == place, 1.0, pick)
             picks.append(pick.astype(BF16))
-        unflat(out_ref, dot(jnp.concatenate(picks, axis=0), tokens_ref[...]).astype(BF16))
+        picks = jnp.concatenate(picks, axis=0)
+        for s, tokens_ref in enumerate(tokens_refs):
+            x = dot(picks, tokens_ref[...]).astype(BF16)
+            unflat(out_ref, x, lane=s * (size // PAIR) * x.shape[1])
 
     return body
 
@@ -139,9 +141,9 @@
         out_ref[...] = dot(hidden, part).astype(BF16)
 
 
-def partial_body(q_ref, own_ref, left_ref, right_ref, gate_ref, up_ref, sums_ref, far_ref):
-    n, width, quarter = gate_ref.shape
-    at = [lax.rem(q_ref[0] + s, n) for s in TURNS]
+def ring_sums_body(q_ref, own_ref, left_ref, right_ref, gate_ref, up_ref, sums_ref, rest_ref):
+    _, width, quarter = gate_ref.shape
+    at = [lax.rem(q_ref[0] + s, len(TURNS)) for s in TURNS]
     half = own_ref.shape[0] // 2
     rows = sums_ref.shape[0] // 2
     for h in range(2):
@@ -150,29 +152,56 @@
         out = pl.ds(h * rows, rows)
         sums_ref[out, :quarter] = sum(dot(x, gate_ref[i]) for x, i in zip(xs, at))
         sums_ref[out, quarter:] = sum(dot(x, up_ref[i]) for x, i in zip(xs, at))
-    far_ref[0] = gate_ref[at[3]]
-    far_ref[1] = up_ref[at[3]]
-
-
-def hidden_body(sums_ref, o0_ref, o1_ref, far_ref, out_ref):
-    _, width, quarter = far_ref.shape
-    rows = sums_ref.shape[0] // 2
-    for h, o_ref in enumerate((o0_ref, o1_ref)):
-        span = pl.ds(h * rows, rows)
-        x = flat(o_ref[...], width)
-        gate = sums_ref[span, :quarter] + dot(x, far_ref[0])
-        up = sums_ref[span, quarter:] + dot(x, far_ref[1])
-        out_ref[span] = silu_times(gate, up)
-
-
-def down_body(*refs):
+    rest_ref[0] = gate_ref[at[3]]
+    rest_ref[1] = up_ref[at[3]]
+
+
+def ring_hidden_body(sums_ref, o0_ref, o1_ref, rest_ref, out_ref):
+    _, width, quarter = rest_ref.shape
+    x = jnp.concatenate([flat(o0_ref[...], width), flat(o1_ref[...], width)], axis=0)
+    gate = sums_ref[:, :quarter] + dot(x, rest_ref[0])
+    up = sums_ref[:, quarter:] + dot(x, rest_ref[1])
+    out_ref[...] = silu_times(gate, up)
+
+
+def pair_sums_body(q_ref, rows_ref, gate_ref, up_ref, sums_ref, rest_ref):
+    _, width, quarter = gate_ref.shape
+    at = [lax.rem(q_ref[0] + s, len(TURNS)) for s in TURNS]
+    lanes = rows_ref.shape[2] // 2
+    own = flat(rows_ref[:, :, :lanes], width)
+    far = flat(rows_ref[:, :, lanes:], width)
+    sums_ref[:, :quarter] = dot(own, gate_ref[at[0]]) + dot(far, gate_ref[at[3]])
+    sums_ref[:, quarter:] = dot(own, up_ref[at[0]]) + dot(far, up_ref[at[3]])
+    for i in range(2):
+        rest_ref[2 * i] = gate_ref[at[1 + i]]
+        rest_ref[2 * i + 1] = up_ref[at[1 + i]]
+
+
+def pair_hidden_body(sums_ref, left_ref, right_ref, rest_ref, out_ref):
+    _, width, quarter = rest_ref.shape
+    left, right = flat(left_ref[...], width), flat(right_ref[...], width)
+    gate = sums_ref[:, :quarter] + dot(left, rest_ref[0]) + dot(right, rest_ref[2])
+    up = sums_ref[:, quarter:] + dot(left, rest_ref[1]) + dot(right, rest_ref[3])
+    out_ref[...] = silu_times(gate, up)
+
+
+def stack_body(*refs):
     *ins, out_ref = refs
-    n = len(TURNS)
-    rows = ins[0].shape[0] // 2
-    for h in range(2):
-        span = pl.ds(h * rows, rows)
-        total = sum(dot(a[span], w[...]) for a, w in zip(ins[:n], ins[n:]))
-        unflat(out_ref, total.astype(BF16), h * out_ref.shape[0] // 2)
+    for s, ref in enumerate(ins):
+        out_ref[s] = ref[...]
+
+
+def down_body(halves):
+    def body(*refs):
+        *ins, down_ref, out_ref = refs
+        count = out_ref.shape[0] // halves
+        rows = ins[0].shape[0] // halves
+        for h in range(halves):
+            span = pl.ds(h * rows, rows)
+            total = sum(dot(a[span], down_ref[s]) for s, a in enumerate(ins))
+            unflat(out_ref.at[pl.ds(h * count, count)], total.astype(BF16))
+
+    return body
 
 
 def combine_body(weight_ref, *refs):
@@ -230,17 +259,18 @@
 
     ids_t = expert_ids.T
     tokens_all = spread(tokens)
+    ids_t = expert_ids.T
     arrived = []
-    for j, size in enumerate(CHUNKS):
+    for j, (size, sources) in enumerate(zip(CHUNKS, ([tokens], [tokens, tokens_all[3]]))):
         (rows,) = kernel_call(
             gather_body(experts, sum(CHUNKS[:j]), size),
-            [(experts, PAIR, size // PAIR * narrow)],
+            [(experts, PAIR, len(sources) * size // PAIR * narrow)],
             ids_t,
-            tokens,
+            *sources,
         )
         arrived.append(exchange(rows, EXPERT))
     columns = kernel_call(columns_body, [(quarter, narrow)] * n, q, w_down, smem=1)
-    down = deal(columns)
+    (down,) = kernel_call(stack_body, [(n, quarter, narrow)], *deal(columns))
     (weight,) = kernel_call(
         weight_body(experts), [(tok_dev, experts * sum(CHUNKS))], expert_ids, gate_values
     )
@@ -257,29 +287,35 @@
     )
 
     returned = []
-    for rows, size in zip(arrived, CHUNKS):
-        left, right, o0, o1 = ring(rows)
-        sums, far = kernel_call(
-            partial_body,
-            [
-                jax.ShapeDtypeStruct((experts * size, 2 * quarter), F32),
-                (2, narrow, quarter),
-            ],
+    for j, (rows, size) in enumerate(zip(arrived, CHUNKS)):
+        count = experts * size
+        sums_shape = jax.ShapeDtypeStruct((count, 2 * quarter), F32)
+        if j == 0:
+            left, right, *last = ring(rows)
+            args = (rows, left, right)
+            bodies = ring_sums_body, ring_hidden_body
+        else:
+            own = rows[:, :, : size // PAIR * narrow]
+            last = shift(own, "tensor", 1), shift(own, "tensor", -1)
+            args = (rows,)
+            bodies = pair_sums_body, pair_hidden_body
+        sums, rest = kernel_call(
+            bodies[0],
+            [sums_shape, (2 * (1 + j), narrow, quarter)],
             q,
-            rows,
-            left,
-            right,
+            *args,
             w_gate,
             w_up,
             smem=1,
             flops=10**9,
         )
-        (hidden,) = kernel_call(
-            hidden_body, [(experts * size, quarter)], sums, o0, o1, far, flops=10**9
-        )
-        hidden_all = spread(hidden)
+        (hidden,) = kernel_call(bodies[1], [(count, quarter)], sums, *last, rest, flops=10**9)
         (out,) = kernel_call(
-            down_body, [(experts, PAIR, size // PAIR * narrow)], *hidden_all, *down, flops=10**9
+            down_body(2 - j),
+            [(experts, PAIR, size // PAIR * narrow)],
+            *spread(hidden),
+            down,
+            flops=10**9,
         )
         returned.append(exchange(out, EXPERT))
     shared_all = deal(shared_parts)

time: 199 us -> 193 us (0.970)
  starting transfers between devices: 64.6 us -> 80.2 us
  waiting for transfers between devices: 92.8 us -> 78.6 us
  local copies, waits for them, and re-layouts: 21.2 us -> 16.9 us
  Pallas kernels: 18.9 us -> 16.2 us
    ppermute x23 -> x21, starting transfers between devices: 25.9 us -> 41.4 us  [shift(): return lax.ppermute(x, axis, [(i, (i + by) % n) for i in range(n)])]
    all_to_all x4, waiting for transfers between devices: 19.2 us -> 8.86 us  [exchange(): return lax.all_to_all(x, axis, split_axis=0, concat_axis=0, tiled=True)]
    ppermute x23 -> x21, waiting for transfers between devices: 73.7 us -> 69.8 us  [shift(): return lax.ppermute(x, axis, [(i, (i + by) % n) for i in range(n)])]
    pallas_call x12 -> x13, Pallas kernels: 18.9 us -> 16.2 us  [kernel_call(): pl.pallas_call(body, in_specs=[pl.BlockSpec(memory_space=m) for m in plac...]
    unnamed x52 -> x42, local copies, waits for them, and re-layouts: 16.3 us -> 14 us
  transfers between devices with their start and end apart: 27 -> 25, of which waited for: 13 -> 14; matrix products, arithmetic and copies ran while one was open for 3% -> 2% of each run, Pallas kernels for 8% -> 6%
where the time goes in v5:
time: 193 us; the launch traced here: 192 us
  starting transfers between devices  80.2 us (42%)
  waiting for transfers between devices  78.6 us (41%)
  local copies, waits for them, and re-layouts  16.9 us (9%)
  Pallas kernels  16.2 us (8%)
    ppermute x21, waiting for transfers between devices, shift(): return lax.ppermute(x, axis, [(i, (i + by) % n) for i in range(n)])  69.8 us
    ppermute x21, starting transfers between devices, shift(): return lax.ppermute(x, axis, [(i, (i + by) % n) for i in range(n)])  41.4 us
    all_to_all x4, starting transfers between devices, exchange(): return lax.all_to_all(x, axis, split_axis=0, concat_axis=0, tiled=True)  38.8 us
    pallas_call x13, Pallas kernels, kernel_call(): pl.pallas_call(body, in_specs=[pl.BlockSpec(memory_space=m) for m in plac...  16.2 us
    unnamed x42, local copies, waits for them, and re-layouts  14 us
    all_to_all x4, waiting for transfers between devices, exchange(): return lax.all_to_all(x, axis, split_axis=0, concat_axis=0, tiled=True)  8.86 us
  transfers between devices with their start and end apart: 25, of which 14 were waited for; matrix products, arithmetic and copies ran while one was open for 2% of the time, Pallas kernels for 6%

profile of v5, /device:TPU:32, one launch (start us, length us, event | category | flops | bytes accessed | tf_op | source)
XLA Modules:
  0.0 192.1 jit_solution(1777241559517669453)
XLA Ops:
  0.0 0.9 copy-done.5
  0.9 0.7 copy-done.17
  1.6 1.4 shard_map.92
  3.0 11.6 %all-to-all-start = ((bf16[64,2,2688]{2,1,0:T(2,128)(2,1)}), bf16[64,2,2688]{2,1,0:T(2,128)(2,1)S(1)}, u32[]{:S(2)}, u32[]{:S(2)}) async-start(bf16[64,2,2688]{2,1,0:T(2,128)(2,1)} %shard_map.92), calls=%async_computation | async-start | bytes 1376256 | tf_op jit(solution)/shard_map/all_to_all | solution.py:220
  14.6 3.3 %collective-permute-start.10 = (bf16[128,896]{1,0:T(8,128)(2,1)S(1)}, bf16[128,896]{1,0:T(8,128)(2,1)S(1)}, u32[]{:S(2)}, u32[]{:S(2)}) collective-permute-start(bf16[128,896]{1,0:T(8,128)(2,1)S(1)} %copy-done.6), channel_id=1, source_target_pairs={{0,2},{1,3},{2,0},{3,1},{4,6},{5,7},{6,4},{7,5},{8,10},{9,11},{10,... | collective-permute-start | bytes 688136 | tf_op jit(solution)/shard_map/ppermute | solution.py:225
  17.9 5.9 %collective-permute-done.10.refs_1_.refs_3_ = bf16[128,896]{1,0:T(8,128)(2,1)S(1)} collective-permute-done((bf16[128,896]{1,0:T(8,128)(2,1)S(1)}, bf16[128,896]{1,0:T(8,128)(2,1)S(1)}, u32[]{:S(2)}, u32[]{:S(2)}) %collective-permute-start.10) | collective-permute-done | bytes 229408 | tf_op jit(solution)/shard_map/ppermute | solution.py:225
  23.8 1.8 shard_map.98
  25.7 0.7 copy-done.13
  26.4 8.9 %all-to-all-done.own_ref = bf16[64,2,2688]{2,1,0:T(2,128)(2,1)S(1)} async-done(((bf16[64,2,2688]{2,1,0:T(2,128)(2,1)}), bf16[64,2,2688]{2,1,0:T(2,128)(2,1)S(1)}, u32[]{:S(2)}, u32[]{:S(2)}) %all-to-all-start) | async-done | bytes 688160 | tf_op jit(solution)/shard_map/all_to_all | solution.py:220
  35.2 0.9 copy-done.3
  36.1 6.5 %all-to-all-start.2 = ((bf16[64,2,5376]{2,1,0:T(2,128)(2,1)}), bf16[64,2,5376]{2,1,0:T(2,128)(2,1)S(1)}, u32[]{:S(2)}, u32[]{:S(2)}) async-start(bf16[64,2,5376]{2,1,0:T(2,128)(2,1)} %shard_map.98), calls=%async_computation.2 | async-start | bytes 2752512 | tf_op jit(solution)/shard_map/all_to_all | solution.py:220
  42.6 1.7 collective-permute-start
  44.2 1.7 collective-permute-start.1
  45.9 1.6 copy-done.9
  47.6 0.4 collective-permute-start.7
  48.0 14.4 %collective-permute-done.left_ref = bf16[64,2,2688]{2,1,0:T(2,128)(2,1)} collective-permute-done((bf16[64,2,2688]{2,1,0:T(2,128)(2,1)}, bf16[64,2,2688]{2,1,0:T(2,128)(2,1)}, u32[]{:S(2)}, u32[]{:S(2)}) %collective-permute-start) | collective-permute-done | bytes 688160 | tf_op jit(solution)/shard_map/ppermute | solution.py:225
  62.5 1.2 slice.12
  63.7 0.4 collective-permute-start.2
  64.1 1.2 slice.13
  65.4 2.9 %collective-permute-start.3 = (bf16[32,2,2688]{2,1,0:T(2,128)(2,1)S(1)}, bf16[32,2,2688]{2,1,0:T(2,128)(2,1)S(1)}, u32[]{:S(2)}, u32[]{:S(2)}) collective-permute-start(bf16[32,2,2688]{2,1,0:T(2,128)(2,1)S(1)} %slice.13), channel_id=1, source_target_pairs={{0,3},{1,0},{2,1},{3,2},{4,7},{5,4},{6,5},{7,6},{8,11},{9,8},{10,9... | collective-permute-start | bytes 1032200 | tf_op jit(solution)/shard_map/ppermute | solution.py:225
  68.3 0.6 collective-permute-start.8
  68.9 0.6 collective-permute-start.9
  69.5 1.5 copy-done.1
  71.0 2.8 %shard_map.93 = (f32[384,512]{1,0:T(8,128)S(1)}, bf16[2,896,256]{2,1,0:T(8,128)(2,1)S(1)}) custom-call(s32[1]{0:T(128)} %bitcast.q_ref, bf16[64,2,2688]{2,1,0:T(2,128)(2,1)S(1)} %copy-done.4, bf16[64,2,2688]{2,1,0:T(2,128)(2,1)} %collective-permute-done.left_ref, bf16[64,2,2688]{2,1,0:T(2,128)(2,1)} %collective-permute-done.1.right_ref, ...), custom_call_target="tpu_custom_call" | custom-call | flops 1000000000 | tf_op jit(solution)/shard_map/pallas_call | solution.py:41
  73.8 5.0 %collective-permute-done.2.o0_ref = bf16[32,2,2688]{2,1,0:T(2,128)(2,1)S(1)} collective-permute-done((bf16[32,2,2688]{2,1,0:T(2,128)(2,1)S(1)}, bf16[32,2,2688]{2,1,0:T(2,128)(2,1)S(1)}, u32[]{:S(2)}, u32[]{:S(2)}) %collective-permute-start.2) | collective-permute-done | bytes 344096 | tf_op jit(solution)/shard_map/ppermute | solution.py:225
  78.8 0.6 shard_map.94.refs_0_
  79.4 1.2 collective-permute-start.4
  80.6 2.1 %collective-permute-start.5 = (bf16[384,256]{1,0:T(8,128)(2,1)S(1)}, bf16[384,256]{1,0:T(8,128)(2,1)S(1)}, u32[]{:S(2)}, u32[]{:S(2)}) collective-permute-start(bf16[384,256]{1,0:T(8,128)(2,1)S(1)} %shard_map.94.refs_0_), channel_id=1, source_target_pairs={{0,3},{1,0},{2,1},{3,2},{4,7},{5,4},{6,5},{7,6},{8,11},{9,8},{10,9... | collective-permute-start | bytes 589832 | tf_op jit(solution)/shard_map/ppermute | solution.py:225
  82.7 9.8 %collective-permute-start.6 = (bf16[384,256]{1,0:T(8,128)(2,1)S(1)}, bf16[384,256]{1,0:T(8,128)(2,1)S(1)}, u32[]{:S(2)}, u32[]{:S(2)}) collective-permute-start(bf16[384,256]{1,0:T(8,128)(2,1)S(1)} %shard_map.94.refs_0_), channel_id=1, source_target_pairs={{0,2},{1,3},{2,0},{3,1},{4,6},{5,7},{6,4},{7,5},{8,10},{9,11},{10,... | collective-permute-start | bytes 589832 | tf_op jit(solution)/shard_map/ppermute | solution.py:225
  92.5 5.2 %collective-permute-done.8.refs_2_ = bf16[256,896]{1,0:T(8,128)(2,1)S(1)} collective-permute-done((bf16[256,896]{1,0:T(8,128)(2,1)S(1)}, bf16[256,896]{1,0:T(8,128)(2,1)S(1)}, u32[]{:S(2)}, u32[]{:S(2)}) %collective-permute-start.8) | collective-permute-done | bytes 458784 | tf_op jit(solution)/shard_map/ppermute | solution.py:225
  97.9 4.2 %collective-permute-done.5.refs_2_ = bf16[384,256]{1,0:T(8,128)(2,1)S(1)} collective-permute-done((bf16[384,256]{1,0:T(8,128)(2,1)S(1)}, bf16[384,256]{1,0:T(8,128)(2,1)S(1)}, u32[]{:S(2)}, u32[]{:S(2)}) %collective-permute-start.5) | collective-permute-done | bytes 196640 | tf_op jit(solution)/shard_map/ppermute | solution.py:225
  102.1 1.0 shard_map.97
  103.2 1.3 copy-done.7
  104.4 0.9 copy-done.15
  105.3 10.5 %all-to-all-start.1 = ((bf16[64,2,2688]{2,1,0:T(2,128)(2,1)}), bf16[64,2,2688]{2,1,0:T(2,128)(2,1)}, u32[]{:S(2)}, u32[]{:S(2)}) async-start(bf16[64,2,2688]{2,1,0:T(2,128)(2,1)} %copy-done.15), calls=%async_computation.1 | async-start | bytes 1376256 | tf_op jit(solution)/shard_map/all_to_all | solution.py:220
  115.8 0.5 slice.14
  116.3 1.9 collective-permute-start.11
  118.2 2.0 %collective-permute-start.12 = (bf16[64,2,2688]{2,1,0:T(2,128)(2,1)S(1)}, bf16[64,2,2688]{2,1,0:T(2,128)(2,1)S(1)}, u32[]{:S(2)}, u32[]{:S(2)}) collective-permute-start(bf16[64,2,2688]{2,1,0:T(2,128)(2,1)S(1)} %slice.14), channel_id=1, source_target_pairs={{0,3},{1,0},{2,1},{3,2},{4,7},{5,4},{6,5},{7,6},{8,11},{9,8},{10,9... | collective-permute-start | bytes 2064392 | tf_op jit(solution)/shard_map/ppermute | solution.py:225
  120.1 1.5 copy-done.2
  121.6 1.1 shard_map.99
  122.8 13.0 %collective-permute-done.11.left_ref = bf16[64,2,2688]{2,1,0:T(2,128)(2,1)S(1)} collective-permute-done((bf16[64,2,2688]{2,1,0:T(2,128)(2,1)S(1)}, bf16[64,2,2688]{2,1,0:T(2,128)(2,1)S(1)}, u32[]{:S(2)}, u32[]{:S(2)}) %collective-permute-start.11) | collective-permute-done | bytes 688160 | tf_op jit(solution)/shard_map/ppermute | solution.py:225
  135.8 1.0 shard_map.100.refs_0_
  136.8 1.2 collective-permute-start.13
  138.1 2.1 %collective-permute-start.14 = (bf16[384,256]{1,0:T(8,128)(2,1)S(1)}, bf16[384,256]{1,0:T(8,128)(2,1)S(1)}, u32[]{:S(2)}, u32[]{:S(2)}) collective-permute-start(bf16[384,256]{1,0:T(8,128)(2,1)S(1)} %shard_map.100.refs_0_), channel_id=1, source_target_pairs={{0,3},{1,0},{2,1},{3,2},{4,7},{5,4},{6,5},{7,6},{8,11},{9,8},{10,9... | collective-permute-start | bytes 589832 | tf_op jit(solution)/shard_map/ppermute | solution.py:225
  140.2 1.7 collective-permute-start.15
  141.9 3.3 %collective-permute-done.13.refs_1_ = bf16[384,256]{1,0:T(8,128)(2,1)S(1)} collective-permute-done((bf16[384,256]{1,0:T(8,128)(2,1)S(1)}, bf16[384,256]{1,0:T(8,128)(2,1)S(1)}, u32[]{:S(2)}, u32[]{:S(2)}) %collective-permute-start.13) | collective-permute-done | bytes 196640 | tf_op jit(solution)/shard_map/ppermute | solution.py:225
  145.2 2.9 %collective-permute-done.14.refs_2_ = bf16[384,256]{1,0:T(8,128)(2,1)S(1)} collective-permute-done((bf16[384,256]{1,0:T(8,128)(2,1)S(1)}, bf16[384,256]{1,0:T(8,128)(2,1)S(1)}, u32[]{:S(2)}, u32[]{:S(2)}) %collective-permute-start.14) | collective-permute-done | bytes 196640 | tf_op jit(solution)/shard_map/ppermute | solution.py:225
  148.1 1.7 collective-permute-done.15.refs_3_
  149.8 1.0 shard_map.101
  150.8 0.8 copy-done.16
  151.6 10.2 %all-to-all-start.3 = ((bf16[64,2,2688]{2,1,0:T(2,128)(2,1)}), bf16[64,2,2688]{2,1,0:T(2,128)(2,1)S(1)}, u32[]{:S(2)}, u32[]{:S(2)}) async-start(bf16[64,2,2688]{2,1,0:T(2,128)(2,1)} %copy-done.16), calls=%async_computation.3 | async-start | bytes 1376256 | tf_op jit(solution)/shard_map/all_to_all | solution.py:220
  161.9 1.2 collective-permute-start.16
  163.1 2.1 %collective-permute-start.17 = (bf16[128,896]{1,0:T(8,128)(2,1)S(1)}, bf16[128,896]{1,0:T(8,128)(2,1)S(1)}, u32[]{:S(2)}, u32[]{:S(2)}) collective-permute-start(bf16[128,896]{1,0:T(8,128)(2,1)S(1)} %copy-done.6), channel_id=1, source_target_pairs={{0,3},{1,0},{2,1},{3,2},{4,7},{5,4},{6,5},{7,6},{8,11},{9,8},{10,9... | collective-permute-start | bytes 688136 | tf_op jit(solution)/shard_map/ppermute | solution.py:225
  165.2 5.6 %collective-permute-done.16.refs_1_ = bf16[128,896]{1,0:T(8,128)(2,1)S(1)} collective-permute-done((bf16[128,896]{1,0:T(8,128)(2,1)S(1)}, bf16[128,896]{1,0:T(8,128)(2,1)S(1)}, u32[]{:S(2)}, u32[]{:S(2)}) %collective-permute-start.16) | collective-permute-done | bytes 229408 | tf_op jit(solution)/shard_map/ppermute | solution.py:225
  170.8 1.5 copy-done.11
  172.3 1.5 copy-done.12
  173.8 1.8 shard_map.102
  175.9 3.0 %collective-permute-start.19 = (bf16[128,896]{1,0:T(8,128)(2,1)}, bf16[128,896]{1,0:T(8,128)(2,1)S(1)}, u32[]{:S(2)}, u32[]{:S(2)}) collective-permute-start(bf16[128,896]{1,0:T(8,128)(2,1)} %get-tuple-element.27), channel_id=1, source_target_pairs={{0,3},{1,0},{2,1},{3,2},{4,7},{5,4},{6,5},{7,6},{8,11},{9,8},{10,9... | collective-permute-start | bytes 688136 | tf_op jit(solution)/shard_map/ppermute | solution.py:225
  178.9 1.2 collective-permute-start.20
  180.3 0.9 shard_map.91.weight_ref
  181.2 3.7 %collective-permute-done.18.refs_3_ = bf16[128,896]{1,0:T(8,128)(2,1)S(1)} collective-permute-done((bf16[128,896]{1,0:T(8,128)(2,1)}, bf16[128,896]{1,0:T(8,128)(2,1)S(1)}, u32[]{:S(2)}, u32[]{:S(2)}) %collective-permute-start.18) | collective-permute-done | bytes 229408 | tf_op jit(solution)/shard_map/ppermute | solution.py:225
  184.9 3.2 %collective-permute-done.19.refs_4_ = bf16[128,896]{1,0:T(8,128)(2,1)S(1)} collective-permute-done((bf16[128,896]{1,0:T(8,128)(2,1)}, bf16[128,896]{1,0:T(8,128)(2,1)S(1)}, u32[]{:S(2)}, u32[]{:S(2)}) %collective-permute-start.19) | collective-permute-done | bytes 229408 | tf_op jit(solution)/shard_map/ppermute | solution.py:225
  188.1 1.5 collective-permute-done.20.refs_5_
  189.6 2.4 %shard_map.103 = bf16[128,896]{1,0:T(8,128)(2,1)} custom-call(bf16[128,768]{1,0:T(8,128)(2,1)S(1)} %shard_map.91.weight_ref, bf16[64,2,2688]{2,1,0:T(2,128)(2,1)} %all-to-all-done.1.refs_0_, bf16[64,2,2688]{2,1,0:T(2,128)(2,1)S(1)} %all-to-all-done.3.refs_1_, bf16[128,896]{1,0:T(8,128)(2,1)S(1)} %get-tuple-element.25.refs_2_, ...), custom_call_target="tpu_custom_call" | custom-call | flops 1 | tf_op jit(solution)/shard_map/pallas_call | solution.py:41
  (44 shorter events, 0.8 us)
Async XLA Ops:
  0.0 0.9 copy-start.5
  0.9 0.7 copy-start.17
  1.6 13.0 %copy-start.6 = (bf16[128,896]{1,0:T(8,128)(2,1)S(1)}, bf16[128,896]{1,0:T(8,128)(2,1)}, u32[]{:S(2)}) copy-start(bf16[128,896]{1,0:T(8,128)(2,1)} %refs_0_.5) | copy-start | bytes 688132
  1.6 22.2 %copy-start.18 = (s32[128,4]{0,1:T(4,128)S(1)}, s32[128,4]{0,1:T(4,128)}, u32[]{:S(2)}) copy-start(s32[128,4]{0,1:T(4,128)} %param.10) | copy-start | bytes 6148
  3.0 32.2 %all-to-all-start = ((bf16[64,2,2688]{2,1,0:T(2,128)(2,1)}), bf16[64,2,2688]{2,1,0:T(2,128)(2,1)S(1)}, u32[]{:S(2)}, u32[]{:S(2)}) async-start(bf16[64,2,2688]{2,1,0:T(2,128)(2,1)} %shard_map.92), calls=%async_computation | async-start | bytes 1376256 | tf_op jit(solution)/shard_map/all_to_all | solution.py:220
  14.6 9.2 %collective-permute-start.10 = (bf16[128,896]{1,0:T(8,128)(2,1)S(1)}, bf16[128,896]{1,0:T(8,128)(2,1)S(1)}, u32[]{:S(2)}, u32[]{:S(2)}) collective-permute-start(bf16[128,896]{1,0:T(8,128)(2,1)S(1)} %copy-done.6), channel_id=1, source_target_pairs={{0,2},{1,3},{2,0},{3,1},{4,6},{5,7},{6,4},{7,5},{8,10},{9,11},{10,... | collective-permute-start | bytes 688136 | tf_op jit(solution)/shard_map/ppermute | solution.py:225
  25.7 0.7 copy-start.13
  35.2 0.9 copy-start.3
  36.1 69.2 %all-to-all-start.2 = ((bf16[64,2,5376]{2,1,0:T(2,128)(2,1)}), bf16[64,2,5376]{2,1,0:T(2,128)(2,1)S(1)}, u32[]{:S(2)}, u32[]{:S(2)}) async-start(bf16[64,2,5376]{2,1,0:T(2,128)(2,1)} %shard_map.98), calls=%async_computation.2 | async-start | bytes 2752512 | tf_op jit(solution)/shard_map/all_to_all | solution.py:220
  42.5 27.0 %copy-start = (bf16[1,3584,256]{2,1,0:T(8,128)(2,1)S(1)}, bf16[1,3584,256]{2,1,0:T(8,128)(2,1)}, u32[]{:S(2)}) copy-start(bf16[1,3584,256]{2,1,0:T(8,128)(2,1)} %param.12) | copy-start | bytes 5505028
  42.6 19.9 %collective-permute-start = (bf16[64,2,2688]{2,1,0:T(2,128)(2,1)}, bf16[64,2,2688]{2,1,0:T(2,128)(2,1)}, u32[]{:S(2)}, u32[]{:S(2)}) collective-permute-start(bf16[64,2,2688]{2,1,0:T(2,128)(2,1)} %copy-done.3), channel_id=1, source_target_pairs={{0,1},{1,2},{2,3},{3,0},{4,5},{5,6},{6,7},{7,4},{8,9},{9,10},{10,1... | collective-permute-start | bytes 2064392 | tf_op jit(solution)/shard_map/ppermute | solution.py:225
  44.2 19.9 %collective-permute-start.1 = (bf16[64,2,2688]{2,1,0:T(2,128)(2,1)}, bf16[64,2,2688]{2,1,0:T(2,128)(2,1)}, u32[]{:S(2)}, u32[]{:S(2)}) collective-permute-start(bf16[64,2,2688]{2,1,0:T(2,128)(2,1)} %copy-done.3), channel_id=1, source_target_pairs={{0,3},{1,0},{2,1},{3,2},{4,7},{5,4},{6,5},{7,6},{8,11},{9,8},{10,9... | collective-permute-start | bytes 2064392 | tf_op jit(solution)/shard_map/ppermute | solution.py:225
  45.9 23.7 %copy-start.4 = (bf16[64,2,2688]{2,1,0:T(2,128)(2,1)S(1)}, bf16[64,2,2688]{2,1,0:T(2,128)(2,1)}, u32[]{:S(2)}) copy-start(bf16[64,2,2688]{2,1,0:T(2,128)(2,1)} %copy-done.3) | copy-start | bytes 2064388
  45.9 1.6 copy-start.9
  47.6 35.2 %collective-permute-start.7 = (bf16[256,896]{1,0:T(8,128)(2,1)S(1)}, bf16[256,896]{1,0:T(8,128)(2,1)S(1)}, u32[]{:S(2)}, u32[]{:S(2)}) collective-permute-start(bf16[256,896]{1,0:T(8,128)(2,1)S(1)} %get-tuple-element.20), channel_id=1, source_target_pairs={{0,1},{1,2},{2,3},{3,0},{4,5},{5,6},{6,7},{7,4},{8,9},{9,10},{10,1... | collective-permute-start | bytes 1376264 | tf_op jit(solution)/shard_map/ppermute | solution.py:225
  63.7 15.1 %collective-permute-start.2 = (bf16[32,2,2688]{2,1,0:T(2,128)(2,1)S(1)}, bf16[32,2,2688]{2,1,0:T(2,128)(2,1)S(1)}, u32[]{:S(2)}, u32[]{:S(2)}) collective-permute-start(bf16[32,2,2688]{2,1,0:T(2,128)(2,1)S(1)} %slice.12), channel_id=1, source_target_pairs={{0,1},{1,2},{2,3},{3,0},{4,5},{5,6},{6,7},{7,4},{8,9},{9,10},{10,1... | collective-permute-start | bytes 1032200 | tf_op jit(solution)/shard_map/ppermute | solution.py:225
  65.4 13.4 %collective-permute-start.3 = (bf16[32,2,2688]{2,1,0:T(2,128)(2,1)S(1)}, bf16[32,2,2688]{2,1,0:T(2,128)(2,1)S(1)}, u32[]{:S(2)}, u32[]{:S(2)}) collective-permute-start(bf16[32,2,2688]{2,1,0:T(2,128)(2,1)S(1)} %slice.13), channel_id=1, source_target_pairs={{0,3},{1,0},{2,1},{3,2},{4,7},{5,4},{6,5},{7,6},{8,11},{9,8},{10,9... | collective-permute-start | bytes 1032200 | tf_op jit(solution)/shard_map/ppermute | solution.py:225
  68.3 29.5 %collective-permute-start.8 = (bf16[256,896]{1,0:T(8,128)(2,1)S(1)}, bf16[256,896]{1,0:T(8,128)(2,1)S(1)}, u32[]{:S(2)}, u32[]{:S(2)}) collective-permute-start(bf16[256,896]{1,0:T(8,128)(2,1)S(1)} %get-tuple-element.21), channel_id=1, source_target_pairs={{0,3},{1,0},{2,1},{3,2},{4,7},{5,4},{6,5},{7,6},{8,11},{9,8},{10,9... | collective-permute-start | bytes 1376264 | tf_op jit(solution)/shard_map/ppermute | solution.py:225
  68.9 28.9 %collective-permute-start.9 = (bf16[256,896]{1,0:T(8,128)(2,1)S(1)}, bf16[256,896]{1,0:T(8,128)(2,1)S(1)}, u32[]{:S(2)}, u32[]{:S(2)}) collective-permute-start(bf16[256,896]{1,0:T(8,128)(2,1)S(1)} %get-tuple-element.22), channel_id=1, source_target_pairs={{0,2},{1,3},{2,0},{3,1},{4,6},{5,7},{6,4},{7,5},{8,10},{9,11},{10,... | collective-permute-start | bytes 1376264 | tf_op jit(solution)/shard_map/ppermute | solution.py:225
  69.5 1.5 copy-start.1
  79.4 18.5 %collective-permute-start.4 = (bf16[384,256]{1,0:T(8,128)(2,1)S(1)}, bf16[384,256]{1,0:T(8,128)(2,1)S(1)}, u32[]{:S(2)}, u32[]{:S(2)}) collective-permute-start(bf16[384,256]{1,0:T(8,128)(2,1)S(1)} %shard_map.94.refs_0_), channel_id=1, source_target_pairs={{0,1},{1,2},{2,3},{3,0},{4,5},{5,6},{6,7},{7,4},{8,9},{9,10},{10,1... | collective-permute-start | bytes 589832 | tf_op jit(solution)/shard_map/ppermute | solution.py:225
  80.6 21.5 %collective-permute-start.5 = (bf16[384,256]{1,0:T(8,128)(2,1)S(1)}, bf16[384,256]{1,0:T(8,128)(2,1)S(1)}, u32[]{:S(2)}, u32[]{:S(2)}) collective-permute-start(bf16[384,256]{1,0:T(8,128)(2,1)S(1)} %shard_map.94.refs_0_), channel_id=1, source_target_pairs={{0,3},{1,0},{2,1},{3,2},{4,7},{5,4},{6,5},{7,6},{8,11},{9,8},{10,9... | collective-permute-start | bytes 589832 | tf_op jit(solution)/shard_map/ppermute | solution.py:225
  82.7 19.4 %collective-permute-start.6 = (bf16[384,256]{1,0:T(8,128)(2,1)S(1)}, bf16[384,256]{1,0:T(8,128)(2,1)S(1)}, u32[]{:S(2)}, u32[]{:S(2)}) collective-permute-start(bf16[384,256]{1,0:T(8,128)(2,1)S(1)} %shard_map.94.refs_0_), channel_id=1, source_target_pairs={{0,2},{1,3},{2,0},{3,1},{4,6},{5,7},{6,4},{7,5},{8,10},{9,11},{10,... | collective-permute-start | bytes 589832 | tf_op jit(solution)/shard_map/ppermute | solution.py:225
  103.2 1.3 copy-start.7
  104.4 0.9 copy-start.15
  105.3 46.4 %all-to-all-start.1 = ((bf16[64,2,2688]{2,1,0:T(2,128)(2,1)}), bf16[64,2,2688]{2,1,0:T(2,128)(2,1)}, u32[]{:S(2)}, u32[]{:S(2)}) async-start(bf16[64,2,2688]{2,1,0:T(2,128)(2,1)} %copy-done.15), calls=%async_computation.1 | async-start | bytes 1376256 | tf_op jit(solution)/shard_map/all_to_all | solution.py:220
  116.3 19.5 %collective-permute-start.11 = (bf16[64,2,2688]{2,1,0:T(2,128)(2,1)S(1)}, bf16[64,2,2688]{2,1,0:T(2,128)(2,1)S(1)}, u32[]{:S(2)}, u32[]{:S(2)}) collective-permute-start(bf16[64,2,2688]{2,1,0:T(2,128)(2,1)S(1)} %slice.14), channel_id=1, source_target_pairs={{0,1},{1,2},{2,3},{3,0},{4,5},{5,6},{6,7},{7,4},{8,9},{9,10},{10,1... | collective-permute-start | bytes 2064392 | tf_op jit(solution)/shard_map/ppermute | solution.py:225
  118.2 17.6 %collective-permute-start.12 = (bf16[64,2,2688]{2,1,0:T(2,128)(2,1)S(1)}, bf16[64,2,2688]{2,1,0:T(2,128)(2,1)S(1)}, u32[]{:S(2)}, u32[]{:S(2)}) collective-permute-start(bf16[64,2,2688]{2,1,0:T(2,128)(2,1)S(1)} %slice.14), channel_id=1, source_target_pairs={{0,3},{1,0},{2,1},{3,2},{4,7},{5,4},{6,5},{7,6},{8,11},{9,8},{10,9... | collective-permute-start | bytes 2064392 | tf_op jit(solution)/shard_map/ppermute | solution.py:225
  120.1 1.5 copy-start.2
  135.8 14.0 %copy-start.8 = (bf16[4,256,896]{2,1,0:T(8,128)(2,1)S(1)}, bf16[4,256,896]{2,1,0:T(8,128)(2,1)}, u32[]{:S(2)}) copy-start(bf16[4,256,896]{2,1,0:T(8,128)(2,1)} %copy-done.7) | copy-start | bytes 5505028
  136.8 34.0 %copy-start.10 = (bf16[3584,256]{1,0:T(8,128)(2,1)S(1)}, bf16[3584,256]{1,0:T(8,128)(2,1)}, u32[]{:S(2)}) copy-start(bf16[3584,256]{1,0:T(8,128)(2,1)} %param.15) | copy-start | bytes 5505028
  136.8 34.0 %copy-start.14 = (bf16[128,896]{1,0:T(8,128)(2,1)S(1)}, bf16[128,896]{1,0:T(8,128)(2,1)}, u32[]{:S(2)}) copy-start(bf16[128,896]{1,0:T(8,128)(2,1)} %copy-done.13) | copy-start | bytes 688132
  136.8 8.4 %collective-permute-start.13 = (bf16[384,256]{1,0:T(8,128)(2,1)S(1)}, bf16[384,256]{1,0:T(8,128)(2,1)S(1)}, u32[]{:S(2)}, u32[]{:S(2)}) collective-permute-start(bf16[384,256]{1,0:T(8,128)(2,1)S(1)} %shard_map.100.refs_0_), channel_id=1, source_target_pairs={{0,1},{1,2},{2,3},{3,0},{4,5},{5,6},{6,7},{7,4},{8,9},{9,10},{10,1... | collective-permute-start | bytes 589832 | tf_op jit(solution)/shard_map/ppermute | solution.py:225
  138.1 10.0 %collective-permute-start.14 = (bf16[384,256]{1,0:T(8,128)(2,1)S(1)}, bf16[384,256]{1,0:T(8,128)(2,1)S(1)}, u32[]{:S(2)}, u32[]{:S(2)}) collective-permute-start(bf16[384,256]{1,0:T(8,128)(2,1)S(1)} %shard_map.100.refs_0_), channel_id=1, source_target_pairs={{0,3},{1,0},{2,1},{3,2},{4,7},{5,4},{6,5},{7,6},{8,11},{9,8},{10,9... | collective-permute-start | bytes 589832 | tf_op jit(solution)/shard_map/ppermute | solution.py:225
  140.2 9.6 %collective-permute-start.15 = (bf16[384,256]{1,0:T(8,128)(2,1)S(1)}, bf16[384,256]{1,0:T(8,128)(2,1)S(1)}, u32[]{:S(2)}, u32[]{:S(2)}) collective-permute-start(bf16[384,256]{1,0:T(8,128)(2,1)S(1)} %shard_map.100.refs_0_), channel_id=1, source_target_pairs={{0,2},{1,3},{2,0},{3,1},{4,6},{5,7},{6,4},{7,5},{8,10},{9,11},{10,... | collective-permute-start | bytes 589832 | tf_op jit(solution)/shard_map/ppermute | solution.py:225
  150.8 0.9 copy-start.16
  151.6 38.0 %all-to-all-start.3 = ((bf16[64,2,2688]{2,1,0:T(2,128)(2,1)}), bf16[64,2,2688]{2,1,0:T(2,128)(2,1)S(1)}, u32[]{:S(2)}, u32[]{:S(2)}) async-start(bf16[64,2,2688]{2,1,0:T(2,128)(2,1)} %copy-done.16), calls=%async_computation.3 | async-start | bytes 1376256 | tf_op jit(solution)/shard_map/all_to_all | solution.py:220
  161.9 8.9 %collective-permute-start.16 = (bf16[128,896]{1,0:T(8,128)(2,1)S(1)}, bf16[128,896]{1,0:T(8,128)(2,1)S(1)}, u32[]{:S(2)}, u32[]{:S(2)}) collective-permute-start(bf16[128,896]{1,0:T(8,128)(2,1)S(1)} %copy-done.6), channel_id=1, source_target_pairs={{0,1},{1,2},{2,3},{3,0},{4,5},{5,6},{6,7},{7,4},{8,9},{9,10},{10,1... | collective-permute-start | bytes 688136 | tf_op jit(solution)/shard_map/ppermute | solution.py:225
  163.1 7.7 %collective-permute-start.17 = (bf16[128,896]{1,0:T(8,128)(2,1)S(1)}, bf16[128,896]{1,0:T(8,128)(2,1)S(1)}, u32[]{:S(2)}, u32[]{:S(2)}) collective-permute-start(bf16[128,896]{1,0:T(8,128)(2,1)S(1)} %copy-done.6), channel_id=1, source_target_pairs={{0,3},{1,0},{2,1},{3,2},{4,7},{5,4},{6,5},{7,6},{8,11},{9,8},{10,9... | collective-permute-start | bytes 688136 | tf_op jit(solution)/shard_map/ppermute | solution.py:225
  170.8 1.5 copy-start.11
  172.3 1.5 copy-start.12
  173.8 6.4 %copy-start.19 = (bf16[128,4]{0,1:T(4,128)(2,1)S(1)}, bf16[128,4]{0,1:T(4,128)(2,1)}, u32[]{:S(2)}) copy-start(bf16[128,4]{0,1:T(4,128)(2,1)} %param.11) | copy-start | bytes 3076
  175.6 9.3 %collective-permute-start.18 = (bf16[128,896]{1,0:T(8,128)(2,1)}, bf16[128,896]{1,0:T(8,128)(2,1)S(1)}, u32[]{:S(2)}, u32[]{:S(2)}) collective-permute-start(bf16[128,896]{1,0:T(8,128)(2,1)} %get-tuple-element.26), channel_id=1, source_target_pairs={{0,1},{1,2},{2,3},{3,0},{4,5},{5,6},{6,7},{7,4},{8,9},{9,10},{10,1... | collective-permute-start | bytes 688136 | tf_op jit(solution)/shard_map/ppermute | solution.py:225
  175.9 12.2 %collective-permute-start.19 = (bf16[128,896]{1,0:T(8,128)(2,1)}, bf16[128,896]{1,0:T(8,128)(2,1)S(1)}, u32[]{:S(2)}, u32[]{:S(2)}) collective-permute-start(bf16[128,896]{1,0:T(8,128)(2,1)} %get-tuple-element.27), channel_id=1, source_target_pairs={{0,3},{1,0},{2,1},{3,2},{4,7},{5,4},{6,5},{7,6},{8,11},{9,8},{10,9... | collective-permute-start | bytes 688136 | tf_op jit(solution)/shard_map/ppermute | solution.py:225
  178.9 10.8 %collective-permute-start.20 = (bf16[128,896]{1,0:T(8,128)(2,1)S(1)}, bf16[128,896]{1,0:T(8,128)(2,1)S(1)}, u32[]{:S(2)}, u32[]{:S(2)}) collective-permute-start(bf16[128,896]{1,0:T(8,128)(2,1)S(1)} %get-tuple-element.28), channel_id=1, source_target_pairs={{0,2},{1,3},{2,0},{3,1},{4,6},{5,7},{6,4},{7,5},{8,10},{9,11},{10,... | collective-permute-start | bytes 688136 | tf_op jit(solution)/shard_map/ppermute | solution.py:225

commit v6 on v5

--- a/solution.py
+++ b/solution.py
@@ -95,7 +95,7 @@
 
 
 def weight_body(experts):
-    def body(ids_ref, gates_ref, out_ref):
+    def body(ids_ref, gates_ref, *outs):
         ids = ids_ref[...]
         gates = gates_ref[...].astype(F32)
         rows, top = ids.shape
@@ -111,14 +111,15 @@
         ]
         width = experts * PAIR
         place = lax.broadcasted_iota(jnp.int32, (rows, width), 1)
-        for i in range(sum(CHUNKS) // PAIR):
+        pairs = [(o, p) for o, size in zip(outs, CHUNKS) for p in range(size // PAIR)]
+        for i, (out_ref, p) in enumerate(pairs):
             weight = jnp.zeros((rows, width), F32)
             for k in range(top):
                 local = slots[k] - i * PAIR
                 inside = (local >= 0) & (local < PAIR)
                 target = jnp.where(inside, ids[:, k : k + 1] * PAIR + local, -1)
                 weight = jnp.where(target == place, gates[:, k : k + 1], weight)
-            out_ref[:, i * width : (i + 1) * width] = weight.astype(BF16)
+            out_ref[:, p * width : (p + 1) * width] = weight.astype(BF16)
 
     return body
 
@@ -204,16 +205,11 @@
     return body
 
 
-def combine_body(weight_ref, *refs):
-    *ins, out_ref = refs
-    rows_refs, parts = ins[: len(CHUNKS)], ins[len(CHUNKS) :]
-    total = sum(p[...].astype(F32) for p in parts)
-    start = 0
-    for rows_ref in rows_refs:
-        rows = flat(rows_ref[...], out_ref.shape[1])
-        total = total + dot(weight_ref[:, start : start + rows.shape[0]], rows)
-        start += rows.shape[0]
-    out_ref[...] = total.astype(BF16)
+def add_body(weight_ref, rows_ref, *refs):
+    *parts, out_ref = refs
+    rows = flat(rows_ref[...], out_ref.shape[1])
+    total = sum((p[...].astype(F32) for p in parts), dot(weight_ref[...], rows))
+    out_ref[...] = total.astype(out_ref.dtype)
 
 
 def exchange(x, axis):
@@ -271,8 +267,11 @@
         arrived.append(exchange(rows, EXPERT))
     columns = kernel_call(columns_body, [(quarter, narrow)] * n, q, w_down, smem=1)
     (down,) = kernel_call(stack_body, [(n, quarter, narrow)], *deal(columns))
-    (weight,) = kernel_call(
-        weight_body(experts), [(tok_dev, experts * sum(CHUNKS))], expert_ids, gate_values
+    weights = kernel_call(
+        weight_body(experts),
+        [(tok_dev, experts * size) for size in CHUNKS],
+        expert_ids,
+        gate_values,
     )
     shared_parts = kernel_call(
         shared_body,
@@ -319,7 +318,9 @@
         )
         returned.append(exchange(out, EXPERT))
     shared_all = deal(shared_parts)
-    return kernel_call(combine_body, [(tok_dev, narrow)], weight, *returned, *shared_all)[0]
+    total_shape = jax.ShapeDtypeStruct((tok_dev, narrow), F32)
+    (total,) = kernel_call(add_body, [total_shape], weights[0], returned[0], *shared_all)
+    return kernel_call(add_body, [(tok_dev, narrow)], weights[1], returned[1], total)[0]
 
 
 def solution(mesh):

time: 193 us -> 194 us (level)
    pallas_call x13 -> x14, Pallas kernels: 16.2 us -> 16.4 us  [kernel_call(): pl.pallas_call(body, in_specs=[pl.BlockSpec(memory_space=m) for m in plac...]
  transfers between devices with their start and end apart: 25 -> 25, of which waited for: 14 -> 14; matrix products, arithmetic and copies ran while one was open for 2% -> 2% of each run, Pallas kernels for 6% -> 7%
where the time goes in v6:
time: 194 us; the launch traced here: 192 us
  starting transfers between devices  80.2 us (41%)
  waiting for transfers between devices  78.6 us (41%)
  local copies, waits for them, and re-layouts  16.9 us (9%)
  Pallas kernels  16.4 us (8%)
    ppermute x21, waiting for transfers between devices, shift(): return lax.ppermute(x, axis, [(i, (i + by) % n) for i in range(n)])  69.8 us
    ppermute x21, starting transfers between devices, shift(): return lax.ppermute(x, axis, [(i, (i + by) % n) for i in range(n)])  41.4 us
    all_to_all x4, starting transfers between devices, exchange(): return lax.all_to_all(x, axis, split_axis=0, concat_axis=0, tiled=True)  38.8 us
    pallas_call x14, Pallas kernels, kernel_call(): pl.pallas_call(body, in_specs=[pl.BlockSpec(memory_space=m) for m in plac...  16.4 us
    unnamed x42, local copies, waits for them, and re-layouts  14 us
    all_to_all x4, waiting for transfers between devices, exchange(): return lax.all_to_all(x, axis, split_axis=0, concat_axis=0, tiled=True)  8.86 us
  transfers between devices with their start and end apart: 25, of which 14 were waited for; matrix products, arithmetic and copies ran while one was open for 2% of the time, Pallas kernels for 7%

profile of v6, /device:TPU:32, one launch (start us, length us, event | category | flops | bytes accessed | tf_op | source)
XLA Modules:
  0.0 192.3 jit_solution(2021776731738958624)
XLA Ops:
  0.0 0.9 copy-done.5
  0.9 0.7 copy-done.17
  1.6 1.4 shard_map.98
  3.0 11.6 %all-to-all-start.2 = ((bf16[64,2,2688]{2,1,0:T(2,128)(2,1)}), bf16[64,2,2688]{2,1,0:T(2,128)(2,1)S(1)}, u32[]{:S(2)}, u32[]{:S(2)}) async-start(bf16[64,2,2688]{2,1,0:T(2,128)(2,1)} %shard_map.98), calls=%async_computation.2 | async-start | bytes 1376256 | tf_op jit(solution)/shard_map/all_to_all | solution.py:216
  14.6 3.3 %collective-permute-start = (bf16[128,896]{1,0:T(8,128)(2,1)S(1)}, bf16[128,896]{1,0:T(8,128)(2,1)S(1)}, u32[]{:S(2)}, u32[]{:S(2)}) collective-permute-start(bf16[128,896]{1,0:T(8,128)(2,1)S(1)} %copy-done.6), channel_id=1, source_target_pairs={{0,2},{1,3},{2,0},{3,1},{4,6},{5,7},{6,4},{7,5},{8,10},{9,11},{10,... | collective-permute-start | bytes 688136 | tf_op jit(solution)/shard_map/ppermute | solution.py:221
  17.9 5.9 %collective-permute-done.refs_1_.refs_3_ = bf16[128,896]{1,0:T(8,128)(2,1)S(1)} collective-permute-done((bf16[128,896]{1,0:T(8,128)(2,1)S(1)}, bf16[128,896]{1,0:T(8,128)(2,1)S(1)}, u32[]{:S(2)}, u32[]{:S(2)}) %collective-permute-start) | collective-permute-done | bytes 229408 | tf_op jit(solution)/shard_map/ppermute | solution.py:221
  23.9 1.8 shard_map.92
  25.7 0.7 copy-done.13
  26.4 8.9 %all-to-all-done.2.own_ref = bf16[64,2,2688]{2,1,0:T(2,128)(2,1)S(1)} async-done(((bf16[64,2,2688]{2,1,0:T(2,128)(2,1)}), bf16[64,2,2688]{2,1,0:T(2,128)(2,1)S(1)}, u32[]{:S(2)}, u32[]{:S(2)}) %all-to-all-start.2) | async-done | bytes 688160 | tf_op jit(solution)/shard_map/all_to_all | solution.py:216
  35.2 0.9 copy-done.3
  36.1 6.5 %all-to-all-start = ((bf16[64,2,5376]{2,1,0:T(2,128)(2,1)}), bf16[64,2,5376]{2,1,0:T(2,128)(2,1)S(1)}, u32[]{:S(2)}, u32[]{:S(2)}) async-start(bf16[64,2,5376]{2,1,0:T(2,128)(2,1)} %shard_map.92), calls=%async_computation | async-start | bytes 2752512 | tf_op jit(solution)/shard_map/all_to_all | solution.py:216
  42.6 1.7 collective-permute-start.9
  44.2 1.7 collective-permute-start.10
  45.9 1.6 copy-done.9
  47.6 0.4 collective-permute-start.6
  48.0 14.4 %collective-permute-done.9.left_ref = bf16[64,2,2688]{2,1,0:T(2,128)(2,1)} collective-permute-done((bf16[64,2,2688]{2,1,0:T(2,128)(2,1)}, bf16[64,2,2688]{2,1,0:T(2,128)(2,1)}, u32[]{:S(2)}, u32[]{:S(2)}) %collective-permute-start.9) | collective-permute-done | bytes 688160 | tf_op jit(solution)/shard_map/ppermute | solution.py:221
  62.5 1.2 slice.13
  64.2 1.2 slice.14
  65.4 2.9 %collective-permute-start.12 = (bf16[32,2,2688]{2,1,0:T(2,128)(2,1)S(1)}, bf16[32,2,2688]{2,1,0:T(2,128)(2,1)S(1)}, u32[]{:S(2)}, u32[]{:S(2)}) collective-permute-start(bf16[32,2,2688]{2,1,0:T(2,128)(2,1)S(1)} %slice.14), channel_id=1, source_target_pairs={{0,3},{1,0},{2,1},{3,2},{4,7},{5,4},{6,5},{7,6},{8,11},{9,8},{10,9... | collective-permute-start | bytes 1032200 | tf_op jit(solution)/shard_map/ppermute | solution.py:221
  68.3 0.6 collective-permute-start.7
  68.9 0.6 collective-permute-start.8
  69.6 1.5 copy-done.1
  71.1 2.8 %shard_map.99 = (f32[384,512]{1,0:T(8,128)S(1)}, bf16[2,896,256]{2,1,0:T(8,128)(2,1)S(1)}) custom-call(s32[1]{0:T(128)} %bitcast.q_ref, bf16[64,2,2688]{2,1,0:T(2,128)(2,1)S(1)} %copy-done.4, bf16[64,2,2688]{2,1,0:T(2,128)(2,1)} %collective-permute-done.9.left_ref, bf16[64,2,2688]{2,1,0:T(2,128)(2,1)} %collective-permute-done.10.right_ref, ...), custom_call_target="tpu_custom_call" | custom-call | flops 1000000000 | tf_op jit(solution)/shard_map/pallas_call | solution.py:41
  73.8 5.0 %collective-permute-done.11.o0_ref = bf16[32,2,2688]{2,1,0:T(2,128)(2,1)S(1)} collective-permute-done((bf16[32,2,2688]{2,1,0:T(2,128)(2,1)S(1)}, bf16[32,2,2688]{2,1,0:T(2,128)(2,1)S(1)}, u32[]{:S(2)}, u32[]{:S(2)}) %collective-permute-start.11) | collective-permute-done | bytes 344096 | tf_op jit(solution)/shard_map/ppermute | solution.py:221
  78.8 0.6 shard_map.100.refs_0_
  79.4 1.2 collective-permute-start.13
  80.7 2.1 %collective-permute-start.14 = (bf16[384,256]{1,0:T(8,128)(2,1)S(1)}, bf16[384,256]{1,0:T(8,128)(2,1)S(1)}, u32[]{:S(2)}, u32[]{:S(2)}) collective-permute-start(bf16[384,256]{1,0:T(8,128)(2,1)S(1)} %shard_map.100.refs_0_), channel_id=1, source_target_pairs={{0,3},{1,0},{2,1},{3,2},{4,7},{5,4},{6,5},{7,6},{8,11},{9,8},{10,9... | collective-permute-start | bytes 589832 | tf_op jit(solution)/shard_map/ppermute | solution.py:221
  82.8 9.8 %collective-permute-start.15 = (bf16[384,256]{1,0:T(8,128)(2,1)S(1)}, bf16[384,256]{1,0:T(8,128)(2,1)S(1)}, u32[]{:S(2)}, u32[]{:S(2)}) collective-permute-start(bf16[384,256]{1,0:T(8,128)(2,1)S(1)} %shard_map.100.refs_0_), channel_id=1, source_target_pairs={{0,2},{1,3},{2,0},{3,1},{4,6},{5,7},{6,4},{7,5},{8,10},{9,11},{10,... | collective-permute-start | bytes 589832 | tf_op jit(solution)/shard_map/ppermute | solution.py:221
  92.6 5.2 %collective-permute-done.7.refs_2_ = bf16[256,896]{1,0:T(8,128)(2,1)S(1)} collective-permute-done((bf16[256,896]{1,0:T(8,128)(2,1)S(1)}, bf16[256,896]{1,0:T(8,128)(2,1)S(1)}, u32[]{:S(2)}, u32[]{:S(2)}) %collective-permute-start.7) | collective-permute-done | bytes 458784 | tf_op jit(solution)/shard_map/ppermute | solution.py:221
  97.9 4.2 %collective-permute-done.14.refs_2_ = bf16[384,256]{1,0:T(8,128)(2,1)S(1)} collective-permute-done((bf16[384,256]{1,0:T(8,128)(2,1)S(1)}, bf16[384,256]{1,0:T(8,128)(2,1)S(1)}, u32[]{:S(2)}, u32[]{:S(2)}) %collective-permute-start.14) | collective-permute-done | bytes 196640 | tf_op jit(solution)/shard_map/ppermute | solution.py:221
  102.2 1.0 shard_map.101
  103.2 1.3 copy-done.7
  104.5 0.8 copy-done.16
  105.3 10.5 %all-to-all-start.3 = ((bf16[64,2,2688]{2,1,0:T(2,128)(2,1)}), bf16[64,2,2688]{2,1,0:T(2,128)(2,1)}, u32[]{:S(2)}, u32[]{:S(2)}) async-start(bf16[64,2,2688]{2,1,0:T(2,128)(2,1)} %copy-done.16), calls=%async_computation.3 | async-start | bytes 1376256 | tf_op jit(solution)/shard_map/all_to_all | solution.py:216
  115.8 0.5 slice.12
  116.3 1.9 collective-permute-start.1
  118.2 2.0 %collective-permute-start.2 = (bf16[64,2,2688]{2,1,0:T(2,128)(2,1)S(1)}, bf16[64,2,2688]{2,1,0:T(2,128)(2,1)S(1)}, u32[]{:S(2)}, u32[]{:S(2)}) collective-permute-start(bf16[64,2,2688]{2,1,0:T(2,128)(2,1)S(1)} %slice.12), channel_id=1, source_target_pairs={{0,3},{1,0},{2,1},{3,2},{4,7},{5,4},{6,5},{7,6},{8,11},{9,8},{10,9... | collective-permute-start | bytes 2064392 | tf_op jit(solution)/shard_map/ppermute | solution.py:221
  120.2 1.5 copy-done.2
  121.7 1.1 shard_map.93
  122.8 13.0 %collective-permute-done.1.left_ref = bf16[64,2,2688]{2,1,0:T(2,128)(2,1)S(1)} collective-permute-done((bf16[64,2,2688]{2,1,0:T(2,128)(2,1)S(1)}, bf16[64,2,2688]{2,1,0:T(2,128)(2,1)S(1)}, u32[]{:S(2)}, u32[]{:S(2)}) %collective-permute-start.1) | collective-permute-done | bytes 688160 | tf_op jit(solution)/shard_map/ppermute | solution.py:221
  135.8 1.0 shard_map.94.refs_0_
  136.9 1.2 collective-permute-start.3
  138.1 2.1 %collective-permute-start.4 = (bf16[384,256]{1,0:T(8,128)(2,1)S(1)}, bf16[384,256]{1,0:T(8,128)(2,1)S(1)}, u32[]{:S(2)}, u32[]{:S(2)}) collective-permute-start(bf16[384,256]{1,0:T(8,128)(2,1)S(1)} %shard_map.94.refs_0_), channel_id=1, source_target_pairs={{0,3},{1,0},{2,1},{3,2},{4,7},{5,4},{6,5},{7,6},{8,11},{9,8},{10,9... | collective-permute-start | bytes 589832 | tf_op jit(solution)/shard_map/ppermute | solution.py:221
  140.2 1.7 collective-permute-start.5
  141.9 3.3 %collective-permute-done.3.refs_1_ = bf16[384,256]{1,0:T(8,128)(2,1)S(1)} collective-permute-done((bf16[384,256]{1,0:T(8,128)(2,1)S(1)}, bf16[384,256]{1,0:T(8,128)(2,1)S(1)}, u32[]{:S(2)}, u32[]{:S(2)}) %collective-permute-start.3) | collective-permute-done | bytes 196640 | tf_op jit(solution)/shard_map/ppermute | solution.py:221
  145.2 2.9 %collective-permute-done.4.refs_2_ = bf16[384,256]{1,0:T(8,128)(2,1)S(1)} collective-permute-done((bf16[384,256]{1,0:T(8,128)(2,1)S(1)}, bf16[384,256]{1,0:T(8,128)(2,1)S(1)}, u32[]{:S(2)}, u32[]{:S(2)}) %collective-permute-start.4) | collective-permute-done | bytes 196640 | tf_op jit(solution)/shard_map/ppermute | solution.py:221
  148.1 1.7 collective-permute-done.5.refs_3_
  149.8 1.0 shard_map.97
  150.8 0.9 copy-done.15
  151.7 10.2 %all-to-all-start.1 = ((bf16[64,2,2688]{2,1,0:T(2,128)(2,1)}), bf16[64,2,2688]{2,1,0:T(2,128)(2,1)S(1)}, u32[]{:S(2)}, u32[]{:S(2)}) async-start(bf16[64,2,2688]{2,1,0:T(2,128)(2,1)} %copy-done.15), calls=%async_computation.1 | async-start | bytes 1376256 | tf_op jit(solution)/shard_map/all_to_all | solution.py:216
  161.9 1.2 collective-permute-start.16
  163.2 2.1 %collective-permute-start.17 = (bf16[128,896]{1,0:T(8,128)(2,1)S(1)}, bf16[128,896]{1,0:T(8,128)(2,1)S(1)}, u32[]{:S(2)}, u32[]{:S(2)}) collective-permute-start(bf16[128,896]{1,0:T(8,128)(2,1)S(1)} %copy-done.6), channel_id=1, source_target_pairs={{0,3},{1,0},{2,1},{3,2},{4,7},{5,4},{6,5},{7,6},{8,11},{9,8},{10,9... | collective-permute-start | bytes 688136 | tf_op jit(solution)/shard_map/ppermute | solution.py:221
  165.3 5.6 %collective-permute-done.16.refs_1_ = bf16[128,896]{1,0:T(8,128)(2,1)S(1)} collective-permute-done((bf16[128,896]{1,0:T(8,128)(2,1)S(1)}, bf16[128,896]{1,0:T(8,128)(2,1)S(1)}, u32[]{:S(2)}, u32[]{:S(2)}) %collective-permute-start.16) | collective-permute-done | bytes 229408 | tf_op jit(solution)/shard_map/ppermute | solution.py:221
  170.9 1.5 copy-done.11
  172.4 1.5 copy-done.12
  173.9 1.8 shard_map.102
  175.9 3.0 %collective-permute-start.19 = (bf16[128,896]{1,0:T(8,128)(2,1)}, bf16[128,896]{1,0:T(8,128)(2,1)S(1)}, u32[]{:S(2)}, u32[]{:S(2)}) collective-permute-start(bf16[128,896]{1,0:T(8,128)(2,1)} %get-tuple-element.31), channel_id=1, source_target_pairs={{0,3},{1,0},{2,1},{3,2},{4,7},{5,4},{6,5},{7,6},{8,11},{9,8},{10,9... | collective-permute-start | bytes 688136 | tf_op jit(solution)/shard_map/ppermute | solution.py:221
  178.9 1.2 collective-permute-start.20
  180.4 0.9 shard_map.91
  181.3 3.7 %collective-permute-done.18.refs_1_ = bf16[128,896]{1,0:T(8,128)(2,1)S(1)} collective-permute-done((bf16[128,896]{1,0:T(8,128)(2,1)}, bf16[128,896]{1,0:T(8,128)(2,1)S(1)}, u32[]{:S(2)}, u32[]{:S(2)}) %collective-permute-start.18) | collective-permute-done | bytes 229408 | tf_op jit(solution)/shard_map/ppermute | solution.py:221
  185.0 3.2 %collective-permute-done.19.refs_2_ = bf16[128,896]{1,0:T(8,128)(2,1)S(1)} collective-permute-done((bf16[128,896]{1,0:T(8,128)(2,1)}, bf16[128,896]{1,0:T(8,128)(2,1)S(1)}, u32[]{:S(2)}, u32[]{:S(2)}) %collective-permute-start.19) | collective-permute-done | bytes 229408 | tf_op jit(solution)/shard_map/ppermute | solution.py:221
  188.2 1.5 collective-permute-done.20.refs_3_
  189.7 1.5 shard_map.103.refs_0_
  191.2 1.1 shard_map.104
  (45 shorter events, 1.3 us)
Async XLA Ops:
  0.0 0.9 copy-start.5
  0.9 0.7 copy-start.17
  1.6 13.0 %copy-start.6 = (bf16[128,896]{1,0:T(8,128)(2,1)S(1)}, bf16[128,896]{1,0:T(8,128)(2,1)}, u32[]{:S(2)}) copy-start(bf16[128,896]{1,0:T(8,128)(2,1)} %refs_0_.5) | copy-start | bytes 688132
  1.6 22.2 %copy-start.18 = (s32[128,4]{0,1:T(4,128)S(1)}, s32[128,4]{0,1:T(4,128)}, u32[]{:S(2)}) copy-start(s32[128,4]{0,1:T(4,128)} %param.10) | copy-start | bytes 6148
  3.0 32.2 %all-to-all-start.2 = ((bf16[64,2,2688]{2,1,0:T(2,128)(2,1)}), bf16[64,2,2688]{2,1,0:T(2,128)(2,1)S(1)}, u32[]{:S(2)}, u32[]{:S(2)}) async-start(bf16[64,2,2688]{2,1,0:T(2,128)(2,1)} %shard_map.98), calls=%async_computation.2 | async-start | bytes 1376256 | tf_op jit(solution)/shard_map/all_to_all | solution.py:216
  14.6 9.2 %collective-permute-start = (bf16[128,896]{1,0:T(8,128)(2,1)S(1)}, bf16[128,896]{1,0:T(8,128)(2,1)S(1)}, u32[]{:S(2)}, u32[]{:S(2)}) collective-permute-start(bf16[128,896]{1,0:T(8,128)(2,1)S(1)} %copy-done.6), channel_id=1, source_target_pairs={{0,2},{1,3},{2,0},{3,1},{4,6},{5,7},{6,4},{7,5},{8,10},{9,11},{10,... | collective-permute-start | bytes 688136 | tf_op jit(solution)/shard_map/ppermute | solution.py:221
  25.7 0.7 copy-start.13
  35.2 0.9 copy-start.3
  36.1 69.2 %all-to-all-start = ((bf16[64,2,5376]{2,1,0:T(2,128)(2,1)}), bf16[64,2,5376]{2,1,0:T(2,128)(2,1)S(1)}, u32[]{:S(2)}, u32[]{:S(2)}) async-start(bf16[64,2,5376]{2,1,0:T(2,128)(2,1)} %shard_map.92), calls=%async_computation | async-start | bytes 2752512 | tf_op jit(solution)/shard_map/all_to_all | solution.py:216
  42.6 27.0 %copy-start = (bf16[1,3584,256]{2,1,0:T(8,128)(2,1)S(1)}, bf16[1,3584,256]{2,1,0:T(8,128)(2,1)}, u32[]{:S(2)}) copy-start(bf16[1,3584,256]{2,1,0:T(8,128)(2,1)} %param.12) | copy-start | bytes 5505028
  42.6 19.9 %collective-permute-start.9 = (bf16[64,2,2688]{2,1,0:T(2,128)(2,1)}, bf16[64,2,2688]{2,1,0:T(2,128)(2,1)}, u32[]{:S(2)}, u32[]{:S(2)}) collective-permute-start(bf16[64,2,2688]{2,1,0:T(2,128)(2,1)} %copy-done.3), channel_id=1, source_target_pairs={{0,1},{1,2},{2,3},{3,0},{4,5},{5,6},{6,7},{7,4},{8,9},{9,10},{10,1... | collective-permute-start | bytes 2064392 | tf_op jit(solution)/shard_map/ppermute | solution.py:221
  44.2 19.9 %collective-permute-start.10 = (bf16[64,2,2688]{2,1,0:T(2,128)(2,1)}, bf16[64,2,2688]{2,1,0:T(2,128)(2,1)}, u32[]{:S(2)}, u32[]{:S(2)}) collective-permute-start(bf16[64,2,2688]{2,1,0:T(2,128)(2,1)} %copy-done.3), channel_id=1, source_target_pairs={{0,3},{1,0},{2,1},{3,2},{4,7},{5,4},{6,5},{7,6},{8,11},{9,8},{10,9... | collective-permute-start | bytes 2064392 | tf_op jit(solution)/shard_map/ppermute | solution.py:221
  45.9 23.7 %copy-start.4 = (bf16[64,2,2688]{2,1,0:T(2,128)(2,1)S(1)}, bf16[64,2,2688]{2,1,0:T(2,128)(2,1)}, u32[]{:S(2)}) copy-start(bf16[64,2,2688]{2,1,0:T(2,128)(2,1)} %copy-done.3) | copy-start | bytes 2064388
  45.9 1.6 copy-start.9
  47.6 35.2 %collective-permute-start.6 = (bf16[256,896]{1,0:T(8,128)(2,1)S(1)}, bf16[256,896]{1,0:T(8,128)(2,1)S(1)}, u32[]{:S(2)}, u32[]{:S(2)}) collective-permute-start(bf16[256,896]{1,0:T(8,128)(2,1)S(1)} %get-tuple-element.23), channel_id=1, source_target_pairs={{0,1},{1,2},{2,3},{3,0},{4,5},{5,6},{6,7},{7,4},{8,9},{9,10},{10,1... | collective-permute-start | bytes 1376264 | tf_op jit(solution)/shard_map/ppermute | solution.py:221
  63.7 15.1 %collective-permute-start.11 = (bf16[32,2,2688]{2,1,0:T(2,128)(2,1)S(1)}, bf16[32,2,2688]{2,1,0:T(2,128)(2,1)S(1)}, u32[]{:S(2)}, u32[]{:S(2)}) collective-permute-start(bf16[32,2,2688]{2,1,0:T(2,128)(2,1)S(1)} %slice.13), channel_id=1, source_target_pairs={{0,1},{1,2},{2,3},{3,0},{4,5},{5,6},{6,7},{7,4},{8,9},{9,10},{10,1... | collective-permute-start | bytes 1032200 | tf_op jit(solution)/shard_map/ppermute | solution.py:221
  65.4 13.4 %collective-permute-start.12 = (bf16[32,2,2688]{2,1,0:T(2,128)(2,1)S(1)}, bf16[32,2,2688]{2,1,0:T(2,128)(2,1)S(1)}, u32[]{:S(2)}, u32[]{:S(2)}) collective-permute-start(bf16[32,2,2688]{2,1,0:T(2,128)(2,1)S(1)} %slice.14), channel_id=1, source_target_pairs={{0,3},{1,0},{2,1},{3,2},{4,7},{5,4},{6,5},{7,6},{8,11},{9,8},{10,9... | collective-permute-start | bytes 1032200 | tf_op jit(solution)/shard_map/ppermute | solution.py:221
  68.3 29.5 %collective-permute-start.7 = (bf16[256,896]{1,0:T(8,128)(2,1)S(1)}, bf16[256,896]{1,0:T(8,128)(2,1)S(1)}, u32[]{:S(2)}, u32[]{:S(2)}) collective-permute-start(bf16[256,896]{1,0:T(8,128)(2,1)S(1)} %get-tuple-element.24), channel_id=1, source_target_pairs={{0,3},{1,0},{2,1},{3,2},{4,7},{5,4},{6,5},{7,6},{8,11},{9,8},{10,9... | collective-permute-start | bytes 1376264 | tf_op jit(solution)/shard_map/ppermute | solution.py:221
  68.9 28.9 %collective-permute-start.8 = (bf16[256,896]{1,0:T(8,128)(2,1)S(1)}, bf16[256,896]{1,0:T(8,128)(2,1)S(1)}, u32[]{:S(2)}, u32[]{:S(2)}) collective-permute-start(bf16[256,896]{1,0:T(8,128)(2,1)S(1)} %get-tuple-element.25), channel_id=1, source_target_pairs={{0,2},{1,3},{2,0},{3,1},{4,6},{5,7},{6,4},{7,5},{8,10},{9,11},{10,... | collective-permute-start | bytes 1376264 | tf_op jit(solution)/shard_map/ppermute | solution.py:221
  69.6 1.5 copy-start.1
  79.4 18.5 %collective-permute-start.13 = (bf16[384,256]{1,0:T(8,128)(2,1)S(1)}, bf16[384,256]{1,0:T(8,128)(2,1)S(1)}, u32[]{:S(2)}, u32[]{:S(2)}) collective-permute-start(bf16[384,256]{1,0:T(8,128)(2,1)S(1)} %shard_map.100.refs_0_), channel_id=1, source_target_pairs={{0,1},{1,2},{2,3},{3,0},{4,5},{5,6},{6,7},{7,4},{8,9},{9,10},{10,1... | collective-permute-start | bytes 589832 | tf_op jit(solution)/shard_map/ppermute | solution.py:221
  80.7 21.5 %collective-permute-start.14 = (bf16[384,256]{1,0:T(8,128)(2,1)S(1)}, bf16[384,256]{1,0:T(8,128)(2,1)S(1)}, u32[]{:S(2)}, u32[]{:S(2)}) collective-permute-start(bf16[384,256]{1,0:T(8,128)(2,1)S(1)} %shard_map.100.refs_0_), channel_id=1, source_target_pairs={{0,3},{1,0},{2,1},{3,2},{4,7},{5,4},{6,5},{7,6},{8,11},{9,8},{10,9... | collective-permute-start | bytes 589832 | tf_op jit(solution)/shard_map/ppermute | solution.py:221
  82.8 19.4 %collective-permute-start.15 = (bf16[384,256]{1,0:T(8,128)(2,1)S(1)}, bf16[384,256]{1,0:T(8,128)(2,1)S(1)}, u32[]{:S(2)}, u32[]{:S(2)}) collective-permute-start(bf16[384,256]{1,0:T(8,128)(2,1)S(1)} %shard_map.100.refs_0_), channel_id=1, source_target_pairs={{0,2},{1,3},{2,0},{3,1},{4,6},{5,7},{6,4},{7,5},{8,10},{9,11},{10,... | collective-permute-start | bytes 589832 | tf_op jit(solution)/shard_map/ppermute | solution.py:221
  103.2 1.3 copy-start.7
  104.5 0.9 copy-start.16
  105.3 46.4 %all-to-all-start.3 = ((bf16[64,2,2688]{2,1,0:T(2,128)(2,1)}), bf16[64,2,2688]{2,1,0:T(2,128)(2,1)}, u32[]{:S(2)}, u32[]{:S(2)}) async-start(bf16[64,2,2688]{2,1,0:T(2,128)(2,1)} %copy-done.16), calls=%async_computation.3 | async-start | bytes 1376256 | tf_op jit(solution)/shard_map/all_to_all | solution.py:216
  116.3 19.5 %collective-permute-start.1 = (bf16[64,2,2688]{2,1,0:T(2,128)(2,1)S(1)}, bf16[64,2,2688]{2,1,0:T(2,128)(2,1)S(1)}, u32[]{:S(2)}, u32[]{:S(2)}) collective-permute-start(bf16[64,2,2688]{2,1,0:T(2,128)(2,1)S(1)} %slice.12), channel_id=1, source_target_pairs={{0,1},{1,2},{2,3},{3,0},{4,5},{5,6},{6,7},{7,4},{8,9},{9,10},{10,1... | collective-permute-start | bytes 2064392 | tf_op jit(solution)/shard_map/ppermute | solution.py:221
  118.2 17.6 %collective-permute-start.2 = (bf16[64,2,2688]{2,1,0:T(2,128)(2,1)S(1)}, bf16[64,2,2688]{2,1,0:T(2,128)(2,1)S(1)}, u32[]{:S(2)}, u32[]{:S(2)}) collective-permute-start(bf16[64,2,2688]{2,1,0:T(2,128)(2,1)S(1)} %slice.12), channel_id=1, source_target_pairs={{0,3},{1,0},{2,1},{3,2},{4,7},{5,4},{6,5},{7,6},{8,11},{9,8},{10,9... | collective-permute-start | bytes 2064392 | tf_op jit(solution)/shard_map/ppermute | solution.py:221
  120.2 1.5 copy-start.2
  135.8 14.0 %copy-start.8 = (bf16[4,256,896]{2,1,0:T(8,128)(2,1)S(1)}, bf16[4,256,896]{2,1,0:T(8,128)(2,1)}, u32[]{:S(2)}) copy-start(bf16[4,256,896]{2,1,0:T(8,128)(2,1)} %copy-done.7) | copy-start | bytes 5505028
  136.9 34.0 %copy-start.10 = (bf16[3584,256]{1,0:T(8,128)(2,1)S(1)}, bf16[3584,256]{1,0:T(8,128)(2,1)}, u32[]{:S(2)}) copy-start(bf16[3584,256]{1,0:T(8,128)(2,1)} %param.15) | copy-start | bytes 5505028
  136.9 34.0 %copy-start.14 = (bf16[128,896]{1,0:T(8,128)(2,1)S(1)}, bf16[128,896]{1,0:T(8,128)(2,1)}, u32[]{:S(2)}) copy-start(bf16[128,896]{1,0:T(8,128)(2,1)} %copy-done.13) | copy-start | bytes 688132
  136.9 8.4 %collective-permute-start.3 = (bf16[384,256]{1,0:T(8,128)(2,1)S(1)}, bf16[384,256]{1,0:T(8,128)(2,1)S(1)}, u32[]{:S(2)}, u32[]{:S(2)}) collective-permute-start(bf16[384,256]{1,0:T(8,128)(2,1)S(1)} %shard_map.94.refs_0_), channel_id=1, source_target_pairs={{0,1},{1,2},{2,3},{3,0},{4,5},{5,6},{6,7},{7,4},{8,9},{9,10},{10,1... | collective-permute-start | bytes 589832 | tf_op jit(solution)/shard_map/ppermute | solution.py:221
  138.1 10.0 %collective-permute-start.4 = (bf16[384,256]{1,0:T(8,128)(2,1)S(1)}, bf16[384,256]{1,0:T(8,128)(2,1)S(1)}, u32[]{:S(2)}, u32[]{:S(2)}) collective-permute-start(bf16[384,256]{1,0:T(8,128)(2,1)S(1)} %shard_map.94.refs_0_), channel_id=1, source_target_pairs={{0,3},{1,0},{2,1},{3,2},{4,7},{5,4},{6,5},{7,6},{8,11},{9,8},{10,9... | collective-permute-start | bytes 589832 | tf_op jit(solution)/shard_map/ppermute | solution.py:221
  140.2 9.6 %collective-permute-start.5 = (bf16[384,256]{1,0:T(8,128)(2,1)S(1)}, bf16[384,256]{1,0:T(8,128)(2,1)S(1)}, u32[]{:S(2)}, u32[]{:S(2)}) collective-permute-start(bf16[384,256]{1,0:T(8,128)(2,1)S(1)} %shard_map.94.refs_0_), channel_id=1, source_target_pairs={{0,2},{1,3},{2,0},{3,1},{4,6},{5,7},{6,4},{7,5},{8,10},{9,11},{10,... | collective-permute-start | bytes 589832 | tf_op jit(solution)/shard_map/ppermute | solution.py:221
  150.8 0.9 copy-start.15
  151.7 39.5 %all-to-all-start.1 = ((bf16[64,2,2688]{2,1,0:T(2,128)(2,1)}), bf16[64,2,2688]{2,1,0:T(2,128)(2,1)S(1)}, u32[]{:S(2)}, u32[]{:S(2)}) async-start(bf16[64,2,2688]{2,1,0:T(2,128)(2,1)} %copy-done.15), calls=%async_computation.1 | async-start | bytes 1376256 | tf_op jit(solution)/shard_map/all_to_all | solution.py:216
  161.9 8.9 %collective-permute-start.16 = (bf16[128,896]{1,0:T(8,128)(2,1)S(1)}, bf16[128,896]{1,0:T(8,128)(2,1)S(1)}, u32[]{:S(2)}, u32[]{:S(2)}) collective-permute-start(bf16[128,896]{1,0:T(8,128)(2,1)S(1)} %copy-done.6), channel_id=1, source_target_pairs={{0,1},{1,2},{2,3},{3,0},{4,5},{5,6},{6,7},{7,4},{8,9},{9,10},{10,1... | collective-permute-start | bytes 688136 | tf_op jit(solution)/shard_map/ppermute | solution.py:221
  163.2 7.7 %collective-permute-start.17 = (bf16[128,896]{1,0:T(8,128)(2,1)S(1)}, bf16[128,896]{1,0:T(8,128)(2,1)S(1)}, u32[]{:S(2)}, u32[]{:S(2)}) collective-permute-start(bf16[128,896]{1,0:T(8,128)(2,1)S(1)} %copy-done.6), channel_id=1, source_target_pairs={{0,3},{1,0},{2,1},{3,2},{4,7},{5,4},{6,5},{7,6},{8,11},{9,8},{10,9... | collective-permute-start | bytes 688136 | tf_op jit(solution)/shard_map/ppermute | solution.py:221
  170.9 1.5 copy-start.11
  172.4 1.5 copy-start.12
  173.9 6.4 %copy-start.19 = (bf16[128,4]{0,1:T(4,128)(2,1)S(1)}, bf16[128,4]{0,1:T(4,128)(2,1)}, u32[]{:S(2)}) copy-start(bf16[128,4]{0,1:T(4,128)(2,1)} %param.11) | copy-start | bytes 3076
  175.7 9.3 %collective-permute-start.18 = (bf16[128,896]{1,0:T(8,128)(2,1)}, bf16[128,896]{1,0:T(8,128)(2,1)S(1)}, u32[]{:S(2)}, u32[]{:S(2)}) collective-permute-start(bf16[128,896]{1,0:T(8,128)(2,1)} %get-tuple-element.30), channel_id=1, source_target_pairs={{0,1},{1,2},{2,3},{3,0},{4,5},{5,6},{6,7},{7,4},{8,9},{9,10},{10,1... | collective-permute-start | bytes 688136 | tf_op jit(solution)/shard_map/ppermute | solution.py:221
  175.9 12.2 %collective-permute-start.19 = (bf16[128,896]{1,0:T(8,128)(2,1)}, bf16[128,896]{1,0:T(8,128)(2,1)S(1)}, u32[]{:S(2)}, u32[]{:S(2)}) collective-permute-start(bf16[128,896]{1,0:T(8,128)(2,1)} %get-tuple-element.31), channel_id=1, source_target_pairs={{0,3},{1,0},{2,1},{3,2},{4,7},{5,4},{6,5},{7,6},{8,11},{9,8},{10,9... | collective-permute-start | bytes 688136 | tf_op jit(solution)/shard_map/ppermute | solution.py:221
  178.9 10.8 %collective-permute-start.20 = (bf16[128,896]{1,0:T(8,128)(2,1)S(1)}, bf16[128,896]{1,0:T(8,128)(2,1)S(1)}, u32[]{:S(2)}, u32[]{:S(2)}) collective-permute-start(bf16[128,896]{1,0:T(8,128)(2,1)S(1)} %get-tuple-element.32), channel_id=1, source_target_pairs={{0,2},{1,3},{2,0},{3,1},{4,6},{5,7},{6,4},{7,5},{8,10},{9,11},{10,... | collective-permute-start | bytes 688136 | tf_op jit(solution)/shard_map/ppermute | solution.py:221

commit v7 on v6

--- a/solution.py
+++ b/solution.py
@@ -36,16 +36,21 @@
     return (gate / (1.0 + jnp.exp(-gate)) * up).astype(BF16)
 
 
-def kernel_call(body, outs, *args, smem=0, vmem=12, flops=1):
-    places = [pltpu.SMEM] * smem + [pltpu.VMEM] * (len(args) - smem)
+def kernel_call(body, outs, *args, smem=0, hbm=0, scratch=(), to_hbm=False, vmem=12, flops=1):
+    places = [pltpu.SMEM] * smem + [pltpu.VMEM] * (len(args) - smem - hbm) + [pltpu.HBM] * hbm
+    last = len(args) - hbm
+    args = args[:last] + tuple(pltpu.with_memory_space_constraint(a, pltpu.HBM) for a in args[last:])
     return pl.pallas_call(
         body,
         in_specs=[pl.BlockSpec(memory_space=m) for m in places],
-        out_specs=[pl.BlockSpec(memory_space=pltpu.VMEM) for _ in outs],
+        out_specs=[pl.BlockSpec(memory_space=pltpu.HBM if to_hbm else pltpu.VMEM) for _ in outs],
         out_shape=[
-            o if isinstance(o, jax.ShapeDtypeStruct) else jax.ShapeDtypeStruct(o, BF16)
+            o
+            if isinstance(o, jax.ShapeDtypeStruct)
+            else (pltpu.HBM if to_hbm else jax.ShapeDtypeStruct)(o, BF16)
             for o in outs
         ],
+        scratch_shapes=scratch,
         compiler_params=pltpu.CompilerParams(vmem_limit_bytes=vmem << 20),
         cost_estimate=pl.CostEstimate(flops=flops, transcendentals=0, bytes_accessed=0),
     )(*args)
@@ -165,42 +170,73 @@
     out_ref[...] = silu_times(gate, up)
 
 
-def pair_sums_body(q_ref, rows_ref, gate_ref, up_ref, sums_ref, rest_ref):
-    _, width, quarter = gate_ref.shape
-    at = [lax.rem(q_ref[0] + s, len(TURNS)) for s in TURNS]
+def pair_sums_body(q_ref, rows_ref, gate_hbm, up_hbm, sums_ref, *scratch):
+    fetched = fetch(q_ref, (gate_hbm, up_hbm), (0, 3), *scratch)
+    width, quarter = gate_hbm.shape[1:]
     lanes = rows_ref.shape[2] // 2
-    own = flat(rows_ref[:, :, :lanes], width)
-    far = flat(rows_ref[:, :, lanes:], width)
-    sums_ref[:, :quarter] = dot(own, gate_ref[at[0]]) + dot(far, gate_ref[at[3]])
-    sums_ref[:, quarter:] = dot(own, up_ref[at[0]]) + dot(far, up_ref[at[3]])
-    for i in range(2):
-        rest_ref[2 * i] = gate_ref[at[1 + i]]
-        rest_ref[2 * i + 1] = up_ref[at[1 + i]]
-
-
-def pair_hidden_body(sums_ref, left_ref, right_ref, rest_ref, out_ref):
-    _, width, quarter = rest_ref.shape
-    left, right = flat(left_ref[...], width), flat(right_ref[...], width)
-    gate = sums_ref[:, :quarter] + dot(left, rest_ref[0]) + dot(right, rest_ref[2])
-    up = sums_ref[:, quarter:] + dot(left, rest_ref[1]) + dot(right, rest_ref[3])
-    out_ref[...] = silu_times(gate, up)
-
-
-def stack_body(*refs):
-    *ins, out_ref = refs
-    for s, ref in enumerate(ins):
-        out_ref[s] = ref[...]
+    xs = [flat(rows_ref[:, :, s * lanes : (s + 1) * lanes], width) for s in range(2)]
+    sums_ref[...] = jnp.zeros_like(sums_ref)
+    for x, pair in zip(xs, fetched):
+        for k, take in enumerate(pair):
+            sums_ref[:, k * quarter : (k + 1) * quarter] += dot(x, take())
+
+
+def pair_hidden_body(q_ref, sums_ref, left_ref, right_ref, gate_hbm, up_hbm, out_ref, *scratch):
+    fetched = fetch(q_ref, (gate_hbm, up_hbm), (1, 2), *scratch)
+    width, quarter = gate_hbm.shape[1:]
+    sums = [sums_ref[:, k * quarter : (k + 1) * quarter] for k in range(2)]
+    for ref, pair in zip((left_ref, right_ref), fetched):
+        x = flat(ref[...], width)
+        sums = [total + dot(x, take()) for total, take in zip(sums, pair)]
+    out_ref[...] = silu_times(*sums)
+
+
+def fetch(q_ref, sources, turns, buffer, sems):
+    def start(i, k, turn):
+        at = lax.rem(q_ref[0] + TURNS[turn], sources[k].shape[0])
+        copy = pltpu.make_async_copy(sources[k].at[at], buffer.at[i, k], sems.at[i, k])
+        copy.start()
+
+        def take():
+            copy.wait()
+            return buffer[i, k]
+
+        return take
+
+    return [[start(i, k, t) for k in range(len(sources))] for i, t in enumerate(turns)]
 
 
 def down_body(halves):
     def body(*refs):
-        *ins, down_ref, out_ref = refs
+        n = len(TURNS)
+        ins, parts, out_hbm = refs[:n], refs[n : 2 * n], refs[2 * n]
+        rows_ref, down_ref, out_ref, in_sems, out_sems = refs[2 * n + 1 :]
+        copies = []
+        for s in range(n):
+            pair = (
+                pltpu.make_async_copy(ins[s], rows_ref.at[s], in_sems.at[0, s]),
+                pltpu.make_async_copy(parts[s], down_ref.at[s], in_sems.at[1, s]),
+            )
+            for c in pair:
+                c.start()
+            copies.append(pair)
+        total = 0.0
+        for s in range(n):
+            for c in copies[s]:
+                c.wait()
+            total = total + dot(rows_ref[s], down_ref[s])
+        total = total.astype(BF16)
         count = out_ref.shape[0] // halves
-        rows = ins[0].shape[0] // halves
+        rows = total.shape[0] // halves
+        leaving = []
         for h in range(halves):
-            span = pl.ds(h * rows, rows)
-            total = sum(dot(a[span], down_ref[s]) for s, a in enumerate(ins))
-            unflat(out_ref.at[pl.ds(h * count, count)], total.astype(BF16))
+            span = pl.ds(h * count, count)
+            unflat(out_ref.at[span], total[h * rows : (h + 1) * rows])
+            c = pltpu.make_async_copy(out_ref.at[span], out_hbm.at[span], out_sems.at[h])
+            c.start()
+            leaving.append(c)
+        for c in leaving:
+            c.wait()
 
     return body
 
@@ -266,7 +302,7 @@
         )
         arrived.append(exchange(rows, EXPERT))
     columns = kernel_call(columns_body, [(quarter, narrow)] * n, q, w_down, smem=1)
-    (down,) = kernel_call(stack_body, [(n, quarter, narrow)], *deal(columns))
+    down = deal(columns)
     weights = kernel_call(
         weight_body(experts),
         [(tok_dev, experts * size) for size in CHUNKS],
@@ -292,28 +328,55 @@
         if j == 0:
             left, right, *last = ring(rows)
             args = (rows, left, right)
-            bodies = ring_sums_body, ring_hidden_body
         else:
             own = rows[:, :, : size // PAIR * narrow]
             last = shift(own, "tensor", 1), shift(own, "tensor", -1)
             args = (rows,)
-            bodies = pair_sums_body, pair_hidden_body
-        sums, rest = kernel_call(
-            bodies[0],
-            [sums_shape, (2 * (1 + j), narrow, quarter)],
-            q,
-            *args,
-            w_gate,
-            w_up,
-            smem=1,
-            flops=10**9,
-        )
-        (hidden,) = kernel_call(bodies[1], [(count, quarter)], sums, *last, rest, flops=10**9)
+        if j == 0:
+            sums, rest = kernel_call(
+                ring_sums_body,
+                [sums_shape, (2, narrow, quarter)],
+                q,
+                *args,
+                w_gate,
+                w_up,
+                smem=1,
+                flops=10**9,
+            )
+            (hidden,) = kernel_call(
+                ring_hidden_body, [(count, quarter)], sums, *last, rest, flops=10**9
+            )
+        else:
+            weights_hbm = dict(
+                smem=1,
+                hbm=2,
+                scratch=[
+                    pltpu.VMEM((2, 2, narrow, quarter), BF16),
+                    pltpu.SemaphoreType.DMA((2, 2)),
+                ],
+                flops=10**9,
+            )
+            (sums,) = kernel_call(
+                pair_sums_body, [sums_shape], q, *args, w_gate, w_up, **weights_hbm
+            )
+            (hidden,) = kernel_call(
+                pair_hidden_body, [(count, quarter)], q, sums, *last, w_gate, w_up, **weights_hbm
+            )
+        out_shape = (experts, PAIR, size // PAIR * narrow)
         (out,) = kernel_call(
             down_body(2 - j),
-            [(experts, PAIR, size // PAIR * narrow)],
+            [out_shape],
             *spread(hidden),
-            down,
+            *down,
+            hbm=2 * n,
+            scratch=[
+                pltpu.VMEM((n, count, quarter), BF16),
+                pltpu.VMEM((n, quarter, narrow), BF16),
+                pltpu.VMEM(out_shape, BF16),
+                pltpu.SemaphoreType.DMA((2, n)),
+                pltpu.SemaphoreType.DMA((2 - j,)),
+            ],
+            to_hbm=True,
             flops=10**9,
         )
         returned.append(exchange(out, EXPERT))

time: 194 us -> 199 us (1.026)
  Pallas kernels: 16.4 us -> 23.9 us
    pallas_call x14 -> x13, Pallas kernels: 16.4 us -> 23.9 us  [kernel_call(): pl.pallas_call(body, in_specs=[pl.BlockSpec(memory_space=m) for m in plac...]
    unnamed x42 -> x56, local copies, waits for them, and re-layouts: 14 us -> 12.4 us
  transfers between devices with their start and end apart: 25 -> 25, of which waited for: 14 -> 14; matrix products, arithmetic and copies ran while one was open for 2% -> 2% of each run, Pallas kernels for 7% -> 11%
where the time goes in v7:
time: 199 us; the launch traced here: 198 us
  starting transfers between devices  80.3 us (40%)
  waiting for transfers between devices  77.8 us (39%)
  Pallas kernels  23.9 us (12%)
  local copies, waits for them, and re-layouts  15.3 us (8%)
    ppermute x21, waiting for transfers between devices, shift(): return lax.ppermute(x, axis, [(i, (i + by) % n) for i in range(n)])  69 us
    ppermute x21, starting transfers between devices, shift(): return lax.ppermute(x, axis, [(i, (i + by) % n) for i in range(n)])  41.6 us
    all_to_all x4, starting transfers between devices, exchange(): return lax.all_to_all(x, axis, split_axis=0, concat_axis=0, tiled=True)  38.8 us
    pallas_call x13, Pallas kernels, kernel_call(): pl.pallas_call(body, in_specs=[pl.BlockSpec(memory_space=m) for m in plac...  23.9 us
    unnamed x56, local copies, waits for them, and re-layouts  12.4 us
    all_to_all x4, waiting for transfers between devices, exchange(): return lax.all_to_all(x, axis, split_axis=0, concat_axis=0, tiled=True)  8.83 us
  transfers between devices with their start and end apart: 25, of which 14 were waited for; matrix products, arithmetic and copies ran while one was open for 2% of the time, Pallas kernels for 11%

profile of v7, /device:TPU:32, one launch (start us, length us, event | category | flops | bytes accessed | tf_op | source)
XLA Modules:
  0.0 197.7 jit_solution(9741677260542702347)
XLA Ops:
  0.0 0.9 copy-done.4
  0.9 0.7 copy-done.13
  1.6 1.4 shard_map.97
  3.0 11.6 %all-to-all-start.2 = ((bf16[64,2,2688]{2,1,0:T(2,128)(2,1)}), bf16[64,2,2688]{2,1,0:T(2,128)(2,1)S(1)}, u32[]{:S(2)}, u32[]{:S(2)}) async-start(bf16[64,2,2688]{2,1,0:T(2,128)(2,1)} %shard_map.97), calls=%async_computation.2 | async-start | bytes 1376256 | tf_op jit(solution)/shard_map/all_to_all | solution.py:252
  14.6 3.3 %collective-permute-start = (bf16[128,896]{1,0:T(8,128)(2,1)S(1)}, bf16[128,896]{1,0:T(8,128)(2,1)S(1)}, u32[]{:S(2)}, u32[]{:S(2)}) collective-permute-start(bf16[128,896]{1,0:T(8,128)(2,1)S(1)} %copy-done.5), channel_id=1, source_target_pairs={{0,2},{1,3},{2,0},{3,1},{4,6},{5,7},{6,4},{7,5},{8,10},{9,11},{10,... | collective-permute-start | bytes 688136 | tf_op jit(solution)/shard_map/ppermute | solution.py:257
  17.9 5.9 %collective-permute-done.refs_1_.refs_3_ = bf16[128,896]{1,0:T(8,128)(2,1)S(1)} collective-permute-done((bf16[128,896]{1,0:T(8,128)(2,1)S(1)}, bf16[128,896]{1,0:T(8,128)(2,1)S(1)}, u32[]{:S(2)}, u32[]{:S(2)}) %collective-permute-start) | collective-permute-done | bytes 229408 | tf_op jit(solution)/shard_map/ppermute | solution.py:257
  23.8 1.9 shard_map.92
  25.7 0.7 copy-done.10
  26.4 8.8 %all-to-all-done.2.own_ref = bf16[64,2,2688]{2,1,0:T(2,128)(2,1)S(1)} async-done(((bf16[64,2,2688]{2,1,0:T(2,128)(2,1)}), bf16[64,2,2688]{2,1,0:T(2,128)(2,1)S(1)}, u32[]{:S(2)}, u32[]{:S(2)}) %all-to-all-start.2) | async-done | bytes 688160 | tf_op jit(solution)/shard_map/all_to_all | solution.py:252
  35.2 0.8 copy-done.2
  36.0 6.5 %all-to-all-start = ((bf16[64,2,5376]{2,1,0:T(2,128)(2,1)}), bf16[64,2,5376]{2,1,0:T(2,128)(2,1)S(1)}, u32[]{:S(2)}, u32[]{:S(2)}) async-start(bf16[64,2,5376]{2,1,0:T(2,128)(2,1)} %shard_map.92), calls=%async_computation | async-start | bytes 2752512 | tf_op jit(solution)/shard_map/all_to_all | solution.py:252
  42.5 1.7 collective-permute-start.9
  44.2 1.7 collective-permute-start.10
  45.8 1.6 copy-done.6
  47.5 0.4 collective-permute-start.6
  48.0 14.4 %collective-permute-done.9.left_ref = bf16[64,2,2688]{2,1,0:T(2,128)(2,1)} collective-permute-done((bf16[64,2,2688]{2,1,0:T(2,128)(2,1)}, bf16[64,2,2688]{2,1,0:T(2,128)(2,1)}, u32[]{:S(2)}, u32[]{:S(2)}) %collective-permute-start.9) | collective-permute-done | bytes 688160 | tf_op jit(solution)/shard_map/ppermute | solution.py:257
  62.4 1.2 slice.13
  63.6 0.4 collective-permute-start.11
  64.1 1.2 slice.14
  65.3 2.9 %collective-permute-start.12 = (bf16[32,2,2688]{2,1,0:T(2,128)(2,1)S(1)}, bf16[32,2,2688]{2,1,0:T(2,128)(2,1)S(1)}, u32[]{:S(2)}, u32[]{:S(2)}) collective-permute-start(bf16[32,2,2688]{2,1,0:T(2,128)(2,1)S(1)} %slice.14), channel_id=1, source_target_pairs={{0,3},{1,0},{2,1},{3,2},{4,7},{5,4},{6,5},{7,6},{8,11},{9,8},{10,9... | collective-permute-start | bytes 1032200 | tf_op jit(solution)/shard_map/ppermute | solution.py:257
  68.3 0.6 collective-permute-start.7
  68.9 0.6 collective-permute-start.8
  69.5 1.5 copy-done.1
  71.0 2.8 %shard_map.98 = (f32[384,512]{1,0:T(8,128)S(1)}, bf16[2,896,256]{2,1,0:T(8,128)(2,1)S(1)}) custom-call(s32[1]{0:T(128)} %bitcast.q_ref, bf16[64,2,2688]{2,1,0:T(2,128)(2,1)S(1)} %copy-done.3, bf16[64,2,2688]{2,1,0:T(2,128)(2,1)} %collective-permute-done.9.left_ref, bf16[64,2,2688]{2,1,0:T(2,128)(2,1)} %collective-permute-done.10.right_ref, ...), custom_call_target="tpu_custom_call" | custom-call | flops 1000000000 | tf_op jit(solution)/shard_map/pallas_call | solution.py:43
  73.8 4.9 %collective-permute-done.11.o0_ref = bf16[32,2,2688]{2,1,0:T(2,128)(2,1)S(1)} collective-permute-done((bf16[32,2,2688]{2,1,0:T(2,128)(2,1)S(1)}, bf16[32,2,2688]{2,1,0:T(2,128)(2,1)S(1)}, u32[]{:S(2)}, u32[]{:S(2)}) %collective-permute-start.11) | collective-permute-done | bytes 344096 | tf_op jit(solution)/shard_map/ppermute | solution.py:257
  78.7 0.6 shard_map.99.refs_0_
  79.4 1.2 collective-permute-start.13
  80.6 2.1 %collective-permute-start.14 = (bf16[384,256]{1,0:T(8,128)(2,1)S(1)}, bf16[384,256]{1,0:T(8,128)(2,1)S(1)}, u32[]{:S(2)}, u32[]{:S(2)}) collective-permute-start(bf16[384,256]{1,0:T(8,128)(2,1)S(1)} %shard_map.99.refs_0_), channel_id=1, source_target_pairs={{0,3},{1,0},{2,1},{3,2},{4,7},{5,4},{6,5},{7,6},{8,11},{9,8},{10,9... | collective-permute-start | bytes 589832 | tf_op jit(solution)/shard_map/ppermute | solution.py:257
  82.7 9.8 %collective-permute-start.15 = (bf16[384,256]{1,0:T(8,128)(2,1)S(1)}, bf16[384,256]{1,0:T(8,128)(2,1)S(1)}, u32[]{:S(2)}, u32[]{:S(2)}) collective-permute-start(bf16[384,256]{1,0:T(8,128)(2,1)S(1)} %shard_map.99.refs_0_), channel_id=1, source_target_pairs={{0,2},{1,3},{2,0},{3,1},{4,6},{5,7},{6,4},{7,5},{8,10},{9,11},{10,... | collective-permute-start | bytes 589832 | tf_op jit(solution)/shard_map/ppermute | solution.py:257
  92.5 5.2 %collective-permute-done.7.refs_6_ = bf16[256,896]{1,0:T(8,128)(2,1)S(1)} collective-permute-done((bf16[256,896]{1,0:T(8,128)(2,1)S(1)}, bf16[256,896]{1,0:T(8,128)(2,1)S(1)}, u32[]{:S(2)}, u32[]{:S(2)}) %collective-permute-start.7) | collective-permute-done | bytes 458784 | tf_op jit(solution)/shard_map/ppermute | solution.py:257
  97.7 4.3 %collective-permute-done.14.refs_2_ = bf16[384,256]{1,0:T(8,128)(2,1)S(1)} collective-permute-done((bf16[384,256]{1,0:T(8,128)(2,1)S(1)}, bf16[384,256]{1,0:T(8,128)(2,1)S(1)}, u32[]{:S(2)}, u32[]{:S(2)}) %collective-permute-start.14) | collective-permute-done | bytes 196640 | tf_op jit(solution)/shard_map/ppermute | solution.py:257
  102.1 0.6 copy-done.22
  102.9 3.3 %shard_map.100 = bf16[64,2,2688]{2,1,0:T(2,128)(2,1)} custom-call(bf16[384,256]{1,0:T(8,128)(2,1)} %copy-done.16, bf16[384,256]{1,0:T(8,128)(2,1)} %copy-done.21, bf16[384,256]{1,0:T(8,128)(2,1)} %copy-done.22, bf16[384,256]{1,0:T(8,128)(2,1)} %copy-done.24, bf16[256,896]{1,0:T(8,128)(2,1)} %copy-done.15, bf16[256,896]{1,0:T(8,128)(2,1)} %copy-done.18, ...), custom_call_target="tpu_custom_call" | custom-call | flops 1000000000 | tf_op jit(solution)/shard_map/pallas_call | solution.py:43
  106.2 10.3 %all-to-all-start.3 = ((bf16[64,2,2688]{2,1,0:T(2,128)(2,1)}), bf16[64,2,2688]{2,1,0:T(2,128)(2,1)S(1)}, u32[]{:S(2)}, u32[]{:S(2)}) async-start(bf16[64,2,2688]{2,1,0:T(2,128)(2,1)} %shard_map.100), calls=%async_computation.3 | async-start | bytes 1376256 | tf_op jit(solution)/shard_map/all_to_all | solution.py:252
  116.5 0.5 slice.12
  117.0 1.8 collective-permute-start.1
  118.8 2.0 %collective-permute-start.2 = (bf16[64,2,2688]{2,1,0:T(2,128)(2,1)S(1)}, bf16[64,2,2688]{2,1,0:T(2,128)(2,1)S(1)}, u32[]{:S(2)}, u32[]{:S(2)}) collective-permute-start(bf16[64,2,2688]{2,1,0:T(2,128)(2,1)S(1)} %slice.12), channel_id=1, source_target_pairs={{0,3},{1,0},{2,1},{3,2},{4,7},{5,4},{6,5},{7,6},{8,11},{9,8},{10,9... | collective-permute-start | bytes 2064392 | tf_op jit(solution)/shard_map/ppermute | solution.py:257
  120.9 3.1 %shard_map.93.sums_ref = f32[384,512]{1,0:T(8,128)S(1)} custom-call(s32[1]{0:T(128)} %bitcast.q_ref, bf16[64,2,5376]{2,1,0:T(2,128)(2,1)S(1)} %all-to-all-done.rows_ref, bf16[4,896,256]{2,1,0:T(8,128)(2,1)} %bitcast.7, bf16[4,896,256]{2,1,0:T(8,128)(2,1)} %bitcast.10), custom_call_target="tpu_custom_call" | custom-call | flops 1000000000 | tf_op jit(solution)/shard_map/pallas_call | solution.py:43
  124.0 12.5 %collective-permute-done.1.left_ref = bf16[64,2,2688]{2,1,0:T(2,128)(2,1)S(1)} collective-permute-done((bf16[64,2,2688]{2,1,0:T(2,128)(2,1)S(1)}, bf16[64,2,2688]{2,1,0:T(2,128)(2,1)S(1)}, u32[]{:S(2)}, u32[]{:S(2)}) %collective-permute-start.1) | collective-permute-done | bytes 688160 | tf_op jit(solution)/shard_map/ppermute | solution.py:257
  136.5 3.1 %shard_map.94.refs_0_ = bf16[384,256]{1,0:T(8,128)(2,1)S(1)} custom-call(s32[1]{0:T(128)} %bitcast.q_ref, f32[384,512]{1,0:T(8,128)S(1)} %shard_map.93.sums_ref, bf16[64,2,2688]{2,1,0:T(2,128)(2,1)S(1)} %collective-permute-done.1.left_ref, bf16[64,2,2688]{2,1,0:T(2,128)(2,1)S(1)} %collective-permute-done.2.right_ref, bf16[4,896,256]{2,1,0:T(8,128)(2,1)} %bitcast.8, ...), custom_call_target="tpu_custom_call" | custom-call | flops 1000000000 | tf_op jit(solution)/shard_map/pallas_call | solution.py:43
  139.6 1.2 collective-permute-start.3
  140.9 2.1 %collective-permute-start.4 = (bf16[384,256]{1,0:T(8,128)(2,1)S(1)}, bf16[384,256]{1,0:T(8,128)(2,1)S(1)}, u32[]{:S(2)}, u32[]{:S(2)}) collective-permute-start(bf16[384,256]{1,0:T(8,128)(2,1)S(1)} %shard_map.94.refs_0_), channel_id=1, source_target_pairs={{0,3},{1,0},{2,1},{3,2},{4,7},{5,4},{6,5},{7,6},{8,11},{9,8},{10,9... | collective-permute-start | bytes 589832 | tf_op jit(solution)/shard_map/ppermute | solution.py:257
  143.0 1.7 collective-permute-start.5
  144.7 3.3 %collective-permute-done.3.refs_1_ = bf16[384,256]{1,0:T(8,128)(2,1)S(1)} collective-permute-done((bf16[384,256]{1,0:T(8,128)(2,1)S(1)}, bf16[384,256]{1,0:T(8,128)(2,1)S(1)}, u32[]{:S(2)}, u32[]{:S(2)}) %collective-permute-start.3) | collective-permute-done | bytes 196640 | tf_op jit(solution)/shard_map/ppermute | solution.py:257
  148.0 2.8 %collective-permute-done.4.refs_2_ = bf16[384,256]{1,0:T(8,128)(2,1)S(1)} collective-permute-done((bf16[384,256]{1,0:T(8,128)(2,1)S(1)}, bf16[384,256]{1,0:T(8,128)(2,1)S(1)}, u32[]{:S(2)}, u32[]{:S(2)}) %collective-permute-start.4) | collective-permute-done | bytes 196640 | tf_op jit(solution)/shard_map/ppermute | solution.py:257
  150.8 1.7 collective-permute-done.5.refs_3_
  152.5 0.7 copy-done.26
  153.2 3.4 %shard_map.96 = bf16[64,2,2688]{2,1,0:T(2,128)(2,1)} custom-call(bf16[384,256]{1,0:T(8,128)(2,1)} %copy-done.12, bf16[384,256]{1,0:T(8,128)(2,1)} %copy-done.23, bf16[384,256]{1,0:T(8,128)(2,1)} %copy-done.25, bf16[384,256]{1,0:T(8,128)(2,1)} %copy-done.26, bf16[256,896]{1,0:T(8,128)(2,1)} %copy-done.15, bf16[256,896]{1,0:T(8,128)(2,1)} %copy-done.18, ...), custom_call_target="tpu_custom_call" | custom-call | flops 1000000000 | tf_op jit(solution)/shard_map/pallas_call | solution.py:43
  156.6 10.3 %all-to-all-start.1 = ((bf16[64,2,2688]{2,1,0:T(2,128)(2,1)}), bf16[64,2,2688]{2,1,0:T(2,128)(2,1)S(1)}, u32[]{:S(2)}, u32[]{:S(2)}) async-start(bf16[64,2,2688]{2,1,0:T(2,128)(2,1)} %shard_map.96), calls=%async_computation.1 | async-start | bytes 1376256 | tf_op jit(solution)/shard_map/all_to_all | solution.py:252
  166.9 1.2 collective-permute-start.16
  168.1 2.1 %collective-permute-start.17 = (bf16[128,896]{1,0:T(8,128)(2,1)S(1)}, bf16[128,896]{1,0:T(8,128)(2,1)S(1)}, u32[]{:S(2)}, u32[]{:S(2)}) collective-permute-start(bf16[128,896]{1,0:T(8,128)(2,1)S(1)} %copy-done.5), channel_id=1, source_target_pairs={{0,3},{1,0},{2,1},{3,2},{4,7},{5,4},{6,5},{7,6},{8,11},{9,8},{10,9... | collective-permute-start | bytes 688136 | tf_op jit(solution)/shard_map/ppermute | solution.py:257
  170.2 5.6 %collective-permute-done.16.refs_1_ = bf16[128,896]{1,0:T(8,128)(2,1)S(1)} collective-permute-done((bf16[128,896]{1,0:T(8,128)(2,1)S(1)}, bf16[128,896]{1,0:T(8,128)(2,1)S(1)}, u32[]{:S(2)}, u32[]{:S(2)}) %collective-permute-start.16) | collective-permute-done | bytes 229408 | tf_op jit(solution)/shard_map/ppermute | solution.py:257
  175.8 1.5 copy-done.7
  177.3 1.5 copy-done.8
  178.8 1.5 copy-done.9
  180.3 1.8 shard_map.101
  182.2 0.8 collective-permute-start.18
  183.0 2.4 %collective-permute-start.19 = (bf16[128,896]{1,0:T(8,128)(2,1)}, bf16[128,896]{1,0:T(8,128)(2,1)S(1)}, u32[]{:S(2)}, u32[]{:S(2)}) collective-permute-start(bf16[128,896]{1,0:T(8,128)(2,1)} %get-tuple-element.27), channel_id=1, source_target_pairs={{0,3},{1,0},{2,1},{3,2},{4,7},{5,4},{6,5},{7,6},{8,11},{9,8},{10,9... | collective-permute-start | bytes 688136 | tf_op jit(solution)/shard_map/ppermute | solution.py:257
  185.4 1.4 collective-permute-start.20
  187.1 0.9 shard_map.91
  188.0 3.4 %collective-permute-done.18.refs_1_ = bf16[128,896]{1,0:T(8,128)(2,1)S(1)} collective-permute-done((bf16[128,896]{1,0:T(8,128)(2,1)}, bf16[128,896]{1,0:T(8,128)(2,1)S(1)}, u32[]{:S(2)}, u32[]{:S(2)}) %collective-permute-start.18) | collective-permute-done | bytes 229408 | tf_op jit(solution)/shard_map/ppermute | solution.py:257
  191.4 3.3 %collective-permute-done.19.refs_2_ = bf16[128,896]{1,0:T(8,128)(2,1)S(1)} collective-permute-done((bf16[128,896]{1,0:T(8,128)(2,1)}, bf16[128,896]{1,0:T(8,128)(2,1)S(1)}, u32[]{:S(2)}, u32[]{:S(2)}) %collective-permute-start.19) | collective-permute-done | bytes 229408 | tf_op jit(solution)/shard_map/ppermute | solution.py:257
  194.7 1.5 collective-permute-done.20.refs_3_
  196.6 1.1 shard_map.103
  (58 shorter events, 1.0 us)
Async XLA Ops:
  0.0 0.9 copy-start.4
  0.9 0.7 copy-start.13
  1.6 13.0 %copy-start.5 = (bf16[128,896]{1,0:T(8,128)(2,1)S(1)}, bf16[128,896]{1,0:T(8,128)(2,1)}, u32[]{:S(2)}) copy-start(bf16[128,896]{1,0:T(8,128)(2,1)} %refs_0_.5) | copy-start | bytes 688132
  1.6 22.2 %copy-start.14 = (s32[128,4]{0,1:T(4,128)S(1)}, s32[128,4]{0,1:T(4,128)}, u32[]{:S(2)}) copy-start(s32[128,4]{0,1:T(4,128)} %param.10) | copy-start | bytes 6148
  3.0 32.2 %all-to-all-start.2 = ((bf16[64,2,2688]{2,1,0:T(2,128)(2,1)}), bf16[64,2,2688]{2,1,0:T(2,128)(2,1)S(1)}, u32[]{:S(2)}, u32[]{:S(2)}) async-start(bf16[64,2,2688]{2,1,0:T(2,128)(2,1)} %shard_map.97), calls=%async_computation.2 | async-start | bytes 1376256 | tf_op jit(solution)/shard_map/all_to_all | solution.py:252
  14.6 9.2 %collective-permute-start = (bf16[128,896]{1,0:T(8,128)(2,1)S(1)}, bf16[128,896]{1,0:T(8,128)(2,1)S(1)}, u32[]{:S(2)}, u32[]{:S(2)}) collective-permute-start(bf16[128,896]{1,0:T(8,128)(2,1)S(1)} %copy-done.5), channel_id=1, source_target_pairs={{0,2},{1,3},{2,0},{3,1},{4,6},{5,7},{6,4},{7,5},{8,10},{9,11},{10,... | collective-permute-start | bytes 688136 | tf_op jit(solution)/shard_map/ppermute | solution.py:257
  25.7 0.7 copy-start.10
  35.2 0.8 copy-start.2
  36.0 70.1 %all-to-all-start = ((bf16[64,2,5376]{2,1,0:T(2,128)(2,1)}), bf16[64,2,5376]{2,1,0:T(2,128)(2,1)S(1)}, u32[]{:S(2)}, u32[]{:S(2)}) async-start(bf16[64,2,5376]{2,1,0:T(2,128)(2,1)} %shard_map.92), calls=%async_computation | async-start | bytes 2752512 | tf_op jit(solution)/shard_map/all_to_all | solution.py:252
  42.5 27.0 %copy-start = (bf16[1,3584,256]{2,1,0:T(8,128)(2,1)S(1)}, bf16[1,3584,256]{2,1,0:T(8,128)(2,1)}, u32[]{:S(2)}) copy-start(bf16[1,3584,256]{2,1,0:T(8,128)(2,1)} %param.12) | copy-start | bytes 5505028
  42.5 19.9 %collective-permute-start.9 = (bf16[64,2,2688]{2,1,0:T(2,128)(2,1)}, bf16[64,2,2688]{2,1,0:T(2,128)(2,1)}, u32[]{:S(2)}, u32[]{:S(2)}) collective-permute-start(bf16[64,2,2688]{2,1,0:T(2,128)(2,1)} %copy-done.2), channel_id=1, source_target_pairs={{0,1},{1,2},{2,3},{3,0},{4,5},{5,6},{6,7},{7,4},{8,9},{9,10},{10,1... | collective-permute-start | bytes 2064392 | tf_op jit(solution)/shard_map/ppermute | solution.py:257
  44.2 19.9 %collective-permute-start.10 = (bf16[64,2,2688]{2,1,0:T(2,128)(2,1)}, bf16[64,2,2688]{2,1,0:T(2,128)(2,1)}, u32[]{:S(2)}, u32[]{:S(2)}) collective-permute-start(bf16[64,2,2688]{2,1,0:T(2,128)(2,1)} %copy-done.2), channel_id=1, source_target_pairs={{0,3},{1,0},{2,1},{3,2},{4,7},{5,4},{6,5},{7,6},{8,11},{9,8},{10,9... | collective-permute-start | bytes 2064392 | tf_op jit(solution)/shard_map/ppermute | solution.py:257
  45.8 23.7 %copy-start.3 = (bf16[64,2,2688]{2,1,0:T(2,128)(2,1)S(1)}, bf16[64,2,2688]{2,1,0:T(2,128)(2,1)}, u32[]{:S(2)}) copy-start(bf16[64,2,2688]{2,1,0:T(2,128)(2,1)} %copy-done.2) | copy-start | bytes 2064388
  45.8 1.6 copy-start.6
  47.5 26.3 %copy-start.15 = (bf16[256,896]{1,0:T(8,128)(2,1)}, bf16[256,896]{1,0:T(8,128)(2,1)S(1)}, u32[]{:S(2)}) copy-start(bf16[256,896]{1,0:T(8,128)(2,1)S(1)} %get-tuple-element.18.refs_4_) | copy-start | bytes 1376260
  47.5 35.2 %collective-permute-start.6 = (bf16[256,896]{1,0:T(8,128)(2,1)S(1)}, bf16[256,896]{1,0:T(8,128)(2,1)S(1)}, u32[]{:S(2)}, u32[]{:S(2)}) collective-permute-start(bf16[256,896]{1,0:T(8,128)(2,1)S(1)} %get-tuple-element.19), channel_id=1, source_target_pairs={{0,1},{1,2},{2,3},{3,0},{4,5},{5,6},{6,7},{7,4},{8,9},{9,10},{10,1... | collective-permute-start | bytes 1376264 | tf_op jit(solution)/shard_map/ppermute | solution.py:257
  63.6 15.1 %collective-permute-start.11 = (bf16[32,2,2688]{2,1,0:T(2,128)(2,1)S(1)}, bf16[32,2,2688]{2,1,0:T(2,128)(2,1)S(1)}, u32[]{:S(2)}, u32[]{:S(2)}) collective-permute-start(bf16[32,2,2688]{2,1,0:T(2,128)(2,1)S(1)} %slice.13), channel_id=1, source_target_pairs={{0,1},{1,2},{2,3},{3,0},{4,5},{5,6},{6,7},{7,4},{8,9},{9,10},{10,1... | collective-permute-start | bytes 1032200 | tf_op jit(solution)/shard_map/ppermute | solution.py:257
  65.3 13.4 %collective-permute-start.12 = (bf16[32,2,2688]{2,1,0:T(2,128)(2,1)S(1)}, bf16[32,2,2688]{2,1,0:T(2,128)(2,1)S(1)}, u32[]{:S(2)}, u32[]{:S(2)}) collective-permute-start(bf16[32,2,2688]{2,1,0:T(2,128)(2,1)S(1)} %slice.14), channel_id=1, source_target_pairs={{0,3},{1,0},{2,1},{3,2},{4,7},{5,4},{6,5},{7,6},{8,11},{9,8},{10,9... | collective-permute-start | bytes 1032200 | tf_op jit(solution)/shard_map/ppermute | solution.py:257
  68.3 29.5 %collective-permute-start.7 = (bf16[256,896]{1,0:T(8,128)(2,1)S(1)}, bf16[256,896]{1,0:T(8,128)(2,1)S(1)}, u32[]{:S(2)}, u32[]{:S(2)}) collective-permute-start(bf16[256,896]{1,0:T(8,128)(2,1)S(1)} %get-tuple-element.20), channel_id=1, source_target_pairs={{0,3},{1,0},{2,1},{3,2},{4,7},{5,4},{6,5},{7,6},{8,11},{9,8},{10,9... | collective-permute-start | bytes 1376264 | tf_op jit(solution)/shard_map/ppermute | solution.py:257
  68.9 28.9 %collective-permute-start.8 = (bf16[256,896]{1,0:T(8,128)(2,1)S(1)}, bf16[256,896]{1,0:T(8,128)(2,1)S(1)}, u32[]{:S(2)}, u32[]{:S(2)}) collective-permute-start(bf16[256,896]{1,0:T(8,128)(2,1)S(1)} %get-tuple-element.21), channel_id=1, source_target_pairs={{0,2},{1,3},{2,0},{3,1},{4,6},{5,7},{6,4},{7,5},{8,10},{9,11},{10,... | collective-permute-start | bytes 1376264 | tf_op jit(solution)/shard_map/ppermute | solution.py:257
  69.5 1.5 copy-start.1
  79.4 22.7 %copy-start.16 = (bf16[384,256]{1,0:T(8,128)(2,1)}, bf16[384,256]{1,0:T(8,128)(2,1)S(1)}, u32[]{:S(2)}) copy-start(bf16[384,256]{1,0:T(8,128)(2,1)S(1)} %shard_map.99.refs_0_) | copy-start | bytes 589828
  79.4 18.3 %collective-permute-start.13 = (bf16[384,256]{1,0:T(8,128)(2,1)S(1)}, bf16[384,256]{1,0:T(8,128)(2,1)S(1)}, u32[]{:S(2)}, u32[]{:S(2)}) collective-permute-start(bf16[384,256]{1,0:T(8,128)(2,1)S(1)} %shard_map.99.refs_0_), channel_id=1, source_target_pairs={{0,1},{1,2},{2,3},{3,0},{4,5},{5,6},{6,7},{7,4},{8,9},{9,10},{10,1... | collective-permute-start | bytes 589832 | tf_op jit(solution)/shard_map/ppermute | solution.py:257
  80.6 21.5 %collective-permute-start.14 = (bf16[384,256]{1,0:T(8,128)(2,1)S(1)}, bf16[384,256]{1,0:T(8,128)(2,1)S(1)}, u32[]{:S(2)}, u32[]{:S(2)}) collective-permute-start(bf16[384,256]{1,0:T(8,128)(2,1)S(1)} %shard_map.99.refs_0_), channel_id=1, source_target_pairs={{0,3},{1,0},{2,1},{3,2},{4,7},{5,4},{6,5},{7,6},{8,11},{9,8},{10,9... | collective-permute-start | bytes 589832 | tf_op jit(solution)/shard_map/ppermute | solution.py:257
  82.7 19.4 %copy-start.18 = (bf16[256,896]{1,0:T(8,128)(2,1)}, bf16[256,896]{1,0:T(8,128)(2,1)S(1)}, u32[]{:S(2)}) copy-start(bf16[256,896]{1,0:T(8,128)(2,1)S(1)} %collective-permute-done.6.refs_5_) | copy-start | bytes 1376260
  82.7 19.4 %collective-permute-start.15 = (bf16[384,256]{1,0:T(8,128)(2,1)S(1)}, bf16[384,256]{1,0:T(8,128)(2,1)S(1)}, u32[]{:S(2)}, u32[]{:S(2)}) collective-permute-start(bf16[384,256]{1,0:T(8,128)(2,1)S(1)} %shard_map.99.refs_0_), channel_id=1, source_target_pairs={{0,2},{1,3},{2,0},{3,1},{4,6},{5,7},{6,4},{7,5},{8,10},{9,11},{10,... | collective-permute-start | bytes 589832 | tf_op jit(solution)/shard_map/ppermute | solution.py:257
  97.7 4.4 %copy-start.19 = (bf16[256,896]{1,0:T(8,128)(2,1)}, bf16[256,896]{1,0:T(8,128)(2,1)S(1)}, u32[]{:S(2)}) copy-start(bf16[256,896]{1,0:T(8,128)(2,1)S(1)} %collective-permute-done.7.refs_6_) | copy-start | bytes 1376260
  97.7 4.4 %copy-start.20 = (bf16[256,896]{1,0:T(8,128)(2,1)}, bf16[256,896]{1,0:T(8,128)(2,1)S(1)}, u32[]{:S(2)}) copy-start(bf16[256,896]{1,0:T(8,128)(2,1)S(1)} %collective-permute-done.8.refs_7_) | copy-start | bytes 1376260
  97.7 4.4 %copy-start.21 = (bf16[384,256]{1,0:T(8,128)(2,1)}, bf16[384,256]{1,0:T(8,128)(2,1)S(1)}, u32[]{:S(2)}) copy-start(bf16[384,256]{1,0:T(8,128)(2,1)S(1)} %collective-permute-done.13.refs_1_) | copy-start | bytes 589828
  102.1 0.7 copy-start.22
  102.1 0.8 copy-start.24
  106.2 50.4 %all-to-all-start.3 = ((bf16[64,2,2688]{2,1,0:T(2,128)(2,1)}), bf16[64,2,2688]{2,1,0:T(2,128)(2,1)S(1)}, u32[]{:S(2)}, u32[]{:S(2)}) async-start(bf16[64,2,2688]{2,1,0:T(2,128)(2,1)} %shard_map.100), calls=%async_computation.3 | async-start | bytes 1376256 | tf_op jit(solution)/shard_map/all_to_all | solution.py:252
  117.0 19.5 %collective-permute-start.1 = (bf16[64,2,2688]{2,1,0:T(2,128)(2,1)S(1)}, bf16[64,2,2688]{2,1,0:T(2,128)(2,1)S(1)}, u32[]{:S(2)}, u32[]{:S(2)}) collective-permute-start(bf16[64,2,2688]{2,1,0:T(2,128)(2,1)S(1)} %slice.12), channel_id=1, source_target_pairs={{0,1},{1,2},{2,3},{3,0},{4,5},{5,6},{6,7},{7,4},{8,9},{9,10},{10,1... | collective-permute-start | bytes 2064392 | tf_op jit(solution)/shard_map/ppermute | solution.py:257
  118.8 17.7 %collective-permute-start.2 = (bf16[64,2,2688]{2,1,0:T(2,128)(2,1)S(1)}, bf16[64,2,2688]{2,1,0:T(2,128)(2,1)S(1)}, u32[]{:S(2)}, u32[]{:S(2)}) collective-permute-start(bf16[64,2,2688]{2,1,0:T(2,128)(2,1)S(1)} %slice.12), channel_id=1, source_target_pairs={{0,3},{1,0},{2,1},{3,2},{4,7},{5,4},{6,5},{7,6},{8,11},{9,8},{10,9... | collective-permute-start | bytes 2064392 | tf_op jit(solution)/shard_map/ppermute | solution.py:257
  139.6 12.9 %copy-start.12 = (bf16[384,256]{1,0:T(8,128)(2,1)}, bf16[384,256]{1,0:T(8,128)(2,1)S(1)}, u32[]{:S(2)}) copy-start(bf16[384,256]{1,0:T(8,128)(2,1)S(1)} %shard_map.94.refs_0_) | copy-start | bytes 589828
  139.6 36.2 %copy-start.11 = (bf16[128,896]{1,0:T(8,128)(2,1)S(1)}, bf16[128,896]{1,0:T(8,128)(2,1)}, u32[]{:S(2)}) copy-start(bf16[128,896]{1,0:T(8,128)(2,1)} %copy-done.10) | copy-start | bytes 688132
  139.6 8.4 %collective-permute-start.3 = (bf16[384,256]{1,0:T(8,128)(2,1)S(1)}, bf16[384,256]{1,0:T(8,128)(2,1)S(1)}, u32[]{:S(2)}, u32[]{:S(2)}) collective-permute-start(bf16[384,256]{1,0:T(8,128)(2,1)S(1)} %shard_map.94.refs_0_), channel_id=1, source_target_pairs={{0,1},{1,2},{2,3},{3,0},{4,5},{5,6},{6,7},{7,4},{8,9},{9,10},{10,1... | collective-permute-start | bytes 589832 | tf_op jit(solution)/shard_map/ppermute | solution.py:257
  140.9 9.9 %collective-permute-start.4 = (bf16[384,256]{1,0:T(8,128)(2,1)S(1)}, bf16[384,256]{1,0:T(8,128)(2,1)S(1)}, u32[]{:S(2)}, u32[]{:S(2)}) collective-permute-start(bf16[384,256]{1,0:T(8,128)(2,1)S(1)} %shard_map.94.refs_0_), channel_id=1, source_target_pairs={{0,3},{1,0},{2,1},{3,2},{4,7},{5,4},{6,5},{7,6},{8,11},{9,8},{10,9... | collective-permute-start | bytes 589832 | tf_op jit(solution)/shard_map/ppermute | solution.py:257
  143.0 9.5 %collective-permute-start.5 = (bf16[384,256]{1,0:T(8,128)(2,1)S(1)}, bf16[384,256]{1,0:T(8,128)(2,1)S(1)}, u32[]{:S(2)}, u32[]{:S(2)}) collective-permute-start(bf16[384,256]{1,0:T(8,128)(2,1)S(1)} %shard_map.94.refs_0_), channel_id=1, source_target_pairs={{0,2},{1,3},{2,0},{3,1},{4,6},{5,7},{6,4},{7,5},{8,10},{9,11},{10,... | collective-permute-start | bytes 589832 | tf_op jit(solution)/shard_map/ppermute | solution.py:257
  148.0 4.5 %copy-start.23 = (bf16[384,256]{1,0:T(8,128)(2,1)}, bf16[384,256]{1,0:T(8,128)(2,1)S(1)}, u32[]{:S(2)}) copy-start(bf16[384,256]{1,0:T(8,128)(2,1)S(1)} %collective-permute-done.3.refs_1_) | copy-start | bytes 589828
  150.8 1.7 copy-start.25
  152.5 0.7 copy-start.26
  156.6 40.1 %all-to-all-start.1 = ((bf16[64,2,2688]{2,1,0:T(2,128)(2,1)}), bf16[64,2,2688]{2,1,0:T(2,128)(2,1)S(1)}, u32[]{:S(2)}, u32[]{:S(2)}) async-start(bf16[64,2,2688]{2,1,0:T(2,128)(2,1)} %shard_map.96), calls=%async_computation.1 | async-start | bytes 1376256 | tf_op jit(solution)/shard_map/all_to_all | solution.py:252
  166.9 8.9 %collective-permute-start.16 = (bf16[128,896]{1,0:T(8,128)(2,1)S(1)}, bf16[128,896]{1,0:T(8,128)(2,1)S(1)}, u32[]{:S(2)}, u32[]{:S(2)}) collective-permute-start(bf16[128,896]{1,0:T(8,128)(2,1)S(1)} %copy-done.5), channel_id=1, source_target_pairs={{0,1},{1,2},{2,3},{3,0},{4,5},{5,6},{6,7},{7,4},{8,9},{9,10},{10,1... | collective-permute-start | bytes 688136 | tf_op jit(solution)/shard_map/ppermute | solution.py:257
  168.1 7.7 %collective-permute-start.17 = (bf16[128,896]{1,0:T(8,128)(2,1)S(1)}, bf16[128,896]{1,0:T(8,128)(2,1)S(1)}, u32[]{:S(2)}, u32[]{:S(2)}) collective-permute-start(bf16[128,896]{1,0:T(8,128)(2,1)S(1)} %copy-done.5), channel_id=1, source_target_pairs={{0,3},{1,0},{2,1},{3,2},{4,7},{5,4},{6,5},{7,6},{8,11},{9,8},{10,9... | collective-permute-start | bytes 688136 | tf_op jit(solution)/shard_map/ppermute | solution.py:257
  175.8 1.5 copy-start.7
  177.3 1.5 copy-start.8
  178.8 1.5 copy-start.9
  180.3 6.6 %copy-start.17 = (bf16[128,4]{0,1:T(4,128)(2,1)S(1)}, bf16[128,4]{0,1:T(4,128)(2,1)}, u32[]{:S(2)}) copy-start(bf16[128,4]{0,1:T(4,128)(2,1)} %param.11) | copy-start | bytes 3076
  182.2 9.3 %collective-permute-start.18 = (bf16[128,896]{1,0:T(8,128)(2,1)}, bf16[128,896]{1,0:T(8,128)(2,1)S(1)}, u32[]{:S(2)}, u32[]{:S(2)}) collective-permute-start(bf16[128,896]{1,0:T(8,128)(2,1)} %get-tuple-element.26), channel_id=1, source_target_pairs={{0,1},{1,2},{2,3},{3,0},{4,5},{5,6},{6,7},{7,4},{8,9},{9,10},{10,1... | collective-permute-start | bytes 688136 | tf_op jit(solution)/shard_map/ppermute | solution.py:257
  183.0 11.7 %collective-permute-start.19 = (bf16[128,896]{1,0:T(8,128)(2,1)}, bf16[128,896]{1,0:T(8,128)(2,1)S(1)}, u32[]{:S(2)}, u32[]{:S(2)}) collective-permute-start(bf16[128,896]{1,0:T(8,128)(2,1)} %get-tuple-element.27), channel_id=1, source_target_pairs={{0,3},{1,0},{2,1},{3,2},{4,7},{5,4},{6,5},{7,6},{8,11},{9,8},{10,9... | collective-permute-start | bytes 688136 | tf_op jit(solution)/shard_map/ppermute | solution.py:257
  185.4 10.8 %collective-permute-start.20 = (bf16[128,896]{1,0:T(8,128)(2,1)S(1)}, bf16[128,896]{1,0:T(8,128)(2,1)S(1)}, u32[]{:S(2)}, u32[]{:S(2)}) collective-permute-start(bf16[128,896]{1,0:T(8,128)(2,1)S(1)} %get-tuple-element.28), channel_id=1, source_target_pairs={{0,2},{1,3},{2,0},{3,1},{4,6},{5,7},{6,4},{7,5},{8,10},{9,11},{10,... | collective-permute-start | bytes 688136 | tf_op jit(solution)/shard_map/ppermute | solution.py:257

commit v8 on v6

--- a/solution.py
+++ b/solution.py
@@ -36,16 +36,21 @@
     return (gate / (1.0 + jnp.exp(-gate)) * up).astype(BF16)
 
 
-def kernel_call(body, outs, *args, smem=0, vmem=12, flops=1):
-    places = [pltpu.SMEM] * smem + [pltpu.VMEM] * (len(args) - smem)
+def kernel_call(body, outs, *args, smem=0, hbm=0, scratch=(), to_hbm=False, vmem=12, flops=1):
+    places = [pltpu.SMEM] * smem + [pltpu.VMEM] * (len(args) - smem - hbm) + [pltpu.HBM] * hbm
+    last = len(args) - hbm
+    args = args[:last] + tuple(pltpu.with_memory_space_constraint(a, pltpu.HBM) for a in args[last:])
     return pl.pallas_call(
         body,
         in_specs=[pl.BlockSpec(memory_space=m) for m in places],
-        out_specs=[pl.BlockSpec(memory_space=pltpu.VMEM) for _ in outs],
+        out_specs=[pl.BlockSpec(memory_space=pltpu.HBM if to_hbm else pltpu.VMEM) for _ in outs],
         out_shape=[
-            o if isinstance(o, jax.ShapeDtypeStruct) else jax.ShapeDtypeStruct(o, BF16)
+            o
+            if isinstance(o, jax.ShapeDtypeStruct)
+            else (pltpu.HBM if to_hbm else jax.ShapeDtypeStruct)(o, BF16)
             for o in outs
         ],
+        scratch_shapes=scratch,
         compiler_params=pltpu.CompilerParams(vmem_limit_bytes=vmem << 20),
         cost_estimate=pl.CostEstimate(flops=flops, transcendentals=0, bytes_accessed=0),
     )(*args)
@@ -194,15 +199,53 @@
 
 def down_body(halves):
     def body(*refs):
-        *ins, down_ref, out_ref = refs
+        n = len(TURNS)
+        ins, parts, out_hbm = refs[:n], refs[n : 2 * n], refs[2 * n]
+        rows_ref, down_ref, out_ref, in_sems, out_sems = refs[2 * n + 1 :]
+        copies = []
+        for s in range(n):
+            pair = (
+                pltpu.make_async_copy(ins[s], rows_ref.at[s], in_sems.at[0, s]),
+                pltpu.make_async_copy(parts[s], down_ref.at[s], in_sems.at[1, s]),
+            )
+            for c in pair:
+                c.start()
+            copies.append(pair)
+        total = 0.0
+        for s in range(n):
+            for c in copies[s]:
+                c.wait()
+            total = total + dot(rows_ref[s], down_ref[s])
+        total = total.astype(BF16)
         count = out_ref.shape[0] // halves
-        rows = ins[0].shape[0] // halves
+        rows = total.shape[0] // halves
+        leaving = []
         for h in range(halves):
-            span = pl.ds(h * rows, rows)
-            total = sum(dot(a[span], down_ref[s]) for s, a in enumerate(ins))
-            unflat(out_ref.at[pl.ds(h * count, count)], total.astype(BF16))
+            span = pl.ds(h * count, count)
+            unflat(out_ref.at[span], total[h * rows : (h + 1) * rows])
+            c = pltpu.make_async_copy(out_ref.at[span], out_hbm.at[span], out_sems.at[h])
+            c.start()
+            leaving.append(c)
+        for c in leaving:
+            c.wait()
 
     return body
+
+
+def near_down_body(*refs):
+    *ins, down_ref, out_ref = refs
+    total = sum(dot(a[...], down_ref[s]) for s, a in enumerate(ins))
+    unflat(out_ref, total.astype(BF16))
+
+
+def halves_body(left_ref, right_ref, out0_ref, out1_ref):
+    half = out0_ref.shape[0]
+    out0_ref[...] = left_ref[pl.ds(0, half)]
+    out1_ref[...] = right_ref[pl.ds(half, half)]
+
+
+def own_body(rows_ref, out_ref):
+    out_ref[...] = rows_ref[:, :, : out_ref.shape[2]]
 
 
 def add_body(weight_ref, rows_ref, *refs):
@@ -233,8 +276,9 @@
     half = x.shape[0] // 2
     left = shift(x, "tensor", 1)
     right = shift(x, "tensor", -1)
-    o0 = shift(left[:half], "tensor", 1)
-    o1 = shift(right[half:], "tensor", -1)
+    h0, h1 = kernel_call(halves_body, [(half, *x.shape[1:])] * 2, left, right)
+    o0 = shift(h0, "tensor", 1)
+    o1 = shift(h1, "tensor", -1)
     return left, right, o0, o1
 
 
@@ -266,7 +310,7 @@
         )
         arrived.append(exchange(rows, EXPERT))
     columns = kernel_call(columns_body, [(quarter, narrow)] * n, q, w_down, smem=1)
-    (down,) = kernel_call(stack_body, [(n, quarter, narrow)], *deal(columns))
+    down = deal(columns)
     weights = kernel_call(
         weight_body(experts),
         [(tok_dev, experts * size) for size in CHUNKS],
@@ -294,7 +338,8 @@
             args = (rows, left, right)
             bodies = ring_sums_body, ring_hidden_body
         else:
-            own = rows[:, :, : size // PAIR * narrow]
+            own_shape = (experts, PAIR, size // PAIR * narrow)
+            (own,) = kernel_call(own_body, [own_shape], rows)
             last = shift(own, "tensor", 1), shift(own, "tensor", -1)
             args = (rows,)
             bodies = pair_sums_body, pair_hidden_body
@@ -309,13 +354,29 @@
             flops=10**9,
         )
         (hidden,) = kernel_call(bodies[1], [(count, quarter)], sums, *last, rest, flops=10**9)
-        (out,) = kernel_call(
-            down_body(2 - j),
-            [(experts, PAIR, size // PAIR * narrow)],
-            *spread(hidden),
-            down,
-            flops=10**9,
-        )
+        hidden_all = spread(hidden)
+        out_shape = (experts, PAIR, size // PAIR * narrow)
+        if j == 0:
+            scratch = [
+                pltpu.VMEM((n, count, quarter), BF16),
+                pltpu.VMEM((n, quarter, narrow), BF16),
+                pltpu.VMEM(out_shape, BF16),
+                pltpu.SemaphoreType.DMA((2, n)),
+                pltpu.SemaphoreType.DMA((2,)),
+            ]
+            (out,) = kernel_call(
+                down_body(2),
+                [out_shape],
+                *hidden_all,
+                *down,
+                hbm=2 * n,
+                scratch=scratch,
+                to_hbm=True,
+                flops=10**9,
+            )
+        else:
+            (stacked,) = kernel_call(stack_body, [(n, quarter, narrow)], *down)
+            (out,) = kernel_call(near_down_body, [out_shape], *hidden_all, stacked, flops=10**9)
         returned.append(exchange(out, EXPERT))
     shared_all = deal(shared_parts)
     total_shape = jax.ShapeDtypeStruct((tok_dev, narrow), F32)

time: 194 us -> 193 us (level)
  local copies, waits for them, and re-layouts: 16.9 us -> 11.9 us
  Pallas kernels: 16.4 us -> 20.2 us
    pallas_call x14 -> x16, Pallas kernels: 16.4 us -> 20.2 us  [kernel_call(): pl.pallas_call(body, in_specs=[pl.BlockSpec(memory_space=m) for m in plac...]
    slice x3 -> x0, local copies, waits for them, and re-layouts: 2.91 us -> none  [the longest x1 1.22 us: ring(): o1 = shift(right[half:], 'tensor', -1)]
    unnamed x42 -> x60, local copies, waits for them, and re-layouts: 14 us -> 11.9 us
  transfers between devices with their start and end apart: 25 -> 25, of which waited for: 14 -> 16; matrix products, arithmetic and copies ran while one was open for 2% -> 0% of each run, Pallas kernels for 7% -> 9%
where the time goes in v8:
time: 193 us; the launch traced here: 192 us
  starting transfers between devices  79.7 us (41%)
  waiting for transfers between devices  79.6 us (41%)
  Pallas kernels  20.2 us (10%)
  local copies, waits for them, and re-layouts  11.9 us (6%)
    ppermute x21, waiting for transfers between devices, shift(): return lax.ppermute(x, axis, [(i, (i + by) % n) for i in range(n)])  70.7 us
    ppermute x21, starting transfers between devices, shift(): return lax.ppermute(x, axis, [(i, (i + by) % n) for i in range(n)])  40.9 us
    all_to_all x4, starting transfers between devices, exchange(): return lax.all_to_all(x, axis, split_axis=0, concat_axis=0, tiled=True)  38.8 us
    pallas_call x16, Pallas kernels, kernel_call(): pl.pallas_call(body, in_specs=[pl.BlockSpec(memory_space=m) for m in plac...  20.2 us
    unnamed x60, local copies, waits for them, and re-layouts  11.9 us
    all_to_all x4, waiting for transfers between devices, exchange(): return lax.all_to_all(x, axis, split_axis=0, concat_axis=0, tiled=True)  8.84 us
  transfers between devices with their start and end apart: 25, of which 16 were waited for; matrix products, arithmetic and copies ran while one was open for 0% of the time, Pallas kernels for 9%

profile of v8, /device:TPU:32, one launch (start us, length us, event | category | flops | bytes accessed | tf_op | source)
XLA Modules:
  0.0 191.7 jit_solution(17225748043114633467)
XLA Ops:
  0.0 0.9 copy-done.5
  0.9 0.7 copy-done.22
  1.6 1.4 shard_map.99
  3.0 11.6 %all-to-all-start.2 = ((bf16[64,2,2688]{2,1,0:T(2,128)(2,1)}), bf16[64,2,2688]{2,1,0:T(2,128)(2,1)S(1)}, u32[]{:S(2)}, u32[]{:S(2)}) async-start(bf16[64,2,2688]{2,1,0:T(2,128)(2,1)} %shard_map.99), calls=%async_computation.2 | async-start | bytes 1376256 | tf_op jit(solution)/shard_map/all_to_all | solution.py:259
  14.6 3.3 %collective-permute-start = (bf16[128,896]{1,0:T(8,128)(2,1)S(1)}, bf16[128,896]{1,0:T(8,128)(2,1)S(1)}, u32[]{:S(2)}, u32[]{:S(2)}) collective-permute-start(bf16[128,896]{1,0:T(8,128)(2,1)S(1)} %copy-done.6), channel_id=1, source_target_pairs={{0,2},{1,3},{2,0},{3,1},{4,6},{5,7},{6,4},{7,5},{8,10},{9,11},{10,... | collective-permute-start | bytes 688136 | tf_op jit(solution)/shard_map/ppermute | solution.py:264
  17.9 5.9 %collective-permute-done.refs_1_.refs_3_ = bf16[128,896]{1,0:T(8,128)(2,1)S(1)} collective-permute-done((bf16[128,896]{1,0:T(8,128)(2,1)S(1)}, bf16[128,896]{1,0:T(8,128)(2,1)S(1)}, u32[]{:S(2)}, u32[]{:S(2)}) %collective-permute-start) | collective-permute-done | bytes 229408 | tf_op jit(solution)/shard_map/ppermute | solution.py:264
  23.8 1.8 shard_map.92
  25.7 0.7 copy-done.11
  26.4 8.8 %all-to-all-done.2.own_ref = bf16[64,2,2688]{2,1,0:T(2,128)(2,1)S(1)} async-done(((bf16[64,2,2688]{2,1,0:T(2,128)(2,1)}), bf16[64,2,2688]{2,1,0:T(2,128)(2,1)S(1)}, u32[]{:S(2)}, u32[]{:S(2)}) %all-to-all-start.2) | async-done | bytes 688160 | tf_op jit(solution)/shard_map/all_to_all | solution.py:259
  35.2 0.9 copy-done.3
  36.1 6.5 %all-to-all-start = ((bf16[64,2,5376]{2,1,0:T(2,128)(2,1)}), bf16[64,2,5376]{2,1,0:T(2,128)(2,1)S(1)}, u32[]{:S(2)}, u32[]{:S(2)}) async-start(bf16[64,2,5376]{2,1,0:T(2,128)(2,1)} %shard_map.92), calls=%async_computation | async-start | bytes 2752512 | tf_op jit(solution)/shard_map/all_to_all | solution.py:259
  42.5 1.7 collective-permute-start.9
  44.2 1.7 collective-permute-start.10
  45.9 1.6 copy-done.7
  47.6 0.8 copy-done.14
  48.3 0.4 collective-permute-start.6
  48.7 13.8 %collective-permute-done.9.left_ref = bf16[64,2,2688]{2,1,0:T(2,128)(2,1)} collective-permute-done((bf16[64,2,2688]{2,1,0:T(2,128)(2,1)}, bf16[64,2,2688]{2,1,0:T(2,128)(2,1)}, u32[]{:S(2)}, u32[]{:S(2)}) %collective-permute-start.9) | collective-permute-done | bytes 688160 | tf_op jit(solution)/shard_map/ppermute | solution.py:264
  62.5 1.4 shard_map.101
  63.8 0.9 collective-permute-start.11
  64.7 2.4 %collective-permute-start.12 = (bf16[32,2,2688]{2,1,0:T(2,128)(2,1)S(1)}, bf16[32,2,2688]{2,1,0:T(2,128)(2,1)S(1)}, u32[]{:S(2)}, u32[]{:S(2)}) collective-permute-start(bf16[32,2,2688]{2,1,0:T(2,128)(2,1)S(1)} %get-tuple-element.31), channel_id=1, source_target_pairs={{0,3},{1,0},{2,1},{3,2},{4,7},{5,4},{6,5},{7,6},{8,11},{9,8},{10,9... | collective-permute-start | bytes 1032200 | tf_op jit(solution)/shard_map/ppermute | solution.py:264
  67.1 1.0 collective-permute-start.7
  68.2 0.6 collective-permute-start.8
  68.8 1.5 copy-done.1
  70.3 2.8 %shard_map.100 = (f32[384,512]{1,0:T(8,128)S(1)}, bf16[2,896,256]{2,1,0:T(8,128)(2,1)S(1)}) custom-call(s32[1]{0:T(128)} %bitcast.q_ref, bf16[64,2,2688]{2,1,0:T(2,128)(2,1)S(1)} %copy-done.4, bf16[64,2,2688]{2,1,0:T(2,128)(2,1)} %collective-permute-done.9.left_ref, bf16[64,2,2688]{2,1,0:T(2,128)(2,1)} %collective-permute-done.10.right_ref, ...), custom_call_target="tpu_custom_call" | custom-call | flops 1000000000 | tf_op jit(solution)/shard_map/pallas_call | solution.py:43
  73.1 5.6 %collective-permute-done.11.o0_ref = bf16[32,2,2688]{2,1,0:T(2,128)(2,1)S(1)} collective-permute-done((bf16[32,2,2688]{2,1,0:T(2,128)(2,1)S(1)}, bf16[32,2,2688]{2,1,0:T(2,128)(2,1)S(1)}, u32[]{:S(2)}, u32[]{:S(2)}) %collective-permute-start.11) | collective-permute-done | bytes 344096 | tf_op jit(solution)/shard_map/ppermute | solution.py:264
  78.8 0.6 shard_map.102.refs_0_
  79.4 1.2 collective-permute-start.13
  80.7 2.1 %collective-permute-start.14 = (bf16[384,256]{1,0:T(8,128)(2,1)S(1)}, bf16[384,256]{1,0:T(8,128)(2,1)S(1)}, u32[]{:S(2)}, u32[]{:S(2)}) collective-permute-start(bf16[384,256]{1,0:T(8,128)(2,1)S(1)} %shard_map.102.refs_0_), channel_id=1, source_target_pairs={{0,3},{1,0},{2,1},{3,2},{4,7},{5,4},{6,5},{7,6},{8,11},{9,8},{10,9... | collective-permute-start | bytes 589832 | tf_op jit(solution)/shard_map/ppermute | solution.py:264
  82.7 9.8 %collective-permute-start.15 = (bf16[384,256]{1,0:T(8,128)(2,1)S(1)}, bf16[384,256]{1,0:T(8,128)(2,1)S(1)}, u32[]{:S(2)}, u32[]{:S(2)}) collective-permute-start(bf16[384,256]{1,0:T(8,128)(2,1)S(1)} %shard_map.102.refs_0_), channel_id=1, source_target_pairs={{0,2},{1,3},{2,0},{3,1},{4,6},{5,7},{6,4},{7,5},{8,10},{9,11},{10,... | collective-permute-start | bytes 589832 | tf_op jit(solution)/shard_map/ppermute | solution.py:264
  92.5 1.3 collective-permute-done.7.refs_2_.refs_6_
  93.9 2.2 %collective-permute-done.13.refs_1_ = bf16[384,256]{1,0:T(8,128)(2,1)S(1)} collective-permute-done((bf16[384,256]{1,0:T(8,128)(2,1)S(1)}, bf16[384,256]{1,0:T(8,128)(2,1)S(1)}, u32[]{:S(2)}, u32[]{:S(2)}) %collective-permute-start.13) | collective-permute-done | bytes 196640 | tf_op jit(solution)/shard_map/ppermute | solution.py:264
  96.1 4.9 %collective-permute-done.14.refs_2_ = bf16[384,256]{1,0:T(8,128)(2,1)S(1)} collective-permute-done((bf16[384,256]{1,0:T(8,128)(2,1)S(1)}, bf16[384,256]{1,0:T(8,128)(2,1)S(1)}, u32[]{:S(2)}, u32[]{:S(2)}) %collective-permute-start.14) | collective-permute-done | bytes 196640 | tf_op jit(solution)/shard_map/ppermute | solution.py:264
  101.1 0.6 copy-done.27
  101.8 3.3 %shard_map.103 = bf16[64,2,2688]{2,1,0:T(2,128)(2,1)} custom-call(bf16[384,256]{1,0:T(8,128)(2,1)} %copy-done.24, bf16[384,256]{1,0:T(8,128)(2,1)} %copy-done.26, bf16[384,256]{1,0:T(8,128)(2,1)} %copy-done.27, bf16[384,256]{1,0:T(8,128)(2,1)} %copy-done.28, bf16[256,896]{1,0:T(8,128)(2,1)} %copy-done.14, bf16[256,896]{1,0:T(8,128)(2,1)} %copy-done.16, ...), custom_call_target="tpu_custom_call" | custom-call | flops 1000000000 | tf_op jit(solution)/shard_map/pallas_call | solution.py:43
  105.1 10.5 %all-to-all-start.3 = ((bf16[64,2,2688]{2,1,0:T(2,128)(2,1)}), bf16[64,2,2688]{2,1,0:T(2,128)(2,1)}, u32[]{:S(2)}, u32[]{:S(2)}) async-start(bf16[64,2,2688]{2,1,0:T(2,128)(2,1)} %shard_map.103), calls=%async_computation.3 | async-start | bytes 1376256 | tf_op jit(solution)/shard_map/all_to_all | solution.py:259
  115.7 3.0 %collective-permute-start.1 = (bf16[64,2,2688]{2,1,0:T(2,128)(2,1)S(1)}, bf16[64,2,2688]{2,1,0:T(2,128)(2,1)S(1)}, u32[]{:S(2)}, u32[]{:S(2)}) collective-permute-start(bf16[64,2,2688]{2,1,0:T(2,128)(2,1)S(1)} %shard_map.94), channel_id=1, source_target_pairs={{0,1},{1,2},{2,3},{3,0},{4,5},{5,6},{6,7},{7,4},{8,9},{9,10},{10,1... | collective-permute-start | bytes 2064392 | tf_op jit(solution)/shard_map/ppermute | solution.py:264
  118.7 0.9 collective-permute-start.2
  119.5 1.1 shard_map.93
  120.7 14.5 %collective-permute-done.1.left_ref = bf16[64,2,2688]{2,1,0:T(2,128)(2,1)S(1)} collective-permute-done((bf16[64,2,2688]{2,1,0:T(2,128)(2,1)S(1)}, bf16[64,2,2688]{2,1,0:T(2,128)(2,1)S(1)}, u32[]{:S(2)}, u32[]{:S(2)}) %collective-permute-start.1) | collective-permute-done | bytes 688160 | tf_op jit(solution)/shard_map/ppermute | solution.py:264
  135.1 0.7 collective-permute-done.2.right_ref
  135.8 1.1 shard_map.95.refs_0_
  136.9 0.5 collective-permute-start.3
  137.4 2.8 %collective-permute-start.4 = (bf16[384,256]{1,0:T(8,128)(2,1)S(1)}, bf16[384,256]{1,0:T(8,128)(2,1)S(1)}, u32[]{:S(2)}, u32[]{:S(2)}) collective-permute-start(bf16[384,256]{1,0:T(8,128)(2,1)S(1)} %shard_map.95.refs_0_), channel_id=1, source_target_pairs={{0,3},{1,0},{2,1},{3,2},{4,7},{5,4},{6,5},{7,6},{8,11},{9,8},{10,9... | collective-permute-start | bytes 589832 | tf_op jit(solution)/shard_map/ppermute | solution.py:264
  140.2 1.0 collective-permute-start.5
  141.4 3.4 %collective-permute-done.3.refs_1_ = bf16[384,256]{1,0:T(8,128)(2,1)S(1)} collective-permute-done((bf16[384,256]{1,0:T(8,128)(2,1)S(1)}, bf16[384,256]{1,0:T(8,128)(2,1)S(1)}, u32[]{:S(2)}, u32[]{:S(2)}) %collective-permute-start.3) | collective-permute-done | bytes 196640 | tf_op jit(solution)/shard_map/ppermute | solution.py:264
  144.9 2.8 %collective-permute-done.4.refs_2_ = bf16[384,256]{1,0:T(8,128)(2,1)S(1)} collective-permute-done((bf16[384,256]{1,0:T(8,128)(2,1)S(1)}, bf16[384,256]{1,0:T(8,128)(2,1)S(1)}, u32[]{:S(2)}, u32[]{:S(2)}) %collective-permute-start.4) | collective-permute-done | bytes 196640 | tf_op jit(solution)/shard_map/ppermute | solution.py:264
  147.6 1.6 collective-permute-done.5.refs_3_
  149.2 1.0 shard_map.98
  150.2 0.9 copy-done.13
  151.0 10.2 %all-to-all-start.1 = ((bf16[64,2,2688]{2,1,0:T(2,128)(2,1)}), bf16[64,2,2688]{2,1,0:T(2,128)(2,1)S(1)}, u32[]{:S(2)}, u32[]{:S(2)}) async-start(bf16[64,2,2688]{2,1,0:T(2,128)(2,1)} %copy-done.13), calls=%async_computation.1 | async-start | bytes 1376256 | tf_op jit(solution)/shard_map/all_to_all | solution.py:259
  161.3 1.2 collective-permute-start.16
  162.5 2.1 %collective-permute-start.17 = (bf16[128,896]{1,0:T(8,128)(2,1)S(1)}, bf16[128,896]{1,0:T(8,128)(2,1)S(1)}, u32[]{:S(2)}, u32[]{:S(2)}) collective-permute-start(bf16[128,896]{1,0:T(8,128)(2,1)S(1)} %copy-done.6), channel_id=1, source_target_pairs={{0,3},{1,0},{2,1},{3,2},{4,7},{5,4},{6,5},{7,6},{8,11},{9,8},{10,9... | collective-permute-start | bytes 688136 | tf_op jit(solution)/shard_map/ppermute | solution.py:264
  164.6 5.6 %collective-permute-done.16.refs_1_ = bf16[128,896]{1,0:T(8,128)(2,1)S(1)} collective-permute-done((bf16[128,896]{1,0:T(8,128)(2,1)S(1)}, bf16[128,896]{1,0:T(8,128)(2,1)S(1)}, u32[]{:S(2)}, u32[]{:S(2)}) %collective-permute-start.16) | collective-permute-done | bytes 229408 | tf_op jit(solution)/shard_map/ppermute | solution.py:264
  170.2 1.5 copy-done.9
  171.7 1.5 copy-done.10
  173.2 1.8 shard_map.104
  175.3 3.0 %collective-permute-start.19 = (bf16[128,896]{1,0:T(8,128)(2,1)}, bf16[128,896]{1,0:T(8,128)(2,1)S(1)}, u32[]{:S(2)}, u32[]{:S(2)}) collective-permute-start(bf16[128,896]{1,0:T(8,128)(2,1)} %get-tuple-element.35), channel_id=1, source_target_pairs={{0,3},{1,0},{2,1},{3,2},{4,7},{5,4},{6,5},{7,6},{8,11},{9,8},{10,9... | collective-permute-start | bytes 688136 | tf_op jit(solution)/shard_map/ppermute | solution.py:264
  178.3 1.2 collective-permute-start.20
  179.7 0.9 shard_map.91
  180.6 3.7 %collective-permute-done.18.refs_1_ = bf16[128,896]{1,0:T(8,128)(2,1)S(1)} collective-permute-done((bf16[128,896]{1,0:T(8,128)(2,1)}, bf16[128,896]{1,0:T(8,128)(2,1)S(1)}, u32[]{:S(2)}, u32[]{:S(2)}) %collective-permute-start.18) | collective-permute-done | bytes 229408 | tf_op jit(solution)/shard_map/ppermute | solution.py:264
  184.3 3.2 %collective-permute-done.19.refs_2_ = bf16[128,896]{1,0:T(8,128)(2,1)S(1)} collective-permute-done((bf16[128,896]{1,0:T(8,128)(2,1)}, bf16[128,896]{1,0:T(8,128)(2,1)S(1)}, u32[]{:S(2)}, u32[]{:S(2)}) %collective-permute-start.19) | collective-permute-done | bytes 229408 | tf_op jit(solution)/shard_map/ppermute | solution.py:264
  187.5 1.5 collective-permute-done.20.refs_3_
  189.0 1.5 shard_map.105.refs_0_
  190.6 1.1 shard_map.106
  (62 shorter events, 1.1 us)
Async XLA Ops:
  0.0 0.9 copy-start.5
  0.9 0.7 copy-start.22
  1.6 13.0 %copy-start.6 = (bf16[128,896]{1,0:T(8,128)(2,1)S(1)}, bf16[128,896]{1,0:T(8,128)(2,1)}, u32[]{:S(2)}) copy-start(bf16[128,896]{1,0:T(8,128)(2,1)} %refs_0_.5) | copy-start | bytes 688132
  1.6 22.2 %copy-start.23 = (s32[128,4]{0,1:T(4,128)S(1)}, s32[128,4]{0,1:T(4,128)}, u32[]{:S(2)}) copy-start(s32[128,4]{0,1:T(4,128)} %param.10) | copy-start | bytes 6148
  3.0 32.2 %all-to-all-start.2 = ((bf16[64,2,2688]{2,1,0:T(2,128)(2,1)}), bf16[64,2,2688]{2,1,0:T(2,128)(2,1)S(1)}, u32[]{:S(2)}, u32[]{:S(2)}) async-start(bf16[64,2,2688]{2,1,0:T(2,128)(2,1)} %shard_map.99), calls=%async_computation.2 | async-start | bytes 1376256 | tf_op jit(solution)/shard_map/all_to_all | solution.py:259
  14.6 9.2 %collective-permute-start = (bf16[128,896]{1,0:T(8,128)(2,1)S(1)}, bf16[128,896]{1,0:T(8,128)(2,1)S(1)}, u32[]{:S(2)}, u32[]{:S(2)}) collective-permute-start(bf16[128,896]{1,0:T(8,128)(2,1)S(1)} %copy-done.6), channel_id=1, source_target_pairs={{0,2},{1,3},{2,0},{3,1},{4,6},{5,7},{6,4},{7,5},{8,10},{9,11},{10,... | collective-permute-start | bytes 688136 | tf_op jit(solution)/shard_map/ppermute | solution.py:264
  25.7 0.7 copy-start.11
  35.2 0.9 copy-start.3
  36.1 69.0 %all-to-all-start = ((bf16[64,2,5376]{2,1,0:T(2,128)(2,1)}), bf16[64,2,5376]{2,1,0:T(2,128)(2,1)S(1)}, u32[]{:S(2)}, u32[]{:S(2)}) async-start(bf16[64,2,5376]{2,1,0:T(2,128)(2,1)} %shard_map.92), calls=%async_computation | async-start | bytes 2752512 | tf_op jit(solution)/shard_map/all_to_all | solution.py:259
  42.5 26.3 %copy-start = (bf16[1,3584,256]{2,1,0:T(8,128)(2,1)S(1)}, bf16[1,3584,256]{2,1,0:T(8,128)(2,1)}, u32[]{:S(2)}) copy-start(bf16[1,3584,256]{2,1,0:T(8,128)(2,1)} %param.12) | copy-start | bytes 5505028
  42.5 19.9 %collective-permute-start.9 = (bf16[64,2,2688]{2,1,0:T(2,128)(2,1)}, bf16[64,2,2688]{2,1,0:T(2,128)(2,1)}, u32[]{:S(2)}, u32[]{:S(2)}) collective-permute-start(bf16[64,2,2688]{2,1,0:T(2,128)(2,1)} %copy-done.3), channel_id=1, source_target_pairs={{0,1},{1,2},{2,3},{3,0},{4,5},{5,6},{6,7},{7,4},{8,9},{9,10},{10,1... | collective-permute-start | bytes 2064392 | tf_op jit(solution)/shard_map/ppermute | solution.py:264
  44.2 18.3 %collective-permute-start.10 = (bf16[64,2,2688]{2,1,0:T(2,128)(2,1)}, bf16[64,2,2688]{2,1,0:T(2,128)(2,1)}, u32[]{:S(2)}, u32[]{:S(2)}) collective-permute-start(bf16[64,2,2688]{2,1,0:T(2,128)(2,1)} %copy-done.3), channel_id=1, source_target_pairs={{0,3},{1,0},{2,1},{3,2},{4,7},{5,4},{6,5},{7,6},{8,11},{9,8},{10,9... | collective-permute-start | bytes 2064392 | tf_op jit(solution)/shard_map/ppermute | solution.py:264
  45.9 22.9 %copy-start.4 = (bf16[64,2,2688]{2,1,0:T(2,128)(2,1)S(1)}, bf16[64,2,2688]{2,1,0:T(2,128)(2,1)}, u32[]{:S(2)}) copy-start(bf16[64,2,2688]{2,1,0:T(2,128)(2,1)} %copy-done.3) | copy-start | bytes 2064388
  45.9 1.6 copy-start.7
  47.6 0.8 copy-start.14
  48.3 34.4 %collective-permute-start.6 = (bf16[256,896]{1,0:T(8,128)(2,1)S(1)}, bf16[256,896]{1,0:T(8,128)(2,1)S(1)}, u32[]{:S(2)}, u32[]{:S(2)}) collective-permute-start(bf16[256,896]{1,0:T(8,128)(2,1)S(1)} %get-tuple-element.25), channel_id=1, source_target_pairs={{0,1},{1,2},{2,3},{3,0},{4,5},{5,6},{6,7},{7,4},{8,9},{9,10},{10,1... | collective-permute-start | bytes 1376264 | tf_op jit(solution)/shard_map/ppermute | solution.py:264
  63.8 14.9 %collective-permute-start.11 = (bf16[32,2,2688]{2,1,0:T(2,128)(2,1)S(1)}, bf16[32,2,2688]{2,1,0:T(2,128)(2,1)S(1)}, u32[]{:S(2)}, u32[]{:S(2)}) collective-permute-start(bf16[32,2,2688]{2,1,0:T(2,128)(2,1)S(1)} %get-tuple-element.30), channel_id=1, source_target_pairs={{0,1},{1,2},{2,3},{3,0},{4,5},{5,6},{6,7},{7,4},{8,9},{9,10},{10,1... | collective-permute-start | bytes 1032200 | tf_op jit(solution)/shard_map/ppermute | solution.py:264
  64.7 14.1 %collective-permute-start.12 = (bf16[32,2,2688]{2,1,0:T(2,128)(2,1)S(1)}, bf16[32,2,2688]{2,1,0:T(2,128)(2,1)S(1)}, u32[]{:S(2)}, u32[]{:S(2)}) collective-permute-start(bf16[32,2,2688]{2,1,0:T(2,128)(2,1)S(1)} %get-tuple-element.31), channel_id=1, source_target_pairs={{0,3},{1,0},{2,1},{3,2},{4,7},{5,4},{6,5},{7,6},{8,11},{9,8},{10,9... | collective-permute-start | bytes 1032200 | tf_op jit(solution)/shard_map/ppermute | solution.py:264
  67.1 26.7 %collective-permute-start.7 = (bf16[256,896]{1,0:T(8,128)(2,1)S(1)}, bf16[256,896]{1,0:T(8,128)(2,1)S(1)}, u32[]{:S(2)}, u32[]{:S(2)}) collective-permute-start(bf16[256,896]{1,0:T(8,128)(2,1)S(1)} %get-tuple-element.26), channel_id=1, source_target_pairs={{0,3},{1,0},{2,1},{3,2},{4,7},{5,4},{6,5},{7,6},{8,11},{9,8},{10,9... | collective-permute-start | bytes 1376264 | tf_op jit(solution)/shard_map/ppermute | solution.py:264
  68.2 25.7 %collective-permute-start.8 = (bf16[256,896]{1,0:T(8,128)(2,1)S(1)}, bf16[256,896]{1,0:T(8,128)(2,1)S(1)}, u32[]{:S(2)}, u32[]{:S(2)}) collective-permute-start(bf16[256,896]{1,0:T(8,128)(2,1)S(1)} %get-tuple-element.27), channel_id=1, source_target_pairs={{0,2},{1,3},{2,0},{3,1},{4,6},{5,7},{6,4},{7,5},{8,10},{9,11},{10,... | collective-permute-start | bytes 1376264 | tf_op jit(solution)/shard_map/ppermute | solution.py:264
  68.8 1.5 copy-start.1
  79.4 21.6 %copy-start.24 = (bf16[384,256]{1,0:T(8,128)(2,1)}, bf16[384,256]{1,0:T(8,128)(2,1)S(1)}, u32[]{:S(2)}) copy-start(bf16[384,256]{1,0:T(8,128)(2,1)S(1)} %shard_map.102.refs_0_) | copy-start | bytes 589828
  79.4 16.7 %collective-permute-start.13 = (bf16[384,256]{1,0:T(8,128)(2,1)S(1)}, bf16[384,256]{1,0:T(8,128)(2,1)S(1)}, u32[]{:S(2)}, u32[]{:S(2)}) collective-permute-start(bf16[384,256]{1,0:T(8,128)(2,1)S(1)} %shard_map.102.refs_0_), channel_id=1, source_target_pairs={{0,1},{1,2},{2,3},{3,0},{4,5},{5,6},{6,7},{7,4},{8,9},{9,10},{10,1... | collective-permute-start | bytes 589832 | tf_op jit(solution)/shard_map/ppermute | solution.py:264
  80.7 20.3 %collective-permute-start.14 = (bf16[384,256]{1,0:T(8,128)(2,1)S(1)}, bf16[384,256]{1,0:T(8,128)(2,1)S(1)}, u32[]{:S(2)}, u32[]{:S(2)}) collective-permute-start(bf16[384,256]{1,0:T(8,128)(2,1)S(1)} %shard_map.102.refs_0_), channel_id=1, source_target_pairs={{0,3},{1,0},{2,1},{3,2},{4,7},{5,4},{6,5},{7,6},{8,11},{9,8},{10,9... | collective-permute-start | bytes 589832 | tf_op jit(solution)/shard_map/ppermute | solution.py:264
  82.7 18.3 %copy-start.16 = (bf16[256,896]{1,0:T(8,128)(2,1)}, bf16[256,896]{1,0:T(8,128)(2,1)S(1)}, u32[]{:S(2)}) copy-start(bf16[256,896]{1,0:T(8,128)(2,1)S(1)} %collective-permute-done.6.refs_1_.refs_5_) | copy-start | bytes 1376260
  82.7 18.3 %collective-permute-start.15 = (bf16[384,256]{1,0:T(8,128)(2,1)S(1)}, bf16[384,256]{1,0:T(8,128)(2,1)S(1)}, u32[]{:S(2)}, u32[]{:S(2)}) collective-permute-start(bf16[384,256]{1,0:T(8,128)(2,1)S(1)} %shard_map.102.refs_0_), channel_id=1, source_target_pairs={{0,2},{1,3},{2,0},{3,1},{4,6},{5,7},{6,4},{7,5},{8,10},{9,11},{10,... | collective-permute-start | bytes 589832 | tf_op jit(solution)/shard_map/ppermute | solution.py:264
  93.9 7.2 %copy-start.18 = (bf16[256,896]{1,0:T(8,128)(2,1)}, bf16[256,896]{1,0:T(8,128)(2,1)S(1)}, u32[]{:S(2)}) copy-start(bf16[256,896]{1,0:T(8,128)(2,1)S(1)} %collective-permute-done.7.refs_2_.refs_6_) | copy-start | bytes 1376260
  93.9 7.2 %copy-start.20 = (bf16[256,896]{1,0:T(8,128)(2,1)}, bf16[256,896]{1,0:T(8,128)(2,1)S(1)}, u32[]{:S(2)}) copy-start(bf16[256,896]{1,0:T(8,128)(2,1)S(1)} %collective-permute-done.8.refs_3_.refs_7_) | copy-start | bytes 1376260
  96.1 5.0 %copy-start.26 = (bf16[384,256]{1,0:T(8,128)(2,1)}, bf16[384,256]{1,0:T(8,128)(2,1)S(1)}, u32[]{:S(2)}) copy-start(bf16[384,256]{1,0:T(8,128)(2,1)S(1)} %collective-permute-done.13.refs_1_) | copy-start | bytes 589828
  101.0 0.7 copy-start.27
  101.0 0.7 copy-start.28
  105.1 46.0 %all-to-all-start.3 = ((bf16[64,2,2688]{2,1,0:T(2,128)(2,1)}), bf16[64,2,2688]{2,1,0:T(2,128)(2,1)}, u32[]{:S(2)}, u32[]{:S(2)}) async-start(bf16[64,2,2688]{2,1,0:T(2,128)(2,1)} %shard_map.103), calls=%async_computation.3 | async-start | bytes 1376256 | tf_op jit(solution)/shard_map/all_to_all | solution.py:259
  115.6 3.9 %copy-start.2 = (bf16[1,3584,256]{2,1,0:T(8,128)(2,1)S(1)}, bf16[1,3584,256]{2,1,0:T(8,128)(2,1)}, u32[]{:S(2)}) copy-start(bf16[1,3584,256]{2,1,0:T(8,128)(2,1)} %param.13) | copy-start | bytes 5505028
  115.7 19.5 %collective-permute-start.1 = (bf16[64,2,2688]{2,1,0:T(2,128)(2,1)S(1)}, bf16[64,2,2688]{2,1,0:T(2,128)(2,1)S(1)}, u32[]{:S(2)}, u32[]{:S(2)}) collective-permute-start(bf16[64,2,2688]{2,1,0:T(2,128)(2,1)S(1)} %shard_map.94), channel_id=1, source_target_pairs={{0,1},{1,2},{2,3},{3,0},{4,5},{5,6},{6,7},{7,4},{8,9},{9,10},{10,1... | collective-permute-start | bytes 2064392 | tf_op jit(solution)/shard_map/ppermute | solution.py:264
  118.7 17.2 %collective-permute-start.2 = (bf16[64,2,2688]{2,1,0:T(2,128)(2,1)S(1)}, bf16[64,2,2688]{2,1,0:T(2,128)(2,1)S(1)}, u32[]{:S(2)}, u32[]{:S(2)}) collective-permute-start(bf16[64,2,2688]{2,1,0:T(2,128)(2,1)S(1)} %shard_map.94), channel_id=1, source_target_pairs={{0,3},{1,0},{2,1},{3,2},{4,7},{5,4},{6,5},{7,6},{8,11},{9,8},{10,9... | collective-permute-start | bytes 2064392 | tf_op jit(solution)/shard_map/ppermute | solution.py:264
  135.8 5.4 %copy-start.15 = (bf16[256,896]{1,0:T(8,128)(2,1)S(1)}, bf16[256,896]{1,0:T(8,128)(2,1)}, u32[]{:S(2)}) copy-start(bf16[256,896]{1,0:T(8,128)(2,1)} %copy-done.14) | copy-start | bytes 1376260
  135.8 5.4 %copy-start.17 = (bf16[256,896]{1,0:T(8,128)(2,1)S(1)}, bf16[256,896]{1,0:T(8,128)(2,1)}, u32[]{:S(2)}) copy-start(bf16[256,896]{1,0:T(8,128)(2,1)} %copy-done.16) | copy-start | bytes 1376260
  135.8 5.4 %copy-start.19 = (bf16[256,896]{1,0:T(8,128)(2,1)S(1)}, bf16[256,896]{1,0:T(8,128)(2,1)}, u32[]{:S(2)}) copy-start(bf16[256,896]{1,0:T(8,128)(2,1)} %copy-done.18) | copy-start | bytes 1376260
  135.8 5.4 %copy-start.21 = (bf16[256,896]{1,0:T(8,128)(2,1)S(1)}, bf16[256,896]{1,0:T(8,128)(2,1)}, u32[]{:S(2)}) copy-start(bf16[256,896]{1,0:T(8,128)(2,1)} %copy-done.20) | copy-start | bytes 1376260
  136.9 7.9 %collective-permute-start.3 = (bf16[384,256]{1,0:T(8,128)(2,1)S(1)}, bf16[384,256]{1,0:T(8,128)(2,1)S(1)}, u32[]{:S(2)}, u32[]{:S(2)}) collective-permute-start(bf16[384,256]{1,0:T(8,128)(2,1)S(1)} %shard_map.95.refs_0_), channel_id=1, source_target_pairs={{0,1},{1,2},{2,3},{3,0},{4,5},{5,6},{6,7},{7,4},{8,9},{9,10},{10,1... | collective-permute-start | bytes 589832 | tf_op jit(solution)/shard_map/ppermute | solution.py:264
  137.4 10.2 %collective-permute-start.4 = (bf16[384,256]{1,0:T(8,128)(2,1)S(1)}, bf16[384,256]{1,0:T(8,128)(2,1)S(1)}, u32[]{:S(2)}, u32[]{:S(2)}) collective-permute-start(bf16[384,256]{1,0:T(8,128)(2,1)S(1)} %shard_map.95.refs_0_), channel_id=1, source_target_pairs={{0,3},{1,0},{2,1},{3,2},{4,7},{5,4},{6,5},{7,6},{8,11},{9,8},{10,9... | collective-permute-start | bytes 589832 | tf_op jit(solution)/shard_map/ppermute | solution.py:264
  140.2 8.9 %collective-permute-start.5 = (bf16[384,256]{1,0:T(8,128)(2,1)S(1)}, bf16[384,256]{1,0:T(8,128)(2,1)S(1)}, u32[]{:S(2)}, u32[]{:S(2)}) collective-permute-start(bf16[384,256]{1,0:T(8,128)(2,1)S(1)} %shard_map.95.refs_0_), channel_id=1, source_target_pairs={{0,2},{1,3},{2,0},{3,1},{4,6},{5,7},{6,4},{7,5},{8,10},{9,11},{10,... | collective-permute-start | bytes 589832 | tf_op jit(solution)/shard_map/ppermute | solution.py:264
  141.4 28.8 %copy-start.8 = (bf16[3584,256]{1,0:T(8,128)(2,1)S(1)}, bf16[3584,256]{1,0:T(8,128)(2,1)}, u32[]{:S(2)}) copy-start(bf16[3584,256]{1,0:T(8,128)(2,1)} %param.15) | copy-start | bytes 5505028
  141.4 28.8 %copy-start.12 = (bf16[128,896]{1,0:T(8,128)(2,1)S(1)}, bf16[128,896]{1,0:T(8,128)(2,1)}, u32[]{:S(2)}) copy-start(bf16[128,896]{1,0:T(8,128)(2,1)} %copy-done.11) | copy-start | bytes 688132
  150.2 0.9 copy-start.13
  151.0 39.5 %all-to-all-start.1 = ((bf16[64,2,2688]{2,1,0:T(2,128)(2,1)}), bf16[64,2,2688]{2,1,0:T(2,128)(2,1)S(1)}, u32[]{:S(2)}, u32[]{:S(2)}) async-start(bf16[64,2,2688]{2,1,0:T(2,128)(2,1)} %copy-done.13), calls=%async_computation.1 | async-start | bytes 1376256 | tf_op jit(solution)/shard_map/all_to_all | solution.py:259
  161.3 8.9 %collective-permute-start.16 = (bf16[128,896]{1,0:T(8,128)(2,1)S(1)}, bf16[128,896]{1,0:T(8,128)(2,1)S(1)}, u32[]{:S(2)}, u32[]{:S(2)}) collective-permute-start(bf16[128,896]{1,0:T(8,128)(2,1)S(1)} %copy-done.6), channel_id=1, source_target_pairs={{0,1},{1,2},{2,3},{3,0},{4,5},{5,6},{6,7},{7,4},{8,9},{9,10},{10,1... | collective-permute-start | bytes 688136 | tf_op jit(solution)/shard_map/ppermute | solution.py:264
  162.5 7.7 %collective-permute-start.17 = (bf16[128,896]{1,0:T(8,128)(2,1)S(1)}, bf16[128,896]{1,0:T(8,128)(2,1)S(1)}, u32[]{:S(2)}, u32[]{:S(2)}) collective-permute-start(bf16[128,896]{1,0:T(8,128)(2,1)S(1)} %copy-done.6), channel_id=1, source_target_pairs={{0,3},{1,0},{2,1},{3,2},{4,7},{5,4},{6,5},{7,6},{8,11},{9,8},{10,9... | collective-permute-start | bytes 688136 | tf_op jit(solution)/shard_map/ppermute | solution.py:264
  170.2 1.5 copy-start.9
  171.7 1.5 copy-start.10
  173.2 6.4 %copy-start.25 = (bf16[128,4]{0,1:T(4,128)(2,1)S(1)}, bf16[128,4]{0,1:T(4,128)(2,1)}, u32[]{:S(2)}) copy-start(bf16[128,4]{0,1:T(4,128)(2,1)} %param.11) | copy-start | bytes 3076
  175.0 9.3 %collective-permute-start.18 = (bf16[128,896]{1,0:T(8,128)(2,1)}, bf16[128,896]{1,0:T(8,128)(2,1)S(1)}, u32[]{:S(2)}, u32[]{:S(2)}) collective-permute-start(bf16[128,896]{1,0:T(8,128)(2,1)} %get-tuple-element.34), channel_id=1, source_target_pairs={{0,1},{1,2},{2,3},{3,0},{4,5},{5,6},{6,7},{7,4},{8,9},{9,10},{10,1... | collective-permute-start | bytes 688136 | tf_op jit(solution)/shard_map/ppermute | solution.py:264
  175.3 12.2 %collective-permute-start.19 = (bf16[128,896]{1,0:T(8,128)(2,1)}, bf16[128,896]{1,0:T(8,128)(2,1)S(1)}, u32[]{:S(2)}, u32[]{:S(2)}) collective-permute-start(bf16[128,896]{1,0:T(8,128)(2,1)} %get-tuple-element.35), channel_id=1, source_target_pairs={{0,3},{1,0},{2,1},{3,2},{4,7},{5,4},{6,5},{7,6},{8,11},{9,8},{10,9... | collective-permute-start | bytes 688136 | tf_op jit(solution)/shard_map/ppermute | solution.py:264
  178.3 10.8 %collective-permute-start.20 = (bf16[128,896]{1,0:T(8,128)(2,1)S(1)}, bf16[128,896]{1,0:T(8,128)(2,1)S(1)}, u32[]{:S(2)}, u32[]{:S(2)}) collective-permute-start(bf16[128,896]{1,0:T(8,128)(2,1)S(1)} %get-tuple-element.36), channel_id=1, source_target_pairs={{0,2},{1,3},{2,0},{3,1},{4,6},{5,7},{6,4},{7,5},{8,10},{9,11},{10,... | collective-permute-start | bytes 688136 | tf_op jit(solution)/shard_map/ppermute | solution.py:264

commit v9 on v8

--- a/solution.py
+++ b/solution.py
@@ -67,9 +67,24 @@
 
 
 def gather_body(experts, first, size):
+    def fetching(ids_hbm, tokens_hbm, out_ref, ids_ref, tokens_ref, sems):
+        pairs = ((ids_hbm, ids_ref), (tokens_hbm, tokens_ref))
+        copies = [pltpu.make_async_copy(a, b, sems.at[i]) for i, (a, b) in enumerate(pairs)]
+        for c in copies:
+            c.start()
+        copies[0].wait()
+        picks = choose(ids_ref[...])
+        copies[1].wait()
+        unflat(out_ref, dot(picks, tokens_ref[...]).astype(BF16))
+
     def body(ids_ref, *refs):
         *tokens_refs, out_ref = refs
-        ids = ids_ref[...]
+        picks = choose(ids_ref[...])
+        for s, tokens_ref in enumerate(tokens_refs):
+            x = dot(picks, tokens_ref[...]).astype(BF16)
+            unflat(out_ref, x, lane=s * (size // PAIR) * x.shape[1])
+
+    def choose(ids):
         top, rows = ids.shape
         numbers = lax.broadcasted_iota(jnp.int32, (experts, rows), 0)
         onehot = [jnp.where(ids[k : k + 1] == numbers, 1.0, 0.0) for k in range(top)]
@@ -91,12 +106,9 @@
                 target = jnp.where(inside, ids[k : k + 1] * PAIR + local, -1)
                 pick = jnp.where(target == place, 1.0, pick)
             picks.append(pick.astype(BF16))
-        picks = jnp.concatenate(picks, axis=0)
-        for s, tokens_ref in enumerate(tokens_refs):
-            x = dot(picks, tokens_ref[...]).astype(BF16)
-            unflat(out_ref, x, lane=s * (size // PAIR) * x.shape[1])
-
-    return body
+        return jnp.concatenate(picks, axis=0)
+
+    return body if first else fetching
 
 
 def weight_body(experts):
@@ -302,11 +314,17 @@
     ids_t = expert_ids.T
     arrived = []
     for j, (size, sources) in enumerate(zip(CHUNKS, ([tokens], [tokens, tokens_all[3]]))):
+        scratch = [
+            pltpu.VMEM(ids_t.shape, jnp.int32),
+            pltpu.VMEM(tokens.shape, BF16),
+            pltpu.SemaphoreType.DMA((2,)),
+        ]
         (rows,) = kernel_call(
             gather_body(experts, sum(CHUNKS[:j]), size),
             [(experts, PAIR, len(sources) * size // PAIR * narrow)],
             ids_t,
             *sources,
+            **({} if j else dict(hbm=2, scratch=scratch)),
         )
         arrived.append(exchange(rows, EXPERT))
     columns = kernel_call(columns_body, [(quarter, narrow)] * n, q, w_down, smem=1)

time: 193 us -> 192 us (level)
    unnamed x60 -> x56, local copies, waits for them, and re-layouts: 11.9 us -> 10.2 us
where the time goes in v9:
time: 192 us; the launch traced here: 191 us
  starting transfers between devices  79.7 us (42%)
  waiting for transfers between devices  79.5 us (41%)
  Pallas kernels  21.1 us (11%)
  local copies, waits for them, and re-layouts  10.2 us (5%)
    ppermute x21, waiting for transfers between devices, shift(): return lax.ppermute(x, axis, [(i, (i + by) % n) for i in range(n)])  70.7 us
    ppermute x21, starting transfers between devices, shift(): return lax.ppermute(x, axis, [(i, (i + by) % n) for i in range(n)])  40.9 us
    all_to_all x4, starting transfers between devices, exchange(): return lax.all_to_all(x, axis, split_axis=0, concat_axis=0, tiled=True)  38.8 us
    pallas_call x16, Pallas kernels, kernel_call(): pl.pallas_call(body, in_specs=[pl.BlockSpec(memory_space=m) for m in plac...  21.1 us
    unnamed x56, local copies, waits for them, and re-layouts  10.2 us
    all_to_all x4, waiting for transfers between devices, exchange(): return lax.all_to_all(x, axis, split_axis=0, concat_axis=0, tiled=True)  8.82 us
  transfers between devices with their start and end apart: 25, of which 16 were waited for; matrix products, arithmetic and copies ran while one was open for 0% of the time, Pallas kernels for 9%

profile of v9, /device:TPU:32, one launch (start us, length us, event | category | flops | bytes accessed | tf_op | source)
XLA Modules:
  0.0 190.9 jit_solution(2711237203569175630)
XLA Ops:
  0.0 2.3 %shard_map.99 = bf16[64,2,2688]{2,1,0:T(2,128)(2,1)} custom-call(s32[4,128]{1,0:T(4,128)} %bitcast.14, bf16[128,896]{1,0:T(8,128)(2,1)} %refs_0_.3), custom_call_target="tpu_custom_call" | custom-call | flops 1 | tf_op jit(solution)/shard_map/pallas_call | solution.py:43
  2.3 11.6 %all-to-all-start.2 = ((bf16[64,2,2688]{2,1,0:T(2,128)(2,1)}), bf16[64,2,2688]{2,1,0:T(2,128)(2,1)S(1)}, u32[]{:S(2)}, u32[]{:S(2)}) async-start(bf16[64,2,2688]{2,1,0:T(2,128)(2,1)} %shard_map.99), calls=%async_computation.2 | async-start | bytes 1376256 | tf_op jit(solution)/shard_map/all_to_all | solution.py:271
  13.9 3.3 %collective-permute-start = (bf16[128,896]{1,0:T(8,128)(2,1)S(1)}, bf16[128,896]{1,0:T(8,128)(2,1)S(1)}, u32[]{:S(2)}, u32[]{:S(2)}) collective-permute-start(bf16[128,896]{1,0:T(8,128)(2,1)S(1)} %copy-done.5), channel_id=1, source_target_pairs={{0,2},{1,3},{2,0},{3,1},{4,6},{5,7},{6,4},{7,5},{8,10},{9,11},{10,... | collective-permute-start | bytes 688136 | tf_op jit(solution)/shard_map/ppermute | solution.py:276
  17.2 5.9 %collective-permute-done.refs_1_.refs_3_ = bf16[128,896]{1,0:T(8,128)(2,1)S(1)} collective-permute-done((bf16[128,896]{1,0:T(8,128)(2,1)S(1)}, bf16[128,896]{1,0:T(8,128)(2,1)S(1)}, u32[]{:S(2)}, u32[]{:S(2)}) %collective-permute-start) | collective-permute-done | bytes 229408 | tf_op jit(solution)/shard_map/ppermute | solution.py:276
  23.1 1.9 shard_map.92
  25.0 0.7 copy-done.10
  25.7 8.8 %all-to-all-done.2.own_ref = bf16[64,2,2688]{2,1,0:T(2,128)(2,1)S(1)} async-done(((bf16[64,2,2688]{2,1,0:T(2,128)(2,1)}), bf16[64,2,2688]{2,1,0:T(2,128)(2,1)S(1)}, u32[]{:S(2)}, u32[]{:S(2)}) %all-to-all-start.2) | async-done | bytes 688160 | tf_op jit(solution)/shard_map/all_to_all | solution.py:271
  34.5 0.8 copy-done.3
  35.3 6.5 %all-to-all-start = ((bf16[64,2,5376]{2,1,0:T(2,128)(2,1)}), bf16[64,2,5376]{2,1,0:T(2,128)(2,1)S(1)}, u32[]{:S(2)}, u32[]{:S(2)}) async-start(bf16[64,2,5376]{2,1,0:T(2,128)(2,1)} %shard_map.92), calls=%async_computation | async-start | bytes 2752512 | tf_op jit(solution)/shard_map/all_to_all | solution.py:271
  41.8 1.7 collective-permute-start.9
  43.5 1.7 collective-permute-start.10
  45.1 1.6 copy-done.6
  46.8 0.8 copy-done.13
  47.6 0.4 collective-permute-start.6
  48.0 13.7 %collective-permute-done.9.left_ref = bf16[64,2,2688]{2,1,0:T(2,128)(2,1)} collective-permute-done((bf16[64,2,2688]{2,1,0:T(2,128)(2,1)}, bf16[64,2,2688]{2,1,0:T(2,128)(2,1)}, u32[]{:S(2)}, u32[]{:S(2)}) %collective-permute-start.9) | collective-permute-done | bytes 688160 | tf_op jit(solution)/shard_map/ppermute | solution.py:276
  61.7 1.4 shard_map.101
  63.1 0.9 collective-permute-start.11
  64.0 2.4 %collective-permute-start.12 = (bf16[32,2,2688]{2,1,0:T(2,128)(2,1)S(1)}, bf16[32,2,2688]{2,1,0:T(2,128)(2,1)S(1)}, u32[]{:S(2)}, u32[]{:S(2)}) collective-permute-start(bf16[32,2,2688]{2,1,0:T(2,128)(2,1)S(1)} %get-tuple-element.31), channel_id=1, source_target_pairs={{0,3},{1,0},{2,1},{3,2},{4,7},{5,4},{6,5},{7,6},{8,11},{9,8},{10,9... | collective-permute-start | bytes 1032200 | tf_op jit(solution)/shard_map/ppermute | solution.py:276
  66.4 1.0 collective-permute-start.7
  67.4 0.6 collective-permute-start.8
  68.1 1.5 copy-done.1
  69.6 2.8 %shard_map.100 = (f32[384,512]{1,0:T(8,128)S(1)}, bf16[2,896,256]{2,1,0:T(8,128)(2,1)S(1)}) custom-call(s32[1]{0:T(128)} %bitcast.q_ref, bf16[64,2,2688]{2,1,0:T(2,128)(2,1)S(1)} %copy-done.4, bf16[64,2,2688]{2,1,0:T(2,128)(2,1)} %collective-permute-done.9.left_ref, bf16[64,2,2688]{2,1,0:T(2,128)(2,1)} %collective-permute-done.10.right_ref, ...), custom_call_target="tpu_custom_call" | custom-call | flops 1000000000 | tf_op jit(solution)/shard_map/pallas_call | solution.py:43
  72.4 5.6 %collective-permute-done.11.o0_ref = bf16[32,2,2688]{2,1,0:T(2,128)(2,1)S(1)} collective-permute-done((bf16[32,2,2688]{2,1,0:T(2,128)(2,1)S(1)}, bf16[32,2,2688]{2,1,0:T(2,128)(2,1)S(1)}, u32[]{:S(2)}, u32[]{:S(2)}) %collective-permute-start.11) | collective-permute-done | bytes 344096 | tf_op jit(solution)/shard_map/ppermute | solution.py:276
  78.0 0.6 shard_map.102.refs_0_
  78.7 1.2 collective-permute-start.13
  79.9 2.1 %collective-permute-start.14 = (bf16[384,256]{1,0:T(8,128)(2,1)S(1)}, bf16[384,256]{1,0:T(8,128)(2,1)S(1)}, u32[]{:S(2)}, u32[]{:S(2)}) collective-permute-start(bf16[384,256]{1,0:T(8,128)(2,1)S(1)} %shard_map.102.refs_0_), channel_id=1, source_target_pairs={{0,3},{1,0},{2,1},{3,2},{4,7},{5,4},{6,5},{7,6},{8,11},{9,8},{10,9... | collective-permute-start | bytes 589832 | tf_op jit(solution)/shard_map/ppermute | solution.py:276
  82.0 9.8 %collective-permute-start.15 = (bf16[384,256]{1,0:T(8,128)(2,1)S(1)}, bf16[384,256]{1,0:T(8,128)(2,1)S(1)}, u32[]{:S(2)}, u32[]{:S(2)}) collective-permute-start(bf16[384,256]{1,0:T(8,128)(2,1)S(1)} %shard_map.102.refs_0_), channel_id=1, source_target_pairs={{0,2},{1,3},{2,0},{3,1},{4,6},{5,7},{6,4},{7,5},{8,10},{9,11},{10,... | collective-permute-start | bytes 589832 | tf_op jit(solution)/shard_map/ppermute | solution.py:276
  91.8 1.3 collective-permute-done.7.refs_2_.refs_6_
  93.1 2.2 %collective-permute-done.13.refs_1_ = bf16[384,256]{1,0:T(8,128)(2,1)S(1)} collective-permute-done((bf16[384,256]{1,0:T(8,128)(2,1)S(1)}, bf16[384,256]{1,0:T(8,128)(2,1)S(1)}, u32[]{:S(2)}, u32[]{:S(2)}) %collective-permute-start.13) | collective-permute-done | bytes 196640 | tf_op jit(solution)/shard_map/ppermute | solution.py:276
  95.4 4.9 %collective-permute-done.14.refs_2_ = bf16[384,256]{1,0:T(8,128)(2,1)S(1)} collective-permute-done((bf16[384,256]{1,0:T(8,128)(2,1)S(1)}, bf16[384,256]{1,0:T(8,128)(2,1)S(1)}, u32[]{:S(2)}, u32[]{:S(2)}) %collective-permute-start.14) | collective-permute-done | bytes 196640 | tf_op jit(solution)/shard_map/ppermute | solution.py:276
  100.3 0.6 copy-done.25
  101.0 3.3 %shard_map.103 = bf16[64,2,2688]{2,1,0:T(2,128)(2,1)} custom-call(bf16[384,256]{1,0:T(8,128)(2,1)} %copy-done.22, bf16[384,256]{1,0:T(8,128)(2,1)} %copy-done.24, bf16[384,256]{1,0:T(8,128)(2,1)} %copy-done.25, bf16[384,256]{1,0:T(8,128)(2,1)} %copy-done.26, bf16[256,896]{1,0:T(8,128)(2,1)} %copy-done.13, bf16[256,896]{1,0:T(8,128)(2,1)} %copy-done.15, ...), custom_call_target="tpu_custom_call" | custom-call | flops 1000000000 | tf_op jit(solution)/shard_map/pallas_call | solution.py:43
  104.3 10.5 %all-to-all-start.3 = ((bf16[64,2,2688]{2,1,0:T(2,128)(2,1)}), bf16[64,2,2688]{2,1,0:T(2,128)(2,1)}, u32[]{:S(2)}, u32[]{:S(2)}) async-start(bf16[64,2,2688]{2,1,0:T(2,128)(2,1)} %shard_map.103), calls=%async_computation.3 | async-start | bytes 1376256 | tf_op jit(solution)/shard_map/all_to_all | solution.py:271
  114.9 3.0 %collective-permute-start.1 = (bf16[64,2,2688]{2,1,0:T(2,128)(2,1)S(1)}, bf16[64,2,2688]{2,1,0:T(2,128)(2,1)S(1)}, u32[]{:S(2)}, u32[]{:S(2)}) collective-permute-start(bf16[64,2,2688]{2,1,0:T(2,128)(2,1)S(1)} %shard_map.94), channel_id=1, source_target_pairs={{0,1},{1,2},{2,3},{3,0},{4,5},{5,6},{6,7},{7,4},{8,9},{9,10},{10,1... | collective-permute-start | bytes 2064392 | tf_op jit(solution)/shard_map/ppermute | solution.py:276
  117.9 0.9 collective-permute-start.2
  118.8 1.1 shard_map.93
  119.9 14.5 %collective-permute-done.1.left_ref = bf16[64,2,2688]{2,1,0:T(2,128)(2,1)S(1)} collective-permute-done((bf16[64,2,2688]{2,1,0:T(2,128)(2,1)S(1)}, bf16[64,2,2688]{2,1,0:T(2,128)(2,1)S(1)}, u32[]{:S(2)}, u32[]{:S(2)}) %collective-permute-start.1) | collective-permute-done | bytes 688160 | tf_op jit(solution)/shard_map/ppermute | solution.py:276
  134.4 0.7 collective-permute-done.2.right_ref
  135.1 1.1 shard_map.95.refs_0_
  136.2 0.5 collective-permute-start.3
  136.7 2.8 %collective-permute-start.4 = (bf16[384,256]{1,0:T(8,128)(2,1)S(1)}, bf16[384,256]{1,0:T(8,128)(2,1)S(1)}, u32[]{:S(2)}, u32[]{:S(2)}) collective-permute-start(bf16[384,256]{1,0:T(8,128)(2,1)S(1)} %shard_map.95.refs_0_), channel_id=1, source_target_pairs={{0,3},{1,0},{2,1},{3,2},{4,7},{5,4},{6,5},{7,6},{8,11},{9,8},{10,9... | collective-permute-start | bytes 589832 | tf_op jit(solution)/shard_map/ppermute | solution.py:276
  139.5 1.0 collective-permute-start.5
  140.5 0.1 shard_map.97.refs_4_
  140.7 3.4 %collective-permute-done.3.refs_1_ = bf16[384,256]{1,0:T(8,128)(2,1)S(1)} collective-permute-done((bf16[384,256]{1,0:T(8,128)(2,1)S(1)}, bf16[384,256]{1,0:T(8,128)(2,1)S(1)}, u32[]{:S(2)}, u32[]{:S(2)}) %collective-permute-start.3) | collective-permute-done | bytes 196640 | tf_op jit(solution)/shard_map/ppermute | solution.py:276
  144.1 2.8 %collective-permute-done.4.refs_2_ = bf16[384,256]{1,0:T(8,128)(2,1)S(1)} collective-permute-done((bf16[384,256]{1,0:T(8,128)(2,1)S(1)}, bf16[384,256]{1,0:T(8,128)(2,1)S(1)}, u32[]{:S(2)}, u32[]{:S(2)}) %collective-permute-start.4) | collective-permute-done | bytes 196640 | tf_op jit(solution)/shard_map/ppermute | solution.py:276
  146.9 1.6 collective-permute-done.5.refs_3_
  148.4 1.0 shard_map.98
  149.4 0.9 copy-done.12
  150.3 10.2 %all-to-all-start.1 = ((bf16[64,2,2688]{2,1,0:T(2,128)(2,1)}), bf16[64,2,2688]{2,1,0:T(2,128)(2,1)S(1)}, u32[]{:S(2)}, u32[]{:S(2)}) async-start(bf16[64,2,2688]{2,1,0:T(2,128)(2,1)} %copy-done.12), calls=%async_computation.1 | async-start | bytes 1376256 | tf_op jit(solution)/shard_map/all_to_all | solution.py:271
  160.5 1.2 collective-permute-start.16
  161.7 2.1 %collective-permute-start.17 = (bf16[128,896]{1,0:T(8,128)(2,1)S(1)}, bf16[128,896]{1,0:T(8,128)(2,1)S(1)}, u32[]{:S(2)}, u32[]{:S(2)}) collective-permute-start(bf16[128,896]{1,0:T(8,128)(2,1)S(1)} %copy-done.5), channel_id=1, source_target_pairs={{0,3},{1,0},{2,1},{3,2},{4,7},{5,4},{6,5},{7,6},{8,11},{9,8},{10,9... | collective-permute-start | bytes 688136 | tf_op jit(solution)/shard_map/ppermute | solution.py:276
  163.8 5.6 %collective-permute-done.16.refs_1_ = bf16[128,896]{1,0:T(8,128)(2,1)S(1)} collective-permute-done((bf16[128,896]{1,0:T(8,128)(2,1)S(1)}, bf16[128,896]{1,0:T(8,128)(2,1)S(1)}, u32[]{:S(2)}, u32[]{:S(2)}) %collective-permute-start.16) | collective-permute-done | bytes 229408 | tf_op jit(solution)/shard_map/ppermute | solution.py:276
  169.5 1.5 copy-done.8
  171.0 1.5 copy-done.9
  172.5 1.8 shard_map.104
  174.3 0.3 collective-permute-start.18
  174.6 2.9 %collective-permute-start.19 = (bf16[128,896]{1,0:T(8,128)(2,1)}, bf16[128,896]{1,0:T(8,128)(2,1)S(1)}, u32[]{:S(2)}, u32[]{:S(2)}) collective-permute-start(bf16[128,896]{1,0:T(8,128)(2,1)} %get-tuple-element.35), channel_id=1, source_target_pairs={{0,3},{1,0},{2,1},{3,2},{4,7},{5,4},{6,5},{7,6},{8,11},{9,8},{10,9... | collective-permute-start | bytes 688136 | tf_op jit(solution)/shard_map/ppermute | solution.py:276
  177.5 1.2 collective-permute-start.20
  178.9 0.9 shard_map.91
  179.9 3.7 %collective-permute-done.18.refs_1_ = bf16[128,896]{1,0:T(8,128)(2,1)S(1)} collective-permute-done((bf16[128,896]{1,0:T(8,128)(2,1)}, bf16[128,896]{1,0:T(8,128)(2,1)S(1)}, u32[]{:S(2)}, u32[]{:S(2)}) %collective-permute-start.18) | collective-permute-done | bytes 229408 | tf_op jit(solution)/shard_map/ppermute | solution.py:276
  183.6 3.2 %collective-permute-done.19.refs_2_ = bf16[128,896]{1,0:T(8,128)(2,1)S(1)} collective-permute-done((bf16[128,896]{1,0:T(8,128)(2,1)}, bf16[128,896]{1,0:T(8,128)(2,1)S(1)}, u32[]{:S(2)}, u32[]{:S(2)}) %collective-permute-start.19) | collective-permute-done | bytes 229408 | tf_op jit(solution)/shard_map/ppermute | solution.py:276
  186.8 1.5 collective-permute-done.20.refs_3_
  188.3 1.5 shard_map.105.refs_0_
  189.8 1.1 shard_map.106
  (58 shorter events, 0.6 us)
Async XLA Ops:
  0.0 23.1 %copy-start.21 = (s32[128,4]{0,1:T(4,128)S(1)}, s32[128,4]{0,1:T(4,128)}, u32[]{:S(2)}) copy-start(s32[128,4]{0,1:T(4,128)} %param.10) | copy-start | bytes 6148
  0.0 13.9 %copy-start.5 = (bf16[128,896]{1,0:T(8,128)(2,1)S(1)}, bf16[128,896]{1,0:T(8,128)(2,1)}, u32[]{:S(2)}) copy-start(bf16[128,896]{1,0:T(8,128)(2,1)} %refs_0_.3) | copy-start | bytes 688132
  2.3 32.2 %all-to-all-start.2 = ((bf16[64,2,2688]{2,1,0:T(2,128)(2,1)}), bf16[64,2,2688]{2,1,0:T(2,128)(2,1)S(1)}, u32[]{:S(2)}, u32[]{:S(2)}) async-start(bf16[64,2,2688]{2,1,0:T(2,128)(2,1)} %shard_map.99), calls=%async_computation.2 | async-start | bytes 1376256 | tf_op jit(solution)/shard_map/all_to_all | solution.py:271
  13.9 9.2 %collective-permute-start = (bf16[128,896]{1,0:T(8,128)(2,1)S(1)}, bf16[128,896]{1,0:T(8,128)(2,1)S(1)}, u32[]{:S(2)}, u32[]{:S(2)}) collective-permute-start(bf16[128,896]{1,0:T(8,128)(2,1)S(1)} %copy-done.5), channel_id=1, source_target_pairs={{0,2},{1,3},{2,0},{3,1},{4,6},{5,7},{6,4},{7,5},{8,10},{9,11},{10,... | collective-permute-start | bytes 688136 | tf_op jit(solution)/shard_map/ppermute | solution.py:276
  25.0 0.7 copy-start.10
  34.5 0.9 copy-start.3
  35.3 69.0 %all-to-all-start = ((bf16[64,2,5376]{2,1,0:T(2,128)(2,1)}), bf16[64,2,5376]{2,1,0:T(2,128)(2,1)S(1)}, u32[]{:S(2)}, u32[]{:S(2)}) async-start(bf16[64,2,5376]{2,1,0:T(2,128)(2,1)} %shard_map.92), calls=%async_computation | async-start | bytes 2752512 | tf_op jit(solution)/shard_map/all_to_all | solution.py:271
  41.8 26.3 %copy-start = (bf16[1,3584,256]{2,1,0:T(8,128)(2,1)S(1)}, bf16[1,3584,256]{2,1,0:T(8,128)(2,1)}, u32[]{:S(2)}) copy-start(bf16[1,3584,256]{2,1,0:T(8,128)(2,1)} %param.12) | copy-start | bytes 5505028
  41.8 19.9 %collective-permute-start.9 = (bf16[64,2,2688]{2,1,0:T(2,128)(2,1)}, bf16[64,2,2688]{2,1,0:T(2,128)(2,1)}, u32[]{:S(2)}, u32[]{:S(2)}) collective-permute-start(bf16[64,2,2688]{2,1,0:T(2,128)(2,1)} %copy-done.3), channel_id=1, source_target_pairs={{0,1},{1,2},{2,3},{3,0},{4,5},{5,6},{6,7},{7,4},{8,9},{9,10},{10,1... | collective-permute-start | bytes 2064392 | tf_op jit(solution)/shard_map/ppermute | solution.py:276
  43.5 18.3 %collective-permute-start.10 = (bf16[64,2,2688]{2,1,0:T(2,128)(2,1)}, bf16[64,2,2688]{2,1,0:T(2,128)(2,1)}, u32[]{:S(2)}, u32[]{:S(2)}) collective-permute-start(bf16[64,2,2688]{2,1,0:T(2,128)(2,1)} %copy-done.3), channel_id=1, source_target_pairs={{0,3},{1,0},{2,1},{3,2},{4,7},{5,4},{6,5},{7,6},{8,11},{9,8},{10,9... | collective-permute-start | bytes 2064392 | tf_op jit(solution)/shard_map/ppermute | solution.py:276
  45.1 22.9 %copy-start.4 = (bf16[64,2,2688]{2,1,0:T(2,128)(2,1)S(1)}, bf16[64,2,2688]{2,1,0:T(2,128)(2,1)}, u32[]{:S(2)}) copy-start(bf16[64,2,2688]{2,1,0:T(2,128)(2,1)} %copy-done.3) | copy-start | bytes 2064388
  45.1 1.6 copy-start.6
  46.8 0.8 copy-start.13
  47.6 34.4 %collective-permute-start.6 = (bf16[256,896]{1,0:T(8,128)(2,1)S(1)}, bf16[256,896]{1,0:T(8,128)(2,1)S(1)}, u32[]{:S(2)}, u32[]{:S(2)}) collective-permute-start(bf16[256,896]{1,0:T(8,128)(2,1)S(1)} %get-tuple-element.25), channel_id=1, source_target_pairs={{0,1},{1,2},{2,3},{3,0},{4,5},{5,6},{6,7},{7,4},{8,9},{9,10},{10,1... | collective-permute-start | bytes 1376264 | tf_op jit(solution)/shard_map/ppermute | solution.py:276
  63.1 14.9 %collective-permute-start.11 = (bf16[32,2,2688]{2,1,0:T(2,128)(2,1)S(1)}, bf16[32,2,2688]{2,1,0:T(2,128)(2,1)S(1)}, u32[]{:S(2)}, u32[]{:S(2)}) collective-permute-start(bf16[32,2,2688]{2,1,0:T(2,128)(2,1)S(1)} %get-tuple-element.30), channel_id=1, source_target_pairs={{0,1},{1,2},{2,3},{3,0},{4,5},{5,6},{6,7},{7,4},{8,9},{9,10},{10,1... | collective-permute-start | bytes 1032200 | tf_op jit(solution)/shard_map/ppermute | solution.py:276
  64.0 14.1 %collective-permute-start.12 = (bf16[32,2,2688]{2,1,0:T(2,128)(2,1)S(1)}, bf16[32,2,2688]{2,1,0:T(2,128)(2,1)S(1)}, u32[]{:S(2)}, u32[]{:S(2)}) collective-permute-start(bf16[32,2,2688]{2,1,0:T(2,128)(2,1)S(1)} %get-tuple-element.31), channel_id=1, source_target_pairs={{0,3},{1,0},{2,1},{3,2},{4,7},{5,4},{6,5},{7,6},{8,11},{9,8},{10,9... | collective-permute-start | bytes 1032200 | tf_op jit(solution)/shard_map/ppermute | solution.py:276
  66.4 26.7 %collective-permute-start.7 = (bf16[256,896]{1,0:T(8,128)(2,1)S(1)}, bf16[256,896]{1,0:T(8,128)(2,1)S(1)}, u32[]{:S(2)}, u32[]{:S(2)}) collective-permute-start(bf16[256,896]{1,0:T(8,128)(2,1)S(1)} %get-tuple-element.26), channel_id=1, source_target_pairs={{0,3},{1,0},{2,1},{3,2},{4,7},{5,4},{6,5},{7,6},{8,11},{9,8},{10,9... | collective-permute-start | bytes 1376264 | tf_op jit(solution)/shard_map/ppermute | solution.py:276
  67.4 25.7 %collective-permute-start.8 = (bf16[256,896]{1,0:T(8,128)(2,1)S(1)}, bf16[256,896]{1,0:T(8,128)(2,1)S(1)}, u32[]{:S(2)}, u32[]{:S(2)}) collective-permute-start(bf16[256,896]{1,0:T(8,128)(2,1)S(1)} %get-tuple-element.27), channel_id=1, source_target_pairs={{0,2},{1,3},{2,0},{3,1},{4,6},{5,7},{6,4},{7,5},{8,10},{9,11},{10,... | collective-permute-start | bytes 1376264 | tf_op jit(solution)/shard_map/ppermute | solution.py:276
  68.1 1.5 copy-start.1
  78.7 21.6 %copy-start.22 = (bf16[384,256]{1,0:T(8,128)(2,1)}, bf16[384,256]{1,0:T(8,128)(2,1)S(1)}, u32[]{:S(2)}) copy-start(bf16[384,256]{1,0:T(8,128)(2,1)S(1)} %shard_map.102.refs_0_) | copy-start | bytes 589828
  78.7 16.7 %collective-permute-start.13 = (bf16[384,256]{1,0:T(8,128)(2,1)S(1)}, bf16[384,256]{1,0:T(8,128)(2,1)S(1)}, u32[]{:S(2)}, u32[]{:S(2)}) collective-permute-start(bf16[384,256]{1,0:T(8,128)(2,1)S(1)} %shard_map.102.refs_0_), channel_id=1, source_target_pairs={{0,1},{1,2},{2,3},{3,0},{4,5},{5,6},{6,7},{7,4},{8,9},{9,10},{10,1... | collective-permute-start | bytes 589832 | tf_op jit(solution)/shard_map/ppermute | solution.py:276
  79.9 20.3 %collective-permute-start.14 = (bf16[384,256]{1,0:T(8,128)(2,1)S(1)}, bf16[384,256]{1,0:T(8,128)(2,1)S(1)}, u32[]{:S(2)}, u32[]{:S(2)}) collective-permute-start(bf16[384,256]{1,0:T(8,128)(2,1)S(1)} %shard_map.102.refs_0_), channel_id=1, source_target_pairs={{0,3},{1,0},{2,1},{3,2},{4,7},{5,4},{6,5},{7,6},{8,11},{9,8},{10,9... | collective-permute-start | bytes 589832 | tf_op jit(solution)/shard_map/ppermute | solution.py:276
  82.0 18.3 %copy-start.15 = (bf16[256,896]{1,0:T(8,128)(2,1)}, bf16[256,896]{1,0:T(8,128)(2,1)S(1)}, u32[]{:S(2)}) copy-start(bf16[256,896]{1,0:T(8,128)(2,1)S(1)} %collective-permute-done.6.refs_1_.refs_5_) | copy-start | bytes 1376260
  82.0 18.3 %collective-permute-start.15 = (bf16[384,256]{1,0:T(8,128)(2,1)S(1)}, bf16[384,256]{1,0:T(8,128)(2,1)S(1)}, u32[]{:S(2)}, u32[]{:S(2)}) collective-permute-start(bf16[384,256]{1,0:T(8,128)(2,1)S(1)} %shard_map.102.refs_0_), channel_id=1, source_target_pairs={{0,2},{1,3},{2,0},{3,1},{4,6},{5,7},{6,4},{7,5},{8,10},{9,11},{10,... | collective-permute-start | bytes 589832 | tf_op jit(solution)/shard_map/ppermute | solution.py:276
  93.1 7.2 %copy-start.17 = (bf16[256,896]{1,0:T(8,128)(2,1)}, bf16[256,896]{1,0:T(8,128)(2,1)S(1)}, u32[]{:S(2)}) copy-start(bf16[256,896]{1,0:T(8,128)(2,1)S(1)} %collective-permute-done.7.refs_2_.refs_6_) | copy-start | bytes 1376260
  93.1 7.2 %copy-start.19 = (bf16[256,896]{1,0:T(8,128)(2,1)}, bf16[256,896]{1,0:T(8,128)(2,1)S(1)}, u32[]{:S(2)}) copy-start(bf16[256,896]{1,0:T(8,128)(2,1)S(1)} %collective-permute-done.8.refs_3_.refs_7_) | copy-start | bytes 1376260
  95.4 5.0 %copy-start.24 = (bf16[384,256]{1,0:T(8,128)(2,1)}, bf16[384,256]{1,0:T(8,128)(2,1)S(1)}, u32[]{:S(2)}) copy-start(bf16[384,256]{1,0:T(8,128)(2,1)S(1)} %collective-permute-done.13.refs_1_) | copy-start | bytes 589828
  100.3 0.7 copy-start.25
  100.3 0.7 copy-start.26
  104.3 45.9 %all-to-all-start.3 = ((bf16[64,2,2688]{2,1,0:T(2,128)(2,1)}), bf16[64,2,2688]{2,1,0:T(2,128)(2,1)}, u32[]{:S(2)}, u32[]{:S(2)}) async-start(bf16[64,2,2688]{2,1,0:T(2,128)(2,1)} %shard_map.103), calls=%async_computation.3 | async-start | bytes 1376256 | tf_op jit(solution)/shard_map/all_to_all | solution.py:271
  114.9 3.9 %copy-start.2 = (bf16[1,3584,256]{2,1,0:T(8,128)(2,1)S(1)}, bf16[1,3584,256]{2,1,0:T(8,128)(2,1)}, u32[]{:S(2)}) copy-start(bf16[1,3584,256]{2,1,0:T(8,128)(2,1)} %param.13) | copy-start | bytes 5505028
  114.9 19.5 %collective-permute-start.1 = (bf16[64,2,2688]{2,1,0:T(2,128)(2,1)S(1)}, bf16[64,2,2688]{2,1,0:T(2,128)(2,1)S(1)}, u32[]{:S(2)}, u32[]{:S(2)}) collective-permute-start(bf16[64,2,2688]{2,1,0:T(2,128)(2,1)S(1)} %shard_map.94), channel_id=1, source_target_pairs={{0,1},{1,2},{2,3},{3,0},{4,5},{5,6},{6,7},{7,4},{8,9},{9,10},{10,1... | collective-permute-start | bytes 2064392 | tf_op jit(solution)/shard_map/ppermute | solution.py:276
  117.9 17.2 %collective-permute-start.2 = (bf16[64,2,2688]{2,1,0:T(2,128)(2,1)S(1)}, bf16[64,2,2688]{2,1,0:T(2,128)(2,1)S(1)}, u32[]{:S(2)}, u32[]{:S(2)}) collective-permute-start(bf16[64,2,2688]{2,1,0:T(2,128)(2,1)S(1)} %shard_map.94), channel_id=1, source_target_pairs={{0,3},{1,0},{2,1},{3,2},{4,7},{5,4},{6,5},{7,6},{8,11},{9,8},{10,9... | collective-permute-start | bytes 2064392 | tf_op jit(solution)/shard_map/ppermute | solution.py:276
  135.1 5.4 %copy-start.14 = (bf16[256,896]{1,0:T(8,128)(2,1)S(1)}, bf16[256,896]{1,0:T(8,128)(2,1)}, u32[]{:S(2)}) copy-start(bf16[256,896]{1,0:T(8,128)(2,1)} %copy-done.13) | copy-start | bytes 1376260
  135.1 5.4 %copy-start.16 = (bf16[256,896]{1,0:T(8,128)(2,1)S(1)}, bf16[256,896]{1,0:T(8,128)(2,1)}, u32[]{:S(2)}) copy-start(bf16[256,896]{1,0:T(8,128)(2,1)} %copy-done.15) | copy-start | bytes 1376260
  135.1 5.4 %copy-start.18 = (bf16[256,896]{1,0:T(8,128)(2,1)S(1)}, bf16[256,896]{1,0:T(8,128)(2,1)}, u32[]{:S(2)}) copy-start(bf16[256,896]{1,0:T(8,128)(2,1)} %copy-done.17) | copy-start | bytes 1376260
  135.1 5.4 %copy-start.20 = (bf16[256,896]{1,0:T(8,128)(2,1)S(1)}, bf16[256,896]{1,0:T(8,128)(2,1)}, u32[]{:S(2)}) copy-start(bf16[256,896]{1,0:T(8,128)(2,1)} %copy-done.19) | copy-start | bytes 1376260
  136.2 7.9 %collective-permute-start.3 = (bf16[384,256]{1,0:T(8,128)(2,1)S(1)}, bf16[384,256]{1,0:T(8,128)(2,1)S(1)}, u32[]{:S(2)}, u32[]{:S(2)}) collective-permute-start(bf16[384,256]{1,0:T(8,128)(2,1)S(1)} %shard_map.95.refs_0_), channel_id=1, source_target_pairs={{0,1},{1,2},{2,3},{3,0},{4,5},{5,6},{6,7},{7,4},{8,9},{9,10},{10,1... | collective-permute-start | bytes 589832 | tf_op jit(solution)/shard_map/ppermute | solution.py:276
  136.7 10.2 %collective-permute-start.4 = (bf16[384,256]{1,0:T(8,128)(2,1)S(1)}, bf16[384,256]{1,0:T(8,128)(2,1)S(1)}, u32[]{:S(2)}, u32[]{:S(2)}) collective-permute-start(bf16[384,256]{1,0:T(8,128)(2,1)S(1)} %shard_map.95.refs_0_), channel_id=1, source_target_pairs={{0,3},{1,0},{2,1},{3,2},{4,7},{5,4},{6,5},{7,6},{8,11},{9,8},{10,9... | collective-permute-start | bytes 589832 | tf_op jit(solution)/shard_map/ppermute | solution.py:276
  139.5 8.9 %collective-permute-start.5 = (bf16[384,256]{1,0:T(8,128)(2,1)S(1)}, bf16[384,256]{1,0:T(8,128)(2,1)S(1)}, u32[]{:S(2)}, u32[]{:S(2)}) collective-permute-start(bf16[384,256]{1,0:T(8,128)(2,1)S(1)} %shard_map.95.refs_0_), channel_id=1, source_target_pairs={{0,2},{1,3},{2,0},{3,1},{4,6},{5,7},{6,4},{7,5},{8,10},{9,11},{10,... | collective-permute-start | bytes 589832 | tf_op jit(solution)/shard_map/ppermute | solution.py:276
  140.7 28.8 %copy-start.7 = (bf16[3584,256]{1,0:T(8,128)(2,1)S(1)}, bf16[3584,256]{1,0:T(8,128)(2,1)}, u32[]{:S(2)}) copy-start(bf16[3584,256]{1,0:T(8,128)(2,1)} %param.15) | copy-start | bytes 5505028
  140.7 28.8 %copy-start.11 = (bf16[128,896]{1,0:T(8,128)(2,1)S(1)}, bf16[128,896]{1,0:T(8,128)(2,1)}, u32[]{:S(2)}) copy-start(bf16[128,896]{1,0:T(8,128)(2,1)} %copy-done.10) | copy-start | bytes 688132
  149.4 0.9 copy-start.12
  150.3 39.5 %all-to-all-start.1 = ((bf16[64,2,2688]{2,1,0:T(2,128)(2,1)}), bf16[64,2,2688]{2,1,0:T(2,128)(2,1)S(1)}, u32[]{:S(2)}, u32[]{:S(2)}) async-start(bf16[64,2,2688]{2,1,0:T(2,128)(2,1)} %copy-done.12), calls=%async_computation.1 | async-start | bytes 1376256 | tf_op jit(solution)/shard_map/all_to_all | solution.py:271
  160.5 8.9 %collective-permute-start.16 = (bf16[128,896]{1,0:T(8,128)(2,1)S(1)}, bf16[128,896]{1,0:T(8,128)(2,1)S(1)}, u32[]{:S(2)}, u32[]{:S(2)}) collective-permute-start(bf16[128,896]{1,0:T(8,128)(2,1)S(1)} %copy-done.5), channel_id=1, source_target_pairs={{0,1},{1,2},{2,3},{3,0},{4,5},{5,6},{6,7},{7,4},{8,9},{9,10},{10,1... | collective-permute-start | bytes 688136 | tf_op jit(solution)/shard_map/ppermute | solution.py:276
  161.7 7.7 %collective-permute-start.17 = (bf16[128,896]{1,0:T(8,128)(2,1)S(1)}, bf16[128,896]{1,0:T(8,128)(2,1)S(1)}, u32[]{:S(2)}, u32[]{:S(2)}) collective-permute-start(bf16[128,896]{1,0:T(8,128)(2,1)S(1)} %copy-done.5), channel_id=1, source_target_pairs={{0,3},{1,0},{2,1},{3,2},{4,7},{5,4},{6,5},{7,6},{8,11},{9,8},{10,9... | collective-permute-start | bytes 688136 | tf_op jit(solution)/shard_map/ppermute | solution.py:276
  169.5 1.5 copy-start.8
  171.0 1.5 copy-start.9
  172.5 6.4 %copy-start.23 = (bf16[128,4]{0,1:T(4,128)(2,1)S(1)}, bf16[128,4]{0,1:T(4,128)(2,1)}, u32[]{:S(2)}) copy-start(bf16[128,4]{0,1:T(4,128)(2,1)} %param.11) | copy-start | bytes 3076
  174.3 9.3 %collective-permute-start.18 = (bf16[128,896]{1,0:T(8,128)(2,1)}, bf16[128,896]{1,0:T(8,128)(2,1)S(1)}, u32[]{:S(2)}, u32[]{:S(2)}) collective-permute-start(bf16[128,896]{1,0:T(8,128)(2,1)} %get-tuple-element.34), channel_id=1, source_target_pairs={{0,1},{1,2},{2,3},{3,0},{4,5},{5,6},{6,7},{7,4},{8,9},{9,10},{10,1... | collective-permute-start | bytes 688136 | tf_op jit(solution)/shard_map/ppermute | solution.py:276
  174.6 12.2 %collective-permute-start.19 = (bf16[128,896]{1,0:T(8,128)(2,1)}, bf16[128,896]{1,0:T(8,128)(2,1)S(1)}, u32[]{:S(2)}, u32[]{:S(2)}) collective-permute-start(bf16[128,896]{1,0:T(8,128)(2,1)} %get-tuple-element.35), channel_id=1, source_target_pairs={{0,3},{1,0},{2,1},{3,2},{4,7},{5,4},{6,5},{7,6},{8,11},{9,8},{10,9... | collective-permute-start | bytes 688136 | tf_op jit(solution)/shard_map/ppermute | solution.py:276
  177.5 10.8 %collective-permute-start.20 = (bf16[128,896]{1,0:T(8,128)(2,1)S(1)}, bf16[128,896]{1,0:T(8,128)(2,1)S(1)}, u32[]{:S(2)}, u32[]{:S(2)}) collective-permute-start(bf16[128,896]{1,0:T(8,128)(2,1)S(1)} %get-tuple-element.36), channel_id=1, source_target_pairs={{0,2},{1,3},{2,0},{3,1},{4,6},{5,7},{6,4},{7,5},{8,10},{9,11},{10,... | collective-permute-start | bytes 688136 | tf_op jit(solution)/shard_map/ppermute | solution.py:276

commit v10 on v9

--- a/solution.py
+++ b/solution.py
@@ -209,24 +209,28 @@
         out_ref[s] = ref[...]
 
 
+def stack_copies_body(*refs):
+    *ins, out_ref, sems = refs
+    copies = [pltpu.make_async_copy(a, out_ref.at[s], sems.at[s]) for s, a in enumerate(ins)]
+    for c in copies:
+        c.start()
+    for c in copies:
+        c.wait()
+
+
 def down_body(halves):
-    def body(*refs):
+    def body(down_ref, *refs):
         n = len(TURNS)
-        ins, parts, out_hbm = refs[:n], refs[n : 2 * n], refs[2 * n]
-        rows_ref, down_ref, out_ref, in_sems, out_sems = refs[2 * n + 1 :]
-        copies = []
-        for s in range(n):
-            pair = (
-                pltpu.make_async_copy(ins[s], rows_ref.at[s], in_sems.at[0, s]),
-                pltpu.make_async_copy(parts[s], down_ref.at[s], in_sems.at[1, s]),
-            )
-            for c in pair:
-                c.start()
-            copies.append(pair)
+        ins, out_hbm = refs[:n], refs[n]
+        rows_ref, out_ref, in_sems, out_sems = refs[n + 1 :]
+        copies = [
+            pltpu.make_async_copy(ins[s], rows_ref.at[s], in_sems.at[s]) for s in range(n)
+        ]
+        for c in copies:
+            c.start()
         total = 0.0
         for s in range(n):
-            for c in copies[s]:
-                c.wait()
+            copies[s].wait()
             total = total + dot(rows_ref[s], down_ref[s])
         total = total.astype(BF16)
         count = out_ref.shape[0] // halves
@@ -375,19 +379,25 @@
         hidden_all = spread(hidden)
         out_shape = (experts, PAIR, size // PAIR * narrow)
         if j == 0:
+            (stacked,) = kernel_call(
+                stack_copies_body,
+                [(n, quarter, narrow)],
+                *down,
+                hbm=n,
+                scratch=[pltpu.SemaphoreType.DMA((n,))],
+            )
             scratch = [
                 pltpu.VMEM((n, count, quarter), BF16),
-                pltpu.VMEM((n, quarter, narrow), BF16),
                 pltpu.VMEM(out_shape, BF16),
-                pltpu.SemaphoreType.DMA((2, n)),
+                pltpu.SemaphoreType.DMA((n,)),
                 pltpu.SemaphoreType.DMA((2,)),
             ]
             (out,) = kernel_call(
                 down_body(2),
                 [out_shape],
+                stacked,
                 *hidden_all,
-                *down,
-                hbm=2 * n,
+                hbm=n,
                 scratch=scratch,
                 to_hbm=True,
                 flops=10**9,

time: 192 us -> 192 us (level)
  waiting for transfers between devices: 79.5 us -> 76.5 us
    ppermute x21, waiting for transfers between devices: 70.7 us -> 67.7 us  [shift(): return lax.ppermute(x, axis, [(i, (i + by) % n) for i in range(n)])]
    pallas_call x16 -> x17, Pallas kernels: 21.1 us -> 22.2 us  [kernel_call(): pl.pallas_call(body, in_specs=[pl.BlockSpec(memory_space=m) for m in plac...]
  transfers between devices with their start and end apart: 25 -> 25, of which waited for: 16 -> 15; matrix products, arithmetic and copies ran while one was open for 0% -> 0% of each run, Pallas kernels for 9% -> 10%
where the time goes in v10:
time: 192 us; the launch traced here: 191 us
  starting transfers between devices  80.3 us (42%)
  waiting for transfers between devices  76.5 us (40%)
  Pallas kernels  22.2 us (12%)
  local copies, waits for them, and re-layouts  11.8 us (6%)
    ppermute x21, waiting for transfers between devices, shift(): return lax.ppermute(x, axis, [(i, (i + by) % n) for i in range(n)])  67.7 us
    ppermute x21, starting transfers between devices, shift(): return lax.ppermute(x, axis, [(i, (i + by) % n) for i in range(n)])  41.5 us
    all_to_all x4, starting transfers between devices, exchange(): return lax.all_to_all(x, axis, split_axis=0, concat_axis=0, tiled=True)  38.8 us
    pallas_call x17, Pallas kernels, kernel_call(): pl.pallas_call(body, in_specs=[pl.BlockSpec(memory_space=m) for m in plac...  22.2 us
    unnamed x56, local copies, waits for them, and re-layouts  11.8 us
    all_to_all x4, waiting for transfers between devices, exchange(): return lax.all_to_all(x, axis, split_axis=0, concat_axis=0, tiled=True)  8.82 us
  transfers between devices with their start and end apart: 25, of which 15 were waited for; matrix products, arithmetic and copies ran while one was open for 0% of the time, Pallas kernels for 10%

profile of v10, /device:TPU:32, one launch (start us, length us, event | category | flops | bytes accessed | tf_op | source)
XLA Modules:
  0.0 191.2 jit_solution(16459048624688625316)
XLA Ops:
  0.0 2.3 %shard_map.100 = bf16[64,2,2688]{2,1,0:T(2,128)(2,1)} custom-call(s32[4,128]{1,0:T(4,128)} %bitcast.14, bf16[128,896]{1,0:T(8,128)(2,1)} %refs_0_.3), custom_call_target="tpu_custom_call" | custom-call | flops 1 | tf_op jit(solution)/shard_map/pallas_call | solution.py:43
  2.3 11.6 %all-to-all-start.2 = ((bf16[64,2,2688]{2,1,0:T(2,128)(2,1)}), bf16[64,2,2688]{2,1,0:T(2,128)(2,1)S(1)}, u32[]{:S(2)}, u32[]{:S(2)}) async-start(bf16[64,2,2688]{2,1,0:T(2,128)(2,1)} %shard_map.100), calls=%async_computation.2 | async-start | bytes 1376256 | tf_op jit(solution)/shard_map/all_to_all | solution.py:275
  13.9 3.3 %collective-permute-start = (bf16[128,896]{1,0:T(8,128)(2,1)S(1)}, bf16[128,896]{1,0:T(8,128)(2,1)S(1)}, u32[]{:S(2)}, u32[]{:S(2)}) collective-permute-start(bf16[128,896]{1,0:T(8,128)(2,1)S(1)} %copy-done.5), channel_id=1, source_target_pairs={{0,2},{1,3},{2,0},{3,1},{4,6},{5,7},{6,4},{7,5},{8,10},{9,11},{10,... | collective-permute-start | bytes 688136 | tf_op jit(solution)/shard_map/ppermute | solution.py:280
  17.2 5.9 %collective-permute-done.refs_1_.refs_3_ = bf16[128,896]{1,0:T(8,128)(2,1)S(1)} collective-permute-done((bf16[128,896]{1,0:T(8,128)(2,1)S(1)}, bf16[128,896]{1,0:T(8,128)(2,1)S(1)}, u32[]{:S(2)}, u32[]{:S(2)}) %collective-permute-start) | collective-permute-done | bytes 229408 | tf_op jit(solution)/shard_map/ppermute | solution.py:280
  23.1 1.9 shard_map.92
  25.0 0.7 copy-done.18
  25.7 8.8 %all-to-all-done.2.own_ref = bf16[64,2,2688]{2,1,0:T(2,128)(2,1)S(1)} async-done(((bf16[64,2,2688]{2,1,0:T(2,128)(2,1)}), bf16[64,2,2688]{2,1,0:T(2,128)(2,1)S(1)}, u32[]{:S(2)}, u32[]{:S(2)}) %all-to-all-start.2) | async-done | bytes 688160 | tf_op jit(solution)/shard_map/all_to_all | solution.py:275
  34.5 0.8 copy-done.3
  35.3 6.5 %all-to-all-start = ((bf16[64,2,5376]{2,1,0:T(2,128)(2,1)}), bf16[64,2,5376]{2,1,0:T(2,128)(2,1)S(1)}, u32[]{:S(2)}, u32[]{:S(2)}) async-start(bf16[64,2,5376]{2,1,0:T(2,128)(2,1)} %shard_map.92), calls=%async_computation | async-start | bytes 2752512 | tf_op jit(solution)/shard_map/all_to_all | solution.py:275
  41.8 1.7 collective-permute-start.9
  43.5 1.7 collective-permute-start.10
  45.1 1.6 copy-done.14
  46.8 0.8 copy-done.6
  47.6 0.4 collective-permute-start.6
  48.0 13.7 %collective-permute-done.9.left_ref = bf16[64,2,2688]{2,1,0:T(2,128)(2,1)} collective-permute-done((bf16[64,2,2688]{2,1,0:T(2,128)(2,1)}, bf16[64,2,2688]{2,1,0:T(2,128)(2,1)}, u32[]{:S(2)}, u32[]{:S(2)}) %collective-permute-start.9) | collective-permute-done | bytes 688160 | tf_op jit(solution)/shard_map/ppermute | solution.py:280
  61.7 1.4 shard_map.102
  63.1 0.9 collective-permute-start.11
  64.0 2.4 %collective-permute-start.12 = (bf16[32,2,2688]{2,1,0:T(2,128)(2,1)S(1)}, bf16[32,2,2688]{2,1,0:T(2,128)(2,1)S(1)}, u32[]{:S(2)}, u32[]{:S(2)}) collective-permute-start(bf16[32,2,2688]{2,1,0:T(2,128)(2,1)S(1)} %get-tuple-element.31), channel_id=1, source_target_pairs={{0,3},{1,0},{2,1},{3,2},{4,7},{5,4},{6,5},{7,6},{8,11},{9,8},{10,9... | collective-permute-start | bytes 1032200 | tf_op jit(solution)/shard_map/ppermute | solution.py:280
  66.4 1.0 collective-permute-start.7
  67.4 0.6 collective-permute-start.8
  68.1 1.5 copy-done.1
  69.6 2.8 %shard_map.101 = (f32[384,512]{1,0:T(8,128)S(1)}, bf16[2,896,256]{2,1,0:T(8,128)(2,1)S(1)}) custom-call(s32[1]{0:T(128)} %bitcast.q_ref, bf16[64,2,2688]{2,1,0:T(2,128)(2,1)S(1)} %copy-done.4, bf16[64,2,2688]{2,1,0:T(2,128)(2,1)} %collective-permute-done.9.left_ref, bf16[64,2,2688]{2,1,0:T(2,128)(2,1)} %collective-permute-done.10.right_ref, ...), custom_call_target="tpu_custom_call" | custom-call | flops 1000000000 | tf_op jit(solution)/shard_map/pallas_call | solution.py:43
  72.4 5.6 %collective-permute-done.11.o0_ref = bf16[32,2,2688]{2,1,0:T(2,128)(2,1)S(1)} collective-permute-done((bf16[32,2,2688]{2,1,0:T(2,128)(2,1)S(1)}, bf16[32,2,2688]{2,1,0:T(2,128)(2,1)S(1)}, u32[]{:S(2)}, u32[]{:S(2)}) %collective-permute-start.11) | collective-permute-done | bytes 344096 | tf_op jit(solution)/shard_map/ppermute | solution.py:280
  78.0 0.6 shard_map.103.refs_0_
  78.7 1.2 collective-permute-start.13
  79.9 2.1 %collective-permute-start.14 = (bf16[384,256]{1,0:T(8,128)(2,1)S(1)}, bf16[384,256]{1,0:T(8,128)(2,1)S(1)}, u32[]{:S(2)}, u32[]{:S(2)}) collective-permute-start(bf16[384,256]{1,0:T(8,128)(2,1)S(1)} %shard_map.103.refs_0_), channel_id=1, source_target_pairs={{0,3},{1,0},{2,1},{3,2},{4,7},{5,4},{6,5},{7,6},{8,11},{9,8},{10,9... | collective-permute-start | bytes 589832 | tf_op jit(solution)/shard_map/ppermute | solution.py:280
  82.0 9.8 %collective-permute-start.15 = (bf16[384,256]{1,0:T(8,128)(2,1)S(1)}, bf16[384,256]{1,0:T(8,128)(2,1)S(1)}, u32[]{:S(2)}, u32[]{:S(2)}) collective-permute-start(bf16[384,256]{1,0:T(8,128)(2,1)S(1)} %shard_map.103.refs_0_), channel_id=1, source_target_pairs={{0,2},{1,3},{2,0},{3,1},{4,6},{5,7},{6,4},{7,5},{8,10},{9,11},{10,... | collective-permute-start | bytes 589832 | tf_op jit(solution)/shard_map/ppermute | solution.py:280
  91.8 1.3 collective-permute-done.7.refs_2_
  93.1 0.8 copy-done.10
  93.9 0.2 copy-done.12
  94.1 1.5 shard_map.99.down_ref
  95.6 4.7 %collective-permute-done.14.refs_2_ = bf16[384,256]{1,0:T(8,128)(2,1)S(1)} collective-permute-done((bf16[384,256]{1,0:T(8,128)(2,1)S(1)}, bf16[384,256]{1,0:T(8,128)(2,1)S(1)}, u32[]{:S(2)}, u32[]{:S(2)}) %collective-permute-start.14) | collective-permute-done | bytes 196640 | tf_op jit(solution)/shard_map/ppermute | solution.py:280
  100.3 0.7 copy-done.25
  100.9 0.7 copy-done.26
  101.6 3.0 %shard_map.104 = bf16[64,2,2688]{2,1,0:T(2,128)(2,1)} custom-call(bf16[4,256,896]{2,1,0:T(8,128)(2,1)S(1)} %shard_map.99.down_ref, bf16[384,256]{1,0:T(8,128)(2,1)} %copy-done.22, bf16[384,256]{1,0:T(8,128)(2,1)} %copy-done.24, bf16[384,256]{1,0:T(8,128)(2,1)} %copy-done.25, bf16[384,256]{1,0:T(8,128)(2,1)} %copy-done.26), custom_call_target="tpu_custom_call" | custom-call | flops 1000000000 | tf_op jit(solution)/shard_map/pallas_call | solution.py:43
  104.6 10.5 %all-to-all-start.3 = ((bf16[64,2,2688]{2,1,0:T(2,128)(2,1)}), bf16[64,2,2688]{2,1,0:T(2,128)(2,1)}, u32[]{:S(2)}, u32[]{:S(2)}) async-start(bf16[64,2,2688]{2,1,0:T(2,128)(2,1)} %shard_map.104), calls=%async_computation.3 | async-start | bytes 1376256 | tf_op jit(solution)/shard_map/all_to_all | solution.py:275
  115.2 2.4 %collective-permute-start.1 = (bf16[64,2,2688]{2,1,0:T(2,128)(2,1)S(1)}, bf16[64,2,2688]{2,1,0:T(2,128)(2,1)S(1)}, u32[]{:S(2)}, u32[]{:S(2)}) collective-permute-start(bf16[64,2,2688]{2,1,0:T(2,128)(2,1)S(1)} %shard_map.94), channel_id=1, source_target_pairs={{0,1},{1,2},{2,3},{3,0},{4,5},{5,6},{6,7},{7,4},{8,9},{9,10},{10,1... | collective-permute-start | bytes 2064392 | tf_op jit(solution)/shard_map/ppermute | solution.py:280
  117.6 1.5 collective-permute-start.2
  119.0 1.1 shard_map.93
  120.2 14.5 %collective-permute-done.1.left_ref = bf16[64,2,2688]{2,1,0:T(2,128)(2,1)S(1)} collective-permute-done((bf16[64,2,2688]{2,1,0:T(2,128)(2,1)S(1)}, bf16[64,2,2688]{2,1,0:T(2,128)(2,1)S(1)}, u32[]{:S(2)}, u32[]{:S(2)}) %collective-permute-start.1) | collective-permute-done | bytes 688160 | tf_op jit(solution)/shard_map/ppermute | solution.py:280
  134.8 1.1 shard_map.95.refs_0_
  135.8 1.1 collective-permute-start.3
  137.0 2.2 %collective-permute-start.4 = (bf16[384,256]{1,0:T(8,128)(2,1)S(1)}, bf16[384,256]{1,0:T(8,128)(2,1)S(1)}, u32[]{:S(2)}, u32[]{:S(2)}) collective-permute-start(bf16[384,256]{1,0:T(8,128)(2,1)S(1)} %shard_map.95.refs_0_), channel_id=1, source_target_pairs={{0,3},{1,0},{2,1},{3,2},{4,7},{5,4},{6,5},{7,6},{8,11},{9,8},{10,9... | collective-permute-start | bytes 589832 | tf_op jit(solution)/shard_map/ppermute | solution.py:280
  139.2 1.6 collective-permute-start.5
  141.0 3.2 %collective-permute-done.3.refs_1_ = bf16[384,256]{1,0:T(8,128)(2,1)S(1)} collective-permute-done((bf16[384,256]{1,0:T(8,128)(2,1)S(1)}, bf16[384,256]{1,0:T(8,128)(2,1)S(1)}, u32[]{:S(2)}, u32[]{:S(2)}) %collective-permute-start.3) | collective-permute-done | bytes 196640 | tf_op jit(solution)/shard_map/ppermute | solution.py:280
  144.1 2.9 %collective-permute-done.4.refs_2_ = bf16[384,256]{1,0:T(8,128)(2,1)S(1)} collective-permute-done((bf16[384,256]{1,0:T(8,128)(2,1)S(1)}, bf16[384,256]{1,0:T(8,128)(2,1)S(1)}, u32[]{:S(2)}, u32[]{:S(2)}) %collective-permute-start.4) | collective-permute-done | bytes 196640 | tf_op jit(solution)/shard_map/ppermute | solution.py:280
  147.0 1.7 collective-permute-done.5.refs_3_
  148.7 1.0 shard_map.98
  149.7 0.9 copy-done.20
  150.6 10.2 %all-to-all-start.1 = ((bf16[64,2,2688]{2,1,0:T(2,128)(2,1)}), bf16[64,2,2688]{2,1,0:T(2,128)(2,1)S(1)}, u32[]{:S(2)}, u32[]{:S(2)}) async-start(bf16[64,2,2688]{2,1,0:T(2,128)(2,1)} %copy-done.20), calls=%async_computation.1 | async-start | bytes 1376256 | tf_op jit(solution)/shard_map/all_to_all | solution.py:275
  160.8 1.2 collective-permute-start.16
  162.0 2.1 %collective-permute-start.17 = (bf16[128,896]{1,0:T(8,128)(2,1)S(1)}, bf16[128,896]{1,0:T(8,128)(2,1)S(1)}, u32[]{:S(2)}, u32[]{:S(2)}) collective-permute-start(bf16[128,896]{1,0:T(8,128)(2,1)S(1)} %copy-done.5), channel_id=1, source_target_pairs={{0,3},{1,0},{2,1},{3,2},{4,7},{5,4},{6,5},{7,6},{8,11},{9,8},{10,9... | collective-permute-start | bytes 688136 | tf_op jit(solution)/shard_map/ppermute | solution.py:280
  164.1 5.6 %collective-permute-done.16.refs_1_ = bf16[128,896]{1,0:T(8,128)(2,1)S(1)} collective-permute-done((bf16[128,896]{1,0:T(8,128)(2,1)S(1)}, bf16[128,896]{1,0:T(8,128)(2,1)S(1)}, u32[]{:S(2)}, u32[]{:S(2)}) %collective-permute-start.16) | collective-permute-done | bytes 229408 | tf_op jit(solution)/shard_map/ppermute | solution.py:280
  169.7 1.5 copy-done.16
  171.2 1.5 copy-done.17
  172.7 1.8 shard_map.105
  174.7 3.1 %collective-permute-start.19 = (bf16[128,896]{1,0:T(8,128)(2,1)}, bf16[128,896]{1,0:T(8,128)(2,1)S(1)}, u32[]{:S(2)}, u32[]{:S(2)}) collective-permute-start(bf16[128,896]{1,0:T(8,128)(2,1)} %get-tuple-element.35), channel_id=1, source_target_pairs={{0,3},{1,0},{2,1},{3,2},{4,7},{5,4},{6,5},{7,6},{8,11},{9,8},{10,9... | collective-permute-start | bytes 688136 | tf_op jit(solution)/shard_map/ppermute | solution.py:280
  177.8 1.2 collective-permute-start.20
  179.2 0.9 shard_map.91
  180.1 3.7 %collective-permute-done.18.refs_1_ = bf16[128,896]{1,0:T(8,128)(2,1)S(1)} collective-permute-done((bf16[128,896]{1,0:T(8,128)(2,1)}, bf16[128,896]{1,0:T(8,128)(2,1)S(1)}, u32[]{:S(2)}, u32[]{:S(2)}) %collective-permute-start.18) | collective-permute-done | bytes 229408 | tf_op jit(solution)/shard_map/ppermute | solution.py:280
  183.9 3.2 %collective-permute-done.19.refs_2_ = bf16[128,896]{1,0:T(8,128)(2,1)S(1)} collective-permute-done((bf16[128,896]{1,0:T(8,128)(2,1)}, bf16[128,896]{1,0:T(8,128)(2,1)S(1)}, u32[]{:S(2)}, u32[]{:S(2)}) %collective-permute-start.19) | collective-permute-done | bytes 229408 | tf_op jit(solution)/shard_map/ppermute | solution.py:280
  187.0 1.5 collective-permute-done.20.refs_3_
  188.6 1.5 shard_map.106.refs_0_
  190.1 1.1 shard_map.107
  (59 shorter events, 1.0 us)
Async XLA Ops:
  0.0 23.1 %copy-start.21 = (s32[128,4]{0,1:T(4,128)S(1)}, s32[128,4]{0,1:T(4,128)}, u32[]{:S(2)}) copy-start(s32[128,4]{0,1:T(4,128)} %param.10) | copy-start | bytes 6148
  0.0 13.9 %copy-start.5 = (bf16[128,896]{1,0:T(8,128)(2,1)S(1)}, bf16[128,896]{1,0:T(8,128)(2,1)}, u32[]{:S(2)}) copy-start(bf16[128,896]{1,0:T(8,128)(2,1)} %refs_0_.3) | copy-start | bytes 688132
  2.3 32.2 %all-to-all-start.2 = ((bf16[64,2,2688]{2,1,0:T(2,128)(2,1)}), bf16[64,2,2688]{2,1,0:T(2,128)(2,1)S(1)}, u32[]{:S(2)}, u32[]{:S(2)}) async-start(bf16[64,2,2688]{2,1,0:T(2,128)(2,1)} %shard_map.100), calls=%async_computation.2 | async-start | bytes 1376256 | tf_op jit(solution)/shard_map/all_to_all | solution.py:275
  13.9 9.2 %collective-permute-start = (bf16[128,896]{1,0:T(8,128)(2,1)S(1)}, bf16[128,896]{1,0:T(8,128)(2,1)S(1)}, u32[]{:S(2)}, u32[]{:S(2)}) collective-permute-start(bf16[128,896]{1,0:T(8,128)(2,1)S(1)} %copy-done.5), channel_id=1, source_target_pairs={{0,2},{1,3},{2,0},{3,1},{4,6},{5,7},{6,4},{7,5},{8,10},{9,11},{10,... | collective-permute-start | bytes 688136 | tf_op jit(solution)/shard_map/ppermute | solution.py:280
  25.0 0.7 copy-start.18
  34.5 0.9 copy-start.3
  35.3 69.3 %all-to-all-start = ((bf16[64,2,5376]{2,1,0:T(2,128)(2,1)}), bf16[64,2,5376]{2,1,0:T(2,128)(2,1)S(1)}, u32[]{:S(2)}, u32[]{:S(2)}) async-start(bf16[64,2,5376]{2,1,0:T(2,128)(2,1)} %shard_map.92), calls=%async_computation | async-start | bytes 2752512 | tf_op jit(solution)/shard_map/all_to_all | solution.py:275
  41.8 26.3 %copy-start = (bf16[1,3584,256]{2,1,0:T(8,128)(2,1)S(1)}, bf16[1,3584,256]{2,1,0:T(8,128)(2,1)}, u32[]{:S(2)}) copy-start(bf16[1,3584,256]{2,1,0:T(8,128)(2,1)} %param.12) | copy-start | bytes 5505028
  41.8 19.9 %collective-permute-start.9 = (bf16[64,2,2688]{2,1,0:T(2,128)(2,1)}, bf16[64,2,2688]{2,1,0:T(2,128)(2,1)}, u32[]{:S(2)}, u32[]{:S(2)}) collective-permute-start(bf16[64,2,2688]{2,1,0:T(2,128)(2,1)} %copy-done.3), channel_id=1, source_target_pairs={{0,1},{1,2},{2,3},{3,0},{4,5},{5,6},{6,7},{7,4},{8,9},{9,10},{10,1... | collective-permute-start | bytes 2064392 | tf_op jit(solution)/shard_map/ppermute | solution.py:280
  43.5 18.3 %collective-permute-start.10 = (bf16[64,2,2688]{2,1,0:T(2,128)(2,1)}, bf16[64,2,2688]{2,1,0:T(2,128)(2,1)}, u32[]{:S(2)}, u32[]{:S(2)}) collective-permute-start(bf16[64,2,2688]{2,1,0:T(2,128)(2,1)} %copy-done.3), channel_id=1, source_target_pairs={{0,3},{1,0},{2,1},{3,2},{4,7},{5,4},{6,5},{7,6},{8,11},{9,8},{10,9... | collective-permute-start | bytes 2064392 | tf_op jit(solution)/shard_map/ppermute | solution.py:280
  45.1 22.9 %copy-start.4 = (bf16[64,2,2688]{2,1,0:T(2,128)(2,1)S(1)}, bf16[64,2,2688]{2,1,0:T(2,128)(2,1)}, u32[]{:S(2)}) copy-start(bf16[64,2,2688]{2,1,0:T(2,128)(2,1)} %copy-done.3) | copy-start | bytes 2064388
  45.1 1.6 copy-start.14
  46.8 0.8 copy-start.6
  47.6 34.4 %collective-permute-start.6 = (bf16[256,896]{1,0:T(8,128)(2,1)S(1)}, bf16[256,896]{1,0:T(8,128)(2,1)S(1)}, u32[]{:S(2)}, u32[]{:S(2)}) collective-permute-start(bf16[256,896]{1,0:T(8,128)(2,1)S(1)} %get-tuple-element.25), channel_id=1, source_target_pairs={{0,1},{1,2},{2,3},{3,0},{4,5},{5,6},{6,7},{7,4},{8,9},{9,10},{10,1... | collective-permute-start | bytes 1376264 | tf_op jit(solution)/shard_map/ppermute | solution.py:280
  63.1 14.9 %collective-permute-start.11 = (bf16[32,2,2688]{2,1,0:T(2,128)(2,1)S(1)}, bf16[32,2,2688]{2,1,0:T(2,128)(2,1)S(1)}, u32[]{:S(2)}, u32[]{:S(2)}) collective-permute-start(bf16[32,2,2688]{2,1,0:T(2,128)(2,1)S(1)} %get-tuple-element.30), channel_id=1, source_target_pairs={{0,1},{1,2},{2,3},{3,0},{4,5},{5,6},{6,7},{7,4},{8,9},{9,10},{10,1... | collective-permute-start | bytes 1032200 | tf_op jit(solution)/shard_map/ppermute | solution.py:280
  64.0 14.1 %collective-permute-start.12 = (bf16[32,2,2688]{2,1,0:T(2,128)(2,1)S(1)}, bf16[32,2,2688]{2,1,0:T(2,128)(2,1)S(1)}, u32[]{:S(2)}, u32[]{:S(2)}) collective-permute-start(bf16[32,2,2688]{2,1,0:T(2,128)(2,1)S(1)} %get-tuple-element.31), channel_id=1, source_target_pairs={{0,3},{1,0},{2,1},{3,2},{4,7},{5,4},{6,5},{7,6},{8,11},{9,8},{10,9... | collective-permute-start | bytes 1032200 | tf_op jit(solution)/shard_map/ppermute | solution.py:280
  66.4 26.7 %collective-permute-start.7 = (bf16[256,896]{1,0:T(8,128)(2,1)S(1)}, bf16[256,896]{1,0:T(8,128)(2,1)S(1)}, u32[]{:S(2)}, u32[]{:S(2)}) collective-permute-start(bf16[256,896]{1,0:T(8,128)(2,1)S(1)} %get-tuple-element.26), channel_id=1, source_target_pairs={{0,3},{1,0},{2,1},{3,2},{4,7},{5,4},{6,5},{7,6},{8,11},{9,8},{10,9... | collective-permute-start | bytes 1376264 | tf_op jit(solution)/shard_map/ppermute | solution.py:280
  67.4 25.7 %collective-permute-start.8 = (bf16[256,896]{1,0:T(8,128)(2,1)S(1)}, bf16[256,896]{1,0:T(8,128)(2,1)S(1)}, u32[]{:S(2)}, u32[]{:S(2)}) collective-permute-start(bf16[256,896]{1,0:T(8,128)(2,1)S(1)} %get-tuple-element.27), channel_id=1, source_target_pairs={{0,2},{1,3},{2,0},{3,1},{4,6},{5,7},{6,4},{7,5},{8,10},{9,11},{10,... | collective-permute-start | bytes 1376264 | tf_op jit(solution)/shard_map/ppermute | solution.py:280
  68.1 1.5 copy-start.1
  78.7 21.6 %copy-start.22 = (bf16[384,256]{1,0:T(8,128)(2,1)}, bf16[384,256]{1,0:T(8,128)(2,1)S(1)}, u32[]{:S(2)}) copy-start(bf16[384,256]{1,0:T(8,128)(2,1)S(1)} %shard_map.103.refs_0_) | copy-start | bytes 589828
  78.7 16.8 %collective-permute-start.13 = (bf16[384,256]{1,0:T(8,128)(2,1)S(1)}, bf16[384,256]{1,0:T(8,128)(2,1)S(1)}, u32[]{:S(2)}, u32[]{:S(2)}) collective-permute-start(bf16[384,256]{1,0:T(8,128)(2,1)S(1)} %shard_map.103.refs_0_), channel_id=1, source_target_pairs={{0,1},{1,2},{2,3},{3,0},{4,5},{5,6},{6,7},{7,4},{8,9},{9,10},{10,1... | collective-permute-start | bytes 589832 | tf_op jit(solution)/shard_map/ppermute | solution.py:280
  79.9 20.3 %collective-permute-start.14 = (bf16[384,256]{1,0:T(8,128)(2,1)S(1)}, bf16[384,256]{1,0:T(8,128)(2,1)S(1)}, u32[]{:S(2)}, u32[]{:S(2)}) collective-permute-start(bf16[384,256]{1,0:T(8,128)(2,1)S(1)} %shard_map.103.refs_0_), channel_id=1, source_target_pairs={{0,3},{1,0},{2,1},{3,2},{4,7},{5,4},{6,5},{7,6},{8,11},{9,8},{10,9... | collective-permute-start | bytes 589832 | tf_op jit(solution)/shard_map/ppermute | solution.py:280
  82.0 11.1 %copy-start.8 = (bf16[256,896]{1,0:T(8,128)(2,1)}, bf16[256,896]{1,0:T(8,128)(2,1)S(1)}, u32[]{:S(2)}) copy-start(bf16[256,896]{1,0:T(8,128)(2,1)S(1)} %collective-permute-done.6.refs_1_) | copy-start | bytes 1376260
  82.0 18.3 %collective-permute-start.15 = (bf16[384,256]{1,0:T(8,128)(2,1)S(1)}, bf16[384,256]{1,0:T(8,128)(2,1)S(1)}, u32[]{:S(2)}, u32[]{:S(2)}) collective-permute-start(bf16[384,256]{1,0:T(8,128)(2,1)S(1)} %shard_map.103.refs_0_), channel_id=1, source_target_pairs={{0,2},{1,3},{2,0},{3,1},{4,6},{5,7},{6,4},{7,5},{8,10},{9,11},{10,... | collective-permute-start | bytes 589832 | tf_op jit(solution)/shard_map/ppermute | solution.py:280
  93.1 0.8 copy-start.10
  93.1 0.9 copy-start.12
  95.5 4.7 %copy-start.24 = (bf16[384,256]{1,0:T(8,128)(2,1)}, bf16[384,256]{1,0:T(8,128)(2,1)S(1)}, u32[]{:S(2)}) copy-start(bf16[384,256]{1,0:T(8,128)(2,1)S(1)} %collective-permute-done.13.refs_1_) | copy-start | bytes 589828
  100.3 0.7 copy-start.25
  100.9 0.7 copy-start.26
  104.6 45.9 %all-to-all-start.3 = ((bf16[64,2,2688]{2,1,0:T(2,128)(2,1)}), bf16[64,2,2688]{2,1,0:T(2,128)(2,1)}, u32[]{:S(2)}, u32[]{:S(2)}) async-start(bf16[64,2,2688]{2,1,0:T(2,128)(2,1)} %shard_map.104), calls=%async_computation.3 | async-start | bytes 1376256 | tf_op jit(solution)/shard_map/all_to_all | solution.py:275
  115.1 3.9 %copy-start.2 = (bf16[1,3584,256]{2,1,0:T(8,128)(2,1)S(1)}, bf16[1,3584,256]{2,1,0:T(8,128)(2,1)}, u32[]{:S(2)}) copy-start(bf16[1,3584,256]{2,1,0:T(8,128)(2,1)} %param.13) | copy-start | bytes 5505028
  115.2 19.5 %collective-permute-start.1 = (bf16[64,2,2688]{2,1,0:T(2,128)(2,1)S(1)}, bf16[64,2,2688]{2,1,0:T(2,128)(2,1)S(1)}, u32[]{:S(2)}, u32[]{:S(2)}) collective-permute-start(bf16[64,2,2688]{2,1,0:T(2,128)(2,1)S(1)} %shard_map.94), channel_id=1, source_target_pairs={{0,1},{1,2},{2,3},{3,0},{4,5},{5,6},{6,7},{7,4},{8,9},{9,10},{10,1... | collective-permute-start | bytes 2064392 | tf_op jit(solution)/shard_map/ppermute | solution.py:280
  117.6 17.2 %collective-permute-start.2 = (bf16[64,2,2688]{2,1,0:T(2,128)(2,1)S(1)}, bf16[64,2,2688]{2,1,0:T(2,128)(2,1)S(1)}, u32[]{:S(2)}, u32[]{:S(2)}) collective-permute-start(bf16[64,2,2688]{2,1,0:T(2,128)(2,1)S(1)} %shard_map.94), channel_id=1, source_target_pairs={{0,3},{1,0},{2,1},{3,2},{4,7},{5,4},{6,5},{7,6},{8,11},{9,8},{10,9... | collective-permute-start | bytes 2064392 | tf_op jit(solution)/shard_map/ppermute | solution.py:280
  134.8 6.0 %copy-start.7 = (bf16[256,896]{1,0:T(8,128)(2,1)S(1)}, bf16[256,896]{1,0:T(8,128)(2,1)}, u32[]{:S(2)}) copy-start(bf16[256,896]{1,0:T(8,128)(2,1)} %copy-done.6) | copy-start | bytes 1376260
  134.8 6.0 %copy-start.9 = (bf16[256,896]{1,0:T(8,128)(2,1)S(1)}, bf16[256,896]{1,0:T(8,128)(2,1)}, u32[]{:S(2)}) copy-start(bf16[256,896]{1,0:T(8,128)(2,1)} %copy-done.8) | copy-start | bytes 1376260
  134.8 6.0 %copy-start.11 = (bf16[256,896]{1,0:T(8,128)(2,1)S(1)}, bf16[256,896]{1,0:T(8,128)(2,1)}, u32[]{:S(2)}) copy-start(bf16[256,896]{1,0:T(8,128)(2,1)} %copy-done.10) | copy-start | bytes 1376260
  134.8 6.0 %copy-start.13 = (bf16[256,896]{1,0:T(8,128)(2,1)S(1)}, bf16[256,896]{1,0:T(8,128)(2,1)}, u32[]{:S(2)}) copy-start(bf16[256,896]{1,0:T(8,128)(2,1)} %copy-done.12) | copy-start | bytes 1376260
  135.8 8.3 %collective-permute-start.3 = (bf16[384,256]{1,0:T(8,128)(2,1)S(1)}, bf16[384,256]{1,0:T(8,128)(2,1)S(1)}, u32[]{:S(2)}, u32[]{:S(2)}) collective-permute-start(bf16[384,256]{1,0:T(8,128)(2,1)S(1)} %shard_map.95.refs_0_), channel_id=1, source_target_pairs={{0,1},{1,2},{2,3},{3,0},{4,5},{5,6},{6,7},{7,4},{8,9},{9,10},{10,1... | collective-permute-start | bytes 589832 | tf_op jit(solution)/shard_map/ppermute | solution.py:280
  137.0 10.1 %collective-permute-start.4 = (bf16[384,256]{1,0:T(8,128)(2,1)S(1)}, bf16[384,256]{1,0:T(8,128)(2,1)S(1)}, u32[]{:S(2)}, u32[]{:S(2)}) collective-permute-start(bf16[384,256]{1,0:T(8,128)(2,1)S(1)} %shard_map.95.refs_0_), channel_id=1, source_target_pairs={{0,3},{1,0},{2,1},{3,2},{4,7},{5,4},{6,5},{7,6},{8,11},{9,8},{10,9... | collective-permute-start | bytes 589832 | tf_op jit(solution)/shard_map/ppermute | solution.py:280
  139.2 9.5 %collective-permute-start.5 = (bf16[384,256]{1,0:T(8,128)(2,1)S(1)}, bf16[384,256]{1,0:T(8,128)(2,1)S(1)}, u32[]{:S(2)}, u32[]{:S(2)}) collective-permute-start(bf16[384,256]{1,0:T(8,128)(2,1)S(1)} %shard_map.95.refs_0_), channel_id=1, source_target_pairs={{0,2},{1,3},{2,0},{3,1},{4,6},{5,7},{6,4},{7,5},{8,10},{9,11},{10,... | collective-permute-start | bytes 589832 | tf_op jit(solution)/shard_map/ppermute | solution.py:280
  140.9 28.8 %copy-start.15 = (bf16[3584,256]{1,0:T(8,128)(2,1)S(1)}, bf16[3584,256]{1,0:T(8,128)(2,1)}, u32[]{:S(2)}) copy-start(bf16[3584,256]{1,0:T(8,128)(2,1)} %param.15) | copy-start | bytes 5505028
  141.0 28.8 %copy-start.19 = (bf16[128,896]{1,0:T(8,128)(2,1)S(1)}, bf16[128,896]{1,0:T(8,128)(2,1)}, u32[]{:S(2)}) copy-start(bf16[128,896]{1,0:T(8,128)(2,1)} %copy-done.18) | copy-start | bytes 688132
  149.7 0.9 copy-start.20
  150.6 39.5 %all-to-all-start.1 = ((bf16[64,2,2688]{2,1,0:T(2,128)(2,1)}), bf16[64,2,2688]{2,1,0:T(2,128)(2,1)S(1)}, u32[]{:S(2)}, u32[]{:S(2)}) async-start(bf16[64,2,2688]{2,1,0:T(2,128)(2,1)} %copy-done.20), calls=%async_computation.1 | async-start | bytes 1376256 | tf_op jit(solution)/shard_map/all_to_all | solution.py:275
  160.8 8.9 %collective-permute-start.16 = (bf16[128,896]{1,0:T(8,128)(2,1)S(1)}, bf16[128,896]{1,0:T(8,128)(2,1)S(1)}, u32[]{:S(2)}, u32[]{:S(2)}) collective-permute-start(bf16[128,896]{1,0:T(8,128)(2,1)S(1)} %copy-done.5), channel_id=1, source_target_pairs={{0,1},{1,2},{2,3},{3,0},{4,5},{5,6},{6,7},{7,4},{8,9},{9,10},{10,1... | collective-permute-start | bytes 688136 | tf_op jit(solution)/shard_map/ppermute | solution.py:280
  162.0 7.7 %collective-permute-start.17 = (bf16[128,896]{1,0:T(8,128)(2,1)S(1)}, bf16[128,896]{1,0:T(8,128)(2,1)S(1)}, u32[]{:S(2)}, u32[]{:S(2)}) collective-permute-start(bf16[128,896]{1,0:T(8,128)(2,1)S(1)} %copy-done.5), channel_id=1, source_target_pairs={{0,3},{1,0},{2,1},{3,2},{4,7},{5,4},{6,5},{7,6},{8,11},{9,8},{10,9... | collective-permute-start | bytes 688136 | tf_op jit(solution)/shard_map/ppermute | solution.py:280
  169.7 1.5 copy-start.16
  171.2 1.5 copy-start.17
  172.7 6.4 %copy-start.23 = (bf16[128,4]{0,1:T(4,128)(2,1)S(1)}, bf16[128,4]{0,1:T(4,128)(2,1)}, u32[]{:S(2)}) copy-start(bf16[128,4]{0,1:T(4,128)(2,1)} %param.11) | copy-start | bytes 3076
  174.6 9.3 %collective-permute-start.18 = (bf16[128,896]{1,0:T(8,128)(2,1)}, bf16[128,896]{1,0:T(8,128)(2,1)S(1)}, u32[]{:S(2)}, u32[]{:S(2)}) collective-permute-start(bf16[128,896]{1,0:T(8,128)(2,1)} %get-tuple-element.34), channel_id=1, source_target_pairs={{0,1},{1,2},{2,3},{3,0},{4,5},{5,6},{6,7},{7,4},{8,9},{9,10},{10,1... | collective-permute-start | bytes 688136 | tf_op jit(solution)/shard_map/ppermute | solution.py:280
  174.7 12.3 %collective-permute-start.19 = (bf16[128,896]{1,0:T(8,128)(2,1)}, bf16[128,896]{1,0:T(8,128)(2,1)S(1)}, u32[]{:S(2)}, u32[]{:S(2)}) collective-permute-start(bf16[128,896]{1,0:T(8,128)(2,1)} %get-tuple-element.35), channel_id=1, source_target_pairs={{0,3},{1,0},{2,1},{3,2},{4,7},{5,4},{6,5},{7,6},{8,11},{9,8},{10,9... | collective-permute-start | bytes 688136 | tf_op jit(solution)/shard_map/ppermute | solution.py:280
  177.8 10.8 %collective-permute-start.20 = (bf16[128,896]{1,0:T(8,128)(2,1)S(1)}, bf16[128,896]{1,0:T(8,128)(2,1)S(1)}, u32[]{:S(2)}, u32[]{:S(2)}) collective-permute-start(bf16[128,896]{1,0:T(8,128)(2,1)S(1)} %get-tuple-element.36), channel_id=1, source_target_pairs={{0,2},{1,3},{2,0},{3,1},{4,6},{5,7},{6,4},{7,5},{8,10},{9,11},{10,... | collective-permute-start | bytes 688136 | tf_op jit(solution)/shard_map/ppermute | solution.py:280
